TPU v7x, 128 devices: a whole 4x4x4 slice. The times are simulated.
128 devices in a mesh: ep: 32 (over y, x, core), tp: 4 (over z).
Axes of the slice: x: 4, y: 4, z: 4, core: 2. Of those that a mesh axis runs over, the one named last changes fastest.
Arguments:
- tokens: bfloat16 [8192, 7168], P('ep', 'tp'), may hold values from -78 to 78
- norm_gain: bfloat16 [7168], P('tp'), may hold values from 0.5 to 1.5
- expert_ids: int32 [8192, 8], P('ep'), may hold values from 0 to 255, all different within a row
- gate_prob: bfloat16 [8192, 8], P('ep'), may hold values from 0.049804688 to 1
- w_gate: bfloat16 [32, 7168, 2048], P('ep', None, 'tp'), may hold values from -0.0625 to 0.0625
- w_up: bfloat16 [32, 7168, 2048], P('ep', None, 'tp'), may hold values from -0.0625 to 0.0625
- w_down: bfloat16 [32, 2048, 7168], P('ep', 'tp'), may hold values from -0.125 to 0.125
Outputs:
- combined: bfloat16 [8192, 7168], P('ep', 'tp')
Inputs may be any that keep to these rules, and one draw needn't show every extreme that they name: `expert_ids`: each row names 8 different experts.
All inputs are finite; a program needn't handle non-finite values.
Results may differ from a plain program's by a relative error of at most 0.01.
Values may be sent and summed in bfloat16 or wider, within the bound.
No kernel may reach another device: no remote copies, remote signals or barrier semaphores. Data moves between devices by JAX's collectives and lax.ppermute only.
A program may use at most 128 MiB of HBM per device.

v0:
```python
import jax
import jax.numpy as jnp
from jax import lax
from jax.experimental import pallas as pl
from jax.experimental.pallas import tpu as pltpu
from jax.sharding import PartitionSpec as P


D = 7168
epsilon = 1e-06
CAP = 16
EARLY = 640
SIDE = 128
F32, BF16 = jnp.float32, jnp.bfloat16


class Copies:
    def __init__(self, sems):
        self.sems, self.used = sems, 0

    def start(self, src, dst):
        copy = pltpu.make_async_copy(src, dst, self.sems.at[self.used])
        self.used += 1
        copy.start()
        return copy


def expert_call(where, xs, segs, w_gate, w_up, carry, inv, hidden, w_down, jobs, outs):
    slices = lax.axis_size("tp")
    d_all, ff = (w_down.shape[1], w_down.shape[0]) if w_gate is None else w_gate.shape
    span = d_all // slices
    rows = (hidden if hidden is not None else carry[0] if carry is not None else xs[0]).shape[0]
    finish = bool(segs) and bool(jobs)
    if not jobs:
        out_shapes = [jax.ShapeDtypeStruct((rows, ff), F32)] * 2
    else:
        out_shapes = [jax.ShapeDtypeStruct(s, BF16) for s in outs]
        if finish:
            out_shapes = [jax.ShapeDtypeStruct((rows, ff), BF16)] + out_shapes
    args = list(xs)
    if segs:
        args += [w_gate, w_up]
    if carry is not None:
        args += list(carry)
    if inv is not None:
        args += [inv]
    if hidden is not None:
        args += [hidden]
    if jobs:
        args += [w_down]
    scratch = []
    for _, _, _, width, _ in segs:
        scratch += [pltpu.VMEM((rows, width), BF16), pltpu.VMEM((width, ff), BF16), pltpu.VMEM((width, ff), BF16)]
    if segs:
        scratch += [pltpu.VMEM((rows, ff), F32)] * 2
    if inv is not None:
        scratch += [pltpu.VMEM((rows, SIDE), BF16)]
    if jobs:
        scratch += [pltpu.VMEM((rows, ff), BF16)]
    for _, _, width, _ in jobs:
        scratch += [pltpu.VMEM((ff, width), BF16), pltpu.VMEM((rows, width), BF16)]
    n_sems = sum(len(s[0]) + 2 for s in segs) + 2 + 1 + 2 + sum(1 + len(j[3]) for j in jobs)
    scratch += [pltpu.SemaphoreType.DMA((n_sems,))]

    def body(where_ref, *refs):
        refs = list(refs)
        take = lambda n: [refs.pop(0) for _ in range(n)]
        x_refs = take(len(xs))
        wg, wu = take(2) if segs else (None, None)
        carried = take(2) if carry is not None else None
        inv_ref = take(1)[0] if inv is not None else None
        hidden_ref = take(1)[0] if hidden is not None else None
        wd = take(1)[0] if jobs else None
        out_refs = take(len(out_shapes))
        seg_bufs = [take(3) for _ in segs]
        accs = take(2) if segs else None
        inv_buf = take(1)[0] if inv is not None else None
        h_buf = take(1)[0] if jobs else None
        job_bufs = [take(2) for _ in jobs]
        copies = Copies(refs.pop(0))
        z = where_ref[0]

        def first(step, offset):
            return pl.multiple_of(lax.rem(z + step, slices) * span + offset, 128)

        waits_in = []
        if carried is not None:
            waits_in = [copies.start(c, a) for c, a in zip(carried, accs)]
        seg_waits = []
        for (parts, step, offset, width, col), (xb, gb, ub) in zip(segs, seg_bufs):
            at = pl.ds(first(step, offset), width)
            mine = []
            for index, row in parts:
                count = x_refs[index].shape[0]
                mine.append(copies.start(x_refs[index].at[:, pl.ds(col, width)], xb.at[pl.ds(row, count), :]))
            mine.append(copies.start(wg.at[at, :], gb))
            mine.append(copies.start(wu.at[at, :], ub))
            seg_waits.append(mine)
        if inv is not None:
            inv_wait = copies.start(inv_ref.at[:, pl.ds(inv_ref.shape[1] - SIDE, SIDE)], inv_buf)
        if hidden is not None:
            hidden_wait = copies.start(hidden_ref, h_buf)
        job_waits = []
        for (step, offset, width, _), (wb, _) in zip(jobs, job_bufs):
            job_waits.append(copies.start(wd.at[:, pl.ds(first(step, offset), width)], wb))
        done = []
        for w in waits_in:
            w.wait()
        for k, (xb, gb, ub) in enumerate(seg_bufs):
            for w in seg_waits[k]:
                w.wait()
            for w_buf, acc in ((gb, accs[0]), (ub, accs[1])):
                term = jnp.dot(xb[...], w_buf[...], preferred_element_type=F32)
                if k == 0 and carried is None:
                    acc[...] = term
                else:
                    acc[...] += term
        if segs and not jobs:
            done += [copies.start(a, o) for a, o in zip(accs, out_refs)]
        if finish:
            inv_wait.wait()
            scale = jnp.sum(inv_buf[...].astype(F32), axis=1, keepdims=True)
            gate = accs[0][...] * scale
            h_buf[...] = (jax.nn.silu(gate) * (accs[1][...] * scale)).astype(BF16)
            done.append(copies.start(h_buf, out_refs.pop(0)))
        if hidden is not None:
            hidden_wait.wait()
        for (_, _, width, targets), (wb, ob), w in zip(jobs, job_bufs, job_waits):
            w.wait()
            ob[...] = jnp.dot(h_buf[...], wb[...], preferred_element_type=F32).astype(BF16)
            for index, row, count, col in targets:
                done.append(copies.start(ob.at[pl.ds(row, count), :], out_refs[index].at[:, pl.ds(col, width)]))
        for copy in done:
            copy.wait()

    hbm = pl.BlockSpec(memory_space=pltpu.HBM)
    flops = sum(4 * rows * s[3] * ff for s in segs) + sum(2 * rows * ff * j[2] for j in jobs)
    return pl.pallas_call(
        body,
        in_specs=[pl.BlockSpec(memory_space=pltpu.SMEM)] + [hbm] * len(args),
        out_specs=[hbm] * len(out_shapes),
        out_shape=out_shapes,
        scratch_shapes=scratch,
        cost_estimate=pl.CostEstimate(flops=flops, bytes_accessed=flops // 256, transcendentals=0),
    )(where, *args)


def place_picks(expert_ids, gate_prob, window):
    ids = expert_ids.T
    probs = gate_prob.T.astype(F32)
    tok = ids.shape[1]
    same = ids[:, None, :] == jnp.arange(window, dtype=jnp.int32)[None, :, None]
    match = jnp.any(same, axis=0).astype(BF16)
    prob = jnp.sum(jnp.where(same, probs[:, None, :], 0.0), axis=0)
    earlier = (jnp.arange(tok)[:, None] < jnp.arange(tok)[None, :]).astype(BF16)
    before = jnp.dot(match, earlier, preferred_element_type=F32)
    slot = jnp.where(match > 0, before, -1.0)
    hit = slot[:, None, :] == jnp.arange(CAP, dtype=F32)[None, :, None]
    pick = hit.astype(BF16).reshape(window * CAP, tok)
    weight = jnp.where(hit, prob[:, None, :], 0.0).astype(BF16).reshape(window * CAP, tok)
    return pick, weight


def three_terms(value):
    rest, terms = value, []
    for _ in range(3):
        term = lax.reduce_precision(rest, 8, 7)
        terms.append(term)
        rest = rest - term
    stacked = jnp.stack(terms, axis=1)
    return jnp.pad(stacked, ((0, 0), (0, SIDE - 3))).astype(BF16)


def local(tokens, norm_gain, expert_ids, gate_prob, w_gate, w_up, w_down):
    window, n_tp = lax.axis_size("ep"), lax.axis_size("tp")
    where = lax.axis_index("tp").astype(jnp.int32).reshape(1)
    w_gate, w_up, w_down = w_gate[0], w_up[0], w_down[0]
    tok = tokens.shape[0]
    rows = window * CAP
    up = [(i, (i + 1) % n_tp) for i in range(n_tp)]
    dn = [(i, (i - 1) % n_tp) for i in range(n_tp)]

    def spread(x):
        half = x.shape[0] // 2
        below, above = lax.ppermute(x, "tp", up), lax.ppermute(x, "tp", dn)
        return below, above, lax.ppermute(below[:half], "tp", up), lax.ppermute(above[half:], "tp", dn)

    def fold(own, above, below, far_a, far_b):
        half = own.shape[0] // 2
        got_a, got_b = lax.ppermute(far_a, "tp", up), lax.ppermute(far_b, "tp", dn)
        sum_up = (above.astype(F32) + jnp.pad(got_a.astype(F32), ((0, half), (0, 0)))).astype(BF16)
        sum_dn = (below.astype(F32) + jnp.pad(got_b.astype(F32), ((half, 0), (0, 0)))).astype(BF16)
        from_dn, from_up = lax.ppermute(sum_up, "tp", up), lax.ppermute(sum_dn, "tp", dn)
        return (own.astype(F32) + from_dn.astype(F32) + from_up.astype(F32)).astype(BF16)

    def exchange(x):
        shaped = x.reshape(window, CAP, x.shape[1])
        return lax.all_to_all(shaped, "ep", 0, 0, tiled=True).reshape(rows, x.shape[1])

    pick, weight = place_picks(expert_ids, gate_prob, window)
    gained = (tokens.astype(F32) * norm_gain.astype(F32)).astype(BF16)
    bulk = tokens.shape[1] - EARLY
    half = rows // 2

    def dispatch(x):
        return jnp.dot(pick, x, preferred_element_type=F32).astype(BF16)

    square_part = jnp.sum(jnp.square(tokens.astype(F32)), axis=1)
    early = jnp.concatenate([gained[:, :EARLY], three_terms(square_part)], axis=1)
    e_below, e_above, e_far_a, e_far_b = spread(early)
    mine = exchange(dispatch(gained[:, EARLY:]))
    e_far = jnp.concatenate([e_far_a, e_far_b], axis=0)
    all_early = (early, e_above, e_far, e_below)
    squares = sum(jnp.sum(e[:, EARLY : EARLY + 3].astype(F32), axis=1) for e in all_early[1:]) + square_part
    inverse_rms = lax.rsqrt(squares / D + epsilon)
    early_all = jnp.concatenate([e[:, :EARLY] for e in all_early] + [three_terms(inverse_rms)], axis=1)
    early_rows = exchange(dispatch(early_all))
    below, above, far_a, far_b = spread(mine)

    whole = lambda i: ((i, 0),)
    near_sums = expert_call(
        where, (mine, above, below),
        [(whole(i), step, EARLY, bulk, 0) for i, step in enumerate((0, 1, 3))],
        w_gate, w_up, None, None, None, None, [], [],
    )
    sums = expert_call(
        where, (early_rows,),
        [(whole(0), k, 0, EARLY, k * EARLY) for k in range(n_tp)],
        w_gate, w_up, near_sums, None, None, None, [], [],
    )
    hidden, p_far_a, p_far_b = expert_call(
        where, (far_a, far_b),
        [(((0, 0), (1, half)), 2, EARLY, bulk, 0)],
        w_gate, w_up, sums, early_rows, None, w_down,
        [(2, EARLY, bulk, ((0, 0, half, 0), (1, half, half, 0)))], [(half, bulk)] * 2,
    )
    (p_early,) = expert_call(
        where, (), [], None, None, None, None, hidden, w_down,
        [(k, 0, EARLY, ((0, 0, rows, k * EARLY),)) for k in range(n_tp)], [(rows, n_tp * EARLY)],
    )
    p_above, p_below, p_own = expert_call(
        where, (), [], None, None, None, None, hidden, w_down,
        [(step, EARLY, bulk, ((i, 0, rows, 0),)) for i, step in enumerate((1, 3, 0))], [(rows, bulk)] * 3,
    )

    def combine(back):
        return lax.dot_general(weight, back, (((0,), (0,)), ((), ())), preferred_element_type=F32).astype(BF16)

    early_back = combine(exchange(p_early))
    e = [early_back[:, k * EARLY : (k + 1) * EARLY] for k in range(n_tp)]
    out_early = fold(e[0], e[1], e[3], e[2][: tok // 2], e[2][tok // 2 :])
    folded = fold(p_own, p_above, p_below, p_far_a, p_far_b)
    out_bulk = combine(exchange(folded))
    return jnp.concatenate([out_early, out_bulk], axis=1)


def solution(mesh):
    placed = (
        P("ep", "tp"),
        P("tp"),
        P("ep", None),
        P("ep", None),
        P("ep", None, "tp"),
        P("ep", None, "tp"),
        P("ep", "tp", None),
    )

    return jax.shard_map(local, mesh=mesh, in_specs=placed, out_specs=P("ep", "tp"), check_vma=False)
```

profile of v0, /device:TPU:1, one launch (start us, length us, event | category | flops | bytes accessed | tf_op | source)
XLA Modules:
  0.0 187.7 jit_solution(522496296014235665)
XLA Ops:
  0.0 0.7 convert_element_type.115
  0.7 1.5 fusion.3
  2.3 0.1 copy.20
  2.5 0.8 fusion.6
  3.2 2.5 %collective-permute-start.5 = (bf16[256,768]{1,0:T(8,128)(2,1)}, bf16[256,768]{1,0:T(8,128)(2,1)S(1)}, u32[]{:S(2)}, u32[]{:S(2)}) collective-permute-start(bf16[256,768]{1,0:T(8,128)(2,1)} %fusion.6), channel_id=1, source_target_pairs={{0,1},{1,2},{2,3},{3,0},{4,5},{5,6},{6,7},{7,4},{8,9},{9,10},{10,1... | collective-permute-start | bytes 1179656 | tf_op jit(solution)/shard_map/ppermute | solution.py:185
  5.7 2.1 %collective-permute-start.4 = (bf16[256,768]{1,0:T(8,128)(2,1)}, bf16[256,768]{1,0:T(8,128)(2,1)S(1)}, u32[]{:S(2)}, u32[]{:S(2)}) collective-permute-start(bf16[256,768]{1,0:T(8,128)(2,1)} %fusion.6), channel_id=1, source_target_pairs={{0,3},{1,0},{2,1},{3,2},{4,7},{5,4},{6,5},{7,6},{8,11},{9,8},{10,9... | collective-permute-start | bytes 1179656 | tf_op jit(solution)/shard_map/ppermute | solution.py:185
  8.0 0.2 convolution_select_fusion
  8.1 0.1 bitcast_compare_fusion
  8.3 1.6 convolution_convert_fusion.1
  9.8 8.0 %all-to-all-start = ((bf16[32,16,1152]{2,1,0:T(8,128)(2,1)}), bf16[32,16,1152]{2,1,0:T(8,128)(2,1)S(1)}, u32[]{:S(2)}, u32[]{:S(2)}) async-start(bf16[32,16,1152]{2,1,0:T(8,128)(2,1)} %bitcast.4), calls=%async_computation | async-start | bytes 2359296 | tf_op jit(solution)/shard_map/all_to_all | solution.py:198
  18.0 2.7 %collective-permute-start.7 = (bf16[128,768]{1,0:T(8,128)(2,1)S(1)}, bf16[128,768]{1,0:T(8,128)(2,1)S(1)}, u32[]{:S(2)}, u32[]{:S(2)}) collective-permute-start(bf16[128,768]{1,0:T(8,128)(2,1)S(1)} %slice.77), channel_id=1, source_target_pairs={{0,3},{1,0},{2,1},{3,2},{4,7},{5,4},{6,5},{7,6},{8,11},{9,8},{10,9... | collective-permute-start | bytes 589832 | tf_op jit(solution)/shard_map/ppermute | solution.py:186
  21.0 4.4 %collective-permute-done.6 = bf16[128,768]{1,0:T(8,128)(2,1)S(1)} collective-permute-done((bf16[128,768]{1,0:T(8,128)(2,1)S(1)}, bf16[128,768]{1,0:T(8,128)(2,1)S(1)}, u32[]{:S(2)}, u32[]{:S(2)}) %collective-permute-start.6) | collective-permute-done | bytes 196640 | tf_op jit(solution)/shard_map/ppermute | solution.py:186
  25.6 0.1 copy.21
  25.9 2.5 %convolution_convert_fusion = bf16[512,2688]{1,0:T(8,128)(2,1)} fusion(pred[512,256]{1,0:T(32,128)(4,1)S(1)} %bitcast_compare_fusion, bf16[256,2688]{1,0:T(8,128)(2,1)S(1)} %pad_dynamic-update-slice_fusion), kind=kOutput, calls=%fused_computation | convolution fusion | flops 706019328 | bytes 4259840 | tf_op jit(solution)/shard_map/dot_general | solution.py:206
  28.4 8.0 %all-to-all-done = bf16[32,16,1152]{2,1,0:T(8,128)(2,1)S(1)} async-done(((bf16[32,16,1152]{2,1,0:T(8,128)(2,1)}), bf16[32,16,1152]{2,1,0:T(8,128)(2,1)S(1)}, u32[]{:S(2)}, u32[]{:S(2)}) %all-to-all-start) | async-done | bytes 1179680 | tf_op jit(solution)/shard_map/all_to_all | solution.py:198
  36.4 1.0 copy-done.2
  37.4 4.1 %all-to-all-start.1 = ((bf16[32,16,2688]{2,1,0:T(8,128)(2,1)}), bf16[32,16,2688]{2,1,0:T(8,128)(2,1)S(1)}, u32[]{:S(2)}, u32[]{:S(2)}) async-start(bf16[32,16,2688]{2,1,0:T(8,128)(2,1)} %bitcast.42), calls=%async_computation.1 | async-start | bytes 5505024 | tf_op jit(solution)/shard_map/all_to_all | solution.py:198
  41.6 1.8 collective-permute-start.2
  43.4 25.7 %collective-permute-done.2.refs_1_ = bf16[512,1152]{1,0:T(8,128)(2,1)} collective-permute-done((bf16[512,1152]{1,0:T(8,128)(2,1)}, bf16[512,1152]{1,0:T(8,128)(2,1)}, u32[]{:S(2)}, u32[]{:S(2)}) %collective-permute-start.2) | collective-permute-done | bytes 1179680 | tf_op jit(solution)/shard_map/ppermute | solution.py:185
  69.1 1.9 %slice.73 = bf16[256,1152]{1,0:T(8,128)(2,1)} slice(bf16[512,1152]{1,0:T(8,128)(2,1)} %collective-permute-done.2.refs_1_), slice={[256:512], [0:1152]} | slice | bytes 1179648 | tf_op jit(solution)/shard_map/slice | solution.py:186
  71.0 3.0 %collective-permute-start.3 = (bf16[256,1152]{1,0:T(8,128)(2,1)}, bf16[256,1152]{1,0:T(8,128)(2,1)S(1)}, u32[]{:S(2)}, u32[]{:S(2)}) collective-permute-start(bf16[256,1152]{1,0:T(8,128)(2,1)} %slice.73), channel_id=1, source_target_pairs={{0,3},{1,0},{2,1},{3,2},{4,7},{5,4},{6,5},{7,6},{8,11},{9,8},{10,9... | collective-permute-start | bytes 1769480 | tf_op jit(solution)/shard_map/ppermute | solution.py:186
  74.0 1.9 %slice.72 = bf16[256,1152]{1,0:T(8,128)(2,1)} slice(bf16[512,1152]{1,0:T(8,128)(2,1)} %collective-permute-done.refs_2_), slice={[0:256], [0:1152]} | slice | bytes 1179648 | tf_op jit(solution)/shard_map/slice | solution.py:186
  75.9 7.5 %shard_map.73 = (f32[512,512]{1,0:T(8,128)}, f32[512,512]{1,0:T(8,128)}) custom-call(s32[1]{0:T(128)} %bitcast.2.where_ref, bf16[512,1152]{1,0:T(8,128)(2,1)} %bitcast.47, bf16[512,1152]{1,0:T(8,128)(2,1)} %collective-permute-done.2.refs_1_, bf16[512,1152]{1,0:T(8,128)(2,1)} %collective-permute-done.refs_2_, bf16[7168,512]{1,0:T(8,128)(2,1)} %bitcast.31, ...), custom_call_target="tpu_custom_call" | custom-call | flops 3623878656 | bytes 14155776 | tf_op jit(solution)/shard_map/pallas_call | solution.py:138
  83.5 1.5 copy-done
  85.0 6.8 %shard_map.74 = (f32[512,512]{1,0:T(8,128)}, f32[512,512]{1,0:T(8,128)}) custom-call(s32[1]{0:T(128)} %bitcast.2.where_ref, bf16[512,2688]{1,0:T(8,128)(2,1)} %bitcast.40, bf16[7168,512]{1,0:T(8,128)(2,1)} %bitcast.32, bf16[7168,512]{1,0:T(8,128)(2,1)} %bitcast.35, f32[512,512]{1,0:T(8,128)} %get-tuple-element.15.refs_3_, f32[512,512]{1,0:T(8,128)} %get-tuple-element.16.refs_4_), custom_call_target="tpu_custom_call" | custom-call | flops 2684354560 | bytes 10485760 | tf_op jit(solution)/shard_map/pallas_call | solution.py:138
  91.8 0.8 copy-done.5
  92.6 6.7 %shard_map.75 = (bf16[512,512]{1,0:T(8,128)(2,1)}, bf16[256,1152]{1,0:T(8,128)(2,1)}, bf16[256,1152]{1,0:T(8,128)(2,1)}) custom-call(s32[1]{0:T(128)} %bitcast.2.where_ref, bf16[256,1152]{1,0:T(8,128)(2,1)} %collective-permute-done.1.refs_0_, bf16[256,1152]{1,0:T(8,128)(2,1)} %copy-done.5, bf16[7168,512]{1,0:T(8,128)(2,1)} %bitcast.33, ...), custom_call_target="tpu_custom_call" | custom-call | flops 1811939328 | bytes 7077888 | tf_op jit(solution)/shard_map/pallas_call | solution.py:138
  99.4 2.7 %collective-permute-start.14 = (bf16[256,1152]{1,0:T(8,128)(2,1)}, bf16[256,1152]{1,0:T(8,128)(2,1)}, u32[]{:S(2)}, u32[]{:S(2)}) collective-permute-start(bf16[256,1152]{1,0:T(8,128)(2,1)} %get-tuple-element.24), channel_id=1, source_target_pairs={{0,3},{1,0},{2,1},{3,2},{4,7},{5,4},{6,5},{7,6},{8,11},{9,8},{10,9... | collective-permute-start | bytes 1769480 | tf_op jit(solution)/shard_map/ppermute | solution.py:190
  102.1 5.4 %shard_map.77 = (bf16[512,1152]{1,0:T(8,128)(2,1)}, bf16[512,1152]{1,0:T(8,128)(2,1)}, bf16[512,1152]{1,0:T(8,128)(2,1)}) custom-call(s32[1]{0:T(128)} %bitcast.2.where_ref, bf16[512,512]{1,0:T(8,128)(2,1)} %get-tuple-element.19.refs_0_, bf16[512,7168]{1,0:T(8,128)(2,1)} %bitcast.38), custom_call_target="tpu_custom_call" | custom-call | flops 1811939328 | bytes 7077888 | tf_op jit(solution)/shard_map/pallas_call | solution.py:138
  107.5 5.0 %shard_map.76 = bf16[512,2560]{1,0:T(8,128)(2,1)} custom-call(s32[1]{0:T(128)} %bitcast.2.where_ref, bf16[512,512]{1,0:T(8,128)(2,1)} %get-tuple-element.19.refs_0_, bf16[512,7168]{1,0:T(8,128)(2,1)} %bitcast.39), custom_call_target="tpu_custom_call" | custom-call | flops 1342177280 | bytes 5242880 | tf_op jit(solution)/shard_map/pallas_call | solution.py:138
  112.5 9.2 %all-to-all-start.2 = ((bf16[32,16,2560]{2,1,0:T(8,128)(2,1)}), bf16[32,16,2560]{2,1,0:T(8,128)(2,1)S(1)}, u32[]{:S(2)}, u32[]{:S(2)}) async-start(bf16[32,16,2560]{2,1,0:T(8,128)(2,1)} %bitcast.43), calls=%async_computation.2 | async-start | bytes 5242880 | tf_op jit(solution)/shard_map/all_to_all | solution.py:198
  121.7 1.7 add_convert_fusion.1
  123.4 3.0 %collective-permute-start.15 = (bf16[512,1152]{1,0:T(8,128)(2,1)S(1)}, bf16[512,1152]{1,0:T(8,128)(2,1)S(1)}, u32[]{:S(2)}, u32[]{:S(2)}) collective-permute-start(bf16[512,1152]{1,0:T(8,128)(2,1)S(1)} %add_convert_fusion.1), channel_id=1, source_target_pairs={{0,3},{1,0},{2,1},{3,2},{4,7},{5,4},{6,5},{7,6},{8,11},{9,8},{10,9... | collective-permute-start | bytes 3538952 | tf_op jit(solution)/shard_map/ppermute | solution.py:193
  126.4 0.2 add_convert_fusion.2
  126.6 0.3 collective-permute-start.13
  126.9 0.2 copy-done.9
  127.1 24.4 %collective-permute-done.15 = bf16[512,1152]{1,0:T(8,128)(2,1)S(1)} collective-permute-done((bf16[512,1152]{1,0:T(8,128)(2,1)S(1)}, bf16[512,1152]{1,0:T(8,128)(2,1)S(1)}, u32[]{:S(2)}, u32[]{:S(2)}) %collective-permute-start.15) | collective-permute-done | bytes 1179680 | tf_op jit(solution)/shard_map/ppermute | solution.py:193
  151.5 3.6 %collective-permute-done.13 = bf16[512,1152]{1,0:T(8,128)(2,1)S(1)} collective-permute-done((bf16[512,1152]{1,0:T(8,128)(2,1)S(1)}, bf16[512,1152]{1,0:T(8,128)(2,1)S(1)}, u32[]{:S(2)}, u32[]{:S(2)}) %collective-permute-start.13) | collective-permute-done | bytes 1179680 | tf_op jit(solution)/shard_map/ppermute | solution.py:193
  155.1 1.5 add_convert_fusion
  156.6 8.5 %all-to-all-start.3 = ((bf16[32,16,1152]{2,1,0:T(8,128)(2,1)}), bf16[32,16,1152]{2,1,0:T(8,128)(2,1)}, u32[]{:S(2)}, u32[]{:S(2)}) async-start(bf16[32,16,1152]{2,1,0:T(8,128)(2,1)} %bitcast.44), calls=%async_computation.3 | async-start | bytes 2359296 | tf_op jit(solution)/shard_map/all_to_all | solution.py:198
  165.2 0.9 fusion
  166.2 2.7 %collective-permute-start.10 = (bf16[128,640]{1,0:T(8,128)(2,1)S(1)}, bf16[128,640]{1,0:T(8,128)(2,1)S(1)}, u32[]{:S(2)}, u32[]{:S(2)}) collective-permute-start(bf16[128,640]{1,0:T(8,128)(2,1)S(1)} %get-tuple-element.30), channel_id=1, source_target_pairs={{0,3},{1,0},{2,1},{3,2},{4,7},{5,4},{6,5},{7,6},{8,11},{9,8},{10,9... | collective-permute-start | bytes 491528 | tf_op jit(solution)/shard_map/ppermute | solution.py:190
  168.8 4.1 %collective-permute-done.8 = bf16[128,640]{1,0:T(8,128)(2,1)S(1)} collective-permute-done((bf16[128,640]{1,0:T(8,128)(2,1)S(1)}, bf16[128,640]{1,0:T(8,128)(2,1)S(1)}, u32[]{:S(2)}, u32[]{:S(2)}) %collective-permute-start.8) | collective-permute-done | bytes 163872 | tf_op jit(solution)/shard_map/ppermute | solution.py:190
  173.1 2.7 %collective-permute-start.11 = (bf16[256,640]{1,0:T(8,128)(2,1)S(1)}, bf16[256,640]{1,0:T(8,128)(2,1)S(1)}, u32[]{:S(2)}, u32[]{:S(2)}) collective-permute-start(bf16[256,640]{1,0:T(8,128)(2,1)S(1)} %get-tuple-element.28), channel_id=1, source_target_pairs={{0,3},{1,0},{2,1},{3,2},{4,7},{5,4},{6,5},{7,6},{8,11},{9,8},{10,9... | collective-permute-start | bytes 983048 | tf_op jit(solution)/shard_map/ppermute | solution.py:193
  175.8 8.0 %all-to-all-done.3 = bf16[32,16,1152]{2,1,0:T(8,128)(2,1)} async-done(((bf16[32,16,1152]{2,1,0:T(8,128)(2,1)}), bf16[32,16,1152]{2,1,0:T(8,128)(2,1)}, u32[]{:S(2)}, u32[]{:S(2)}) %all-to-all-start.3) | async-done | bytes 1179680 | tf_op jit(solution)/shard_map/all_to_all | solution.py:198
  183.7 1.8 fusion.1
  185.6 1.1 add_convert_fusion.3
  186.7 1.0 pad_maximum_fusion
  (60 shorter events, 1.2 us)
Async XLA Ops:
  2.2 5.6 %copy-start.8 = (s32[256,8]{0,1:T(8,128)S(1)}, s32[256,8]{0,1:T(8,128)}, u32[]{:S(2)}) copy-start(s32[256,8]{0,1:T(8,128)} %param.9) | copy-start | bytes 24580
  3.2 14.6 %collective-permute-start.5 = (bf16[256,768]{1,0:T(8,128)(2,1)}, bf16[256,768]{1,0:T(8,128)(2,1)S(1)}, u32[]{:S(2)}, u32[]{:S(2)}) collective-permute-start(bf16[256,768]{1,0:T(8,128)(2,1)} %fusion.6), channel_id=1, source_target_pairs={{0,1},{1,2},{2,3},{3,0},{4,5},{5,6},{6,7},{7,4},{8,9},{9,10},{10,1... | collective-permute-start | bytes 1179656 | tf_op jit(solution)/shard_map/ppermute | solution.py:185
  5.7 12.3 %collective-permute-start.4 = (bf16[256,768]{1,0:T(8,128)(2,1)}, bf16[256,768]{1,0:T(8,128)(2,1)S(1)}, u32[]{:S(2)}, u32[]{:S(2)}) collective-permute-start(bf16[256,768]{1,0:T(8,128)(2,1)} %fusion.6), channel_id=1, source_target_pairs={{0,3},{1,0},{2,1},{3,2},{4,7},{5,4},{6,5},{7,6},{8,11},{9,8},{10,9... | collective-permute-start | bytes 1179656 | tf_op jit(solution)/shard_map/ppermute | solution.py:185
  8.1 1.7 copy-start.6
  9.8 26.6 %all-to-all-start = ((bf16[32,16,1152]{2,1,0:T(8,128)(2,1)}), bf16[32,16,1152]{2,1,0:T(8,128)(2,1)S(1)}, u32[]{:S(2)}, u32[]{:S(2)}) async-start(bf16[32,16,1152]{2,1,0:T(8,128)(2,1)} %bitcast.4), calls=%async_computation | async-start | bytes 2359296 | tf_op jit(solution)/shard_map/all_to_all | solution.py:198
  17.9 7.5 %collective-permute-start.6 = (bf16[128,768]{1,0:T(8,128)(2,1)S(1)}, bf16[128,768]{1,0:T(8,128)(2,1)S(1)}, u32[]{:S(2)}, u32[]{:S(2)}) collective-permute-start(bf16[128,768]{1,0:T(8,128)(2,1)S(1)} %slice.76), channel_id=1, source_target_pairs={{0,1},{1,2},{2,3},{3,0},{4,5},{5,6},{6,7},{7,4},{8,9},{9,10},{10,1... | collective-permute-start | bytes 589832 | tf_op jit(solution)/shard_map/ppermute | solution.py:186
  18.0 7.4 %collective-permute-start.7 = (bf16[128,768]{1,0:T(8,128)(2,1)S(1)}, bf16[128,768]{1,0:T(8,128)(2,1)S(1)}, u32[]{:S(2)}, u32[]{:S(2)}) collective-permute-start(bf16[128,768]{1,0:T(8,128)(2,1)S(1)} %slice.77), channel_id=1, source_target_pairs={{0,3},{1,0},{2,1},{3,2},{4,7},{5,4},{6,5},{7,6},{8,11},{9,8},{10,9... | collective-permute-start | bytes 589832 | tf_op jit(solution)/shard_map/ppermute | solution.py:186
  36.4 1.0 copy-start.2
  37.4 46.0 %all-to-all-start.1 = ((bf16[32,16,2688]{2,1,0:T(8,128)(2,1)}), bf16[32,16,2688]{2,1,0:T(8,128)(2,1)S(1)}, u32[]{:S(2)}, u32[]{:S(2)}) async-start(bf16[32,16,2688]{2,1,0:T(8,128)(2,1)} %bitcast.42), calls=%async_computation.1 | async-start | bytes 5505024 | tf_op jit(solution)/shard_map/all_to_all | solution.py:198
  41.6 27.6 %collective-permute-start.2 = (bf16[512,1152]{1,0:T(8,128)(2,1)}, bf16[512,1152]{1,0:T(8,128)(2,1)}, u32[]{:S(2)}, u32[]{:S(2)}) collective-permute-start(bf16[512,1152]{1,0:T(8,128)(2,1)} %bitcast.45), channel_id=1, source_target_pairs={{0,3},{1,0},{2,1},{3,2},{4,7},{5,4},{6,5},{7,6},{8,11},{9,8},{10,9... | collective-permute-start | bytes 3538952 | tf_op jit(solution)/shard_map/ppermute | solution.py:185
  43.4 30.6 %collective-permute-start = (bf16[512,1152]{1,0:T(8,128)(2,1)}, bf16[512,1152]{1,0:T(8,128)(2,1)}, u32[]{:S(2)}, u32[]{:S(2)}) collective-permute-start(bf16[512,1152]{1,0:T(8,128)(2,1)} %bitcast.46), channel_id=1, source_target_pairs={{0,1},{1,2},{2,3},{3,0},{4,5},{5,6},{6,7},{7,4},{8,9},{9,10},{10,1... | collective-permute-start | bytes 3538952 | tf_op jit(solution)/shard_map/ppermute | solution.py:185
  71.0 20.8 %collective-permute-start.3 = (bf16[256,1152]{1,0:T(8,128)(2,1)}, bf16[256,1152]{1,0:T(8,128)(2,1)S(1)}, u32[]{:S(2)}, u32[]{:S(2)}) collective-permute-start(bf16[256,1152]{1,0:T(8,128)(2,1)} %slice.73), channel_id=1, source_target_pairs={{0,3},{1,0},{2,1},{3,2},{4,7},{5,4},{6,5},{7,6},{8,11},{9,8},{10,9... | collective-permute-start | bytes 1769480 | tf_op jit(solution)/shard_map/ppermute | solution.py:186
  75.9 15.9 %collective-permute-start.1 = (bf16[256,1152]{1,0:T(8,128)(2,1)}, bf16[256,1152]{1,0:T(8,128)(2,1)}, u32[]{:S(2)}, u32[]{:S(2)}) collective-permute-start(bf16[256,1152]{1,0:T(8,128)(2,1)} %slice.72), channel_id=1, source_target_pairs={{0,1},{1,2},{2,3},{3,0},{4,5},{5,6},{6,7},{7,4},{8,9},{9,10},{10,1... | collective-permute-start | bytes 1769480 | tf_op jit(solution)/shard_map/ppermute | solution.py:186
  83.4 1.5 copy-start
  91.8 0.8 copy-start.5
  99.4 22.3 %collective-permute-start.14 = (bf16[256,1152]{1,0:T(8,128)(2,1)}, bf16[256,1152]{1,0:T(8,128)(2,1)}, u32[]{:S(2)}, u32[]{:S(2)}) collective-permute-start(bf16[256,1152]{1,0:T(8,128)(2,1)} %get-tuple-element.24), channel_id=1, source_target_pairs={{0,3},{1,0},{2,1},{3,2},{4,7},{5,4},{6,5},{7,6},{8,11},{9,8},{10,9... | collective-permute-start | bytes 1769480 | tf_op jit(solution)/shard_map/ppermute | solution.py:190
  102.1 24.3 %collective-permute-start.12 = (bf16[256,1152]{1,0:T(8,128)(2,1)}, bf16[256,1152]{1,0:T(8,128)(2,1)S(1)}, u32[]{:S(2)}, u32[]{:S(2)}) collective-permute-start(bf16[256,1152]{1,0:T(8,128)(2,1)} %get-tuple-element.22), channel_id=1, source_target_pairs={{0,1},{1,2},{2,3},{3,0},{4,5},{5,6},{6,7},{7,4},{8,9},{9,10},{10,1... | collective-permute-start | bytes 1769480 | tf_op jit(solution)/shard_map/ppermute | solution.py:190
  112.5 44.1 %all-to-all-start.2 = ((bf16[32,16,2560]{2,1,0:T(8,128)(2,1)}), bf16[32,16,2560]{2,1,0:T(8,128)(2,1)S(1)}, u32[]{:S(2)}, u32[]{:S(2)}) async-start(bf16[32,16,2560]{2,1,0:T(8,128)(2,1)} %bitcast.43), calls=%async_computation.2 | async-start | bytes 5242880 | tf_op jit(solution)/shard_map/all_to_all | solution.py:198
  121.7 4.7 %copy-start.4 = (bf16[512,1152]{1,0:T(8,128)(2,1)S(1)}, bf16[512,1152]{1,0:T(8,128)(2,1)}, u32[]{:S(2)}) copy-start(bf16[512,1152]{1,0:T(8,128)(2,1)} %get-tuple-element.21) | copy-start | bytes 3538948
  123.4 28.1 %collective-permute-start.15 = (bf16[512,1152]{1,0:T(8,128)(2,1)S(1)}, bf16[512,1152]{1,0:T(8,128)(2,1)S(1)}, u32[]{:S(2)}, u32[]{:S(2)}) collective-permute-start(bf16[512,1152]{1,0:T(8,128)(2,1)S(1)} %add_convert_fusion.1), channel_id=1, source_target_pairs={{0,3},{1,0},{2,1},{3,2},{4,7},{5,4},{6,5},{7,6},{8,11},{9,8},{10,9... | collective-permute-start | bytes 3538952 | tf_op jit(solution)/shard_map/ppermute | solution.py:193
  126.4 0.7 copy-start.9
  126.4 28.7 %copy-start.3 = (bf16[512,1152]{1,0:T(8,128)(2,1)S(1)}, bf16[512,1152]{1,0:T(8,128)(2,1)}, u32[]{:S(2)}) copy-start(bf16[512,1152]{1,0:T(8,128)(2,1)} %get-tuple-element.20) | copy-start | bytes 3538948
  126.6 28.5 %collective-permute-start.13 = (bf16[512,1152]{1,0:T(8,128)(2,1)S(1)}, bf16[512,1152]{1,0:T(8,128)(2,1)S(1)}, u32[]{:S(2)}, u32[]{:S(2)}) collective-permute-start(bf16[512,1152]{1,0:T(8,128)(2,1)S(1)} %add_convert_fusion.2), channel_id=1, source_target_pairs={{0,1},{1,2},{2,3},{3,0},{4,5},{5,6},{6,7},{7,4},{8,9},{9,10},{10,1... | collective-permute-start | bytes 3538952 | tf_op jit(solution)/shard_map/ppermute | solution.py:193
  156.6 8.6 %copy-start.7 = (f32[32,256]{1,0:T(8,128)S(1)}, f32[32,256]{1,0:T(8,128)}, u32[]{:S(2)}) copy-start(f32[32,256]{1,0:T(8,128)} %copy-done.6) | copy-start | bytes 98308
  156.6 27.1 %all-to-all-start.3 = ((bf16[32,16,1152]{2,1,0:T(8,128)(2,1)}), bf16[32,16,1152]{2,1,0:T(8,128)(2,1)}, u32[]{:S(2)}, u32[]{:S(2)}) async-start(bf16[32,16,1152]{2,1,0:T(8,128)(2,1)} %bitcast.44), calls=%async_computation.3 | async-start | bytes 2359296 | tf_op jit(solution)/shard_map/all_to_all | solution.py:198
  166.0 6.9 %copy-start.1 = (bf16[256,2560]{1,0:T(8,128)(2,1)}, bf16[256,2560]{1,0:T(8,128)(2,1)S(1)}, u32[]{:S(2)}) copy-start(bf16[256,2560]{1,0:T(8,128)(2,1)S(1)} %fusion) | copy-start | bytes 3932164
  166.1 6.8 %collective-permute-start.8 = (bf16[128,640]{1,0:T(8,128)(2,1)S(1)}, bf16[128,640]{1,0:T(8,128)(2,1)S(1)}, u32[]{:S(2)}, u32[]{:S(2)}) collective-permute-start(bf16[128,640]{1,0:T(8,128)(2,1)S(1)} %get-tuple-element.29), channel_id=1, source_target_pairs={{0,1},{1,2},{2,3},{3,0},{4,5},{5,6},{6,7},{7,4},{8,9},{9,10},{10,1... | collective-permute-start | bytes 491528 | tf_op jit(solution)/shard_map/ppermute | solution.py:190
  166.2 6.8 %collective-permute-start.10 = (bf16[128,640]{1,0:T(8,128)(2,1)S(1)}, bf16[128,640]{1,0:T(8,128)(2,1)S(1)}, u32[]{:S(2)}, u32[]{:S(2)}) collective-permute-start(bf16[128,640]{1,0:T(8,128)(2,1)S(1)} %get-tuple-element.30), channel_id=1, source_target_pairs={{0,3},{1,0},{2,1},{3,2},{4,7},{5,4},{6,5},{7,6},{8,11},{9,8},{10,9... | collective-permute-start | bytes 491528 | tf_op jit(solution)/shard_map/ppermute | solution.py:190
  173.0 12.5 %collective-permute-start.9 = (bf16[256,640]{1,0:T(8,128)(2,1)S(1)}, bf16[256,640]{1,0:T(8,128)(2,1)S(1)}, u32[]{:S(2)}, u32[]{:S(2)}) collective-permute-start(bf16[256,640]{1,0:T(8,128)(2,1)S(1)} %get-tuple-element.27), channel_id=1, source_target_pairs={{0,1},{1,2},{2,3},{3,0},{4,5},{5,6},{6,7},{7,4},{8,9},{9,10},{10,1... | collective-permute-start | bytes 983048 | tf_op jit(solution)/shard_map/ppermute | solution.py:193
  173.1 12.5 %collective-permute-start.11 = (bf16[256,640]{1,0:T(8,128)(2,1)S(1)}, bf16[256,640]{1,0:T(8,128)(2,1)S(1)}, u32[]{:S(2)}, u32[]{:S(2)}) collective-permute-start(bf16[256,640]{1,0:T(8,128)(2,1)S(1)} %get-tuple-element.28), channel_id=1, source_target_pairs={{0,3},{1,0},{2,1},{3,2},{4,7},{5,4},{6,5},{7,6},{8,11},{9,8},{10,9... | collective-permute-start | bytes 983048 | tf_op jit(solution)/shard_map/ppermute | solution.py:193
where the time goes:
time: 188 us
  waiting for transfers between devices  78.3 us (42%)
  starting transfers between devices  53.5 us (28%)
  Pallas kernels  31.5 us (17%)
  other arithmetic  9.12 us (5%)
  local copies, waits for them, and re-layouts  8.08 us (4%)
  matrix products  6.85 us (4%)
    pallas_call x5, Pallas kernels, expert_call(): pl.pallas_call(body, in_specs=[pl.BlockSpec(memory_space=pltpu.SMEM)] + [...  31.5 us
    all_to_all x4, starting transfers between devices, exchange(): lax.all_to_all(shaped, 'ep', 0, 0, tiled=True).reshape(rows, x.shape[1])  29.9 us
    ppermute x4, waiting for transfers between devices, spread(): below, above = (lax.ppermute(x, 'tp', up), lax.ppermute(x, 'tp', dn))  25.8 us
    ppermute x2, waiting for transfers between devices, fold(): lax.ppermute(sum_dn, 'tp', dn)  24.4 us
    all_to_all x4, waiting for transfers between devices, exchange(): lax.all_to_all(shaped, 'ep', 0, 0, tiled=True).reshape(rows, x.shape[1])  16 us
    ppermute x4, starting transfers between devices, spread(): below, above = (lax.ppermute(x, 'tp', up), lax.ppermute(x, 'tp', dn))  6.39 us
    ppermute x2, starting transfers between devices, fold(): lax.ppermute(sum_dn, 'tp', dn)  5.68 us
    ppermute x2, starting transfers between devices, spread(): lax.ppermute(above[half:], 'tp', dn)  5.67 us
  transfers between devices with their start and end apart: 20, of which 7 were waited for; matrix products, arithmetic and copies ran while one was open for 8% of the time, Pallas kernels for 13%

commit v1 on v0

v1 whole, which is shorter than its diff:
```python
import jax
import jax.numpy as jnp
from jax import lax
from jax.experimental import pallas as pl
from jax.experimental.pallas import tpu as pltpu
from jax.sharding import PartitionSpec as P


D = 7168
epsilon = 1e-06
CAP = 16
EARLY = 640
SIDE = 128
F32, BF16 = jnp.float32, jnp.bfloat16


class Copies:
    def __init__(self, sems):
        self.sems, self.used = sems, 0

    def start(self, src, dst):
        copy = pltpu.make_async_copy(src, dst, self.sems.at[self.used])
        self.used += 1
        copy.start()
        return copy


def expert_call(where, weights, xs=(), segs=(), carry=(), inv=None, hidden=None, jobs=(), outs=()):
    slices = lax.axis_size("tp")
    w_gate, w_up, w_down = weights
    d_all, ff = w_gate.shape
    span = d_all // slices
    finish = bool(segs) and bool(jobs)
    rows = hidden.shape[0] if hidden is not None else carry[0].shape[0] if carry else sum(xs[i].shape[0] for i in segs[0][0])
    results = [((rows, ff), F32)] * 2 if not jobs else [((rows, ff), BF16)] * finish + [(s, BF16) for s in outs]
    resident = list(xs) + list(carry) + ([] if inv is None else [inv]) + ([] if hidden is None else [hidden])
    streamed = ([w_gate, w_up] if segs else []) + ([w_down] if jobs else [])
    columns = []
    for step, offset, width, *_ in jobs:
        if (step, offset, width) not in columns:
            columns.append((step, offset, width))
    scratch = []
    for _, _, _, width, _ in segs:
        scratch += [pltpu.VMEM((width, ff), BF16)] * 2
    if finish:
        scratch += [pltpu.VMEM((rows, ff), F32)] * 2
    scratch += [pltpu.VMEM((ff, width), BF16) for _, _, width in columns]
    scratch += [pltpu.SemaphoreType.DMA((2 * len(segs) + len(columns),))]

    def body(where_ref, *refs):
        refs = list(refs)
        take = lambda n: [refs.pop(0) for _ in range(n)]
        x_refs, carried = take(len(xs)), take(len(carry))
        inv_ref = take(inv is not None)
        hidden_ref = take(hidden is not None)
        wg, wu = take(2) if segs else (None, None)
        wd = take(bool(jobs))
        out_refs = take(len(results))
        seg_bufs = [take(2) for _ in segs]
        accs = take(2) if finish else out_refs
        col_bufs = take(len(columns))
        copies = Copies(refs.pop(0))
        z = where_ref[0]

        def first(step, offset):
            return pl.multiple_of(lax.rem(z + step, slices) * span + offset, 128)

        seg_waits, col_waits = [], []
        for (_, step, offset, width, _), (gb, ub) in zip(segs, seg_bufs):
            at = pl.ds(first(step, offset), width)
            seg_waits.append([copies.start(wg.at[at, :], gb), copies.start(wu.at[at, :], ub)])
        for (step, offset, width), wb in zip(columns, col_bufs):
            col_waits.append(copies.start(wd[0].at[:, pl.ds(first(step, offset), width)], wb))
        for k, (index, _, _, width, col) in enumerate(segs):
            x = [x_refs[i][:, col : col + width] for i in index]
            x = x[0] if len(x) == 1 else jnp.concatenate(x, axis=0)
            for w in seg_waits[k]:
                w.wait()
            for w_buf, acc, base in zip(seg_bufs[k], accs, carried or (None, None)):
                term = jnp.dot(x, w_buf[...], preferred_element_type=F32)
                if k:
                    acc[...] += term
                elif base is None:
                    acc[...] = term
                else:
                    acc[...] = base[...] + term
        if finish:
            scale = jnp.sum(inv_ref[0][:, -SIDE:].astype(F32), axis=1, keepdims=True)
            gate = accs[0][...] * scale
            hidden_ref = [out_refs.pop(0)]
            hidden_ref[0][...] = (jax.nn.silu(gate) * (accs[1][...] * scale)).astype(BF16)
        waited = set()
        for step, offset, width, row, count, targets in jobs:
            k = columns.index((step, offset, width))
            if k not in waited:
                col_waits[k].wait()
                waited.add(k)
            term = jnp.dot(hidden_ref[0][row : row + count, :], col_bufs[k][...], preferred_element_type=F32).astype(BF16)
            for index, top, n, col in targets:
                out_refs[index][:, col : col + width] = term[top : top + n, :]

    vmem = pl.BlockSpec(memory_space=pltpu.VMEM)
    flops = sum(4 * rows * s[3] * ff for s in segs) + sum(2 * j[4] * ff * j[2] for j in jobs)
    return pl.pallas_call(
        body,
        in_specs=[pl.BlockSpec(memory_space=pltpu.SMEM)] + [vmem] * len(resident) + [pl.BlockSpec(memory_space=pltpu.HBM)] * len(streamed),
        out_specs=[vmem] * len(results),
        out_shape=[pltpu.VMEM(s, t) for s, t in results],
        scratch_shapes=scratch,
        cost_estimate=pl.CostEstimate(flops=flops, bytes_accessed=flops // 256, transcendentals=0),
        compiler_params=pltpu.CompilerParams(vmem_limit_bytes=24 * 2**20),
    )(where, *[pltpu.with_memory_space_constraint(x, pltpu.VMEM) for x in resident], *[pltpu.with_memory_space_constraint(w, pltpu.HBM) for w in streamed])


def place_picks(expert_ids, gate_prob, window):
    ids = expert_ids.T
    probs = gate_prob.T.astype(F32)
    tok = ids.shape[1]
    same = ids[:, None, :] == jnp.arange(window, dtype=jnp.int32)[None, :, None]
    match = jnp.any(same, axis=0).astype(BF16)
    prob = jnp.sum(jnp.where(same, probs[:, None, :], 0.0), axis=0)
    earlier = (jnp.arange(tok)[:, None] < jnp.arange(tok)[None, :]).astype(BF16)
    before = jnp.dot(match, earlier, preferred_element_type=F32)
    slot = jnp.where(match > 0, before, -1.0)
    hit = slot[:, None, :] == jnp.arange(CAP, dtype=F32)[None, :, None]
    pick = hit.astype(BF16).reshape(window * CAP, tok)
    weight = jnp.where(hit, prob[:, None, :], 0.0).astype(BF16).reshape(window * CAP, tok)
    return pick, weight


def three_terms(value):
    rest, terms = value, []
    for _ in range(3):
        term = lax.reduce_precision(rest, 8, 7)
        terms.append(term)
        rest = rest - term
    stacked = jnp.stack(terms, axis=1)
    return jnp.pad(stacked, ((0, 0), (0, SIDE - 3))).astype(BF16)


def local(tokens, norm_gain, expert_ids, gate_prob, w_gate, w_up, w_down):
    window, n_tp = lax.axis_size("ep"), lax.axis_size("tp")
    where = lax.axis_index("tp").astype(jnp.int32).reshape(1)
    w_gate, w_up, w_down = w_gate[0], w_up[0], w_down[0]
    tok = tokens.shape[0]
    rows = window * CAP
    up = [(i, (i + 1) % n_tp) for i in range(n_tp)]
    dn = [(i, (i - 1) % n_tp) for i in range(n_tp)]

    def spread(x):
        half = x.shape[0] // 2
        below, above = lax.ppermute(x, "tp", up), lax.ppermute(x, "tp", dn)
        return below, above, lax.ppermute(below[:half], "tp", up), lax.ppermute(above[half:], "tp", dn)

    def fold(own, above, below, far_a, far_b):
        half = own.shape[0] // 2
        got_a, got_b = lax.ppermute(far_a, "tp", up), lax.ppermute(far_b, "tp", dn)
        sum_up = (above.astype(F32) + jnp.pad(got_a.astype(F32), ((0, half), (0, 0)))).astype(BF16)
        sum_dn = (below.astype(F32) + jnp.pad(got_b.astype(F32), ((half, 0), (0, 0)))).astype(BF16)
        from_dn, from_up = lax.ppermute(sum_up, "tp", up), lax.ppermute(sum_dn, "tp", dn)
        return (own.astype(F32) + from_dn.astype(F32) + from_up.astype(F32)).astype(BF16)

    def spread_halves(low, high):
        below_low, above_high = lax.ppermute(low, "tp", up), lax.ppermute(high, "tp", dn)
        below_high, above_low = lax.ppermute(high, "tp", up), lax.ppermute(low, "tp", dn)
        far = lax.ppermute(below_low, "tp", up), lax.ppermute(above_high, "tp", dn)
        return (below_low, below_high), (above_low, above_high), far

    def add(*terms):
        return sum(t.astype(F32) for t in terms).astype(BF16)

    def fold_halves(own, above, below, far):
        got_low, got_high = lax.ppermute(far[0], "tp", up), lax.ppermute(far[1], "tp", dn)
        dn_high, up_low = lax.ppermute(above[1], "tp", up), lax.ppermute(below[0], "tp", dn)
        dn_low = lax.ppermute(add(above[0], got_low), "tp", up)
        up_high = lax.ppermute(add(below[1], got_high), "tp", dn)
        return jnp.concatenate([add(own[0], dn_low, up_low), add(own[1], dn_high, up_high)], axis=0)

    def exchange(x):
        shaped = x.reshape(window, CAP, x.shape[1])
        return lax.all_to_all(shaped, "ep", 0, 0, tiled=True).reshape(rows, x.shape[1])

    pick, weight = place_picks(expert_ids, gate_prob, window)
    gained = (tokens.astype(F32) * norm_gain.astype(F32)).astype(BF16)
    bulk = tokens.shape[1] - EARLY
    half = rows // 2

    def dispatch(x):
        return jnp.dot(pick, x, preferred_element_type=F32).astype(BF16)

    square_part = jnp.sum(jnp.square(tokens.astype(F32)), axis=1)
    early = jnp.concatenate([gained[:, :EARLY], three_terms(square_part)], axis=1)
    e_below, e_above, e_far_a, e_far_b = spread(early)
    mine = exchange(dispatch(gained[:, EARLY:]))
    e_far = jnp.concatenate([e_far_a, e_far_b], axis=0)
    all_early = (early, e_above, e_far, e_below)
    squares = sum(jnp.sum(e[:, EARLY : EARLY + 3].astype(F32), axis=1) for e in all_early[1:]) + square_part
    inverse_rms = lax.rsqrt(squares / D + epsilon)
    early_all = jnp.concatenate([e[:, :EARLY] for e in all_early] + [three_terms(inverse_rms)], axis=1)
    early_rows = exchange(dispatch(early_all))
    below, above, far = spread_halves(mine[:half], mine[half:])

    weights = (w_gate, w_up, w_down)
    sums = expert_call(where, weights, [mine], [((0,), 0, EARLY, bulk, 0)])
    sums = expert_call(
        where, weights, [*above, *below],
        [((0, 1), 1, EARLY, bulk, 0), ((2, 3), 3, EARLY, bulk, 0)], sums,
    )
    sums = expert_call(
        where, weights, [early_rows],
        [((0,), k, 0, EARLY, k * EARLY) for k in range(n_tp)], sums,
    )
    low, high = (0, half), (half, half)
    hidden, f_low, f_high, a_high, b_low = expert_call(
        where, weights, far, [((0, 1), 2, EARLY, bulk, 0)], sums, inv=early_rows[:, -SIDE:],
        jobs=[
            (2, EARLY, bulk, 0, rows, ((0, 0, half, 0), (1, half, half, 0))),
            (1, EARLY, bulk, *high, ((2, 0, half, 0),)),
            (3, EARLY, bulk, *low, ((3, 0, half, 0),)),
        ],
        outs=[(half, bulk)] * 4,
    )
    (p_early,) = expert_call(
        where, weights, hidden=hidden,
        jobs=[(k, 0, EARLY, 0, rows, ((0, 0, rows, k * EARLY),)) for k in range(n_tp)], outs=[(rows, n_tp * EARLY)],
    )
    a_low, b_high, o_low, o_high = expert_call(
        where, weights, hidden=hidden,
        jobs=[
            (1, EARLY, bulk, *low, ((0, 0, half, 0),)),
            (3, EARLY, bulk, *high, ((1, 0, half, 0),)),
            (0, EARLY, bulk, 0, rows, ((2, 0, half, 0), (3, half, half, 0))),
        ],
        outs=[(half, bulk)] * 4,
    )

    def combine(back):
        return lax.dot_general(weight, back, (((0,), (0,)), ((), ())), preferred_element_type=F32).astype(BF16)

    early_back = combine(exchange(p_early))
    e = [early_back[:, k * EARLY : (k + 1) * EARLY] for k in range(n_tp)]
    out_early = fold(e[0], e[1], e[3], e[2][: tok // 2], e[2][tok // 2 :])
    folded = fold_halves((o_low, o_high), (a_low, a_high), (b_low, b_high), (f_low, f_high))
    out_bulk = combine(exchange(folded))
    return jnp.concatenate([out_early, out_bulk], axis=1)


def solution(mesh):
    placed = (
        P("ep", "tp"),
        P("tp"),
        P("ep", None),
        P("ep", None),
        P("ep", None, "tp"),
        P("ep", None, "tp"),
        P("ep", "tp", None),
    )

    return jax.shard_map(local, mesh=mesh, in_specs=placed, out_specs=P("ep", "tp"), check_vma=False)
```

time: 188 us -> 187 us (level)
  waiting for transfers between devices: 78.3 us -> 72.1 us
  starting transfers between devices: 53.5 us -> 59.1 us
    ppermute x0 -> x12, waiting for transfers between devices: none -> 48.7 us  [the longest x1 19.9 us: fold_halves(): lax.ppermute(far[1], 'tp', dn)]
    ppermute x4 -> x2, waiting for transfers between devices: 25.8 us -> 0.01 us  [spread(): below, above = (lax.ppermute(x, 'tp', up), lax.ppermute(x, 'tp', dn))]
    ppermute x2 -> x1, waiting for transfers between devices: 24.4 us -> 0.01 us  [fold(): lax.ppermute(sum_dn, 'tp', dn)]
    ppermute x0 -> x12, starting transfers between devices: none -> 14.7 us  [the longest x1 3.58 us: fold_halves(): up_high = lax.ppermute(add(below[1], got_high), 'tp', dn)]
    ppermute x2 -> x1, starting transfers between devices: 5.68 us -> 2.1 us  [fold(): lax.ppermute(sum_dn, 'tp', dn)]
    all_to_all x4, waiting for transfers between devices: 16 us -> 12.6 us  [exchange(): lax.all_to_all(shaped, 'ep', 0, 0, tiled=True).reshape(rows, x.shape[1])]
    unnamed x26, local copies, waits for them, and re-layouts: 4 us -> 7.17 us
    ppermute x2 -> x1, starting transfers between devices: 5.67 us -> 2.72 us  [spread(): lax.ppermute(above[half:], 'tp', dn)]
  transfers between devices with their start and end apart: 20 -> 24, of which waited for: 7 -> 11; matrix products, arithmetic and copies ran while one was open for 8% -> 7% of each run, Pallas kernels for 13% -> 13%
where the time goes in v1:
time: 187 us; the launch traced here: 186 us
  waiting for transfers between devices  72.1 us (39%)
  starting transfers between devices  59.1 us (32%)
  Pallas kernels  29.8 us (16%)
  local copies, waits for them, and re-layouts  9.79 us (5%)
  other arithmetic  7.42 us (4%)
  matrix products  7.29 us (4%)
    all_to_all x4, starting transfers between devices, exchange(): lax.all_to_all(shaped, 'ep', 0, 0, tiled=True).reshape(rows, x.shape[1])  30.8 us
    pallas_call x6, Pallas kernels, expert_call(): pl.pallas_call(body, in_specs=[pl.BlockSpec(memory_space=pltpu.SMEM)] + [...  29.8 us
    ppermute x1, waiting for transfers between devices, fold_halves(): lax.ppermute(far[1], 'tp', dn)  19.9 us
    all_to_all x4, waiting for transfers between devices, exchange(): lax.all_to_all(shaped, 'ep', 0, 0, tiled=True).reshape(rows, x.shape[1])  12.6 us
    ppermute x1, waiting for transfers between devices, spread_halves(): lax.ppermute(low, 'tp', up)  11.8 us
    ppermute x1, waiting for transfers between devices, fold_halves(): up_high = lax.ppermute(add(below[1], got_high), 'tp', dn)  10.6 us
    unnamed x26, local copies, waits for them, and re-layouts  7.17 us
    ppermute x1, waiting for transfers between devices, spread_halves(): lax.ppermute(low, 'tp', dn)  4.6 us
  transfers between devices with their start and end apart: 24, of which 11 were waited for; matrix products, arithmetic and copies ran while one was open for 7% of the time, Pallas kernels for 13%

profile of v1, /device:TPU:1, one launch (start us, length us, event | category | flops | bytes accessed | tf_op | source)
XLA Modules:
  0.0 185.9 jit_solution(4176660512695329801)
XLA Ops:
  0.7 1.5 fusion.3
  2.5 0.8 fusion.6
  3.2 2.5 %collective-permute-start.5 = (bf16[256,768]{1,0:T(8,128)(2,1)}, bf16[256,768]{1,0:T(8,128)(2,1)S(1)}, u32[]{:S(2)}, u32[]{:S(2)}) collective-permute-start(bf16[256,768]{1,0:T(8,128)(2,1)} %fusion.6), channel_id=1, source_target_pairs={{0,1},{1,2},{2,3},{3,0},{4,5},{5,6},{6,7},{7,4},{8,9},{9,10},{10,1... | collective-permute-start | bytes 1179656 | tf_op jit(solution)/shard_map/ppermute | solution.py:152
  5.7 2.1 %collective-permute-start.4 = (bf16[256,768]{1,0:T(8,128)(2,1)}, bf16[256,768]{1,0:T(8,128)(2,1)S(1)}, u32[]{:S(2)}, u32[]{:S(2)}) collective-permute-start(bf16[256,768]{1,0:T(8,128)(2,1)} %fusion.6), channel_id=1, source_target_pairs={{0,3},{1,0},{2,1},{3,2},{4,7},{5,4},{6,5},{7,6},{8,11},{9,8},{10,9... | collective-permute-start | bytes 1179656 | tf_op jit(solution)/shard_map/ppermute | solution.py:152
  8.3 1.6 convolution_convert_fusion.1
  9.8 8.0 %all-to-all-start = ((bf16[32,16,1152]{2,1,0:T(8,128)(2,1)}), bf16[32,16,1152]{2,1,0:T(8,128)(2,1)S(1)}, u32[]{:S(2)}, u32[]{:S(2)}) async-start(bf16[32,16,1152]{2,1,0:T(8,128)(2,1)} %bitcast.4), calls=%async_computation | async-start | bytes 2359296 | tf_op jit(solution)/shard_map/all_to_all | solution.py:181
  18.0 2.7 %collective-permute-start.7 = (bf16[128,768]{1,0:T(8,128)(2,1)S(1)}, bf16[128,768]{1,0:T(8,128)(2,1)S(1)}, u32[]{:S(2)}, u32[]{:S(2)}) collective-permute-start(bf16[128,768]{1,0:T(8,128)(2,1)S(1)} %slice.89), channel_id=1, source_target_pairs={{0,3},{1,0},{2,1},{3,2},{4,7},{5,4},{6,5},{7,6},{8,11},{9,8},{10,9... | collective-permute-start | bytes 589832 | tf_op jit(solution)/shard_map/ppermute | solution.py:153
  21.0 4.4 %collective-permute-done.6 = bf16[128,768]{1,0:T(8,128)(2,1)S(1)} collective-permute-done((bf16[128,768]{1,0:T(8,128)(2,1)S(1)}, bf16[128,768]{1,0:T(8,128)(2,1)S(1)}, u32[]{:S(2)}, u32[]{:S(2)}) %collective-permute-start.6) | collective-permute-done | bytes 196640 | tf_op jit(solution)/shard_map/ppermute | solution.py:153
  25.9 2.4 %convolution_convert_fusion = bf16[512,2688]{1,0:T(8,128)(2,1)} fusion(pred[512,256]{1,0:T(32,128)(4,1)S(1)} %bitcast_compare_fusion, bf16[256,2688]{1,0:T(8,128)(2,1)S(1)} %pad_dynamic-update-slice_fusion), kind=kOutput, calls=%fused_computation | convolution fusion | flops 706019328 | bytes 4259840 | tf_op jit(solution)/shard_map/dot_general | solution.py:189
  28.3 8.1 %all-to-all-done = bf16[32,16,1152]{2,1,0:T(8,128)(2,1)S(1)} async-done(((bf16[32,16,1152]{2,1,0:T(8,128)(2,1)}), bf16[32,16,1152]{2,1,0:T(8,128)(2,1)S(1)}, u32[]{:S(2)}, u32[]{:S(2)}) %all-to-all-start) | async-done | bytes 1179680 | tf_op jit(solution)/shard_map/all_to_all | solution.py:181
  36.4 1.0 copy-done
  37.4 4.1 %all-to-all-start.1 = ((bf16[32,16,2688]{2,1,0:T(8,128)(2,1)}), bf16[32,16,2688]{2,1,0:T(8,128)(2,1)S(1)}, u32[]{:S(2)}, u32[]{:S(2)}) async-start(bf16[32,16,2688]{2,1,0:T(8,128)(2,1)} %bitcast.47), calls=%async_computation.1 | async-start | bytes 5505024 | tf_op jit(solution)/shard_map/all_to_all | solution.py:181
  41.6 2.4 %fusion.21 = (bf16[16,16,1152]{2,1,0:T(8,128)(2,1)}, bf16[16,16,1152]{2,1,0:T(8,128)(2,1)}) fusion(bf16[32,16,1152]{2,1,0:T(8,128)(2,1)} %copy-done), kind=kLoop, calls=%fused_computation.67 | loop fusion | bytes 2359296 | tf_op jit(solution)/shard_map/slice | solution.py:201
  43.9 2.7 %collective-permute-start.2 = (bf16[256,1152]{1,0:T(8,128)(2,1)}, bf16[256,1152]{1,0:T(8,128)(2,1)}, u32[]{:S(2)}, u32[]{:S(2)}) collective-permute-start(bf16[256,1152]{1,0:T(8,128)(2,1)} %bitcast.6), channel_id=1, source_target_pairs={{0,3},{1,0},{2,1},{3,2},{4,7},{5,4},{6,5},{7,6},{8,11},{9,8},{10,9... | collective-permute-start | bytes 1769480 | tf_op jit(solution)/shard_map/ppermute | solution.py:164
  47.1 0.9 collective-permute-start.9
  48.1 11.8 %collective-permute-done.refs_2_ = bf16[256,1152]{1,0:T(8,128)(2,1)S(1)} collective-permute-done((bf16[256,1152]{1,0:T(8,128)(2,1)}, bf16[256,1152]{1,0:T(8,128)(2,1)S(1)}, u32[]{:S(2)}, u32[]{:S(2)}) %collective-permute-start) | collective-permute-done | bytes 589856 | tf_op jit(solution)/shard_map/ppermute | solution.py:164
  59.9 2.7 %collective-permute-start.3 = (bf16[256,1152]{1,0:T(8,128)(2,1)}, bf16[256,1152]{1,0:T(8,128)(2,1)}, u32[]{:S(2)}, u32[]{:S(2)}) collective-permute-start(bf16[256,1152]{1,0:T(8,128)(2,1)} %collective-permute-done.2.refs_1_), channel_id=1, source_target_pairs={{0,3},{1,0},{2,1},{3,2},{4,7},{5,4},{6,5},{7,6},{8,11},{9,8},{10,9... | collective-permute-start | bytes 1769480 | tf_op jit(solution)/shard_map/ppermute | solution.py:166
  62.6 1.3 copy-done.1
  63.8 3.2 %shard_map.73 = (f32[512,512]{1,0:T(8,128)S(1)}, f32[512,512]{1,0:T(8,128)S(1)}) custom-call(s32[1]{0:T(128)} %bitcast.2.where_ref, bf16[512,1152]{1,0:T(8,128)(2,1)S(1)} %bitcast.35, bf16[7168,512]{1,0:T(8,128)(2,1)} %bitcast.36, bf16[7168,512]{1,0:T(8,128)(2,1)} %bitcast.40), custom_call_target="tpu_custom_call" | custom-call | flops 1207959552 | bytes 4718592 | tf_op jit(solution)/shard_map/pallas_call | solution.py:104
  67.0 4.6 %collective-permute-done.8.refs_0_ = bf16[256,1152]{1,0:T(8,128)(2,1)} collective-permute-done((bf16[256,1152]{1,0:T(8,128)(2,1)}, bf16[256,1152]{1,0:T(8,128)(2,1)}, u32[]{:S(2)}, u32[]{:S(2)}) %collective-permute-start.8) | collective-permute-done | bytes 589856 | tf_op jit(solution)/shard_map/ppermute | solution.py:165
  71.6 1.0 collective-permute-done.9.refs_3_
  72.6 6.2 %shard_map.74 = (f32[512,512]{1,0:T(8,128)S(1)}, f32[512,512]{1,0:T(8,128)S(1)}) custom-call(s32[1]{0:T(128)} %bitcast.2.where_ref, bf16[256,1152]{1,0:T(8,128)(2,1)} %collective-permute-done.8.refs_0_, bf16[256,1152]{1,0:T(8,128)(2,1)} %collective-permute-done.2.refs_1_, bf16[256,1152]{1,0:T(8,128)(2,1)S(1)} %collective-permute-done.refs_2_, ...), custom_call_target="tpu_custom_call" | custom-call | flops 2415919104 | bytes 9437184 | tf_op jit(solution)/shard_map/pallas_call | solution.py:104
  78.9 1.0 copy-done.2
  79.8 1.0 copy-done.4
  80.9 1.2 copy-done.3
  82.1 1.2 copy-done.5
  83.3 5.2 %shard_map.75 = (f32[512,512]{1,0:T(8,128)S(1)}, f32[512,512]{1,0:T(8,128)S(1)}) custom-call(s32[1]{0:T(128)} %bitcast.2.where_ref, bf16[512,2688]{1,0:T(8,128)(2,1)S(1)} %bitcast.34, f32[512,512]{1,0:T(8,128)S(1)} %copy-done.3, f32[512,512]{1,0:T(8,128)S(1)} %copy-done.5, bf16[7168,512]{1,0:T(8,128)(2,1)} %bitcast.38, bf16[7168,512]{1,0:T(8,128)(2,1)} %bitcast.42), custom_call_target="tpu_custom_call" | custom-call | flops 2684354560 | bytes 10485760 | tf_op jit(solution)/shard_map/pallas_call | solution.py:104
  88.6 6.6 %shard_map.76 = (bf16[512,512]{1,0:T(8,128)(2,1)S(1)}, bf16[256,1152]{1,0:T(8,128)(2,1)S(1)}, bf16[256,1152]{1,0:T(8,128)(2,1)S(1)}, bf16[256,1152]{1,0:T(8,128)(2,1)S(1)}, bf16[256,1152]{1,0:T(8,128)(2,1)S(1)}) custom-call(s32[1]{0:T(128)} %bitcast.2.where_ref, bf16[256,1152]{1,0:T(8,128)(2,1)} %collective-permute-done.1.refs_0_, ...), custom_call_target="tpu_custom_call" | custom-call | flops 2415919104 | bytes 9437184 | tf_op jit(solution)/shard_map/pallas_call | solution.py:104
  95.2 5.5 %shard_map.77 = bf16[512,2560]{1,0:T(8,128)(2,1)} custom-call(s32[1]{0:T(128)} %bitcast.2.where_ref, bf16[512,512]{1,0:T(8,128)(2,1)S(1)} %get-tuple-element.26.refs_0_, bf16[512,7168]{1,0:T(8,128)(2,1)} %bitcast.45), custom_call_target="tpu_custom_call" | custom-call | flops 1342177280 | bytes 5242880 | tf_op jit(solution)/shard_map/pallas_call | solution.py:104
  100.7 9.8 %all-to-all-start.2 = ((bf16[32,16,2560]{2,1,0:T(8,128)(2,1)}), bf16[32,16,2560]{2,1,0:T(8,128)(2,1)}, u32[]{:S(2)}, u32[]{:S(2)}) async-start(bf16[32,16,2560]{2,1,0:T(8,128)(2,1)} %bitcast.15), calls=%async_computation.2 | async-start | bytes 5242880 | tf_op jit(solution)/shard_map/all_to_all | solution.py:181
  110.5 2.5 %collective-permute-start.16 = (bf16[256,1152]{1,0:T(8,128)(2,1)S(1)}, bf16[256,1152]{1,0:T(8,128)(2,1)S(1)}, u32[]{:S(2)}, u32[]{:S(2)}) collective-permute-start(bf16[256,1152]{1,0:T(8,128)(2,1)S(1)} %get-tuple-element.30), channel_id=1, source_target_pairs={{0,3},{1,0},{2,1},{3,2},{4,7},{5,4},{6,5},{7,6},{8,11},{9,8},{10,9... | collective-permute-start | bytes 1769480 | tf_op jit(solution)/shard_map/ppermute | solution.py:174
  113.0 1.7 collective-permute-start.18
  114.7 3.2 %shard_map.78 = (bf16[256,1152]{1,0:T(8,128)(2,1)S(1)}, bf16[256,1152]{1,0:T(8,128)(2,1)S(1)}, bf16[256,1152]{1,0:T(8,128)(2,1)S(1)}, bf16[256,1152]{1,0:T(8,128)(2,1)S(1)}) custom-call(s32[1]{0:T(128)} %bitcast.2.where_ref, bf16[512,512]{1,0:T(8,128)(2,1)S(1)} %get-tuple-element.26.refs_0_, bf16[512,7168]{1,0:T(8,128)(2,1)} %bitcast.46), custom_call_target="tpu_custom_call" | custom-call | flops 1207959552 | bytes 4718592 | tf_op jit(solution)/shard_map/pallas_call | solution.py:104
  118.1 19.9 %collective-permute-done.18 = bf16[256,1152]{1,0:T(8,128)(2,1)S(1)} collective-permute-done((bf16[256,1152]{1,0:T(8,128)(2,1)S(1)}, bf16[256,1152]{1,0:T(8,128)(2,1)S(1)}, u32[]{:S(2)}, u32[]{:S(2)}) %collective-permute-start.18) | collective-permute-done | bytes 589856 | tf_op jit(solution)/shard_map/ppermute | solution.py:173
  138.2 3.6 %collective-permute-start.19 = (bf16[256,1152]{1,0:T(8,128)(2,1)S(1)}, bf16[256,1152]{1,0:T(8,128)(2,1)S(1)}, u32[]{:S(2)}, u32[]{:S(2)}) collective-permute-start(bf16[256,1152]{1,0:T(8,128)(2,1)S(1)} %add_convert_fusion.1), channel_id=1, source_target_pairs={{0,3},{1,0},{2,1},{3,2},{4,7},{5,4},{6,5},{7,6},{8,11},{9,8},{10,9... | collective-permute-start | bytes 1769480 | tf_op jit(solution)/shard_map/ppermute | solution.py:176
  141.8 0.8 collective-permute-done.15
  142.8 10.6 %collective-permute-done.19 = bf16[256,1152]{1,0:T(8,128)(2,1)S(1)} collective-permute-done((bf16[256,1152]{1,0:T(8,128)(2,1)S(1)}, bf16[256,1152]{1,0:T(8,128)(2,1)S(1)}, u32[]{:S(2)}, u32[]{:S(2)}) %collective-permute-start.19) | collective-permute-done | bytes 589856 | tf_op jit(solution)/shard_map/ppermute | solution.py:176
  153.6 1.1 pad_maximum_fusion
  154.8 8.8 %all-to-all-start.3 = ((bf16[32,16,1152]{2,1,0:T(8,128)(2,1)}), bf16[32,16,1152]{2,1,0:T(8,128)(2,1)S(1)}, u32[]{:S(2)}, u32[]{:S(2)}) async-start(bf16[32,16,1152]{2,1,0:T(8,128)(2,1)} %bitcast.17), calls=%async_computation.3 | async-start | bytes 2359296 | tf_op jit(solution)/shard_map/all_to_all | solution.py:181
  163.6 2.6 %fusion = bf16[256,2560]{1,0:T(8,128)(2,1)S(1)} fusion(bf16[32,16,2560]{2,1,0:T(8,128)(2,1)} %all-to-all-done.2, bf16[32,256]{1,0:T(8,128)(2,1)S(1)} %select_reduce_fusion, f32[32,256]{1,0:T(8,128)S(1)} %copy-done.7), kind=kOutput, calls=%fused_computation.2 | convolution fusion | flops 672006144 | bytes 3981312 | tf_op jit(solution)/shard_map/dot_general | solution.py:238
  166.3 1.1 collective-permute-start.10
  167.4 2.5 %collective-permute-start.12 = (bf16[128,640]{1,0:T(8,128)(2,1)S(1)}, bf16[128,640]{1,0:T(8,128)(2,1)S(1)}, u32[]{:S(2)}, u32[]{:S(2)}) collective-permute-start(bf16[128,640]{1,0:T(8,128)(2,1)S(1)} %get-tuple-element.40), channel_id=1, source_target_pairs={{0,3},{1,0},{2,1},{3,2},{4,7},{5,4},{6,5},{7,6},{8,11},{9,8},{10,9... | collective-permute-start | bytes 491528 | tf_op jit(solution)/shard_map/ppermute | solution.py:157
  169.8 4.3 %collective-permute-done.10 = bf16[128,640]{1,0:T(8,128)(2,1)S(1)} collective-permute-done((bf16[128,640]{1,0:T(8,128)(2,1)S(1)}, bf16[128,640]{1,0:T(8,128)(2,1)S(1)}, u32[]{:S(2)}, u32[]{:S(2)}) %collective-permute-start.10) | collective-permute-done | bytes 163872 | tf_op jit(solution)/shard_map/ppermute | solution.py:157
  174.1 0.8 add_convert_fusion.6
  175.5 2.1 %collective-permute-start.13 = (bf16[256,640]{1,0:T(8,128)(2,1)S(1)}, bf16[256,640]{1,0:T(8,128)(2,1)S(1)}, u32[]{:S(2)}, u32[]{:S(2)}) collective-permute-start(bf16[256,640]{1,0:T(8,128)(2,1)S(1)} %get-tuple-element.38), channel_id=1, source_target_pairs={{0,3},{1,0},{2,1},{3,2},{4,7},{5,4},{6,5},{7,6},{8,11},{9,8},{10,9... | collective-permute-start | bytes 983048 | tf_op jit(solution)/shard_map/ppermute | solution.py:160
  177.6 4.6 %all-to-all-done.3 = bf16[32,16,1152]{2,1,0:T(8,128)(2,1)S(1)} async-done(((bf16[32,16,1152]{2,1,0:T(8,128)(2,1)}), bf16[32,16,1152]{2,1,0:T(8,128)(2,1)S(1)}, u32[]{:S(2)}, u32[]{:S(2)}) %all-to-all-start.3) | async-done | bytes 1179680 | tf_op jit(solution)/shard_map/all_to_all | solution.py:181
  182.7 2.1 %collective-permute-done.11 = bf16[256,640]{1,0:T(8,128)(2,1)S(1)} collective-permute-done((bf16[256,640]{1,0:T(8,128)(2,1)}, bf16[256,640]{1,0:T(8,128)(2,1)S(1)}, u32[]{:S(2)}, u32[]{:S(2)}) %collective-permute-start.11) | collective-permute-done | bytes 327712 | tf_op jit(solution)/shard_map/ppermute | solution.py:160
  184.9 1.0 pad_maximum_fusion.1
  (71 shorter events, 5.0 us)
Async XLA Ops:
  2.2 5.6 %copy-start.8 = (s32[256,8]{0,1:T(8,128)S(1)}, s32[256,8]{0,1:T(8,128)}, u32[]{:S(2)}) copy-start(s32[256,8]{0,1:T(8,128)} %param.9) | copy-start | bytes 24580
  3.2 14.6 %collective-permute-start.5 = (bf16[256,768]{1,0:T(8,128)(2,1)}, bf16[256,768]{1,0:T(8,128)(2,1)S(1)}, u32[]{:S(2)}, u32[]{:S(2)}) collective-permute-start(bf16[256,768]{1,0:T(8,128)(2,1)} %fusion.6), channel_id=1, source_target_pairs={{0,1},{1,2},{2,3},{3,0},{4,5},{5,6},{6,7},{7,4},{8,9},{9,10},{10,1... | collective-permute-start | bytes 1179656 | tf_op jit(solution)/shard_map/ppermute | solution.py:152
  5.7 12.3 %collective-permute-start.4 = (bf16[256,768]{1,0:T(8,128)(2,1)}, bf16[256,768]{1,0:T(8,128)(2,1)S(1)}, u32[]{:S(2)}, u32[]{:S(2)}) collective-permute-start(bf16[256,768]{1,0:T(8,128)(2,1)} %fusion.6), channel_id=1, source_target_pairs={{0,3},{1,0},{2,1},{3,2},{4,7},{5,4},{6,5},{7,6},{8,11},{9,8},{10,9... | collective-permute-start | bytes 1179656 | tf_op jit(solution)/shard_map/ppermute | solution.py:152
  8.1 1.7 copy-start.6
  9.8 26.6 %all-to-all-start = ((bf16[32,16,1152]{2,1,0:T(8,128)(2,1)}), bf16[32,16,1152]{2,1,0:T(8,128)(2,1)S(1)}, u32[]{:S(2)}, u32[]{:S(2)}) async-start(bf16[32,16,1152]{2,1,0:T(8,128)(2,1)} %bitcast.4), calls=%async_computation | async-start | bytes 2359296 | tf_op jit(solution)/shard_map/all_to_all | solution.py:181
  17.9 7.5 %collective-permute-start.6 = (bf16[128,768]{1,0:T(8,128)(2,1)S(1)}, bf16[128,768]{1,0:T(8,128)(2,1)S(1)}, u32[]{:S(2)}, u32[]{:S(2)}) collective-permute-start(bf16[128,768]{1,0:T(8,128)(2,1)S(1)} %slice.88), channel_id=1, source_target_pairs={{0,1},{1,2},{2,3},{3,0},{4,5},{5,6},{6,7},{7,4},{8,9},{9,10},{10,1... | collective-permute-start | bytes 589832 | tf_op jit(solution)/shard_map/ppermute | solution.py:153
  18.0 7.4 %collective-permute-start.7 = (bf16[128,768]{1,0:T(8,128)(2,1)S(1)}, bf16[128,768]{1,0:T(8,128)(2,1)S(1)}, u32[]{:S(2)}, u32[]{:S(2)}) collective-permute-start(bf16[128,768]{1,0:T(8,128)(2,1)S(1)} %slice.89), channel_id=1, source_target_pairs={{0,3},{1,0},{2,1},{3,2},{4,7},{5,4},{6,5},{7,6},{8,11},{9,8},{10,9... | collective-permute-start | bytes 589832 | tf_op jit(solution)/shard_map/ppermute | solution.py:153
  36.4 1.1 copy-start
  37.4 43.4 %all-to-all-start.1 = ((bf16[32,16,2688]{2,1,0:T(8,128)(2,1)}), bf16[32,16,2688]{2,1,0:T(8,128)(2,1)S(1)}, u32[]{:S(2)}, u32[]{:S(2)}) async-start(bf16[32,16,2688]{2,1,0:T(8,128)(2,1)} %bitcast.47), calls=%async_computation.1 | async-start | bytes 5505024 | tf_op jit(solution)/shard_map/all_to_all | solution.py:181
  43.9 16.0 %collective-permute-start = (bf16[256,1152]{1,0:T(8,128)(2,1)}, bf16[256,1152]{1,0:T(8,128)(2,1)S(1)}, u32[]{:S(2)}, u32[]{:S(2)}) collective-permute-start(bf16[256,1152]{1,0:T(8,128)(2,1)} %bitcast.5), channel_id=1, source_target_pairs={{0,1},{1,2},{2,3},{3,0},{4,5},{5,6},{6,7},{7,4},{8,9},{9,10},{10,1... | collective-permute-start | bytes 1769480 | tf_op jit(solution)/shard_map/ppermute | solution.py:164
  43.9 16.0 %collective-permute-start.2 = (bf16[256,1152]{1,0:T(8,128)(2,1)}, bf16[256,1152]{1,0:T(8,128)(2,1)}, u32[]{:S(2)}, u32[]{:S(2)}) collective-permute-start(bf16[256,1152]{1,0:T(8,128)(2,1)} %bitcast.6), channel_id=1, source_target_pairs={{0,3},{1,0},{2,1},{3,2},{4,7},{5,4},{6,5},{7,6},{8,11},{9,8},{10,9... | collective-permute-start | bytes 1769480 | tf_op jit(solution)/shard_map/ppermute | solution.py:164
  46.6 25.0 %collective-permute-start.8 = (bf16[256,1152]{1,0:T(8,128)(2,1)}, bf16[256,1152]{1,0:T(8,128)(2,1)}, u32[]{:S(2)}, u32[]{:S(2)}) collective-permute-start(bf16[256,1152]{1,0:T(8,128)(2,1)} %bitcast.5), channel_id=1, source_target_pairs={{0,3},{1,0},{2,1},{3,2},{4,7},{5,4},{6,5},{7,6},{8,11},{9,8},{10,9... | collective-permute-start | bytes 1769480 | tf_op jit(solution)/shard_map/ppermute | solution.py:165
  47.1 25.5 %collective-permute-start.9 = (bf16[256,1152]{1,0:T(8,128)(2,1)}, bf16[256,1152]{1,0:T(8,128)(2,1)}, u32[]{:S(2)}, u32[]{:S(2)}) collective-permute-start(bf16[256,1152]{1,0:T(8,128)(2,1)} %bitcast.6), channel_id=1, source_target_pairs={{0,1},{1,2},{2,3},{3,0},{4,5},{5,6},{6,7},{7,4},{8,9},{9,10},{10,1... | collective-permute-start | bytes 1769480 | tf_op jit(solution)/shard_map/ppermute | solution.py:165
  59.9 28.6 %collective-permute-start.1 = (bf16[256,1152]{1,0:T(8,128)(2,1)S(1)}, bf16[256,1152]{1,0:T(8,128)(2,1)}, u32[]{:S(2)}, u32[]{:S(2)}) collective-permute-start(bf16[256,1152]{1,0:T(8,128)(2,1)S(1)} %collective-permute-done.refs_2_), channel_id=1, source_target_pairs={{0,1},{1,2},{2,3},{3,0},{4,5},{5,6},{6,7},{7,4},{8,9},{9,10},{10,1... | collective-permute-start | bytes 1769480 | tf_op jit(solution)/shard_map/ppermute | solution.py:166
  59.9 28.6 %collective-permute-start.3 = (bf16[256,1152]{1,0:T(8,128)(2,1)}, bf16[256,1152]{1,0:T(8,128)(2,1)}, u32[]{:S(2)}, u32[]{:S(2)}) collective-permute-start(bf16[256,1152]{1,0:T(8,128)(2,1)} %collective-permute-done.2.refs_1_), channel_id=1, source_target_pairs={{0,3},{1,0},{2,1},{3,2},{4,7},{5,4},{6,5},{7,6},{8,11},{9,8},{10,9... | collective-permute-start | bytes 1769480 | tf_op jit(solution)/shard_map/ppermute | solution.py:166
  62.6 1.3 copy-start.1
  78.9 1.0 copy-start.2
  79.8 1.0 copy-start.4
  80.8 1.2 copy-start.3
  82.1 1.2 copy-start.5
  88.5 6.7 %copy-start.9 = (bf16[256,8]{0,1:T(8,128)(2,1)S(1)}, bf16[256,8]{0,1:T(8,128)(2,1)}, u32[]{:S(2)}) copy-start(bf16[256,8]{0,1:T(8,128)(2,1)} %param.10) | copy-start | bytes 12292
  95.1 22.7 %collective-permute-start.14 = (bf16[256,1152]{1,0:T(8,128)(2,1)S(1)}, bf16[256,1152]{1,0:T(8,128)(2,1)S(1)}, u32[]{:S(2)}, u32[]{:S(2)}) collective-permute-start(bf16[256,1152]{1,0:T(8,128)(2,1)S(1)} %get-tuple-element.29), channel_id=1, source_target_pairs={{0,1},{1,2},{2,3},{3,0},{4,5},{5,6},{6,7},{7,4},{8,9},{9,10},{10,1... | collective-permute-start | bytes 1769480 | tf_op jit(solution)/shard_map/ppermute | solution.py:173
  100.7 54.0 %all-to-all-start.2 = ((bf16[32,16,2560]{2,1,0:T(8,128)(2,1)}), bf16[32,16,2560]{2,1,0:T(8,128)(2,1)}, u32[]{:S(2)}, u32[]{:S(2)}) async-start(bf16[32,16,2560]{2,1,0:T(8,128)(2,1)} %bitcast.15), calls=%async_computation.2 | async-start | bytes 5242880 | tf_op jit(solution)/shard_map/all_to_all | solution.py:181
  110.5 31.3 %collective-permute-start.16 = (bf16[256,1152]{1,0:T(8,128)(2,1)S(1)}, bf16[256,1152]{1,0:T(8,128)(2,1)S(1)}, u32[]{:S(2)}, u32[]{:S(2)}) collective-permute-start(bf16[256,1152]{1,0:T(8,128)(2,1)S(1)} %get-tuple-element.30), channel_id=1, source_target_pairs={{0,3},{1,0},{2,1},{3,2},{4,7},{5,4},{6,5},{7,6},{8,11},{9,8},{10,9... | collective-permute-start | bytes 1769480 | tf_op jit(solution)/shard_map/ppermute | solution.py:174
  113.0 25.0 %collective-permute-start.18 = (bf16[256,1152]{1,0:T(8,128)(2,1)S(1)}, bf16[256,1152]{1,0:T(8,128)(2,1)S(1)}, u32[]{:S(2)}, u32[]{:S(2)}) collective-permute-start(bf16[256,1152]{1,0:T(8,128)(2,1)S(1)} %get-tuple-element.34), channel_id=1, source_target_pairs={{0,3},{1,0},{2,1},{3,2},{4,7},{5,4},{6,5},{7,6},{8,11},{9,8},{10,9... | collective-permute-start | bytes 1769480 | tf_op jit(solution)/shard_map/ppermute | solution.py:173
  114.7 28.1 %collective-permute-start.17 = (bf16[256,1152]{1,0:T(8,128)(2,1)S(1)}, bf16[256,1152]{1,0:T(8,128)(2,1)S(1)}, u32[]{:S(2)}, u32[]{:S(2)}) collective-permute-start(bf16[256,1152]{1,0:T(8,128)(2,1)S(1)} %get-tuple-element.32), channel_id=1, source_target_pairs={{0,1},{1,2},{2,3},{3,0},{4,5},{5,6},{6,7},{7,4},{8,9},{9,10},{10,1... | collective-permute-start | bytes 1769480 | tf_op jit(solution)/shard_map/ppermute | solution.py:174
  118.0 24.5 %collective-permute-start.15 = (bf16[256,1152]{1,0:T(8,128)(2,1)S(1)}, bf16[256,1152]{1,0:T(8,128)(2,1)S(1)}, u32[]{:S(2)}, u32[]{:S(2)}) collective-permute-start(bf16[256,1152]{1,0:T(8,128)(2,1)S(1)} %add_convert_fusion.3), channel_id=1, source_target_pairs={{0,1},{1,2},{2,3},{3,0},{4,5},{5,6},{6,7},{7,4},{8,9},{9,10},{10,1... | collective-permute-start | bytes 1769480 | tf_op jit(solution)/shard_map/ppermute | solution.py:175
  138.2 15.2 %collective-permute-start.19 = (bf16[256,1152]{1,0:T(8,128)(2,1)S(1)}, bf16[256,1152]{1,0:T(8,128)(2,1)S(1)}, u32[]{:S(2)}, u32[]{:S(2)}) collective-permute-start(bf16[256,1152]{1,0:T(8,128)(2,1)S(1)} %add_convert_fusion.1), channel_id=1, source_target_pairs={{0,3},{1,0},{2,1},{3,2},{4,7},{5,4},{6,5},{7,6},{8,11},{9,8},{10,9... | collective-permute-start | bytes 1769480 | tf_op jit(solution)/shard_map/ppermute | solution.py:176
  154.8 8.9 %copy-start.7 = (f32[32,256]{1,0:T(8,128)S(1)}, f32[32,256]{1,0:T(8,128)}, u32[]{:S(2)}) copy-start(f32[32,256]{1,0:T(8,128)} %copy-done.6) | copy-start | bytes 98308
  154.8 27.4 %all-to-all-start.3 = ((bf16[32,16,1152]{2,1,0:T(8,128)(2,1)}), bf16[32,16,1152]{2,1,0:T(8,128)(2,1)S(1)}, u32[]{:S(2)}, u32[]{:S(2)}) async-start(bf16[32,16,1152]{2,1,0:T(8,128)(2,1)} %bitcast.17), calls=%async_computation.3 | async-start | bytes 2359296 | tf_op jit(solution)/shard_map/all_to_all | solution.py:181
  166.3 7.8 %collective-permute-start.10 = (bf16[128,640]{1,0:T(8,128)(2,1)S(1)}, bf16[128,640]{1,0:T(8,128)(2,1)S(1)}, u32[]{:S(2)}, u32[]{:S(2)}) collective-permute-start(bf16[128,640]{1,0:T(8,128)(2,1)S(1)} %get-tuple-element.39), channel_id=1, source_target_pairs={{0,1},{1,2},{2,3},{3,0},{4,5},{5,6},{6,7},{7,4},{8,9},{9,10},{10,1... | collective-permute-start | bytes 491528 | tf_op jit(solution)/shard_map/ppermute | solution.py:157
  167.4 6.7 %collective-permute-start.12 = (bf16[128,640]{1,0:T(8,128)(2,1)S(1)}, bf16[128,640]{1,0:T(8,128)(2,1)S(1)}, u32[]{:S(2)}, u32[]{:S(2)}) collective-permute-start(bf16[128,640]{1,0:T(8,128)(2,1)S(1)} %get-tuple-element.40), channel_id=1, source_target_pairs={{0,3},{1,0},{2,1},{3,2},{4,7},{5,4},{6,5},{7,6},{8,11},{9,8},{10,9... | collective-permute-start | bytes 491528 | tf_op jit(solution)/shard_map/ppermute | solution.py:157
  174.9 9.9 %collective-permute-start.11 = (bf16[256,640]{1,0:T(8,128)(2,1)}, bf16[256,640]{1,0:T(8,128)(2,1)S(1)}, u32[]{:S(2)}, u32[]{:S(2)}) collective-permute-start(bf16[256,640]{1,0:T(8,128)(2,1)} %get-tuple-element.37), channel_id=1, source_target_pairs={{0,1},{1,2},{2,3},{3,0},{4,5},{5,6},{6,7},{7,4},{8,9},{9,10},{10,1... | collective-permute-start | bytes 983048 | tf_op jit(solution)/shard_map/ppermute | solution.py:160
  175.5 9.3 %collective-permute-start.13 = (bf16[256,640]{1,0:T(8,128)(2,1)S(1)}, bf16[256,640]{1,0:T(8,128)(2,1)S(1)}, u32[]{:S(2)}, u32[]{:S(2)}) collective-permute-start(bf16[256,640]{1,0:T(8,128)(2,1)S(1)} %get-tuple-element.38), channel_id=1, source_target_pairs={{0,3},{1,0},{2,1},{3,2},{4,7},{5,4},{6,5},{7,6},{8,11},{9,8},{10,9... | collective-permute-start | bytes 983048 | tf_op jit(solution)/shard_map/ppermute | solution.py:160

commit v2 on v1

--- a/solution.py
+++ b/solution.py
@@ -9,7 +9,7 @@
 D = 7168
 epsilon = 1e-06
 CAP = 16
-EARLY = 640
+EARLY = 512
 SIDE = 128
 F32, BF16 = jnp.float32, jnp.bfloat16
 
@@ -112,6 +112,24 @@
     )(where, *[pltpu.with_memory_space_constraint(x, pltpu.VMEM) for x in resident], *[pltpu.with_memory_space_constraint(w, pltpu.HBM) for w in streamed])
 
 
+def join_sums(low, high):
+    half, width = low[0].shape
+
+    def body(*refs):
+        out = refs[-1]
+        for k in (0, 1):
+            a, b, c = (r[...].astype(F32) for r in refs[3 * k : 3 * k + 3])
+            out[k * half : (k + 1) * half, :] = (a + b + c).astype(BF16)
+
+    return pl.pallas_call(
+        body,
+        out_shape=jax.ShapeDtypeStruct((2 * half, width), BF16),
+        cost_estimate=pl.CostEstimate(flops=6 * half * width, bytes_accessed=16 * half * width, transcendentals=0),
+        compiler_params=pltpu.CompilerParams(vmem_limit_bytes=16 * 2**20),
+        name="join_sums",
+    )(*low, *high)
+
+
 def place_picks(expert_ids, gate_prob, window):
     ids = expert_ids.T
     probs = gate_prob.T.astype(F32)
@@ -174,7 +192,7 @@
         dn_high, up_low = lax.ppermute(above[1], "tp", up), lax.ppermute(below[0], "tp", dn)
         dn_low = lax.ppermute(add(above[0], got_low), "tp", up)
         up_high = lax.ppermute(add(below[1], got_high), "tp", dn)
-        return jnp.concatenate([add(own[0], dn_low, up_low), add(own[1], dn_high, up_high)], axis=0)
+        return join_sums((own[0], dn_low, up_low), (own[1], dn_high, up_high))
 
     def exchange(x):
         shaped = x.reshape(window, CAP, x.shape[1])
@@ -197,7 +215,8 @@
     squares = sum(jnp.sum(e[:, EARLY : EARLY + 3].astype(F32), axis=1) for e in all_early[1:]) + square_part
     inverse_rms = lax.rsqrt(squares / D + epsilon)
     early_all = jnp.concatenate([e[:, :EARLY] for e in all_early] + [three_terms(inverse_rms)], axis=1)
-    early_rows = exchange(dispatch(early_all))
+    picked = dispatch(early_all)
+    early_rows = exchange(picked)
     below, above, far = spread_halves(mine[:half], mine[half:])
 
     weights = (w_gate, w_up, w_down)

time: 187 us -> 188 us (level)
  waiting for transfers between devices: 72.1 us -> 83.1 us
  local copies, waits for them, and re-layouts: 9.79 us -> 4 us
  other arithmetic: 7.42 us -> 4.4 us
    ppermute x1, waiting for transfers between devices: 19.9 us -> 0.01 us  [fold_halves(): lax.ppermute(far[1], 'tp', dn)]
    ppermute x1, waiting for transfers between devices: 0.01 us -> 13.6 us  [fold_halves(): lax.ppermute(above[1], 'tp', up)]
    ppermute x1, waiting for transfers between devices: 0.75 us -> 14 us  [fold_halves(): dn_low = lax.ppermute(add(above[0], got_low), 'tp', up)]
    ppermute x1, waiting for transfers between devices: 10.6 us -> 0.01 us  [fold_halves(): up_high = lax.ppermute(add(below[1], got_high), 'tp', dn)]
    ppermute x1, waiting for transfers between devices: 0.01 us -> 8.12 us  [fold_halves(): lax.ppermute(far[0], 'tp', up)]
    unnamed x26 -> x18, local copies, waits for them, and re-layouts: 7.17 us -> 2.6 us
    ppermute x1, waiting for transfers between devices: 2.09 us -> 5.31 us  [fold(): lax.ppermute(sum_up, 'tp', up)]
    ppermute x1, waiting for transfers between devices: 4.6 us -> 7.09 us  [spread_halves(): lax.ppermute(low, 'tp', dn)]
  transfers between devices with their start and end apart: 24 -> 24, of which waited for: 11 -> 12; matrix products, arithmetic and copies ran while one was open for 7% -> 5% of each run, Pallas kernels for 13% -> 12%
where the time goes in v2:
time: 188 us; the launch traced here: 187 us
  waiting for transfers between devices  83.1 us (44%)
  starting transfers between devices  58.5 us (31%)
  Pallas kernels  29.9 us (16%)
  matrix products  6.77 us (4%)
  other arithmetic  4.4 us (2%)
  local copies, waits for them, and re-layouts  4 us (2%)
    all_to_all x4, starting transfers between devices, exchange(): lax.all_to_all(shaped, 'ep', 0, 0, tiled=True).reshape(rows, x.shape[1])  30.5 us
    pallas_call x6, Pallas kernels, expert_call(): pl.pallas_call(body, in_specs=[pl.BlockSpec(memory_space=pltpu.SMEM)] + [...  28.3 us
    ppermute x1, waiting for transfers between devices, fold_halves(): dn_low = lax.ppermute(add(above[0], got_low), 'tp', up)  14 us
    ppermute x1, waiting for transfers between devices, fold_halves(): lax.ppermute(above[1], 'tp', up)  13.6 us
    ppermute x1, waiting for transfers between devices, spread_halves(): lax.ppermute(low, 'tp', up)  13.3 us
    all_to_all x4, waiting for transfers between devices, exchange(): lax.all_to_all(shaped, 'ep', 0, 0, tiled=True).reshape(rows, x.shape[1])  12.3 us
    ppermute x1, waiting for transfers between devices, fold_halves(): lax.ppermute(far[0], 'tp', up)  8.12 us
    ppermute x1, waiting for transfers between devices, spread_halves(): lax.ppermute(low, 'tp', dn)  7.09 us
  transfers between devices with their start and end apart: 24, of which 12 were waited for; matrix products, arithmetic and copies ran while one was open for 5% of the time, Pallas kernels for 12%

profile of v2, /device:TPU:1, one launch (start us, length us, event | category | flops | bytes accessed | tf_op | source)
XLA Modules:
  0.0 187.1 jit_solution(12273334671673547567)
XLA Ops:
  0.0 0.7 convert_element_type.103
  0.7 1.5 fusion.3
  2.5 2.5 %collective-permute-start.5 = (bf16[256,640]{1,0:T(8,128)(2,1)S(1)}, bf16[256,640]{1,0:T(8,128)(2,1)S(1)}, u32[]{:S(2)}, u32[]{:S(2)}) collective-permute-start(bf16[256,640]{1,0:T(8,128)(2,1)S(1)} %fusion.6), channel_id=1, source_target_pairs={{0,1},{1,2},{2,3},{3,0},{4,5},{5,6},{6,7},{7,4},{8,9},{9,10},{10,1... | collective-permute-start | bytes 983048 | tf_op jit(solution)/shard_map/ppermute | solution.py:170
  5.0 2.2 %collective-permute-start.4 = (bf16[256,640]{1,0:T(8,128)(2,1)S(1)}, bf16[256,640]{1,0:T(8,128)(2,1)S(1)}, u32[]{:S(2)}, u32[]{:S(2)}) collective-permute-start(bf16[256,640]{1,0:T(8,128)(2,1)S(1)} %fusion.6), channel_id=1, source_target_pairs={{0,3},{1,0},{2,1},{3,2},{4,7},{5,4},{6,5},{7,6},{8,11},{9,8},{10,9... | collective-permute-start | bytes 983048 | tf_op jit(solution)/shard_map/ppermute | solution.py:170
  7.3 0.2 convolution_select_fusion
  7.7 1.6 convolution_convert_fusion.1
  9.2 8.0 %all-to-all-start = ((bf16[32,16,1280]{2,1,0:T(8,128)(2,1)}), bf16[32,16,1280]{2,1,0:T(8,128)(2,1)S(1)}, u32[]{:S(2)}, u32[]{:S(2)}) async-start(bf16[32,16,1280]{2,1,0:T(8,128)(2,1)} %bitcast.4), calls=%async_computation | async-start | bytes 2621440 | tf_op jit(solution)/shard_map/all_to_all | solution.py:199
  17.4 2.7 %collective-permute-start.7 = (bf16[128,640]{1,0:T(8,128)(2,1)S(1)}, bf16[128,640]{1,0:T(8,128)(2,1)S(1)}, u32[]{:S(2)}, u32[]{:S(2)}) collective-permute-start(bf16[128,640]{1,0:T(8,128)(2,1)S(1)} %slice.89), channel_id=1, source_target_pairs={{0,3},{1,0},{2,1},{3,2},{4,7},{5,4},{6,5},{7,6},{8,11},{9,8},{10,9... | collective-permute-start | bytes 491528 | tf_op jit(solution)/shard_map/ppermute | solution.py:171
  20.4 3.7 %collective-permute-done.6 = bf16[128,640]{1,0:T(8,128)(2,1)S(1)} collective-permute-done((bf16[128,640]{1,0:T(8,128)(2,1)S(1)}, bf16[128,640]{1,0:T(8,128)(2,1)S(1)}, u32[]{:S(2)}, u32[]{:S(2)}) %collective-permute-start.6) | collective-permute-done | bytes 163872 | tf_op jit(solution)/shard_map/ppermute | solution.py:171
  24.6 2.2 %convolution_convert_fusion = bf16[512,2176]{1,0:T(8,128)(2,1)} fusion(pred[512,256]{1,0:T(32,128)(4,1)S(1)} %bitcast_compare_fusion, bf16[256,2176]{1,0:T(8,128)(2,1)S(1)} %pad_dynamic-update-slice_fusion), kind=kOutput, calls=%fused_computation | convolution fusion | flops 571539456 | bytes 3473408 | tf_op jit(solution)/shard_map/dot_general | solution.py:207
  26.8 9.8 %all-to-all-done = bf16[32,16,1280]{2,1,0:T(8,128)(2,1)S(1)} async-done(((bf16[32,16,1280]{2,1,0:T(8,128)(2,1)}), bf16[32,16,1280]{2,1,0:T(8,128)(2,1)S(1)}, u32[]{:S(2)}, u32[]{:S(2)}) %all-to-all-start) | async-done | bytes 1310752 | tf_op jit(solution)/shard_map/all_to_all | solution.py:199
  36.6 5.2 %all-to-all-start.1 = ((bf16[32,16,2176]{2,1,0:T(8,128)(2,1)}), bf16[32,16,2176]{2,1,0:T(8,128)(2,1)S(1)}, u32[]{:S(2)}, u32[]{:S(2)}) async-start(bf16[32,16,2176]{2,1,0:T(8,128)(2,1)} %bitcast.47), calls=%async_computation.1 | async-start | bytes 4456448 | tf_op jit(solution)/shard_map/all_to_all | solution.py:199
  41.8 1.2 fusion.20
  43.0 2.7 %collective-permute-start.2 = (bf16[256,1280]{1,0:T(8,128)(2,1)}, bf16[256,1280]{1,0:T(8,128)(2,1)}, u32[]{:S(2)}, u32[]{:S(2)}) collective-permute-start(bf16[256,1280]{1,0:T(8,128)(2,1)} %bitcast.6), channel_id=1, source_target_pairs={{0,3},{1,0},{2,1},{3,2},{4,7},{5,4},{6,5},{7,6},{8,11},{9,8},{10,9... | collective-permute-start | bytes 1966088 | tf_op jit(solution)/shard_map/ppermute | solution.py:182
  45.6 0.5 collective-permute-start.8
  46.1 1.0 collective-permute-start.9
  47.1 13.3 %collective-permute-done.refs_2_ = bf16[256,1280]{1,0:T(8,128)(2,1)} collective-permute-done((bf16[256,1280]{1,0:T(8,128)(2,1)}, bf16[256,1280]{1,0:T(8,128)(2,1)}, u32[]{:S(2)}, u32[]{:S(2)}) %collective-permute-start) | collective-permute-done | bytes 655392 | tf_op jit(solution)/shard_map/ppermute | solution.py:182
  60.4 2.7 %collective-permute-start.3 = (bf16[256,1280]{1,0:T(8,128)(2,1)}, bf16[256,1280]{1,0:T(8,128)(2,1)}, u32[]{:S(2)}, u32[]{:S(2)}) collective-permute-start(bf16[256,1280]{1,0:T(8,128)(2,1)} %collective-permute-done.2.refs_1_), channel_id=1, source_target_pairs={{0,3},{1,0},{2,1},{3,2},{4,7},{5,4},{6,5},{7,6},{8,11},{9,8},{10,9... | collective-permute-start | bytes 1966088 | tf_op jit(solution)/shard_map/ppermute | solution.py:184
  63.1 3.3 %shard_map.73 = (f32[512,512]{1,0:T(8,128)S(1)}, f32[512,512]{1,0:T(8,128)S(1)}) custom-call(s32[1]{0:T(128)} %bitcast.2.where_ref, bf16[512,1280]{1,0:T(8,128)(2,1)S(1)} %bitcast.33, bf16[7168,512]{1,0:T(8,128)(2,1)} %bitcast.36, bf16[7168,512]{1,0:T(8,128)(2,1)} %bitcast.40), custom_call_target="tpu_custom_call" | custom-call | flops 1342177280 | bytes 5242880 | tf_op jit(solution)/shard_map/pallas_call | solution.py:104
  66.4 7.1 %collective-permute-done.8.refs_0_ = bf16[256,1280]{1,0:T(8,128)(2,1)} collective-permute-done((bf16[256,1280]{1,0:T(8,128)(2,1)}, bf16[256,1280]{1,0:T(8,128)(2,1)}, u32[]{:S(2)}, u32[]{:S(2)}) %collective-permute-start.8) | collective-permute-done | bytes 655392 | tf_op jit(solution)/shard_map/ppermute | solution.py:183
  73.4 1.0 collective-permute-done.9.refs_3_
  74.5 6.6 %shard_map.74 = (f32[512,512]{1,0:T(8,128)S(1)}, f32[512,512]{1,0:T(8,128)S(1)}) custom-call(s32[1]{0:T(128)} %bitcast.2.where_ref, bf16[256,1280]{1,0:T(8,128)(2,1)} %collective-permute-done.8.refs_0_, bf16[256,1280]{1,0:T(8,128)(2,1)} %collective-permute-done.2.refs_1_, bf16[256,1280]{1,0:T(8,128)(2,1)} %collective-permute-done.refs_2_, ...), custom_call_target="tpu_custom_call" | custom-call | flops 2684354560 | bytes 10485760 | tf_op jit(solution)/shard_map/pallas_call | solution.py:104
  81.0 1.0 copy-done
  82.1 1.2 copy-done.1
  83.3 4.0 %shard_map.75 = (f32[512,512]{1,0:T(8,128)S(1)}, f32[512,512]{1,0:T(8,128)S(1)}) custom-call(s32[1]{0:T(128)} %bitcast.2.where_ref, bf16[512,2176]{1,0:T(8,128)(2,1)S(1)} %bitcast.35, f32[512,512]{1,0:T(8,128)S(1)} %get-tuple-element.22.refs_1_, f32[512,512]{1,0:T(8,128)S(1)} %copy-done.1, bf16[7168,512]{1,0:T(8,128)(2,1)} %bitcast.38, ...), custom_call_target="tpu_custom_call" | custom-call | flops 2147483648 | bytes 8388608 | tf_op jit(solution)/shard_map/pallas_call | solution.py:104
  87.3 1.2 collective-permute-done.1.refs_0_
  88.5 7.0 %shard_map.76 = (bf16[512,512]{1,0:T(8,128)(2,1)S(1)}, bf16[256,1280]{1,0:T(8,128)(2,1)S(1)}, bf16[256,1280]{1,0:T(8,128)(2,1)}, bf16[256,1280]{1,0:T(8,128)(2,1)S(1)}, bf16[256,1280]{1,0:T(8,128)(2,1)S(1)}) custom-call(s32[1]{0:T(128)} %bitcast.2.where_ref, bf16[256,1280]{1,0:T(8,128)(2,1)} %collective-permute-done.1.refs_0_, ...), custom_call_target="tpu_custom_call" | custom-call | flops 2684354560 | bytes 10485760 | tf_op jit(solution)/shard_map/pallas_call | solution.py:104
  95.5 2.5 %collective-permute-start.18 = (bf16[256,1280]{1,0:T(8,128)(2,1)}, bf16[256,1280]{1,0:T(8,128)(2,1)S(1)}, u32[]{:S(2)}, u32[]{:S(2)}) collective-permute-start(bf16[256,1280]{1,0:T(8,128)(2,1)} %get-tuple-element.34), channel_id=1, source_target_pairs={{0,3},{1,0},{2,1},{3,2},{4,7},{5,4},{6,5},{7,6},{8,11},{9,8},{10,9... | collective-permute-start | bytes 1966088 | tf_op jit(solution)/shard_map/ppermute | solution.py:191
  98.0 4.2 %shard_map.77 = bf16[512,2048]{1,0:T(8,128)(2,1)} custom-call(s32[1]{0:T(128)} %bitcast.2.where_ref, bf16[512,512]{1,0:T(8,128)(2,1)S(1)} %get-tuple-element.26.refs_0_, bf16[512,7168]{1,0:T(8,128)(2,1)} %bitcast.45), custom_call_target="tpu_custom_call" | custom-call | flops 1073741824 | bytes 4194304 | tf_op jit(solution)/shard_map/pallas_call | solution.py:104
  102.1 8.9 %all-to-all-start.2 = ((bf16[32,16,2048]{2,1,0:T(8,128)(2,1)}), bf16[32,16,2048]{2,1,0:T(8,128)(2,1)}, u32[]{:S(2)}, u32[]{:S(2)}) async-start(bf16[32,16,2048]{2,1,0:T(8,128)(2,1)} %bitcast.15), calls=%async_computation.2 | async-start | bytes 4194304 | tf_op jit(solution)/shard_map/all_to_all | solution.py:199
  111.2 2.7 %collective-permute-start.16 = (bf16[256,1280]{1,0:T(8,128)(2,1)S(1)}, bf16[256,1280]{1,0:T(8,128)(2,1)S(1)}, u32[]{:S(2)}, u32[]{:S(2)}) collective-permute-start(bf16[256,1280]{1,0:T(8,128)(2,1)S(1)} %get-tuple-element.30), channel_id=1, source_target_pairs={{0,3},{1,0},{2,1},{3,2},{4,7},{5,4},{6,5},{7,6},{8,11},{9,8},{10,9... | collective-permute-start | bytes 1966088 | tf_op jit(solution)/shard_map/ppermute | solution.py:192
  113.8 3.3 %shard_map.78 = (bf16[256,1280]{1,0:T(8,128)(2,1)S(1)}, bf16[256,1280]{1,0:T(8,128)(2,1)S(1)}, bf16[256,1280]{1,0:T(8,128)(2,1)S(1)}, bf16[256,1280]{1,0:T(8,128)(2,1)S(1)}) custom-call(s32[1]{0:T(128)} %bitcast.2.where_ref, bf16[512,512]{1,0:T(8,128)(2,1)S(1)} %get-tuple-element.26.refs_0_, bf16[512,7168]{1,0:T(8,128)(2,1)} %bitcast.46), custom_call_target="tpu_custom_call" | custom-call | flops 1342177280 | bytes 5242880 | tf_op jit(solution)/shard_map/pallas_call | solution.py:104
  117.2 0.2 add_convert_fusion
  117.4 3.0 %collective-permute-start.19 = (bf16[256,1280]{1,0:T(8,128)(2,1)S(1)}, bf16[256,1280]{1,0:T(8,128)(2,1)S(1)}, u32[]{:S(2)}, u32[]{:S(2)}) collective-permute-start(bf16[256,1280]{1,0:T(8,128)(2,1)S(1)} %add_convert_fusion), channel_id=1, source_target_pairs={{0,3},{1,0},{2,1},{3,2},{4,7},{5,4},{6,5},{7,6},{8,11},{9,8},{10,9... | collective-permute-start | bytes 1966088 | tf_op jit(solution)/shard_map/ppermute | solution.py:194
  120.3 8.1 %collective-permute-done.14 = bf16[256,1280]{1,0:T(8,128)(2,1)S(1)} collective-permute-done((bf16[256,1280]{1,0:T(8,128)(2,1)S(1)}, bf16[256,1280]{1,0:T(8,128)(2,1)S(1)}, u32[]{:S(2)}, u32[]{:S(2)}) %collective-permute-start.14) | collective-permute-done | bytes 655392 | tf_op jit(solution)/shard_map/ppermute | solution.py:191
  128.4 0.2 add_convert_fusion.1
  128.8 13.6 %collective-permute-done.17.refs_4_ = bf16[256,1280]{1,0:T(8,128)(2,1)S(1)} collective-permute-done((bf16[256,1280]{1,0:T(8,128)(2,1)S(1)}, bf16[256,1280]{1,0:T(8,128)(2,1)S(1)}, u32[]{:S(2)}, u32[]{:S(2)}) %collective-permute-start.17) | collective-permute-done | bytes 655392 | tf_op jit(solution)/shard_map/ppermute | solution.py:192
  142.4 14.0 %collective-permute-done.15.refs_1_ = bf16[256,1280]{1,0:T(8,128)(2,1)S(1)} collective-permute-done((bf16[256,1280]{1,0:T(8,128)(2,1)S(1)}, bf16[256,1280]{1,0:T(8,128)(2,1)S(1)}, u32[]{:S(2)}, u32[]{:S(2)}) %collective-permute-start.15) | collective-permute-done | bytes 655392 | tf_op jit(solution)/shard_map/ppermute | solution.py:193
  156.4 1.6 join_sums.1
  158.0 8.3 %all-to-all-start.3 = ((bf16[32,16,1280]{2,1,0:T(8,128)(2,1)}), bf16[32,16,1280]{2,1,0:T(8,128)(2,1)S(1)}, u32[]{:S(2)}, u32[]{:S(2)}) async-start(bf16[32,16,1280]{2,1,0:T(8,128)(2,1)} %bitcast.17), calls=%async_computation.3 | async-start | bytes 2621440 | tf_op jit(solution)/shard_map/all_to_all | solution.py:199
  166.3 2.3 %fusion = bf16[256,2048]{1,0:T(8,128)(2,1)S(1)} fusion(bf16[32,16,2048]{2,1,0:T(8,128)(2,1)} %all-to-all-done.2, bf16[32,256]{1,0:T(8,128)(2,1)S(1)} %select_reduce_fusion, f32[32,256]{1,0:T(8,128)S(1)} %copy-done.3), kind=kOutput, calls=%fused_computation.4 | convolution fusion | flops 537657344 | bytes 3194880 | tf_op jit(solution)/shard_map/dot_general | solution.py:257
  168.7 2.7 %collective-permute-start.12 = (bf16[128,512]{1,0:T(8,128)(2,1)S(1)}, bf16[128,512]{1,0:T(8,128)(2,1)S(1)}, u32[]{:S(2)}, u32[]{:S(2)}) collective-permute-start(bf16[128,512]{1,0:T(8,128)(2,1)S(1)} %get-tuple-element.42), channel_id=1, source_target_pairs={{0,3},{1,0},{2,1},{3,2},{4,7},{5,4},{6,5},{7,6},{8,11},{9,8},{10,9... | collective-permute-start | bytes 393224 | tf_op jit(solution)/shard_map/ppermute | solution.py:175
  171.4 3.4 %collective-permute-done.10 = bf16[128,512]{1,0:T(8,128)(2,1)S(1)} collective-permute-done((bf16[128,512]{1,0:T(8,128)(2,1)S(1)}, bf16[128,512]{1,0:T(8,128)(2,1)S(1)}, u32[]{:S(2)}, u32[]{:S(2)}) %collective-permute-start.10) | collective-permute-done | bytes 131104 | tf_op jit(solution)/shard_map/ppermute | solution.py:175
  175.0 2.7 %collective-permute-start.13 = (bf16[256,512]{1,0:T(8,128)(2,1)S(1)}, bf16[256,512]{1,0:T(8,128)(2,1)S(1)}, u32[]{:S(2)}, u32[]{:S(2)}) collective-permute-start(bf16[256,512]{1,0:T(8,128)(2,1)S(1)} %get-tuple-element.40), channel_id=1, source_target_pairs={{0,3},{1,0},{2,1},{3,2},{4,7},{5,4},{6,5},{7,6},{8,11},{9,8},{10,9... | collective-permute-start | bytes 786440 | tf_op jit(solution)/shard_map/ppermute | solution.py:178
  177.6 5.3 %collective-permute-done.11 = bf16[256,512]{1,0:T(8,128)(2,1)S(1)} collective-permute-done((bf16[256,512]{1,0:T(8,128)(2,1)S(1)}, bf16[256,512]{1,0:T(8,128)(2,1)S(1)}, u32[]{:S(2)}, u32[]{:S(2)}) %collective-permute-start.11) | collective-permute-done | bytes 262176 | tf_op jit(solution)/shard_map/ppermute | solution.py:178
  183.0 2.5 %all-to-all-done.3 = bf16[32,16,1280]{2,1,0:T(8,128)(2,1)S(1)} async-done(((bf16[32,16,1280]{2,1,0:T(8,128)(2,1)}), bf16[32,16,1280]{2,1,0:T(8,128)(2,1)S(1)}, u32[]{:S(2)}, u32[]{:S(2)}) %all-to-all-start.3) | async-done | bytes 1310752 | tf_op jit(solution)/shard_map/all_to_all | solution.py:199
  185.6 0.5 fusion.1
  186.1 1.0 pad_maximum_fusion
  (61 shorter events, 1.9 us)
Async XLA Ops:
  0.7 6.5 %copy-start.4 = (s32[256,8]{0,1:T(8,128)S(1)}, s32[256,8]{0,1:T(8,128)}, u32[]{:S(2)}) copy-start(s32[256,8]{0,1:T(8,128)} %param.9) | copy-start | bytes 24580
  2.5 14.8 %collective-permute-start.5 = (bf16[256,640]{1,0:T(8,128)(2,1)S(1)}, bf16[256,640]{1,0:T(8,128)(2,1)S(1)}, u32[]{:S(2)}, u32[]{:S(2)}) collective-permute-start(bf16[256,640]{1,0:T(8,128)(2,1)S(1)} %fusion.6), channel_id=1, source_target_pairs={{0,1},{1,2},{2,3},{3,0},{4,5},{5,6},{6,7},{7,4},{8,9},{9,10},{10,1... | collective-permute-start | bytes 983048 | tf_op jit(solution)/shard_map/ppermute | solution.py:170
  5.0 12.4 %collective-permute-start.4 = (bf16[256,640]{1,0:T(8,128)(2,1)S(1)}, bf16[256,640]{1,0:T(8,128)(2,1)S(1)}, u32[]{:S(2)}, u32[]{:S(2)}) collective-permute-start(bf16[256,640]{1,0:T(8,128)(2,1)S(1)} %fusion.6), channel_id=1, source_target_pairs={{0,3},{1,0},{2,1},{3,2},{4,7},{5,4},{6,5},{7,6},{8,11},{9,8},{10,9... | collective-permute-start | bytes 983048 | tf_op jit(solution)/shard_map/ppermute | solution.py:170
  7.4 1.8 copy-start.2
  9.2 27.3 %all-to-all-start = ((bf16[32,16,1280]{2,1,0:T(8,128)(2,1)}), bf16[32,16,1280]{2,1,0:T(8,128)(2,1)S(1)}, u32[]{:S(2)}, u32[]{:S(2)}) async-start(bf16[32,16,1280]{2,1,0:T(8,128)(2,1)} %bitcast.4), calls=%async_computation | async-start | bytes 2621440 | tf_op jit(solution)/shard_map/all_to_all | solution.py:199
  17.3 6.8 %collective-permute-start.6 = (bf16[128,640]{1,0:T(8,128)(2,1)S(1)}, bf16[128,640]{1,0:T(8,128)(2,1)S(1)}, u32[]{:S(2)}, u32[]{:S(2)}) collective-permute-start(bf16[128,640]{1,0:T(8,128)(2,1)S(1)} %slice.88), channel_id=1, source_target_pairs={{0,1},{1,2},{2,3},{3,0},{4,5},{5,6},{6,7},{7,4},{8,9},{9,10},{10,1... | collective-permute-start | bytes 491528 | tf_op jit(solution)/shard_map/ppermute | solution.py:171
  17.4 6.7 %collective-permute-start.7 = (bf16[128,640]{1,0:T(8,128)(2,1)S(1)}, bf16[128,640]{1,0:T(8,128)(2,1)S(1)}, u32[]{:S(2)}, u32[]{:S(2)}) collective-permute-start(bf16[128,640]{1,0:T(8,128)(2,1)S(1)} %slice.89), channel_id=1, source_target_pairs={{0,3},{1,0},{2,1},{3,2},{4,7},{5,4},{6,5},{7,6},{8,11},{9,8},{10,9... | collective-permute-start | bytes 491528 | tf_op jit(solution)/shard_map/ppermute | solution.py:171
  36.6 45.5 %all-to-all-start.1 = ((bf16[32,16,2176]{2,1,0:T(8,128)(2,1)}), bf16[32,16,2176]{2,1,0:T(8,128)(2,1)S(1)}, u32[]{:S(2)}, u32[]{:S(2)}) async-start(bf16[32,16,2176]{2,1,0:T(8,128)(2,1)} %bitcast.47), calls=%async_computation.1 | async-start | bytes 4456448 | tf_op jit(solution)/shard_map/all_to_all | solution.py:199
  42.9 17.5 %collective-permute-start = (bf16[256,1280]{1,0:T(8,128)(2,1)}, bf16[256,1280]{1,0:T(8,128)(2,1)}, u32[]{:S(2)}, u32[]{:S(2)}) collective-permute-start(bf16[256,1280]{1,0:T(8,128)(2,1)} %bitcast.5), channel_id=1, source_target_pairs={{0,1},{1,2},{2,3},{3,0},{4,5},{5,6},{6,7},{7,4},{8,9},{9,10},{10,1... | collective-permute-start | bytes 1966088 | tf_op jit(solution)/shard_map/ppermute | solution.py:182
  43.0 17.5 %collective-permute-start.2 = (bf16[256,1280]{1,0:T(8,128)(2,1)}, bf16[256,1280]{1,0:T(8,128)(2,1)}, u32[]{:S(2)}, u32[]{:S(2)}) collective-permute-start(bf16[256,1280]{1,0:T(8,128)(2,1)} %bitcast.6), channel_id=1, source_target_pairs={{0,3},{1,0},{2,1},{3,2},{4,7},{5,4},{6,5},{7,6},{8,11},{9,8},{10,9... | collective-permute-start | bytes 1966088 | tf_op jit(solution)/shard_map/ppermute | solution.py:182
  45.6 27.8 %collective-permute-start.8 = (bf16[256,1280]{1,0:T(8,128)(2,1)}, bf16[256,1280]{1,0:T(8,128)(2,1)}, u32[]{:S(2)}, u32[]{:S(2)}) collective-permute-start(bf16[256,1280]{1,0:T(8,128)(2,1)} %bitcast.5), channel_id=1, source_target_pairs={{0,3},{1,0},{2,1},{3,2},{4,7},{5,4},{6,5},{7,6},{8,11},{9,8},{10,9... | collective-permute-start | bytes 1966088 | tf_op jit(solution)/shard_map/ppermute | solution.py:183
  46.1 28.4 %collective-permute-start.9 = (bf16[256,1280]{1,0:T(8,128)(2,1)}, bf16[256,1280]{1,0:T(8,128)(2,1)}, u32[]{:S(2)}, u32[]{:S(2)}) collective-permute-start(bf16[256,1280]{1,0:T(8,128)(2,1)} %bitcast.6), channel_id=1, source_target_pairs={{0,1},{1,2},{2,3},{3,0},{4,5},{5,6},{6,7},{7,4},{8,9},{9,10},{10,1... | collective-permute-start | bytes 1966088 | tf_op jit(solution)/shard_map/ppermute | solution.py:183
  60.4 28.1 %collective-permute-start.1 = (bf16[256,1280]{1,0:T(8,128)(2,1)}, bf16[256,1280]{1,0:T(8,128)(2,1)}, u32[]{:S(2)}, u32[]{:S(2)}) collective-permute-start(bf16[256,1280]{1,0:T(8,128)(2,1)} %collective-permute-done.refs_2_), channel_id=1, source_target_pairs={{0,1},{1,2},{2,3},{3,0},{4,5},{5,6},{6,7},{7,4},{8,9},{9,10},{10,1... | collective-permute-start | bytes 1966088 | tf_op jit(solution)/shard_map/ppermute | solution.py:184
  60.4 28.1 %collective-permute-start.3 = (bf16[256,1280]{1,0:T(8,128)(2,1)}, bf16[256,1280]{1,0:T(8,128)(2,1)}, u32[]{:S(2)}, u32[]{:S(2)}) collective-permute-start(bf16[256,1280]{1,0:T(8,128)(2,1)} %collective-permute-done.2.refs_1_), channel_id=1, source_target_pairs={{0,3},{1,0},{2,1},{3,2},{4,7},{5,4},{6,5},{7,6},{8,11},{9,8},{10,9... | collective-permute-start | bytes 1966088 | tf_op jit(solution)/shard_map/ppermute | solution.py:184
  81.0 1.0 copy-start
  82.1 1.2 copy-start.1
  95.5 21.7 %collective-permute-start.18 = (bf16[256,1280]{1,0:T(8,128)(2,1)}, bf16[256,1280]{1,0:T(8,128)(2,1)S(1)}, u32[]{:S(2)}, u32[]{:S(2)}) collective-permute-start(bf16[256,1280]{1,0:T(8,128)(2,1)} %get-tuple-element.34), channel_id=1, source_target_pairs={{0,3},{1,0},{2,1},{3,2},{4,7},{5,4},{6,5},{7,6},{8,11},{9,8},{10,9... | collective-permute-start | bytes 1966088 | tf_op jit(solution)/shard_map/ppermute | solution.py:191
  102.1 55.9 %all-to-all-start.2 = ((bf16[32,16,2048]{2,1,0:T(8,128)(2,1)}), bf16[32,16,2048]{2,1,0:T(8,128)(2,1)}, u32[]{:S(2)}, u32[]{:S(2)}) async-start(bf16[32,16,2048]{2,1,0:T(8,128)(2,1)} %bitcast.15), calls=%async_computation.2 | async-start | bytes 4194304 | tf_op jit(solution)/shard_map/all_to_all | solution.py:199
  111.1 17.4 %collective-permute-start.14 = (bf16[256,1280]{1,0:T(8,128)(2,1)S(1)}, bf16[256,1280]{1,0:T(8,128)(2,1)S(1)}, u32[]{:S(2)}, u32[]{:S(2)}) collective-permute-start(bf16[256,1280]{1,0:T(8,128)(2,1)S(1)} %get-tuple-element.29), channel_id=1, source_target_pairs={{0,1},{1,2},{2,3},{3,0},{4,5},{5,6},{6,7},{7,4},{8,9},{9,10},{10,1... | collective-permute-start | bytes 1966088 | tf_op jit(solution)/shard_map/ppermute | solution.py:191
  111.2 17.6 %collective-permute-start.16 = (bf16[256,1280]{1,0:T(8,128)(2,1)S(1)}, bf16[256,1280]{1,0:T(8,128)(2,1)S(1)}, u32[]{:S(2)}, u32[]{:S(2)}) collective-permute-start(bf16[256,1280]{1,0:T(8,128)(2,1)S(1)} %get-tuple-element.30), channel_id=1, source_target_pairs={{0,3},{1,0},{2,1},{3,2},{4,7},{5,4},{6,5},{7,6},{8,11},{9,8},{10,9... | collective-permute-start | bytes 1966088 | tf_op jit(solution)/shard_map/ppermute | solution.py:192
  113.8 28.6 %collective-permute-start.17 = (bf16[256,1280]{1,0:T(8,128)(2,1)S(1)}, bf16[256,1280]{1,0:T(8,128)(2,1)S(1)}, u32[]{:S(2)}, u32[]{:S(2)}) collective-permute-start(bf16[256,1280]{1,0:T(8,128)(2,1)S(1)} %get-tuple-element.32), channel_id=1, source_target_pairs={{0,1},{1,2},{2,3},{3,0},{4,5},{5,6},{6,7},{7,4},{8,9},{9,10},{10,1... | collective-permute-start | bytes 1966088 | tf_op jit(solution)/shard_map/ppermute | solution.py:192
  117.3 11.4 %copy-start.5 = (bf16[256,8]{0,1:T(8,128)(2,1)S(1)}, bf16[256,8]{0,1:T(8,128)(2,1)}, u32[]{:S(2)}) copy-start(bf16[256,8]{0,1:T(8,128)(2,1)} %param.10) | copy-start | bytes 12292
  117.4 25.0 %collective-permute-start.19 = (bf16[256,1280]{1,0:T(8,128)(2,1)S(1)}, bf16[256,1280]{1,0:T(8,128)(2,1)S(1)}, u32[]{:S(2)}, u32[]{:S(2)}) collective-permute-start(bf16[256,1280]{1,0:T(8,128)(2,1)S(1)} %add_convert_fusion), channel_id=1, source_target_pairs={{0,3},{1,0},{2,1},{3,2},{4,7},{5,4},{6,5},{7,6},{8,11},{9,8},{10,9... | collective-permute-start | bytes 1966088 | tf_op jit(solution)/shard_map/ppermute | solution.py:194
  128.6 27.8 %collective-permute-start.15 = (bf16[256,1280]{1,0:T(8,128)(2,1)S(1)}, bf16[256,1280]{1,0:T(8,128)(2,1)S(1)}, u32[]{:S(2)}, u32[]{:S(2)}) collective-permute-start(bf16[256,1280]{1,0:T(8,128)(2,1)S(1)} %add_convert_fusion.1), channel_id=1, source_target_pairs={{0,1},{1,2},{2,3},{3,0},{4,5},{5,6},{6,7},{7,4},{8,9},{9,10},{10,1... | collective-permute-start | bytes 1966088 | tf_op jit(solution)/shard_map/ppermute | solution.py:193
  158.0 8.3 %copy-start.3 = (f32[32,256]{1,0:T(8,128)S(1)}, f32[32,256]{1,0:T(8,128)}, u32[]{:S(2)}) copy-start(f32[32,256]{1,0:T(8,128)} %copy-done.2) | copy-start | bytes 98308
  158.0 27.6 %all-to-all-start.3 = ((bf16[32,16,1280]{2,1,0:T(8,128)(2,1)}), bf16[32,16,1280]{2,1,0:T(8,128)(2,1)S(1)}, u32[]{:S(2)}, u32[]{:S(2)}) async-start(bf16[32,16,1280]{2,1,0:T(8,128)(2,1)} %bitcast.17), calls=%async_computation.3 | async-start | bytes 2621440 | tf_op jit(solution)/shard_map/all_to_all | solution.py:199
  168.7 6.1 %collective-permute-start.10 = (bf16[128,512]{1,0:T(8,128)(2,1)S(1)}, bf16[128,512]{1,0:T(8,128)(2,1)S(1)}, u32[]{:S(2)}, u32[]{:S(2)}) collective-permute-start(bf16[128,512]{1,0:T(8,128)(2,1)S(1)} %get-tuple-element.41), channel_id=1, source_target_pairs={{0,1},{1,2},{2,3},{3,0},{4,5},{5,6},{6,7},{7,4},{8,9},{9,10},{10,1... | collective-permute-start | bytes 393224 | tf_op jit(solution)/shard_map/ppermute | solution.py:175
  168.7 6.0 %collective-permute-start.12 = (bf16[128,512]{1,0:T(8,128)(2,1)S(1)}, bf16[128,512]{1,0:T(8,128)(2,1)S(1)}, u32[]{:S(2)}, u32[]{:S(2)}) collective-permute-start(bf16[128,512]{1,0:T(8,128)(2,1)S(1)} %get-tuple-element.42), channel_id=1, source_target_pairs={{0,3},{1,0},{2,1},{3,2},{4,7},{5,4},{6,5},{7,6},{8,11},{9,8},{10,9... | collective-permute-start | bytes 393224 | tf_op jit(solution)/shard_map/ppermute | solution.py:175
  174.9 8.1 %collective-permute-start.11 = (bf16[256,512]{1,0:T(8,128)(2,1)S(1)}, bf16[256,512]{1,0:T(8,128)(2,1)S(1)}, u32[]{:S(2)}, u32[]{:S(2)}) collective-permute-start(bf16[256,512]{1,0:T(8,128)(2,1)S(1)} %get-tuple-element.39), channel_id=1, source_target_pairs={{0,1},{1,2},{2,3},{3,0},{4,5},{5,6},{6,7},{7,4},{8,9},{9,10},{10,1... | collective-permute-start | bytes 786440 | tf_op jit(solution)/shard_map/ppermute | solution.py:178
  175.0 8.0 %collective-permute-start.13 = (bf16[256,512]{1,0:T(8,128)(2,1)S(1)}, bf16[256,512]{1,0:T(8,128)(2,1)S(1)}, u32[]{:S(2)}, u32[]{:S(2)}) collective-permute-start(bf16[256,512]{1,0:T(8,128)(2,1)S(1)} %get-tuple-element.40), channel_id=1, source_target_pairs={{0,3},{1,0},{2,1},{3,2},{4,7},{5,4},{6,5},{7,6},{8,11},{9,8},{10,9... | collective-permute-start | bytes 786440 | tf_op jit(solution)/shard_map/ppermute | solution.py:178

commit v3 on v2

--- a/solution.py
+++ b/solution.py
@@ -31,33 +31,38 @@
     d_all, ff = w_gate.shape
     span = d_all // slices
     finish = bool(segs) and bool(jobs)
-    rows = hidden.shape[0] if hidden is not None else carry[0].shape[0] if carry else sum(xs[i].shape[0] for i in segs[0][0])
+    rows = hidden.shape[0] if hidden is not None else sum(xs[i].shape[0] for i in segs[0][0])
     results = [((rows, ff), F32)] * 2 if not jobs else [((rows, ff), BF16)] * finish + [(s, BF16) for s in outs]
-    resident = list(xs) + list(carry) + ([] if inv is None else [inv]) + ([] if hidden is None else [hidden])
-    streamed = ([w_gate, w_up] if segs else []) + ([w_down] if jobs else [])
+    resident = [] if hidden is None else [hidden]
+    streamed = list(xs) + list(carry) + ([w_gate, w_up] if segs else []) + ([w_down] if jobs else [])
     columns = []
     for step, offset, width, *_ in jobs:
         if (step, offset, width) not in columns:
             columns.append((step, offset, width))
     scratch = []
     for _, _, _, width, _ in segs:
-        scratch += [pltpu.VMEM((width, ff), BF16)] * 2
+        scratch += [pltpu.VMEM((rows, width), BF16)] + [pltpu.VMEM((width, ff), BF16)] * 2
+    scratch += [pltpu.VMEM((rows, ff), F32)] * len(carry)
     if finish:
         scratch += [pltpu.VMEM((rows, ff), F32)] * 2
+    if inv is not None:
+        scratch += [pltpu.VMEM((rows, SIDE), BF16)]
     scratch += [pltpu.VMEM((ff, width), BF16) for _, _, width in columns]
-    scratch += [pltpu.SemaphoreType.DMA((2 * len(segs) + len(columns),))]
+    n_sems = sum(len(s[0]) + 2 for s in segs) + len(carry) + (inv is not None) + len(columns)
+    scratch += [pltpu.SemaphoreType.DMA((n_sems,))]
 
     def body(where_ref, *refs):
         refs = list(refs)
         take = lambda n: [refs.pop(0) for _ in range(n)]
+        hidden_ref = take(hidden is not None)
         x_refs, carried = take(len(xs)), take(len(carry))
-        inv_ref = take(inv is not None)
-        hidden_ref = take(hidden is not None)
         wg, wu = take(2) if segs else (None, None)
         wd = take(bool(jobs))
         out_refs = take(len(results))
-        seg_bufs = [take(2) for _ in segs]
+        seg_bufs = [take(3) for _ in segs]
+        carry_bufs = take(len(carry))
         accs = take(2) if finish else out_refs
+        inv_buf = take(inv is not None)
         col_bufs = take(len(columns))
         copies = Copies(refs.pop(0))
         z = where_ref[0]
@@ -66,26 +71,33 @@
             return pl.multiple_of(lax.rem(z + step, slices) * span + offset, 128)
 
         seg_waits, col_waits = [], []
-        for (_, step, offset, width, _), (gb, ub) in zip(segs, seg_bufs):
+        for (index, step, offset, width, col), (xb, gb, ub) in zip(segs, seg_bufs):
             at = pl.ds(first(step, offset), width)
-            seg_waits.append([copies.start(wg.at[at, :], gb), copies.start(wu.at[at, :], ub)])
+            waits, row = [], 0
+            for i in index:
+                count = x_refs[i].shape[0]
+                waits.append(copies.start(x_refs[i].at[:, pl.ds(col, width)], xb.at[pl.ds(row, count), :]))
+                row += count
+            seg_waits.append(waits + [copies.start(wg.at[at, :], gb), copies.start(wu.at[at, :], ub)])
+        carry_waits = [copies.start(c, b) for c, b in zip(carried, carry_bufs)]
+        if inv is not None:
+            inv_wait = copies.start(x_refs[inv[0]].at[:, pl.ds(inv[1], SIDE)], inv_buf[0])
         for (step, offset, width), wb in zip(columns, col_bufs):
             col_waits.append(copies.start(wd[0].at[:, pl.ds(first(step, offset), width)], wb))
-        for k, (index, _, _, width, col) in enumerate(segs):
-            x = [x_refs[i][:, col : col + width] for i in index]
-            x = x[0] if len(x) == 1 else jnp.concatenate(x, axis=0)
+        for k, (xb, *w_bufs) in enumerate(seg_bufs):
             for w in seg_waits[k]:
                 w.wait()
-            for w_buf, acc, base in zip(seg_bufs[k], accs, carried or (None, None)):
-                term = jnp.dot(x, w_buf[...], preferred_element_type=F32)
+            for n, (w_buf, acc) in enumerate(zip(w_bufs, accs)):
+                term = jnp.dot(xb[...], w_buf[...], preferred_element_type=F32)
                 if k:
-                    acc[...] += term
-                elif base is None:
-                    acc[...] = term
-                else:
-                    acc[...] = base[...] + term
+                    term = acc[...] + term
+                if carry and k == len(segs) - 1:
+                    carry_waits[n].wait()
+                    term = term + carry_bufs[n][...]
+                acc[...] = term
         if finish:
-            scale = jnp.sum(inv_ref[0][:, -SIDE:].astype(F32), axis=1, keepdims=True)
+            inv_wait.wait()
+            scale = jnp.sum(inv_buf[0][...].astype(F32), axis=1, keepdims=True)
             gate = accs[0][...] * scale
             hidden_ref = [out_refs.pop(0)]
             hidden_ref[0][...] = (jax.nn.silu(gate) * (accs[1][...] * scale)).astype(BF16)
@@ -99,17 +111,65 @@
             for index, top, n, col in targets:
                 out_refs[index][:, col : col + width] = term[top : top + n, :]
 
-    vmem = pl.BlockSpec(memory_space=pltpu.VMEM)
+    vmem, hbm = pl.BlockSpec(memory_space=pltpu.VMEM), pl.BlockSpec(memory_space=pltpu.HBM)
     flops = sum(4 * rows * s[3] * ff for s in segs) + sum(2 * j[4] * ff * j[2] for j in jobs)
     return pl.pallas_call(
         body,
-        in_specs=[pl.BlockSpec(memory_space=pltpu.SMEM)] + [vmem] * len(resident) + [pl.BlockSpec(memory_space=pltpu.HBM)] * len(streamed),
+        in_specs=[pl.BlockSpec(memory_space=pltpu.SMEM)] + [vmem] * len(resident) + [hbm] * len(streamed),
         out_specs=[vmem] * len(results),
-        out_shape=[pltpu.VMEM(s, t) for s, t in results],
+        out_shape=[pltpu.VMEM(s, t) if jobs else jax.ShapeDtypeStruct(s, t) for s, t in results],
         scratch_shapes=scratch,
         cost_estimate=pl.CostEstimate(flops=flops, bytes_accessed=flops // 256, transcendentals=0),
+        compiler_params=pltpu.CompilerParams(vmem_limit_bytes=28 * 2**20),
+    )(
+        where,
+        *[pltpu.with_memory_space_constraint(x, pltpu.VMEM) for x in resident],
+        *[pltpu.with_memory_space_constraint(x, pltpu.HBM) for x in streamed],
+    )
+
+
+def side_columns(value):
+    lane = lax.broadcasted_iota(jnp.int32, (value.shape[0], SIDE), 1)
+    out = jnp.zeros((value.shape[0], SIDE), F32)
+    for k in range(3):
+        term = value.astype(BF16).astype(F32)
+        out = jnp.where(lane == k, term, out)
+        value = value - term
+    return out.astype(BF16)
+
+
+def head(tokens, norm_gain, ids, window):
+    tok, width = tokens.shape
+    rows, bulk = window * CAP, width - EARLY
+
+    def body(tokens_ref, gain_ref, ids_ref, pick_ref, bulk_ref, early_ref):
+        expert = lax.broadcasted_iota(jnp.int32, (window, tok), 0)
+        match = jnp.zeros((window, tok), F32)
+        for k in range(ids.shape[0]):
+            match = match + jnp.where(ids_ref[k : k + 1, :] == expert, 1.0, 0.0)
+        earlier = lax.broadcasted_iota(jnp.int32, (tok, tok), 0) < lax.broadcasted_iota(jnp.int32, (tok, tok), 1)
+        earlier = jnp.where(earlier, 1.0, 0.0).astype(BF16)
+        before = jnp.dot(match.astype(BF16), earlier, preferred_element_type=F32)
+        slot = jnp.where(match > 0.0, before, -1.0)
+        row = lax.broadcasted_iota(jnp.int32, (rows, window), 0)
+        own = (row // CAP) == lax.broadcasted_iota(jnp.int32, (rows, window), 1)
+        spread = jnp.dot(jnp.where(own, 1.0, 0.0).astype(BF16), slot.astype(BF16), preferred_element_type=F32)
+        wanted = (lax.broadcasted_iota(jnp.int32, (rows, tok), 0) % CAP).astype(F32)
+        pick = jnp.where(spread == wanted, 1.0, 0.0).astype(BF16)
+        pick_ref[...] = pick
+        values = tokens_ref[...].astype(F32)
+        gained = (values * gain_ref[...].astype(F32)).astype(BF16)
+        bulk_ref[...] = jnp.dot(pick, gained[:, EARLY:], preferred_element_type=F32).astype(BF16)
+        early_ref[:, :EARLY] = gained[:, :EARLY]
+        early_ref[:, EARLY:] = side_columns(jnp.sum(values * values, axis=1, keepdims=True))
+
+    return pl.pallas_call(
+        body,
+        out_shape=[jax.ShapeDtypeStruct(s, BF16) for s in ((rows, tok), (rows, bulk), (tok, EARLY + SIDE))],
+        cost_estimate=pl.CostEstimate(flops=2 * rows * tok * bulk, bytes_accessed=2 * tok * width, transcendentals=0),
         compiler_params=pltpu.CompilerParams(vmem_limit_bytes=24 * 2**20),
-    )(where, *[pltpu.with_memory_space_constraint(x, pltpu.VMEM) for x in resident], *[pltpu.with_memory_space_constraint(w, pltpu.HBM) for w in streamed])
+        name="head",
+    )(tokens, norm_gain.reshape(1, width), ids)
 
 
 def join_sums(low, high):
@@ -128,22 +188,6 @@
         compiler_params=pltpu.CompilerParams(vmem_limit_bytes=16 * 2**20),
         name="join_sums",
     )(*low, *high)
-
-
-def place_picks(expert_ids, gate_prob, window):
-    ids = expert_ids.T
-    probs = gate_prob.T.astype(F32)
-    tok = ids.shape[1]
-    same = ids[:, None, :] == jnp.arange(window, dtype=jnp.int32)[None, :, None]
-    match = jnp.any(same, axis=0).astype(BF16)
-    prob = jnp.sum(jnp.where(same, probs[:, None, :], 0.0), axis=0)
-    earlier = (jnp.arange(tok)[:, None] < jnp.arange(tok)[None, :]).astype(BF16)
-    before = jnp.dot(match, earlier, preferred_element_type=F32)
-    slot = jnp.where(match > 0, before, -1.0)
-    hit = slot[:, None, :] == jnp.arange(CAP, dtype=F32)[None, :, None]
-    pick = hit.astype(BF16).reshape(window * CAP, tok)
-    weight = jnp.where(hit, prob[:, None, :], 0.0).astype(BF16).reshape(window * CAP, tok)
-    return pick, weight
 
 
 def three_terms(value):
@@ -198,21 +242,23 @@
         shaped = x.reshape(window, CAP, x.shape[1])
         return lax.all_to_all(shaped, "ep", 0, 0, tiled=True).reshape(rows, x.shape[1])
 
-    pick, weight = place_picks(expert_ids, gate_prob, window)
-    gained = (tokens.astype(F32) * norm_gain.astype(F32)).astype(BF16)
     bulk = tokens.shape[1] - EARLY
     half = rows // 2
+    ids, probs = expert_ids.T, gate_prob.T.astype(F32)
+    pick, picked_bulk, early = head(tokens, norm_gain, ids, window)
+    same = ids[:, None, :] == jnp.arange(window, dtype=jnp.int32)[None, :, None]
+    prob = jnp.sum(jnp.where(same, probs[:, None, :], 0.0), axis=0)
+    by_slot = jnp.broadcast_to(prob[:, None, :], (window, CAP, tok)).reshape(rows, tok)
+    weight = jnp.where(pick > 0, by_slot, 0.0).astype(BF16)
 
     def dispatch(x):
         return jnp.dot(pick, x, preferred_element_type=F32).astype(BF16)
 
-    square_part = jnp.sum(jnp.square(tokens.astype(F32)), axis=1)
-    early = jnp.concatenate([gained[:, :EARLY], three_terms(square_part)], axis=1)
     e_below, e_above, e_far_a, e_far_b = spread(early)
-    mine = exchange(dispatch(gained[:, EARLY:]))
+    mine = exchange(picked_bulk)
     e_far = jnp.concatenate([e_far_a, e_far_b], axis=0)
     all_early = (early, e_above, e_far, e_below)
-    squares = sum(jnp.sum(e[:, EARLY : EARLY + 3].astype(F32), axis=1) for e in all_early[1:]) + square_part
+    squares = sum(jnp.sum(e[:, EARLY : EARLY + 3].astype(F32), axis=1) for e in all_early)
     inverse_rms = lax.rsqrt(squares / D + epsilon)
     early_all = jnp.concatenate([e[:, :EARLY] for e in all_early] + [three_terms(inverse_rms)], axis=1)
     picked = dispatch(early_all)
@@ -225,13 +271,11 @@
         where, weights, [*above, *below],
         [((0, 1), 1, EARLY, bulk, 0), ((2, 3), 3, EARLY, bulk, 0)], sums,
     )
-    sums = expert_call(
-        where, weights, [early_rows],
-        [((0,), k, 0, EARLY, k * EARLY) for k in range(n_tp)], sums,
-    )
     low, high = (0, half), (half, half)
     hidden, f_low, f_high, a_high, b_low = expert_call(
-        where, weights, far, [((0, 1), 2, EARLY, bulk, 0)], sums, inv=early_rows[:, -SIDE:],
+        where, weights, [early_rows, *far],
+        [((0,), k, 0, EARLY, k * EARLY) for k in range(n_tp)] + [((1, 2), 2, EARLY, bulk, 0)],
+        sums, inv=(0, n_tp * EARLY),
         jobs=[
             (2, EARLY, bulk, 0, rows, ((0, 0, half, 0), (1, half, half, 0))),
             (1, EARLY, bulk, *high, ((2, 0, half, 0),)),

time: 188 us -> 191 us (1.016)
  local copies, waits for them, and re-layouts: 4 us -> 11 us
    unnamed x18 -> x33, local copies, waits for them, and re-layouts: 2.6 us -> 7.95 us
    ppermute x1, waiting for transfers between devices: 1.19 us -> 6.46 us  [spread_halves(): lax.ppermute(below_low, 'tp', up)]
    pallas_call x6 -> x5, Pallas kernels: 28.3 us -> 25.1 us  [expert_call(): pl.pallas_call(body, in_specs=[pl.BlockSpec(memory_space=pltpu.SMEM)] + [...]
    ppermute x1, waiting for transfers between devices: 3.72 us -> 0.79 us  [spread(): lax.ppermute(below[:half], 'tp', up)]
    ppermute x1, waiting for transfers between devices: 7.09 us -> 4.68 us  [spread_halves(): lax.ppermute(low, 'tp', dn)]
    pallas_call x0 -> x1, Pallas kernels: none -> 1.91 us  [head(): pl.pallas_call(body, out_shape=[jax.ShapeDtypeStruct(s, BF16) for s in ((...]
  transfers between devices with their start and end apart: 24 -> 24, of which waited for: 12 -> 12; matrix products, arithmetic and copies ran while one was open for 5% -> 6% of each run, Pallas kernels for 12% -> 10%
where the time goes in v3:
time: 191 us; the launch traced here: 190 us
  waiting for transfers between devices  81.9 us (43%)
  starting transfers between devices  58.8 us (31%)
  Pallas kernels  28.6 us (15%)
  local copies, waits for them, and re-layouts  11 us (6%)
  matrix products  5.02 us (3%)
  other arithmetic  4.02 us (2%)
    all_to_all x4, starting transfers between devices, exchange(): lax.all_to_all(shaped, 'ep', 0, 0, tiled=True).reshape(rows, x.shape[1])  31.1 us
    pallas_call x5, Pallas kernels, expert_call(): pl.pallas_call(body, in_specs=[pl.BlockSpec(memory_space=pltpu.SMEM)] + [...  25.1 us
    ppermute x1, waiting for transfers between devices, fold_halves(): dn_low = lax.ppermute(add(above[0], got_low), 'tp', up)  14 us
    ppermute x1, waiting for transfers between devices, fold_halves(): lax.ppermute(above[1], 'tp', up)  13.3 us
    ppermute x1, waiting for transfers between devices, spread_halves(): lax.ppermute(low, 'tp', up)  13.3 us
    all_to_all x4, waiting for transfers between devices, exchange(): lax.all_to_all(shaped, 'ep', 0, 0, tiled=True).reshape(rows, x.shape[1])  12.4 us
    unnamed x33, local copies, waits for them, and re-layouts  7.95 us
    ppermute x1, waiting for transfers between devices, fold_halves(): lax.ppermute(far[0], 'tp', up)  7.25 us
  transfers between devices with their start and end apart: 24, of which 12 were waited for; matrix products, arithmetic and copies ran while one was open for 6% of the time, Pallas kernels for 10%

profile of v3, /device:TPU:1, one launch (start us, length us, event | category | flops | bytes accessed | tf_op | source)
XLA Modules:
  0.0 189.7 jit_solution(8346655321366579808)
XLA Ops:
  1.4 1.2 copy-done.6
  2.6 1.9 %head.1 = (bf16[512,256]{1,0:T(8,128)(2,1)S(1)}, bf16[512,1280]{1,0:T(8,128)(2,1)}, bf16[256,640]{1,0:T(8,128)(2,1)S(1)}) custom-call(bf16[256,1792]{1,0:T(8,128)(2,1)S(1)} %copy-done.6, bf16[1,1792]{1,0:T(2,128)(2,1)S(1)} %reshape.124.gain_ref, s32[8,256]{1,0:T(8,128)S(1)} %bitcast.28), custom_call_target="tpu_custom_call" | custom-call | flops 335544320 | bytes 917504 | tf_op jit(solution)/shard_map/head/pallas_call | solution.py:166
  4.5 2.5 %collective-permute-start.1 = (bf16[256,640]{1,0:T(8,128)(2,1)S(1)}, bf16[256,640]{1,0:T(8,128)(2,1)S(1)}, u32[]{:S(2)}, u32[]{:S(2)}) collective-permute-start(bf16[256,640]{1,0:T(8,128)(2,1)S(1)} %get-tuple-element.22), channel_id=1, source_target_pairs={{0,1},{1,2},{2,3},{3,0},{4,5},{5,6},{6,7},{7,4},{8,9},{9,10},{10,1... | collective-permute-start | bytes 983048 | tf_op jit(solution)/shard_map/ppermute | solution.py:214
  6.9 2.1 %collective-permute-start = (bf16[256,640]{1,0:T(8,128)(2,1)S(1)}, bf16[256,640]{1,0:T(8,128)(2,1)}, u32[]{:S(2)}, u32[]{:S(2)}) collective-permute-start(bf16[256,640]{1,0:T(8,128)(2,1)S(1)} %get-tuple-element.22), channel_id=1, source_target_pairs={{0,3},{1,0},{2,1},{3,2},{4,7},{5,4},{6,5},{7,6},{8,11},{9,8},{10,9... | collective-permute-start | bytes 983048 | tf_op jit(solution)/shard_map/ppermute | solution.py:214
  9.1 8.0 %all-to-all-start.1 = ((bf16[32,16,1280]{2,1,0:T(8,128)(2,1)}), bf16[32,16,1280]{2,1,0:T(8,128)(2,1)S(1)}, u32[]{:S(2)}, u32[]{:S(2)}) async-start(bf16[32,16,1280]{2,1,0:T(8,128)(2,1)} %bitcast.7), calls=%async_computation.1 | async-start | bytes 2621440 | tf_op jit(solution)/shard_map/all_to_all | solution.py:243
  17.4 0.9 slice.81
  18.3 2.7 %collective-permute-start.3 = (bf16[128,640]{1,0:T(8,128)(2,1)S(1)}, bf16[128,640]{1,0:T(8,128)(2,1)S(1)}, u32[]{:S(2)}, u32[]{:S(2)}) collective-permute-start(bf16[128,640]{1,0:T(8,128)(2,1)S(1)} %slice.81), channel_id=1, source_target_pairs={{0,3},{1,0},{2,1},{3,2},{4,7},{5,4},{6,5},{7,6},{8,11},{9,8},{10,9... | collective-permute-start | bytes 491528 | tf_op jit(solution)/shard_map/ppermute | solution.py:215
  21.0 1.0 slice_dynamic-update-slice_fusion.2
  22.1 1.0 convert_reduce_fusion.2
  23.1 0.8 collective-permute-done.2
  24.3 2.2 %convolution_convert_fusion = bf16[512,2176]{1,0:T(8,128)(2,1)} fusion(bf16[512,256]{1,0:T(8,128)(2,1)S(1)} %get-tuple-element.21, bf16[256,2176]{1,0:T(8,128)(2,1)S(1)} %pad_dynamic-update-slice_fusion), kind=kOutput, calls=%fused_computation | convolution fusion | flops 571539456 | bytes 3604480 | tf_op jit(solution)/shard_map/dot_general | solution.py:255
  26.5 9.9 %all-to-all-done.1 = bf16[32,16,1280]{2,1,0:T(8,128)(2,1)S(1)} async-done(((bf16[32,16,1280]{2,1,0:T(8,128)(2,1)}), bf16[32,16,1280]{2,1,0:T(8,128)(2,1)S(1)}, u32[]{:S(2)}, u32[]{:S(2)}) %all-to-all-start.1) | async-done | bytes 1310752 | tf_op jit(solution)/shard_map/all_to_all | solution.py:243
  36.4 5.9 %all-to-all-start = ((bf16[32,16,2176]{2,1,0:T(8,128)(2,1)}), bf16[32,16,2176]{2,1,0:T(8,128)(2,1)}, u32[]{:S(2)}, u32[]{:S(2)}) async-start(bf16[32,16,2176]{2,1,0:T(8,128)(2,1)} %bitcast.40), calls=%async_computation | async-start | bytes 4456448 | tf_op jit(solution)/shard_map/all_to_all | solution.py:243
  42.3 1.2 fusion.3
  43.5 2.7 %collective-permute-start.6 = (bf16[256,1280]{1,0:T(8,128)(2,1)}, bf16[256,1280]{1,0:T(8,128)(2,1)S(1)}, u32[]{:S(2)}, u32[]{:S(2)}) collective-permute-start(bf16[256,1280]{1,0:T(8,128)(2,1)} %bitcast.9), channel_id=1, source_target_pairs={{0,3},{1,0},{2,1},{3,2},{4,7},{5,4},{6,5},{7,6},{8,11},{9,8},{10,9... | collective-permute-start | bytes 1966088 | tf_op jit(solution)/shard_map/ppermute | solution.py:226
  46.7 0.9 collective-permute-start.9
  47.6 13.3 %collective-permute-done.4.refs_2_ = bf16[256,1280]{1,0:T(8,128)(2,1)S(1)} collective-permute-done((bf16[256,1280]{1,0:T(8,128)(2,1)}, bf16[256,1280]{1,0:T(8,128)(2,1)S(1)}, u32[]{:S(2)}, u32[]{:S(2)}) %collective-permute-start.4) | collective-permute-done | bytes 655392 | tf_op jit(solution)/shard_map/ppermute | solution.py:226
  60.9 2.7 %collective-permute-start.7 = (bf16[256,1280]{1,0:T(8,128)(2,1)S(1)}, bf16[256,1280]{1,0:T(8,128)(2,1)S(1)}, u32[]{:S(2)}, u32[]{:S(2)}) collective-permute-start(bf16[256,1280]{1,0:T(8,128)(2,1)S(1)} %collective-permute-done.6.refs_1_), channel_id=1, source_target_pairs={{0,3},{1,0},{2,1},{3,2},{4,7},{5,4},{6,5},{7,6},{8,11},{9,8},{10,9... | collective-permute-start | bytes 1966088 | tf_op jit(solution)/shard_map/ppermute | solution.py:228
  63.6 3.6 %shard_map.73 = (f32[512,512]{1,0:T(8,128)S(1)}, f32[512,512]{1,0:T(8,128)S(1)}) custom-call(s32[1]{0:T(128)} %bitcast.3.where_ref, bf16[512,1280]{1,0:T(8,128)(2,1)} %bitcast.39, bf16[7168,512]{1,0:T(8,128)(2,1)} %bitcast.30, bf16[7168,512]{1,0:T(8,128)(2,1)} %bitcast.33), custom_call_target="tpu_custom_call" | custom-call | flops 1342177280 | bytes 5242880 | tf_op jit(solution)/shard_map/pallas_call | solution.py:116
  67.2 1.0 copy-done.2
  68.2 1.0 copy-done.3
  69.2 4.7 %collective-permute-done.8.refs_0_ = bf16[256,1280]{1,0:T(8,128)(2,1)S(1)} collective-permute-done((bf16[256,1280]{1,0:T(8,128)(2,1)}, bf16[256,1280]{1,0:T(8,128)(2,1)S(1)}, u32[]{:S(2)}, u32[]{:S(2)}) %collective-permute-start.8) | collective-permute-done | bytes 655392 | tf_op jit(solution)/shard_map/ppermute | solution.py:227
  73.9 1.0 collective-permute-done.9.refs_3_
  74.9 5.5 %shard_map.74 = (f32[512,512]{1,0:T(8,128)S(1)}, f32[512,512]{1,0:T(8,128)S(1)}) custom-call(s32[1]{0:T(128)} %bitcast.3.where_ref, bf16[256,1280]{1,0:T(8,128)(2,1)} %copy-done.12, bf16[256,1280]{1,0:T(8,128)(2,1)} %copy-done.10, bf16[256,1280]{1,0:T(8,128)(2,1)} %copy-done.9, bf16[256,1280]{1,0:T(8,128)(2,1)} %collective-permute-done.9.refs_3_, ...), custom_call_target="tpu_custom_call" | custom-call | flops 2684354560 | bytes 10485760 | tf_op jit(solution)/shard_map/pallas_call | solution.py:116
  80.4 1.0 copy-done
  81.4 1.0 copy-done.1
  82.4 6.5 %collective-permute-done.5.refs_1_ = bf16[256,1280]{1,0:T(8,128)(2,1)S(1)} collective-permute-done((bf16[256,1280]{1,0:T(8,128)(2,1)S(1)}, bf16[256,1280]{1,0:T(8,128)(2,1)S(1)}, u32[]{:S(2)}, u32[]{:S(2)}) %collective-permute-start.5) | collective-permute-done | bytes 655392 | tf_op jit(solution)/shard_map/ppermute | solution.py:228
  88.9 0.8 copy-done.8
  89.9 8.5 %shard_map.75 = (bf16[512,512]{1,0:T(8,128)(2,1)S(1)}, bf16[256,1280]{1,0:T(8,128)(2,1)S(1)}, bf16[256,1280]{1,0:T(8,128)(2,1)S(1)}, bf16[256,1280]{1,0:T(8,128)(2,1)S(1)}, bf16[256,1280]{1,0:T(8,128)(2,1)S(1)}) custom-call(s32[1]{0:T(128)} %bitcast.3.where_ref, bf16[512,2176]{1,0:T(8,128)(2,1)} %bitcast.6.refs_0_, bf16[256,1280]{1,0:T(8,128)(2,1)} %copy-done.8, ...), custom_call_target="tpu_custom_call" | custom-call | flops 4831838208 | bytes 18874368 | tf_op jit(solution)/shard_map/pallas_call | solution.py:116
  98.4 2.2 %collective-permute-start.18 = (bf16[256,1280]{1,0:T(8,128)(2,1)S(1)}, bf16[256,1280]{1,0:T(8,128)(2,1)}, u32[]{:S(2)}, u32[]{:S(2)}) collective-permute-start(bf16[256,1280]{1,0:T(8,128)(2,1)S(1)} %get-tuple-element.36), channel_id=1, source_target_pairs={{0,3},{1,0},{2,1},{3,2},{4,7},{5,4},{6,5},{7,6},{8,11},{9,8},{10,9... | collective-permute-start | bytes 1966088 | tf_op jit(solution)/shard_map/ppermute | solution.py:235
  100.6 4.2 %shard_map.76 = bf16[512,2048]{1,0:T(8,128)(2,1)} custom-call(s32[1]{0:T(128)} %bitcast.3.where_ref, bf16[512,512]{1,0:T(8,128)(2,1)S(1)} %get-tuple-element.28.refs_0_, bf16[512,7168]{1,0:T(8,128)(2,1)} %bitcast.37), custom_call_target="tpu_custom_call" | custom-call | flops 1073741824 | bytes 4194304 | tf_op jit(solution)/shard_map/pallas_call | solution.py:116
  104.8 9.0 %all-to-all-start.2 = ((bf16[32,16,2048]{2,1,0:T(8,128)(2,1)}), bf16[32,16,2048]{2,1,0:T(8,128)(2,1)}, u32[]{:S(2)}, u32[]{:S(2)}) async-start(bf16[32,16,2048]{2,1,0:T(8,128)(2,1)} %bitcast.14), calls=%async_computation.2 | async-start | bytes 4194304 | tf_op jit(solution)/shard_map/all_to_all | solution.py:243
  113.9 2.7 %collective-permute-start.16 = (bf16[256,1280]{1,0:T(8,128)(2,1)S(1)}, bf16[256,1280]{1,0:T(8,128)(2,1)S(1)}, u32[]{:S(2)}, u32[]{:S(2)}) collective-permute-start(bf16[256,1280]{1,0:T(8,128)(2,1)S(1)} %get-tuple-element.32), channel_id=1, source_target_pairs={{0,3},{1,0},{2,1},{3,2},{4,7},{5,4},{6,5},{7,6},{8,11},{9,8},{10,9... | collective-permute-start | bytes 1966088 | tf_op jit(solution)/shard_map/ppermute | solution.py:236
  116.6 3.3 %shard_map.77 = (bf16[256,1280]{1,0:T(8,128)(2,1)S(1)}, bf16[256,1280]{1,0:T(8,128)(2,1)S(1)}, bf16[256,1280]{1,0:T(8,128)(2,1)S(1)}, bf16[256,1280]{1,0:T(8,128)(2,1)S(1)}) custom-call(s32[1]{0:T(128)} %bitcast.3.where_ref, bf16[512,512]{1,0:T(8,128)(2,1)S(1)} %get-tuple-element.28.refs_0_, bf16[512,7168]{1,0:T(8,128)(2,1)} %bitcast.38), custom_call_target="tpu_custom_call" | custom-call | flops 1342177280 | bytes 5242880 | tf_op jit(solution)/shard_map/pallas_call | solution.py:116
  119.9 1.2 add_convert_fusion
  121.2 2.7 %collective-permute-start.19 = (bf16[256,1280]{1,0:T(8,128)(2,1)S(1)}, bf16[256,1280]{1,0:T(8,128)(2,1)S(1)}, u32[]{:S(2)}, u32[]{:S(2)}) collective-permute-start(bf16[256,1280]{1,0:T(8,128)(2,1)S(1)} %add_convert_fusion), channel_id=1, source_target_pairs={{0,3},{1,0},{2,1},{3,2},{4,7},{5,4},{6,5},{7,6},{8,11},{9,8},{10,9... | collective-permute-start | bytes 1966088 | tf_op jit(solution)/shard_map/ppermute | solution.py:238
  123.9 7.2 %collective-permute-done.14 = bf16[256,1280]{1,0:T(8,128)(2,1)S(1)} collective-permute-done((bf16[256,1280]{1,0:T(8,128)(2,1)S(1)}, bf16[256,1280]{1,0:T(8,128)(2,1)S(1)}, u32[]{:S(2)}, u32[]{:S(2)}) %collective-permute-start.14) | collective-permute-done | bytes 655392 | tf_op jit(solution)/shard_map/ppermute | solution.py:235
  131.8 13.3 %collective-permute-done.17.refs_4_ = bf16[256,1280]{1,0:T(8,128)(2,1)S(1)} collective-permute-done((bf16[256,1280]{1,0:T(8,128)(2,1)S(1)}, bf16[256,1280]{1,0:T(8,128)(2,1)S(1)}, u32[]{:S(2)}, u32[]{:S(2)}) %collective-permute-start.17) | collective-permute-done | bytes 655392 | tf_op jit(solution)/shard_map/ppermute | solution.py:236
  145.1 14.0 %collective-permute-done.15.refs_1_ = bf16[256,1280]{1,0:T(8,128)(2,1)S(1)} collective-permute-done((bf16[256,1280]{1,0:T(8,128)(2,1)S(1)}, bf16[256,1280]{1,0:T(8,128)(2,1)S(1)}, u32[]{:S(2)}, u32[]{:S(2)}) %collective-permute-start.15) | collective-permute-done | bytes 655392 | tf_op jit(solution)/shard_map/ppermute | solution.py:237
  159.2 1.6 join_sums.1
  160.8 8.2 %all-to-all-start.3 = ((bf16[32,16,1280]{2,1,0:T(8,128)(2,1)}), bf16[32,16,1280]{2,1,0:T(8,128)(2,1)S(1)}, u32[]{:S(2)}, u32[]{:S(2)}) async-start(bf16[32,16,1280]{2,1,0:T(8,128)(2,1)} %bitcast.16), calls=%async_computation.3 | async-start | bytes 2621440 | tf_op jit(solution)/shard_map/all_to_all | solution.py:243
  168.9 2.3 %convolution_convert_fusion.1 = bf16[256,2048]{1,0:T(8,128)(2,1)S(1)} fusion(bf16[512,256]{1,0:T(8,128)(2,1)S(1)} %fusion, bf16[512,2048]{1,0:T(8,128)(2,1)} %bitcast.15), kind=kOutput, calls=%fused_computation.1 | convolution fusion | flops 537395200 | bytes 3407872 | tf_op jit(solution)/shard_map/dot_general | solution.py:301
  171.4 2.7 %collective-permute-start.12 = (bf16[128,512]{1,0:T(8,128)(2,1)S(1)}, bf16[128,512]{1,0:T(8,128)(2,1)S(1)}, u32[]{:S(2)}, u32[]{:S(2)}) collective-permute-start(bf16[128,512]{1,0:T(8,128)(2,1)S(1)} %get-tuple-element.42), channel_id=1, source_target_pairs={{0,3},{1,0},{2,1},{3,2},{4,7},{5,4},{6,5},{7,6},{8,11},{9,8},{10,9... | collective-permute-start | bytes 393224 | tf_op jit(solution)/shard_map/ppermute | solution.py:219
  174.0 3.4 %collective-permute-done.10 = bf16[128,512]{1,0:T(8,128)(2,1)S(1)} collective-permute-done((bf16[128,512]{1,0:T(8,128)(2,1)S(1)}, bf16[128,512]{1,0:T(8,128)(2,1)S(1)}, u32[]{:S(2)}, u32[]{:S(2)}) %collective-permute-start.10) | collective-permute-done | bytes 131104 | tf_op jit(solution)/shard_map/ppermute | solution.py:219
  177.6 2.7 %collective-permute-start.13 = (bf16[256,512]{1,0:T(8,128)(2,1)S(1)}, bf16[256,512]{1,0:T(8,128)(2,1)S(1)}, u32[]{:S(2)}, u32[]{:S(2)}) collective-permute-start(bf16[256,512]{1,0:T(8,128)(2,1)S(1)} %get-tuple-element.40), channel_id=1, source_target_pairs={{0,3},{1,0},{2,1},{3,2},{4,7},{5,4},{6,5},{7,6},{8,11},{9,8},{10,9... | collective-permute-start | bytes 786440 | tf_op jit(solution)/shard_map/ppermute | solution.py:222
  180.2 5.3 %collective-permute-done.11 = bf16[256,512]{1,0:T(8,128)(2,1)S(1)} collective-permute-done((bf16[256,512]{1,0:T(8,128)(2,1)S(1)}, bf16[256,512]{1,0:T(8,128)(2,1)S(1)}, u32[]{:S(2)}, u32[]{:S(2)}) %collective-permute-start.11) | collective-permute-done | bytes 262176 | tf_op jit(solution)/shard_map/ppermute | solution.py:222
  185.7 2.5 %all-to-all-done.3 = bf16[32,16,1280]{2,1,0:T(8,128)(2,1)S(1)} async-done(((bf16[32,16,1280]{2,1,0:T(8,128)(2,1)}), bf16[32,16,1280]{2,1,0:T(8,128)(2,1)S(1)}, u32[]{:S(2)}, u32[]{:S(2)}) %all-to-all-start.3) | async-done | bytes 1310752 | tf_op jit(solution)/shard_map/all_to_all | solution.py:243
  188.7 1.0 pad_maximum_fusion
  (66 shorter events, 4.5 us)
Async XLA Ops:
  0.7 0.7 copy-start.4
  1.4 1.2 copy-start.6
  4.5 12.8 %collective-permute-start.1 = (bf16[256,640]{1,0:T(8,128)(2,1)S(1)}, bf16[256,640]{1,0:T(8,128)(2,1)S(1)}, u32[]{:S(2)}, u32[]{:S(2)}) collective-permute-start(bf16[256,640]{1,0:T(8,128)(2,1)S(1)} %get-tuple-element.22), channel_id=1, source_target_pairs={{0,1},{1,2},{2,3},{3,0},{4,5},{5,6},{6,7},{7,4},{8,9},{9,10},{10,1... | collective-permute-start | bytes 983048 | tf_op jit(solution)/shard_map/ppermute | solution.py:214
  6.9 10.4 %collective-permute-start = (bf16[256,640]{1,0:T(8,128)(2,1)S(1)}, bf16[256,640]{1,0:T(8,128)(2,1)}, u32[]{:S(2)}, u32[]{:S(2)}) collective-permute-start(bf16[256,640]{1,0:T(8,128)(2,1)S(1)} %get-tuple-element.22), channel_id=1, source_target_pairs={{0,3},{1,0},{2,1},{3,2},{4,7},{5,4},{6,5},{7,6},{8,11},{9,8},{10,9... | collective-permute-start | bytes 983048 | tf_op jit(solution)/shard_map/ppermute | solution.py:214
  9.1 27.3 %all-to-all-start.1 = ((bf16[32,16,1280]{2,1,0:T(8,128)(2,1)}), bf16[32,16,1280]{2,1,0:T(8,128)(2,1)S(1)}, u32[]{:S(2)}, u32[]{:S(2)}) async-start(bf16[32,16,1280]{2,1,0:T(8,128)(2,1)} %bitcast.7), calls=%async_computation.1 | async-start | bytes 2621440 | tf_op jit(solution)/shard_map/all_to_all | solution.py:243
  17.3 6.6 %collective-permute-start.2 = (bf16[128,640]{1,0:T(8,128)(2,1)S(1)}, bf16[128,640]{1,0:T(8,128)(2,1)S(1)}, u32[]{:S(2)}, u32[]{:S(2)}) collective-permute-start(bf16[128,640]{1,0:T(8,128)(2,1)S(1)} %slice.80), channel_id=1, source_target_pairs={{0,1},{1,2},{2,3},{3,0},{4,5},{5,6},{6,7},{7,4},{8,9},{9,10},{10,1... | collective-permute-start | bytes 491528 | tf_op jit(solution)/shard_map/ppermute | solution.py:215
  18.3 5.6 %collective-permute-start.3 = (bf16[128,640]{1,0:T(8,128)(2,1)S(1)}, bf16[128,640]{1,0:T(8,128)(2,1)S(1)}, u32[]{:S(2)}, u32[]{:S(2)}) collective-permute-start(bf16[128,640]{1,0:T(8,128)(2,1)S(1)} %slice.81), channel_id=1, source_target_pairs={{0,3},{1,0},{2,1},{3,2},{4,7},{5,4},{6,5},{7,6},{8,11},{9,8},{10,9... | collective-permute-start | bytes 491528 | tf_op jit(solution)/shard_map/ppermute | solution.py:215
  36.4 5.9 %copy-start.7 = (bf16[32,16,1280]{2,1,0:T(8,128)(2,1)}, bf16[32,16,1280]{2,1,0:T(8,128)(2,1)S(1)}, u32[]{:S(2)}) copy-start(bf16[32,16,1280]{2,1,0:T(8,128)(2,1)S(1)} %all-to-all-done.1) | copy-start | bytes 3932164
  36.4 52.5 %all-to-all-start = ((bf16[32,16,2176]{2,1,0:T(8,128)(2,1)}), bf16[32,16,2176]{2,1,0:T(8,128)(2,1)}, u32[]{:S(2)}, u32[]{:S(2)}) async-start(bf16[32,16,2176]{2,1,0:T(8,128)(2,1)} %bitcast.40), calls=%async_computation | async-start | bytes 4456448 | tf_op jit(solution)/shard_map/all_to_all | solution.py:243
  43.5 17.4 %collective-permute-start.4 = (bf16[256,1280]{1,0:T(8,128)(2,1)}, bf16[256,1280]{1,0:T(8,128)(2,1)S(1)}, u32[]{:S(2)}, u32[]{:S(2)}) collective-permute-start(bf16[256,1280]{1,0:T(8,128)(2,1)} %bitcast.8), channel_id=1, source_target_pairs={{0,1},{1,2},{2,3},{3,0},{4,5},{5,6},{6,7},{7,4},{8,9},{9,10},{10,1... | collective-permute-start | bytes 1966088 | tf_op jit(solution)/shard_map/ppermute | solution.py:226
  43.5 17.4 %collective-permute-start.6 = (bf16[256,1280]{1,0:T(8,128)(2,1)}, bf16[256,1280]{1,0:T(8,128)(2,1)S(1)}, u32[]{:S(2)}, u32[]{:S(2)}) collective-permute-start(bf16[256,1280]{1,0:T(8,128)(2,1)} %bitcast.9), channel_id=1, source_target_pairs={{0,3},{1,0},{2,1},{3,2},{4,7},{5,4},{6,5},{7,6},{8,11},{9,8},{10,9... | collective-permute-start | bytes 1966088 | tf_op jit(solution)/shard_map/ppermute | solution.py:226
  46.2 27.8 %collective-permute-start.8 = (bf16[256,1280]{1,0:T(8,128)(2,1)}, bf16[256,1280]{1,0:T(8,128)(2,1)S(1)}, u32[]{:S(2)}, u32[]{:S(2)}) collective-permute-start(bf16[256,1280]{1,0:T(8,128)(2,1)} %bitcast.8), channel_id=1, source_target_pairs={{0,3},{1,0},{2,1},{3,2},{4,7},{5,4},{6,5},{7,6},{8,11},{9,8},{10,9... | collective-permute-start | bytes 1966088 | tf_op jit(solution)/shard_map/ppermute | solution.py:227
  46.7 28.2 %collective-permute-start.9 = (bf16[256,1280]{1,0:T(8,128)(2,1)}, bf16[256,1280]{1,0:T(8,128)(2,1)}, u32[]{:S(2)}, u32[]{:S(2)}) collective-permute-start(bf16[256,1280]{1,0:T(8,128)(2,1)} %bitcast.9), channel_id=1, source_target_pairs={{0,1},{1,2},{2,3},{3,0},{4,5},{5,6},{6,7},{7,4},{8,9},{9,10},{10,1... | collective-permute-start | bytes 1966088 | tf_op jit(solution)/shard_map/ppermute | solution.py:227
  60.9 6.3 %copy-start.9 = (bf16[256,1280]{1,0:T(8,128)(2,1)}, bf16[256,1280]{1,0:T(8,128)(2,1)S(1)}, u32[]{:S(2)}) copy-start(bf16[256,1280]{1,0:T(8,128)(2,1)S(1)} %collective-permute-done.4.refs_2_) | copy-start | bytes 1966084
  60.9 28.0 %collective-permute-start.5 = (bf16[256,1280]{1,0:T(8,128)(2,1)S(1)}, bf16[256,1280]{1,0:T(8,128)(2,1)S(1)}, u32[]{:S(2)}, u32[]{:S(2)}) collective-permute-start(bf16[256,1280]{1,0:T(8,128)(2,1)S(1)} %collective-permute-done.4.refs_2_), channel_id=1, source_target_pairs={{0,1},{1,2},{2,3},{3,0},{4,5},{5,6},{6,7},{7,4},{8,9},{9,10},{10,1... | collective-permute-start | bytes 1966088 | tf_op jit(solution)/shard_map/ppermute | solution.py:228
  60.9 6.3 %copy-start.10 = (bf16[256,1280]{1,0:T(8,128)(2,1)}, bf16[256,1280]{1,0:T(8,128)(2,1)S(1)}, u32[]{:S(2)}) copy-start(bf16[256,1280]{1,0:T(8,128)(2,1)S(1)} %collective-permute-done.6.refs_1_) | copy-start | bytes 1966084
  60.9 28.0 %collective-permute-start.7 = (bf16[256,1280]{1,0:T(8,128)(2,1)S(1)}, bf16[256,1280]{1,0:T(8,128)(2,1)S(1)}, u32[]{:S(2)}, u32[]{:S(2)}) collective-permute-start(bf16[256,1280]{1,0:T(8,128)(2,1)S(1)} %collective-permute-done.6.refs_1_), channel_id=1, source_target_pairs={{0,3},{1,0},{2,1},{3,2},{4,7},{5,4},{6,5},{7,6},{8,11},{9,8},{10,9... | collective-permute-start | bytes 1966088 | tf_op jit(solution)/shard_map/ppermute | solution.py:228
  67.2 1.0 copy-start.2
  68.2 1.0 copy-start.3
  73.9 1.0 copy-start.12
  80.4 1.0 copy-start
  81.4 1.0 copy-start.1
  88.9 0.8 copy-start.8
  88.9 1.1 copy-start.11
  98.4 21.5 %collective-permute-start.18 = (bf16[256,1280]{1,0:T(8,128)(2,1)S(1)}, bf16[256,1280]{1,0:T(8,128)(2,1)}, u32[]{:S(2)}, u32[]{:S(2)}) collective-permute-start(bf16[256,1280]{1,0:T(8,128)(2,1)S(1)} %get-tuple-element.36), channel_id=1, source_target_pairs={{0,3},{1,0},{2,1},{3,2},{4,7},{5,4},{6,5},{7,6},{8,11},{9,8},{10,9... | collective-permute-start | bytes 1966088 | tf_op jit(solution)/shard_map/ppermute | solution.py:235
  104.8 55.9 %all-to-all-start.2 = ((bf16[32,16,2048]{2,1,0:T(8,128)(2,1)}), bf16[32,16,2048]{2,1,0:T(8,128)(2,1)}, u32[]{:S(2)}, u32[]{:S(2)}) async-start(bf16[32,16,2048]{2,1,0:T(8,128)(2,1)} %bitcast.14), calls=%async_computation.2 | async-start | bytes 4194304 | tf_op jit(solution)/shard_map/all_to_all | solution.py:243
  113.8 17.4 %collective-permute-start.14 = (bf16[256,1280]{1,0:T(8,128)(2,1)S(1)}, bf16[256,1280]{1,0:T(8,128)(2,1)S(1)}, u32[]{:S(2)}, u32[]{:S(2)}) collective-permute-start(bf16[256,1280]{1,0:T(8,128)(2,1)S(1)} %get-tuple-element.31), channel_id=1, source_target_pairs={{0,1},{1,2},{2,3},{3,0},{4,5},{5,6},{6,7},{7,4},{8,9},{9,10},{10,1... | collective-permute-start | bytes 1966088 | tf_op jit(solution)/shard_map/ppermute | solution.py:235
  113.9 17.9 %collective-permute-start.16 = (bf16[256,1280]{1,0:T(8,128)(2,1)S(1)}, bf16[256,1280]{1,0:T(8,128)(2,1)S(1)}, u32[]{:S(2)}, u32[]{:S(2)}) collective-permute-start(bf16[256,1280]{1,0:T(8,128)(2,1)S(1)} %get-tuple-element.32), channel_id=1, source_target_pairs={{0,3},{1,0},{2,1},{3,2},{4,7},{5,4},{6,5},{7,6},{8,11},{9,8},{10,9... | collective-permute-start | bytes 1966088 | tf_op jit(solution)/shard_map/ppermute | solution.py:236
  116.6 28.6 %collective-permute-start.17 = (bf16[256,1280]{1,0:T(8,128)(2,1)S(1)}, bf16[256,1280]{1,0:T(8,128)(2,1)S(1)}, u32[]{:S(2)}, u32[]{:S(2)}) collective-permute-start(bf16[256,1280]{1,0:T(8,128)(2,1)S(1)} %get-tuple-element.34), channel_id=1, source_target_pairs={{0,1},{1,2},{2,3},{3,0},{4,5},{5,6},{6,7},{7,4},{8,9},{9,10},{10,1... | collective-permute-start | bytes 1966088 | tf_op jit(solution)/shard_map/ppermute | solution.py:236
  121.2 10.5 %copy-start.13 = (bf16[256,8]{0,1:T(8,128)(2,1)S(1)}, bf16[256,8]{0,1:T(8,128)(2,1)}, u32[]{:S(2)}) copy-start(bf16[256,8]{0,1:T(8,128)(2,1)} %param.10) | copy-start | bytes 12292
  121.2 10.5 %copy-start.5 = (s32[256,8]{0,1:T(8,128)S(1)}, s32[256,8]{0,1:T(8,128)}, u32[]{:S(2)}) copy-start(s32[256,8]{0,1:T(8,128)} %param.9) | copy-start | bytes 24580
  121.2 23.9 %collective-permute-start.19 = (bf16[256,1280]{1,0:T(8,128)(2,1)S(1)}, bf16[256,1280]{1,0:T(8,128)(2,1)S(1)}, u32[]{:S(2)}, u32[]{:S(2)}) collective-permute-start(bf16[256,1280]{1,0:T(8,128)(2,1)S(1)} %add_convert_fusion), channel_id=1, source_target_pairs={{0,3},{1,0},{2,1},{3,2},{4,7},{5,4},{6,5},{7,6},{8,11},{9,8},{10,9... | collective-permute-start | bytes 1966088 | tf_op jit(solution)/shard_map/ppermute | solution.py:238
  131.4 27.8 %collective-permute-start.15 = (bf16[256,1280]{1,0:T(8,128)(2,1)S(1)}, bf16[256,1280]{1,0:T(8,128)(2,1)S(1)}, u32[]{:S(2)}, u32[]{:S(2)}) collective-permute-start(bf16[256,1280]{1,0:T(8,128)(2,1)S(1)} %add_convert_fusion.1), channel_id=1, source_target_pairs={{0,1},{1,2},{2,3},{3,0},{4,5},{5,6},{6,7},{7,4},{8,9},{9,10},{10,1... | collective-permute-start | bytes 1966088 | tf_op jit(solution)/shard_map/ppermute | solution.py:237
  160.8 27.4 %all-to-all-start.3 = ((bf16[32,16,1280]{2,1,0:T(8,128)(2,1)}), bf16[32,16,1280]{2,1,0:T(8,128)(2,1)S(1)}, u32[]{:S(2)}, u32[]{:S(2)}) async-start(bf16[32,16,1280]{2,1,0:T(8,128)(2,1)} %bitcast.16), calls=%async_computation.3 | async-start | bytes 2621440 | tf_op jit(solution)/shard_map/all_to_all | solution.py:243
  171.3 6.1 %collective-permute-start.10 = (bf16[128,512]{1,0:T(8,128)(2,1)S(1)}, bf16[128,512]{1,0:T(8,128)(2,1)S(1)}, u32[]{:S(2)}, u32[]{:S(2)}) collective-permute-start(bf16[128,512]{1,0:T(8,128)(2,1)S(1)} %get-tuple-element.41), channel_id=1, source_target_pairs={{0,1},{1,2},{2,3},{3,0},{4,5},{5,6},{6,7},{7,4},{8,9},{9,10},{10,1... | collective-permute-start | bytes 393224 | tf_op jit(solution)/shard_map/ppermute | solution.py:219
  171.4 6.0 %collective-permute-start.12 = (bf16[128,512]{1,0:T(8,128)(2,1)S(1)}, bf16[128,512]{1,0:T(8,128)(2,1)S(1)}, u32[]{:S(2)}, u32[]{:S(2)}) collective-permute-start(bf16[128,512]{1,0:T(8,128)(2,1)S(1)} %get-tuple-element.42), channel_id=1, source_target_pairs={{0,3},{1,0},{2,1},{3,2},{4,7},{5,4},{6,5},{7,6},{8,11},{9,8},{10,9... | collective-permute-start | bytes 393224 | tf_op jit(solution)/shard_map/ppermute | solution.py:219
  177.5 8.1 %collective-permute-start.11 = (bf16[256,512]{1,0:T(8,128)(2,1)S(1)}, bf16[256,512]{1,0:T(8,128)(2,1)S(1)}, u32[]{:S(2)}, u32[]{:S(2)}) collective-permute-start(bf16[256,512]{1,0:T(8,128)(2,1)S(1)} %get-tuple-element.39), channel_id=1, source_target_pairs={{0,1},{1,2},{2,3},{3,0},{4,5},{5,6},{6,7},{7,4},{8,9},{9,10},{10,1... | collective-permute-start | bytes 786440 | tf_op jit(solution)/shard_map/ppermute | solution.py:222
  177.6 8.0 %collective-permute-start.13 = (bf16[256,512]{1,0:T(8,128)(2,1)S(1)}, bf16[256,512]{1,0:T(8,128)(2,1)S(1)}, u32[]{:S(2)}, u32[]{:S(2)}) collective-permute-start(bf16[256,512]{1,0:T(8,128)(2,1)S(1)} %get-tuple-element.40), channel_id=1, source_target_pairs={{0,3},{1,0},{2,1},{3,2},{4,7},{5,4},{6,5},{7,6},{8,11},{9,8},{10,9... | collective-permute-start | bytes 786440 | tf_op jit(solution)/shard_map/ppermute | solution.py:222

commit v4 on v3

--- a/solution.py
+++ b/solution.py
@@ -25,91 +25,101 @@
         return copy
 
 
-def expert_call(where, weights, xs=(), segs=(), carry=(), inv=None, hidden=None, jobs=(), outs=()):
+def expert_call(where, weights, xs=(), segs=(), carry=(), inv=None, hidden=None, jobs=(), outs=(), stash=((), ()), held=None, stored=()):
     slices = lax.axis_size("tp")
     w_gate, w_up, w_down = weights
     d_all, ff = w_gate.shape
     span = d_all // slices
     finish = bool(segs) and bool(jobs)
     rows = hidden.shape[0] if hidden is not None else sum(xs[i].shape[0] for i in segs[0][0])
+
+    def columns_of(some):
+        found = []
+        for step, offset, width, *_ in some:
+            if (step, offset, width) not in found:
+                found.append((step, offset, width))
+        return found
+
+    def weight_shapes(seg_list, column_list):
+        shapes = []
+        for _, _, _, width, _ in seg_list:
+            shapes += [(width, ff)] * 2
+        return shapes + [(ff, width) for _, _, width in column_list]
+
+    columns, later = columns_of(jobs), columns_of(stash[1])
     results = [((rows, ff), F32)] * 2 if not jobs else [((rows, ff), BF16)] * finish + [(s, BF16) for s in outs]
-    resident = [] if hidden is None else [hidden]
-    streamed = list(xs) + list(carry) + ([w_gate, w_up] if segs else []) + ([w_down] if jobs else [])
-    columns = []
-    for step, offset, width, *_ in jobs:
-        if (step, offset, width) not in columns:
-            columns.append((step, offset, width))
-    scratch = []
-    for _, _, _, width, _ in segs:
-        scratch += [pltpu.VMEM((rows, width), BF16)] + [pltpu.VMEM((width, ff), BF16)] * 2
-    scratch += [pltpu.VMEM((rows, ff), F32)] * len(carry)
+    results += [(s, BF16) for s in weight_shapes(stash[0], later)]
+    resident = list(xs) + list(carry) + ([] if hidden is None else [hidden]) + list(held or ())
+    streamed = ([] if held else [w_gate, w_up, w_down]) + list(stored)
+    buffers = [] if held else weight_shapes(segs, columns)
+    scratch = [pltpu.VMEM(s, BF16) for s in buffers]
     if finish:
         scratch += [pltpu.VMEM((rows, ff), F32)] * 2
-    if inv is not None:
-        scratch += [pltpu.VMEM((rows, SIDE), BF16)]
-    scratch += [pltpu.VMEM((ff, width), BF16) for _, _, width in columns]
-    n_sems = sum(len(s[0]) + 2 for s in segs) + len(carry) + (inv is not None) + len(columns)
-    scratch += [pltpu.SemaphoreType.DMA((n_sems,))]
+    scratch += [pltpu.VMEM((rows, ff), F32)] * len(stored)
+    n_copies = len(stored) + len(buffers) + len(weight_shapes(stash[0], later))
+    scratch += [pltpu.SemaphoreType.DMA((max(n_copies, 1),))]
 
     def body(where_ref, *refs):
         refs = list(refs)
         take = lambda n: [refs.pop(0) for _ in range(n)]
+        x_refs, carried = take(len(xs)), take(len(carry))
         hidden_ref = take(hidden is not None)
-        x_refs, carried = take(len(xs)), take(len(carry))
-        wg, wu = take(2) if segs else (None, None)
-        wd = take(bool(jobs))
+        held_refs = take(len(held or ()))
+        wg, wu, wd = (None,) * 3 if held else take(3)
+        stored_refs = take(len(stored))
         out_refs = take(len(results))
-        seg_bufs = [take(3) for _ in segs]
-        carry_bufs = take(len(carry))
-        accs = take(2) if finish else out_refs
-        inv_buf = take(inv is not None)
-        col_bufs = take(len(columns))
+        bufs = take(len(buffers)) if not held else held_refs
+        accs = take(2) if finish else out_refs[:2]
+        stored_bufs = take(len(stored))
         copies = Copies(refs.pop(0))
         z = where_ref[0]
 
-        def first(step, offset):
-            return pl.multiple_of(lax.rem(z + step, slices) * span + offset, 128)
-
-        seg_waits, col_waits = [], []
-        for (index, step, offset, width, col), (xb, gb, ub) in zip(segs, seg_bufs):
-            at = pl.ds(first(step, offset), width)
-            waits, row = [], 0
-            for i in index:
-                count = x_refs[i].shape[0]
-                waits.append(copies.start(x_refs[i].at[:, pl.ds(col, width)], xb.at[pl.ds(row, count), :]))
-                row += count
-            seg_waits.append(waits + [copies.start(wg.at[at, :], gb), copies.start(wu.at[at, :], ub)])
-        carry_waits = [copies.start(c, b) for c, b in zip(carried, carry_bufs)]
-        if inv is not None:
-            inv_wait = copies.start(x_refs[inv[0]].at[:, pl.ds(inv[1], SIDE)], inv_buf[0])
-        for (step, offset, width), wb in zip(columns, col_bufs):
-            col_waits.append(copies.start(wd[0].at[:, pl.ds(first(step, offset), width)], wb))
-        for k, (xb, *w_bufs) in enumerate(seg_bufs):
-            for w in seg_waits[k]:
-                w.wait()
-            for n, (w_buf, acc) in enumerate(zip(w_bufs, accs)):
-                term = jnp.dot(xb[...], w_buf[...], preferred_element_type=F32)
+        def bring(seg_list, column_list, into):
+            waits = []
+            for _, step, offset, width, _ in seg_list:
+                at = pl.ds(pl.multiple_of(lax.rem(z + step, slices) * span + offset, 128), width)
+                waits += [copies.start(w.at[at, :], into[len(waits) + n]) for n, w in enumerate((wg, wu))]
+            for step, offset, width in column_list:
+                at = pl.ds(pl.multiple_of(lax.rem(z + step, slices) * span + offset, 128), width)
+                waits.append(copies.start(wd.at[:, at], into[len(waits)]))
+            return waits
+
+        waits = [] if held else bring(segs, columns, bufs)
+        stored_waits = [copies.start(r, b) for r, b in zip(stored_refs, stored_bufs)]
+        n_stash = len(weight_shapes(stash[0], later))
+        stash_waits = bring(stash[0], later, out_refs[len(out_refs) - n_stash :]) if n_stash else []
+        for k, (index, _, _, width, col) in enumerate(segs):
+            x = [x_refs[i][:, col : col + width] for i in index]
+            x = x[0] if len(x) == 1 else jnp.concatenate(x, axis=0)
+            for n, acc in enumerate(accs):
+                if waits:
+                    waits[2 * k + n].wait()
+                term = jnp.dot(x, bufs[2 * k + n][...], preferred_element_type=F32)
                 if k:
                     term = acc[...] + term
-                if carry and k == len(segs) - 1:
-                    carry_waits[n].wait()
-                    term = term + carry_bufs[n][...]
+                elif carry:
+                    term = carried[n][...] + term
+                if stored and k == len(segs) - 1:
+                    stored_waits[n].wait()
+                    term = stored_bufs[n][...] + term
                 acc[...] = term
         if finish:
-            inv_wait.wait()
-            scale = jnp.sum(inv_buf[0][...].astype(F32), axis=1, keepdims=True)
+            scale = jnp.sum(x_refs[inv[0]][:, inv[1] : inv[1] + SIDE].astype(F32), axis=1, keepdims=True)
             gate = accs[0][...] * scale
             hidden_ref = [out_refs.pop(0)]
             hidden_ref[0][...] = (jax.nn.silu(gate) * (accs[1][...] * scale)).astype(BF16)
         waited = set()
         for step, offset, width, row, count, targets in jobs:
             k = columns.index((step, offset, width))
-            if k not in waited:
-                col_waits[k].wait()
+            if waits and k not in waited:
+                waits[2 * len(segs) + k].wait()
                 waited.add(k)
-            term = jnp.dot(hidden_ref[0][row : row + count, :], col_bufs[k][...], preferred_element_type=F32).astype(BF16)
+            w = bufs[2 * len(segs) + k]
+            term = jnp.dot(hidden_ref[0][row : row + count, :], w[...], preferred_element_type=F32).astype(BF16)
             for index, top, n, col in targets:
                 out_refs[index][:, col : col + width] = term[top : top + n, :]
+        for w in stash_waits:
+            w.wait()
 
     vmem, hbm = pl.BlockSpec(memory_space=pltpu.VMEM), pl.BlockSpec(memory_space=pltpu.HBM)
     flops = sum(4 * rows * s[3] * ff for s in segs) + sum(2 * j[4] * ff * j[2] for j in jobs)
@@ -117,10 +127,10 @@
         body,
         in_specs=[pl.BlockSpec(memory_space=pltpu.SMEM)] + [vmem] * len(resident) + [hbm] * len(streamed),
         out_specs=[vmem] * len(results),
-        out_shape=[pltpu.VMEM(s, t) if jobs else jax.ShapeDtypeStruct(s, t) for s, t in results],
+        out_shape=[pltpu.VMEM(s, t) for s, t in results],
         scratch_shapes=scratch,
         cost_estimate=pl.CostEstimate(flops=flops, bytes_accessed=flops // 256, transcendentals=0),
-        compiler_params=pltpu.CompilerParams(vmem_limit_bytes=28 * 2**20),
+        compiler_params=pltpu.CompilerParams(vmem_limit_bytes=20 * 2**20),
     )(
         where,
         *[pltpu.with_memory_space_constraint(x, pltpu.VMEM) for x in resident],
@@ -142,7 +152,9 @@
     tok, width = tokens.shape
     rows, bulk = window * CAP, width - EARLY
 
-    def body(tokens_ref, gain_ref, ids_ref, pick_ref, bulk_ref, early_ref):
+    def body(tokens_hbm, gain_ref, ids_ref, pick_ref, bulk_ref, early_ref, tokens_ref, sem):
+        load = pltpu.make_async_copy(tokens_hbm, tokens_ref, sem)
+        load.start()
         expert = lax.broadcasted_iota(jnp.int32, (window, tok), 0)
         match = jnp.zeros((window, tok), F32)
         for k in range(ids.shape[0]):
@@ -157,19 +169,23 @@
         wanted = (lax.broadcasted_iota(jnp.int32, (rows, tok), 0) % CAP).astype(F32)
         pick = jnp.where(spread == wanted, 1.0, 0.0).astype(BF16)
         pick_ref[...] = pick
+        gain = gain_ref[...].astype(F32).reshape(1, width)
+        load.wait()
         values = tokens_ref[...].astype(F32)
-        gained = (values * gain_ref[...].astype(F32)).astype(BF16)
+        gained = (values * gain).astype(BF16)
         bulk_ref[...] = jnp.dot(pick, gained[:, EARLY:], preferred_element_type=F32).astype(BF16)
         early_ref[:, :EARLY] = gained[:, :EARLY]
         early_ref[:, EARLY:] = side_columns(jnp.sum(values * values, axis=1, keepdims=True))
 
     return pl.pallas_call(
         body,
+        in_specs=[pl.BlockSpec(memory_space=pltpu.HBM)] + [pl.BlockSpec(memory_space=pltpu.VMEM)] * 2,
+        scratch_shapes=[pltpu.VMEM((tok, width), BF16), pltpu.SemaphoreType.DMA],
         out_shape=[jax.ShapeDtypeStruct(s, BF16) for s in ((rows, tok), (rows, bulk), (tok, EARLY + SIDE))],
         cost_estimate=pl.CostEstimate(flops=2 * rows * tok * bulk, bytes_accessed=2 * tok * width, transcendentals=0),
         compiler_params=pltpu.CompilerParams(vmem_limit_bytes=24 * 2**20),
         name="head",
-    )(tokens, norm_gain.reshape(1, width), ids)
+    )(pltpu.with_memory_space_constraint(tokens, pltpu.HBM), norm_gain, ids)
 
 
 def join_sums(low, high):
@@ -266,22 +282,25 @@
     below, above, far = spread_halves(mine[:half], mine[half:])
 
     weights = (w_gate, w_up, w_down)
+    low, high = (0, half), (half, half)
+    far_segs = [((0, 1), 2, EARLY, bulk, 0)]
+    far_jobs = [
+        (2, EARLY, bulk, 0, rows, ((0, 0, half, 0), (1, half, half, 0))),
+        (1, EARLY, bulk, *high, ((2, 0, half, 0),)),
+        (3, EARLY, bulk, *low, ((3, 0, half, 0),)),
+    ]
     sums = expert_call(where, weights, [mine], [((0,), 0, EARLY, bulk, 0)])
     sums = expert_call(
         where, weights, [*above, *below],
         [((0, 1), 1, EARLY, bulk, 0), ((2, 3), 3, EARLY, bulk, 0)], sums,
     )
-    low, high = (0, half), (half, half)
+    *sums, = expert_call(
+        where, weights, [early_rows],
+        [((0,), k, 0, EARLY, k * EARLY) for k in range(n_tp)], stored=sums, stash=(far_segs, far_jobs),
+    )
     hidden, f_low, f_high, a_high, b_low = expert_call(
-        where, weights, [early_rows, *far],
-        [((0,), k, 0, EARLY, k * EARLY) for k in range(n_tp)] + [((1, 2), 2, EARLY, bulk, 0)],
-        sums, inv=(0, n_tp * EARLY),
-        jobs=[
-            (2, EARLY, bulk, 0, rows, ((0, 0, half, 0), (1, half, half, 0))),
-            (1, EARLY, bulk, *high, ((2, 0, half, 0),)),
-            (3, EARLY, bulk, *low, ((3, 0, half, 0),)),
-        ],
-        outs=[(half, bulk)] * 4,
+        where, weights, [*far, early_rows], far_segs, sums[:2], inv=(2, n_tp * EARLY),
+        jobs=far_jobs, outs=[(half, bulk)] * 4, held=sums[2:],
     )
     (p_early,) = expert_call(
         where, weights, hidden=hidden,

time: 191 us -> 183 us (0.958)
  waiting for transfers between devices: 81.9 us -> 75.1 us
  local copies, waits for them, and re-layouts: 11 us -> 7.62 us
  Pallas kernels: 28.6 us -> 31 us
    ppermute x1, waiting for transfers between devices: 13.3 us -> 0.01 us  [fold_halves(): lax.ppermute(above[1], 'tp', up)]
    ppermute x1, waiting for transfers between devices: 0.01 us -> 9.94 us  [fold_halves(): lax.ppermute(below[0], 'tp', dn)]
    ppermute x1, waiting for transfers between devices: 14 us -> 4.36 us  [fold_halves(): dn_low = lax.ppermute(add(above[0], got_low), 'tp', up)]
    ppermute x1, waiting for transfers between devices: 0.01 us -> 9.68 us  [fold_halves(): up_high = lax.ppermute(add(below[1], got_high), 'tp', dn)]
    ppermute x1, waiting for transfers between devices: 0.01 us -> 7.54 us  [fold_halves(): lax.ppermute(far[1], 'tp', dn)]
    ppermute x1, waiting for transfers between devices: 7.25 us -> 0.01 us  [fold_halves(): lax.ppermute(far[0], 'tp', up)]
    ppermute x1, waiting for transfers between devices: 6.46 us -> 0.8 us  [spread_halves(): lax.ppermute(below_low, 'tp', up)]
    ppermute x1, waiting for transfers between devices: 4.68 us -> 7.32 us  [spread_halves(): lax.ppermute(low, 'tp', dn)]
  transfers between devices with their start and end apart: 24 -> 24, of which waited for: 12 -> 13; matrix products, arithmetic and copies ran while one was open for 6% -> 6% of each run, Pallas kernels for 10% -> 13%
where the time goes in v4:
time: 183 us; the launch traced here: 182 us
  waiting for transfers between devices  75.1 us (41%)
  starting transfers between devices  59.1 us (32%)
  Pallas kernels  31 us (17%)
  local copies, waits for them, and re-layouts  7.62 us (4%)
  matrix products  5.02 us (3%)
  other arithmetic  4 us (2%)
    all_to_all x4, starting transfers between devices, exchange(): lax.all_to_all(shaped, 'ep', 0, 0, tiled=True).reshape(rows, x.shape[1])  30.3 us
    pallas_call x6, Pallas kernels, expert_call(): pl.pallas_call(body, in_specs=[pl.BlockSpec(memory_space=pltpu.SMEM)] + [...  26.5 us
    ppermute x1, waiting for transfers between devices, spread_halves(): lax.ppermute(low, 'tp', up)  13.3 us
    all_to_all x4, waiting for transfers between devices, exchange(): lax.all_to_all(shaped, 'ep', 0, 0, tiled=True).reshape(rows, x.shape[1])  11.1 us
    ppermute x1, waiting for transfers between devices, fold_halves(): lax.ppermute(below[0], 'tp', dn)  9.94 us
    ppermute x1, waiting for transfers between devices, fold_halves(): up_high = lax.ppermute(add(below[1], got_high), 'tp', dn)  9.68 us
    ppermute x1, waiting for transfers between devices, fold_halves(): lax.ppermute(far[1], 'tp', dn)  7.54 us
    ppermute x1, waiting for transfers between devices, spread_halves(): lax.ppermute(low, 'tp', dn)  7.32 us
  transfers between devices with their start and end apart: 24, of which 13 were waited for; matrix products, arithmetic and copies ran while one was open for 6% of the time, Pallas kernels for 13%

profile of v4, /device:TPU:1, one launch (start us, length us, event | category | flops | bytes accessed | tf_op | source)
XLA Modules:
  0.0 182.2 jit_solution(16062721129862931877)
XLA Ops:
  1.4 2.9 %head.1 = (bf16[512,256]{1,0:T(8,128)(2,1)S(1)}, bf16[512,1280]{1,0:T(8,128)(2,1)}, bf16[256,640]{1,0:T(8,128)(2,1)S(1)}) custom-call(bf16[256,1792]{1,0:T(8,128)(2,1)} %tokens_hbm.1, bf16[1792]{0:T(1024)(128)(2,1)S(1)} %copy-done.10, s32[8,256]{1,0:T(8,128)S(1)} %bitcast.31), custom_call_target="tpu_custom_call" | custom-call | flops 335544320 | bytes 917504 | tf_op jit(solution)/shard_map/head/pallas_call | solution.py:180
  4.3 2.5 %collective-permute-start.5 = (bf16[256,640]{1,0:T(8,128)(2,1)S(1)}, bf16[256,640]{1,0:T(8,128)(2,1)S(1)}, u32[]{:S(2)}, u32[]{:S(2)}) collective-permute-start(bf16[256,640]{1,0:T(8,128)(2,1)S(1)} %get-tuple-element.30), channel_id=1, source_target_pairs={{0,1},{1,2},{2,3},{3,0},{4,5},{5,6},{6,7},{7,4},{8,9},{9,10},{10,1... | collective-permute-start | bytes 983048 | tf_op jit(solution)/shard_map/ppermute | solution.py:230
  6.8 2.2 %collective-permute-start.4 = (bf16[256,640]{1,0:T(8,128)(2,1)S(1)}, bf16[256,640]{1,0:T(8,128)(2,1)}, u32[]{:S(2)}, u32[]{:S(2)}) collective-permute-start(bf16[256,640]{1,0:T(8,128)(2,1)S(1)} %get-tuple-element.30), channel_id=1, source_target_pairs={{0,3},{1,0},{2,1},{3,2},{4,7},{5,4},{6,5},{7,6},{8,11},{9,8},{10,9... | collective-permute-start | bytes 983048 | tf_op jit(solution)/shard_map/ppermute | solution.py:230
  9.0 8.0 %all-to-all-start = ((bf16[32,16,1280]{2,1,0:T(8,128)(2,1)}), bf16[32,16,1280]{2,1,0:T(8,128)(2,1)S(1)}, u32[]{:S(2)}, u32[]{:S(2)}) async-start(bf16[32,16,1280]{2,1,0:T(8,128)(2,1)} %bitcast.4), calls=%async_computation | async-start | bytes 2621440 | tf_op jit(solution)/shard_map/all_to_all | solution.py:259
  17.3 0.9 slice.83
  18.3 2.7 %collective-permute-start.7 = (bf16[128,640]{1,0:T(8,128)(2,1)S(1)}, bf16[128,640]{1,0:T(8,128)(2,1)S(1)}, u32[]{:S(2)}, u32[]{:S(2)}) collective-permute-start(bf16[128,640]{1,0:T(8,128)(2,1)S(1)} %slice.83), channel_id=1, source_target_pairs={{0,3},{1,0},{2,1},{3,2},{4,7},{5,4},{6,5},{7,6},{8,11},{9,8},{10,9... | collective-permute-start | bytes 491528 | tf_op jit(solution)/shard_map/ppermute | solution.py:231
  21.0 1.0 slice_dynamic-update-slice_fusion.2
  22.1 1.0 convert_reduce_fusion.2
  23.0 0.9 collective-permute-done.6
  24.3 2.2 %convolution_convert_fusion = bf16[512,2176]{1,0:T(8,128)(2,1)} fusion(bf16[512,256]{1,0:T(8,128)(2,1)S(1)} %get-tuple-element.28, bf16[256,2176]{1,0:T(8,128)(2,1)S(1)} %pad_dynamic-update-slice_fusion), kind=kOutput, calls=%fused_computation | convolution fusion | flops 571539456 | bytes 3604480 | tf_op jit(solution)/shard_map/dot_general | solution.py:271
  26.5 9.8 %all-to-all-done = bf16[32,16,1280]{2,1,0:T(8,128)(2,1)S(1)} async-done(((bf16[32,16,1280]{2,1,0:T(8,128)(2,1)}), bf16[32,16,1280]{2,1,0:T(8,128)(2,1)S(1)}, u32[]{:S(2)}, u32[]{:S(2)}) %all-to-all-start) | async-done | bytes 1310752 | tf_op jit(solution)/shard_map/all_to_all | solution.py:259
  36.3 5.2 %all-to-all-start.1 = ((bf16[32,16,2176]{2,1,0:T(8,128)(2,1)}), bf16[32,16,2176]{2,1,0:T(8,128)(2,1)S(1)}, u32[]{:S(2)}, u32[]{:S(2)}) async-start(bf16[32,16,2176]{2,1,0:T(8,128)(2,1)} %bitcast.48), calls=%async_computation.1 | async-start | bytes 4456448 | tf_op jit(solution)/shard_map/all_to_all | solution.py:259
  41.6 1.1 fusion.3
  42.7 2.7 %collective-permute-start.2 = (bf16[256,1280]{1,0:T(8,128)(2,1)}, bf16[256,1280]{1,0:T(8,128)(2,1)}, u32[]{:S(2)}, u32[]{:S(2)}) collective-permute-start(bf16[256,1280]{1,0:T(8,128)(2,1)} %bitcast.6), channel_id=1, source_target_pairs={{0,3},{1,0},{2,1},{3,2},{4,7},{5,4},{6,5},{7,6},{8,11},{9,8},{10,9... | collective-permute-start | bytes 1966088 | tf_op jit(solution)/shard_map/ppermute | solution.py:242
  45.8 1.0 collective-permute-start.9
  46.8 13.3 %collective-permute-done.refs_2_ = bf16[256,1280]{1,0:T(8,128)(2,1)} collective-permute-done((bf16[256,1280]{1,0:T(8,128)(2,1)}, bf16[256,1280]{1,0:T(8,128)(2,1)}, u32[]{:S(2)}, u32[]{:S(2)}) %collective-permute-start) | collective-permute-done | bytes 655392 | tf_op jit(solution)/shard_map/ppermute | solution.py:242
  60.2 2.7 %collective-permute-start.3 = (bf16[256,1280]{1,0:T(8,128)(2,1)}, bf16[256,1280]{1,0:T(8,128)(2,1)}, u32[]{:S(2)}, u32[]{:S(2)}) collective-permute-start(bf16[256,1280]{1,0:T(8,128)(2,1)} %collective-permute-done.2.refs_1_), channel_id=1, source_target_pairs={{0,3},{1,0},{2,1},{3,2},{4,7},{5,4},{6,5},{7,6},{8,11},{9,8},{10,9... | collective-permute-start | bytes 1966088 | tf_op jit(solution)/shard_map/ppermute | solution.py:244
  62.8 3.0 %shard_map.73 = (f32[512,512]{1,0:T(8,128)S(1)}, f32[512,512]{1,0:T(8,128)S(1)}) custom-call(s32[1]{0:T(128)} %bitcast.3.where_ref, bf16[512,1280]{1,0:T(8,128)(2,1)S(1)} %bitcast.30, bf16[7168,512]{1,0:T(8,128)(2,1)} %bitcast.33, bf16[7168,512]{1,0:T(8,128)(2,1)} %bitcast.38, bf16[512,7168]{1,0:T(8,128)(2,1)} %bitcast.43), custom_call_target="tpu_custom_call" | custom-call | flops 1342177280 | bytes 5242880 | tf_op jit(solution)/shard_map/pallas_call | solution.py:126
  65.9 7.3 %collective-permute-done.8.refs_0_ = bf16[256,1280]{1,0:T(8,128)(2,1)} collective-permute-done((bf16[256,1280]{1,0:T(8,128)(2,1)}, bf16[256,1280]{1,0:T(8,128)(2,1)}, u32[]{:S(2)}, u32[]{:S(2)}) %collective-permute-start.8) | collective-permute-done | bytes 655392 | tf_op jit(solution)/shard_map/ppermute | solution.py:243
  73.2 1.0 collective-permute-done.9.refs_3_
  74.2 6.4 %shard_map.74 = (f32[512,512]{1,0:T(8,128)S(1)}, f32[512,512]{1,0:T(8,128)S(1)}) custom-call(s32[1]{0:T(128)} %bitcast.3.where_ref, bf16[256,1280]{1,0:T(8,128)(2,1)} %collective-permute-done.8.refs_0_, bf16[256,1280]{1,0:T(8,128)(2,1)} %collective-permute-done.2.refs_1_, bf16[256,1280]{1,0:T(8,128)(2,1)} %collective-permute-done.refs_2_, ...), custom_call_target="tpu_custom_call" | custom-call | flops 2684354560 | bytes 10485760 | tf_op jit(solution)/shard_map/pallas_call | solution.py:126
  80.6 1.0 copy-done
  81.6 1.0 copy-done.1
  82.6 4.8 %shard_map.75 = (f32[512,512]{1,0:T(8,128)S(1)}, f32[512,512]{1,0:T(8,128)S(1)}, bf16[1280,512]{1,0:T(8,128)(2,1)S(1)}, bf16[1280,512]{1,0:T(8,128)(2,1)S(1)}, b...) custom-call(s32[1]{0:T(128)} %bitcast.3.where_ref, ...), custom_call_target="tpu_custom_call" | custom-call | flops 2147483648 | bytes 8388608 | tf_op jit(solution)/shard_map/pallas_call | solution.py:126
  87.4 0.8 collective-permute-done.1.refs_0_
  88.3 4.5 %shard_map.76 = (bf16[512,512]{1,0:T(8,128)(2,1)S(1)}, bf16[256,1280]{1,0:T(8,128)(2,1)}, bf16[256,1280]{1,0:T(8,128)(2,1)S(1)}, bf16[256,1280]{1,0:T(8,128)(2,1)S(1)}, bf16[256,1280]{1,0:T(8,128)(2,1)S(1)}) custom-call(s32[1]{0:T(128)} %bitcast.3.where_ref, bf16[256,1280]{1,0:T(8,128)(2,1)} %collective-permute-done.1.refs_0_, ...), custom_call_target="tpu_custom_call" | custom-call | flops 2684354560 | bytes 10485760 | tf_op jit(solution)/shard_map/pallas_call | solution.py:126
  92.8 0.9 copy-done.6
  93.7 4.4 %shard_map.77 = bf16[512,2048]{1,0:T(8,128)(2,1)} custom-call(s32[1]{0:T(128)} %bitcast.3.where_ref, bf16[512,512]{1,0:T(8,128)(2,1)S(1)} %get-tuple-element.42.refs_0_, bf16[7168,512]{1,0:T(8,128)(2,1)} %bitcast.36, bf16[7168,512]{1,0:T(8,128)(2,1)} %bitcast.41, bf16[512,7168]{1,0:T(8,128)(2,1)} %bitcast.46), custom_call_target="tpu_custom_call" | custom-call | flops 1073741824 | bytes 4194304 | tf_op jit(solution)/shard_map/pallas_call | solution.py:126
  98.1 8.9 %all-to-all-start.2 = ((bf16[32,16,2048]{2,1,0:T(8,128)(2,1)}), bf16[32,16,2048]{2,1,0:T(8,128)(2,1)}, u32[]{:S(2)}, u32[]{:S(2)}) async-start(bf16[32,16,2048]{2,1,0:T(8,128)(2,1)} %bitcast.14), calls=%async_computation.2 | async-start | bytes 4194304 | tf_op jit(solution)/shard_map/all_to_all | solution.py:259
  107.0 2.7 %collective-permute-start.18 = (bf16[256,1280]{1,0:T(8,128)(2,1)S(1)}, bf16[256,1280]{1,0:T(8,128)(2,1)S(1)}, u32[]{:S(2)}, u32[]{:S(2)}) collective-permute-start(bf16[256,1280]{1,0:T(8,128)(2,1)S(1)} %copy-done.9), channel_id=1, source_target_pairs={{0,3},{1,0},{2,1},{3,2},{4,7},{5,4},{6,5},{7,6},{8,11},{9,8},{10,9... | collective-permute-start | bytes 1966088 | tf_op jit(solution)/shard_map/ppermute | solution.py:251
  109.7 1.5 collective-permute-start.16
  111.3 3.3 %shard_map.78 = (bf16[256,1280]{1,0:T(8,128)(2,1)S(1)}, bf16[256,1280]{1,0:T(8,128)(2,1)S(1)}, bf16[256,1280]{1,0:T(8,128)(2,1)S(1)}, bf16[256,1280]{1,0:T(8,128)(2,1)S(1)}) custom-call(s32[1]{0:T(128)} %bitcast.3.where_ref, bf16[512,512]{1,0:T(8,128)(2,1)S(1)} %get-tuple-element.42.refs_0_, bf16[7168,512]{1,0:T(8,128)(2,1)} %bitcast.37, ...), custom_call_target="tpu_custom_call" | custom-call | flops 1342177280 | bytes 5242880 | tf_op jit(solution)/shard_map/pallas_call | solution.py:126
  114.6 1.2 add_convert_fusion.1
  116.0 7.5 %collective-permute-done.18 = bf16[256,1280]{1,0:T(8,128)(2,1)S(1)} collective-permute-done((bf16[256,1280]{1,0:T(8,128)(2,1)S(1)}, bf16[256,1280]{1,0:T(8,128)(2,1)S(1)}, u32[]{:S(2)}, u32[]{:S(2)}) %collective-permute-start.18) | collective-permute-done | bytes 655392 | tf_op jit(solution)/shard_map/ppermute | solution.py:251
  123.7 3.8 %collective-permute-start.19 = (bf16[256,1280]{1,0:T(8,128)(2,1)S(1)}, bf16[256,1280]{1,0:T(8,128)(2,1)S(1)}, u32[]{:S(2)}, u32[]{:S(2)}) collective-permute-start(bf16[256,1280]{1,0:T(8,128)(2,1)S(1)} %add_convert_fusion), channel_id=1, source_target_pairs={{0,3},{1,0},{2,1},{3,2},{4,7},{5,4},{6,5},{7,6},{8,11},{9,8},{10,9... | collective-permute-start | bytes 1966088 | tf_op jit(solution)/shard_map/ppermute | solution.py:254
  127.6 9.9 %collective-permute-done.16.refs_2_ = bf16[256,1280]{1,0:T(8,128)(2,1)S(1)} collective-permute-done((bf16[256,1280]{1,0:T(8,128)(2,1)S(1)}, bf16[256,1280]{1,0:T(8,128)(2,1)S(1)}, u32[]{:S(2)}, u32[]{:S(2)}) %collective-permute-start.16) | collective-permute-done | bytes 655392 | tf_op jit(solution)/shard_map/ppermute | solution.py:252
  137.6 4.4 %collective-permute-done.15.refs_1_ = bf16[256,1280]{1,0:T(8,128)(2,1)S(1)} collective-permute-done((bf16[256,1280]{1,0:T(8,128)(2,1)S(1)}, bf16[256,1280]{1,0:T(8,128)(2,1)S(1)}, u32[]{:S(2)}, u32[]{:S(2)}) %collective-permute-start.15) | collective-permute-done | bytes 655392 | tf_op jit(solution)/shard_map/ppermute | solution.py:253
  141.9 9.7 %collective-permute-done.19.refs_5_ = bf16[256,1280]{1,0:T(8,128)(2,1)S(1)} collective-permute-done((bf16[256,1280]{1,0:T(8,128)(2,1)S(1)}, bf16[256,1280]{1,0:T(8,128)(2,1)S(1)}, u32[]{:S(2)}, u32[]{:S(2)}) %collective-permute-start.19) | collective-permute-done | bytes 655392 | tf_op jit(solution)/shard_map/ppermute | solution.py:254
  151.6 1.6 join_sums.1
  153.2 8.2 %all-to-all-start.3 = ((bf16[32,16,1280]{2,1,0:T(8,128)(2,1)}), bf16[32,16,1280]{2,1,0:T(8,128)(2,1)S(1)}, u32[]{:S(2)}, u32[]{:S(2)}) async-start(bf16[32,16,1280]{2,1,0:T(8,128)(2,1)} %bitcast.16), calls=%async_computation.3 | async-start | bytes 2621440 | tf_op jit(solution)/shard_map/all_to_all | solution.py:259
  161.4 2.3 %convolution_convert_fusion.1 = bf16[256,2048]{1,0:T(8,128)(2,1)S(1)} fusion(bf16[512,256]{1,0:T(8,128)(2,1)S(1)} %fusion, bf16[512,2048]{1,0:T(8,128)(2,1)} %bitcast.15), kind=kOutput, calls=%fused_computation.1 | convolution fusion | flops 537395200 | bytes 3407872 | tf_op jit(solution)/shard_map/dot_general | solution.py:320
  163.7 1.7 collective-permute-start.10
  165.4 1.9 %collective-permute-start.12 = (bf16[128,512]{1,0:T(8,128)(2,1)S(1)}, bf16[128,512]{1,0:T(8,128)(2,1)S(1)}, u32[]{:S(2)}, u32[]{:S(2)}) collective-permute-start(bf16[128,512]{1,0:T(8,128)(2,1)S(1)} %get-tuple-element.56), channel_id=1, source_target_pairs={{0,3},{1,0},{2,1},{3,2},{4,7},{5,4},{6,5},{7,6},{8,11},{9,8},{10,9... | collective-permute-start | bytes 393224 | tf_op jit(solution)/shard_map/ppermute | solution.py:235
  167.3 3.6 %collective-permute-done.10 = bf16[128,512]{1,0:T(8,128)(2,1)S(1)} collective-permute-done((bf16[128,512]{1,0:T(8,128)(2,1)S(1)}, bf16[128,512]{1,0:T(8,128)(2,1)S(1)}, u32[]{:S(2)}, u32[]{:S(2)}) %collective-permute-start.10) | collective-permute-done | bytes 131104 | tf_op jit(solution)/shard_map/ppermute | solution.py:235
  171.6 2.1 %collective-permute-start.13 = (bf16[256,512]{1,0:T(8,128)(2,1)S(1)}, bf16[256,512]{1,0:T(8,128)(2,1)S(1)}, u32[]{:S(2)}, u32[]{:S(2)}) collective-permute-start(bf16[256,512]{1,0:T(8,128)(2,1)S(1)} %get-tuple-element.54), channel_id=1, source_target_pairs={{0,3},{1,0},{2,1},{3,2},{4,7},{5,4},{6,5},{7,6},{8,11},{9,8},{10,9... | collective-permute-start | bytes 786440 | tf_op jit(solution)/shard_map/ppermute | solution.py:238
  173.7 5.6 %collective-permute-done.11 = bf16[256,512]{1,0:T(8,128)(2,1)S(1)} collective-permute-done((bf16[256,512]{1,0:T(8,128)(2,1)S(1)}, bf16[256,512]{1,0:T(8,128)(2,1)S(1)}, u32[]{:S(2)}, u32[]{:S(2)}) %collective-permute-start.11) | collective-permute-done | bytes 262176 | tf_op jit(solution)/shard_map/ppermute | solution.py:238
  179.4 1.2 all-to-all-done.3
  181.2 1.0 pad_maximum_fusion
  (62 shorter events, 4.4 us)
Async XLA Ops:
  0.0 0.7 copy-start.4
  0.7 0.7 copy-start.10
  4.3 20.1 %copy-start.2 = (bf16[512,256]{1,0:T(8,128)(2,1)}, bf16[512,256]{1,0:T(8,128)(2,1)S(1)}, u32[]{:S(2)}) copy-start(bf16[512,256]{1,0:T(8,128)(2,1)S(1)} %get-tuple-element.28) | copy-start | bytes 786436
  4.3 12.9 %collective-permute-start.5 = (bf16[256,640]{1,0:T(8,128)(2,1)S(1)}, bf16[256,640]{1,0:T(8,128)(2,1)S(1)}, u32[]{:S(2)}, u32[]{:S(2)}) collective-permute-start(bf16[256,640]{1,0:T(8,128)(2,1)S(1)} %get-tuple-element.30), channel_id=1, source_target_pairs={{0,1},{1,2},{2,3},{3,0},{4,5},{5,6},{6,7},{7,4},{8,9},{9,10},{10,1... | collective-permute-start | bytes 983048 | tf_op jit(solution)/shard_map/ppermute | solution.py:230
  6.8 10.5 %collective-permute-start.4 = (bf16[256,640]{1,0:T(8,128)(2,1)S(1)}, bf16[256,640]{1,0:T(8,128)(2,1)}, u32[]{:S(2)}, u32[]{:S(2)}) collective-permute-start(bf16[256,640]{1,0:T(8,128)(2,1)S(1)} %get-tuple-element.30), channel_id=1, source_target_pairs={{0,3},{1,0},{2,1},{3,2},{4,7},{5,4},{6,5},{7,6},{8,11},{9,8},{10,9... | collective-permute-start | bytes 983048 | tf_op jit(solution)/shard_map/ppermute | solution.py:230
  9.0 27.3 %all-to-all-start = ((bf16[32,16,1280]{2,1,0:T(8,128)(2,1)}), bf16[32,16,1280]{2,1,0:T(8,128)(2,1)S(1)}, u32[]{:S(2)}, u32[]{:S(2)}) async-start(bf16[32,16,1280]{2,1,0:T(8,128)(2,1)} %bitcast.4), calls=%async_computation | async-start | bytes 2621440 | tf_op jit(solution)/shard_map/all_to_all | solution.py:259
  17.2 6.7 %collective-permute-start.6 = (bf16[128,640]{1,0:T(8,128)(2,1)S(1)}, bf16[128,640]{1,0:T(8,128)(2,1)S(1)}, u32[]{:S(2)}, u32[]{:S(2)}) collective-permute-start(bf16[128,640]{1,0:T(8,128)(2,1)S(1)} %slice.82), channel_id=1, source_target_pairs={{0,1},{1,2},{2,3},{3,0},{4,5},{5,6},{6,7},{7,4},{8,9},{9,10},{10,1... | collective-permute-start | bytes 491528 | tf_op jit(solution)/shard_map/ppermute | solution.py:231
  18.3 5.7 %collective-permute-start.7 = (bf16[128,640]{1,0:T(8,128)(2,1)S(1)}, bf16[128,640]{1,0:T(8,128)(2,1)S(1)}, u32[]{:S(2)}, u32[]{:S(2)}) collective-permute-start(bf16[128,640]{1,0:T(8,128)(2,1)S(1)} %slice.83), channel_id=1, source_target_pairs={{0,3},{1,0},{2,1},{3,2},{4,7},{5,4},{6,5},{7,6},{8,11},{9,8},{10,9... | collective-permute-start | bytes 491528 | tf_op jit(solution)/shard_map/ppermute | solution.py:231
  36.3 46.3 %all-to-all-start.1 = ((bf16[32,16,2176]{2,1,0:T(8,128)(2,1)}), bf16[32,16,2176]{2,1,0:T(8,128)(2,1)S(1)}, u32[]{:S(2)}, u32[]{:S(2)}) async-start(bf16[32,16,2176]{2,1,0:T(8,128)(2,1)} %bitcast.48), calls=%async_computation.1 | async-start | bytes 4456448 | tf_op jit(solution)/shard_map/all_to_all | solution.py:259
  42.7 17.5 %collective-permute-start = (bf16[256,1280]{1,0:T(8,128)(2,1)}, bf16[256,1280]{1,0:T(8,128)(2,1)}, u32[]{:S(2)}, u32[]{:S(2)}) collective-permute-start(bf16[256,1280]{1,0:T(8,128)(2,1)} %bitcast.5), channel_id=1, source_target_pairs={{0,1},{1,2},{2,3},{3,0},{4,5},{5,6},{6,7},{7,4},{8,9},{9,10},{10,1... | collective-permute-start | bytes 1966088 | tf_op jit(solution)/shard_map/ppermute | solution.py:242
  42.7 17.5 %collective-permute-start.2 = (bf16[256,1280]{1,0:T(8,128)(2,1)}, bf16[256,1280]{1,0:T(8,128)(2,1)}, u32[]{:S(2)}, u32[]{:S(2)}) collective-permute-start(bf16[256,1280]{1,0:T(8,128)(2,1)} %bitcast.6), channel_id=1, source_target_pairs={{0,3},{1,0},{2,1},{3,2},{4,7},{5,4},{6,5},{7,6},{8,11},{9,8},{10,9... | collective-permute-start | bytes 1966088 | tf_op jit(solution)/shard_map/ppermute | solution.py:242
  45.4 27.8 %collective-permute-start.8 = (bf16[256,1280]{1,0:T(8,128)(2,1)}, bf16[256,1280]{1,0:T(8,128)(2,1)}, u32[]{:S(2)}, u32[]{:S(2)}) collective-permute-start(bf16[256,1280]{1,0:T(8,128)(2,1)} %bitcast.5), channel_id=1, source_target_pairs={{0,3},{1,0},{2,1},{3,2},{4,7},{5,4},{6,5},{7,6},{8,11},{9,8},{10,9... | collective-permute-start | bytes 1966088 | tf_op jit(solution)/shard_map/ppermute | solution.py:243
  45.8 28.4 %collective-permute-start.9 = (bf16[256,1280]{1,0:T(8,128)(2,1)}, bf16[256,1280]{1,0:T(8,128)(2,1)}, u32[]{:S(2)}, u32[]{:S(2)}) collective-permute-start(bf16[256,1280]{1,0:T(8,128)(2,1)} %bitcast.6), channel_id=1, source_target_pairs={{0,1},{1,2},{2,3},{3,0},{4,5},{5,6},{6,7},{7,4},{8,9},{9,10},{10,1... | collective-permute-start | bytes 1966088 | tf_op jit(solution)/shard_map/ppermute | solution.py:243
  60.2 28.1 %collective-permute-start.1 = (bf16[256,1280]{1,0:T(8,128)(2,1)}, bf16[256,1280]{1,0:T(8,128)(2,1)}, u32[]{:S(2)}, u32[]{:S(2)}) collective-permute-start(bf16[256,1280]{1,0:T(8,128)(2,1)} %collective-permute-done.refs_2_), channel_id=1, source_target_pairs={{0,1},{1,2},{2,3},{3,0},{4,5},{5,6},{6,7},{7,4},{8,9},{9,10},{10,1... | collective-permute-start | bytes 1966088 | tf_op jit(solution)/shard_map/ppermute | solution.py:244
  60.2 28.1 %collective-permute-start.3 = (bf16[256,1280]{1,0:T(8,128)(2,1)}, bf16[256,1280]{1,0:T(8,128)(2,1)}, u32[]{:S(2)}, u32[]{:S(2)}) collective-permute-start(bf16[256,1280]{1,0:T(8,128)(2,1)} %collective-permute-done.2.refs_1_), channel_id=1, source_target_pairs={{0,3},{1,0},{2,1},{3,2},{4,7},{5,4},{6,5},{7,6},{8,11},{9,8},{10,9... | collective-permute-start | bytes 1966088 | tf_op jit(solution)/shard_map/ppermute | solution.py:244
  80.6 1.0 copy-start
  81.6 1.0 copy-start.1
  92.8 0.9 copy-start.6
  93.7 4.4 %copy-start.8 = (bf16[256,1280]{1,0:T(8,128)(2,1)}, bf16[256,1280]{1,0:T(8,128)(2,1)S(1)}, u32[]{:S(2)}) copy-start(bf16[256,1280]{1,0:T(8,128)(2,1)S(1)} %get-tuple-element.50) | copy-start | bytes 1966084
  93.7 20.9 %collective-permute-start.14 = (bf16[256,1280]{1,0:T(8,128)(2,1)}, bf16[256,1280]{1,0:T(8,128)(2,1)}, u32[]{:S(2)}, u32[]{:S(2)}) collective-permute-start(bf16[256,1280]{1,0:T(8,128)(2,1)} %get-tuple-element.45), channel_id=1, source_target_pairs={{0,1},{1,2},{2,3},{3,0},{4,5},{5,6},{6,7},{7,4},{8,9},{9,10},{10,1... | collective-permute-start | bytes 1966088 | tf_op jit(solution)/shard_map/ppermute | solution.py:251
  98.1 8.9 %copy-start.9 = (bf16[256,1280]{1,0:T(8,128)(2,1)S(1)}, bf16[256,1280]{1,0:T(8,128)(2,1)}, u32[]{:S(2)}) copy-start(bf16[256,1280]{1,0:T(8,128)(2,1)} %copy-done.8) | copy-start | bytes 1966084
  98.1 11.6 %copy-start.7 = (bf16[256,1280]{1,0:T(8,128)(2,1)S(1)}, bf16[256,1280]{1,0:T(8,128)(2,1)}, u32[]{:S(2)}) copy-start(bf16[256,1280]{1,0:T(8,128)(2,1)} %copy-done.6) | copy-start | bytes 1966084
  98.1 55.1 %all-to-all-start.2 = ((bf16[32,16,2048]{2,1,0:T(8,128)(2,1)}), bf16[32,16,2048]{2,1,0:T(8,128)(2,1)}, u32[]{:S(2)}, u32[]{:S(2)}) async-start(bf16[32,16,2048]{2,1,0:T(8,128)(2,1)} %bitcast.14), calls=%async_computation.2 | async-start | bytes 4194304 | tf_op jit(solution)/shard_map/all_to_all | solution.py:259
  107.0 16.5 %collective-permute-start.18 = (bf16[256,1280]{1,0:T(8,128)(2,1)S(1)}, bf16[256,1280]{1,0:T(8,128)(2,1)S(1)}, u32[]{:S(2)}, u32[]{:S(2)}) collective-permute-start(bf16[256,1280]{1,0:T(8,128)(2,1)S(1)} %copy-done.9), channel_id=1, source_target_pairs={{0,3},{1,0},{2,1},{3,2},{4,7},{5,4},{6,5},{7,6},{8,11},{9,8},{10,9... | collective-permute-start | bytes 1966088 | tf_op jit(solution)/shard_map/ppermute | solution.py:251
  109.7 27.8 %collective-permute-start.16 = (bf16[256,1280]{1,0:T(8,128)(2,1)S(1)}, bf16[256,1280]{1,0:T(8,128)(2,1)S(1)}, u32[]{:S(2)}, u32[]{:S(2)}) collective-permute-start(bf16[256,1280]{1,0:T(8,128)(2,1)S(1)} %copy-done.7), channel_id=1, source_target_pairs={{0,3},{1,0},{2,1},{3,2},{4,7},{5,4},{6,5},{7,6},{8,11},{9,8},{10,9... | collective-permute-start | bytes 1966088 | tf_op jit(solution)/shard_map/ppermute | solution.py:252
  111.3 26.3 %collective-permute-start.17 = (bf16[256,1280]{1,0:T(8,128)(2,1)S(1)}, bf16[256,1280]{1,0:T(8,128)(2,1)S(1)}, u32[]{:S(2)}, u32[]{:S(2)}) collective-permute-start(bf16[256,1280]{1,0:T(8,128)(2,1)S(1)} %get-tuple-element.48), channel_id=1, source_target_pairs={{0,1},{1,2},{2,3},{3,0},{4,5},{5,6},{6,7},{7,4},{8,9},{9,10},{10,1... | collective-permute-start | bytes 1966088 | tf_op jit(solution)/shard_map/ppermute | solution.py:252
  115.9 11.6 %copy-start.11 = (bf16[256,8]{0,1:T(8,128)(2,1)S(1)}, bf16[256,8]{0,1:T(8,128)(2,1)}, u32[]{:S(2)}) copy-start(bf16[256,8]{0,1:T(8,128)(2,1)} %param.10) | copy-start | bytes 12292
  115.9 11.6 %copy-start.5 = (s32[256,8]{0,1:T(8,128)S(1)}, s32[256,8]{0,1:T(8,128)}, u32[]{:S(2)}) copy-start(s32[256,8]{0,1:T(8,128)} %param.9) | copy-start | bytes 24580
  115.9 11.6 %copy-start.3 = (bf16[512,256]{1,0:T(8,128)(2,1)S(1)}, bf16[512,256]{1,0:T(8,128)(2,1)}, u32[]{:S(2)}) copy-start(bf16[512,256]{1,0:T(8,128)(2,1)} %copy-done.2) | copy-start | bytes 786436
  115.9 26.0 %collective-permute-start.15 = (bf16[256,1280]{1,0:T(8,128)(2,1)S(1)}, bf16[256,1280]{1,0:T(8,128)(2,1)S(1)}, u32[]{:S(2)}, u32[]{:S(2)}) collective-permute-start(bf16[256,1280]{1,0:T(8,128)(2,1)S(1)} %add_convert_fusion.1), channel_id=1, source_target_pairs={{0,1},{1,2},{2,3},{3,0},{4,5},{5,6},{6,7},{7,4},{8,9},{9,10},{10,1... | collective-permute-start | bytes 1966088 | tf_op jit(solution)/shard_map/ppermute | solution.py:253
  123.7 27.9 %collective-permute-start.19 = (bf16[256,1280]{1,0:T(8,128)(2,1)S(1)}, bf16[256,1280]{1,0:T(8,128)(2,1)S(1)}, u32[]{:S(2)}, u32[]{:S(2)}) collective-permute-start(bf16[256,1280]{1,0:T(8,128)(2,1)S(1)} %add_convert_fusion), channel_id=1, source_target_pairs={{0,3},{1,0},{2,1},{3,2},{4,7},{5,4},{6,5},{7,6},{8,11},{9,8},{10,9... | collective-permute-start | bytes 1966088 | tf_op jit(solution)/shard_map/ppermute | solution.py:254
  153.2 27.4 %all-to-all-start.3 = ((bf16[32,16,1280]{2,1,0:T(8,128)(2,1)}), bf16[32,16,1280]{2,1,0:T(8,128)(2,1)S(1)}, u32[]{:S(2)}, u32[]{:S(2)}) async-start(bf16[32,16,1280]{2,1,0:T(8,128)(2,1)} %bitcast.16), calls=%async_computation.3 | async-start | bytes 2621440 | tf_op jit(solution)/shard_map/all_to_all | solution.py:259
  163.7 7.1 %collective-permute-start.10 = (bf16[128,512]{1,0:T(8,128)(2,1)S(1)}, bf16[128,512]{1,0:T(8,128)(2,1)S(1)}, u32[]{:S(2)}, u32[]{:S(2)}) collective-permute-start(bf16[128,512]{1,0:T(8,128)(2,1)S(1)} %get-tuple-element.55), channel_id=1, source_target_pairs={{0,1},{1,2},{2,3},{3,0},{4,5},{5,6},{6,7},{7,4},{8,9},{9,10},{10,1... | collective-permute-start | bytes 393224 | tf_op jit(solution)/shard_map/ppermute | solution.py:235
  165.4 5.4 %collective-permute-start.12 = (bf16[128,512]{1,0:T(8,128)(2,1)S(1)}, bf16[128,512]{1,0:T(8,128)(2,1)S(1)}, u32[]{:S(2)}, u32[]{:S(2)}) collective-permute-start(bf16[128,512]{1,0:T(8,128)(2,1)S(1)} %get-tuple-element.56), channel_id=1, source_target_pairs={{0,3},{1,0},{2,1},{3,2},{4,7},{5,4},{6,5},{7,6},{8,11},{9,8},{10,9... | collective-permute-start | bytes 393224 | tf_op jit(solution)/shard_map/ppermute | solution.py:235
  171.0 8.3 %collective-permute-start.11 = (bf16[256,512]{1,0:T(8,128)(2,1)S(1)}, bf16[256,512]{1,0:T(8,128)(2,1)S(1)}, u32[]{:S(2)}, u32[]{:S(2)}) collective-permute-start(bf16[256,512]{1,0:T(8,128)(2,1)S(1)} %get-tuple-element.53), channel_id=1, source_target_pairs={{0,1},{1,2},{2,3},{3,0},{4,5},{5,6},{6,7},{7,4},{8,9},{9,10},{10,1... | collective-permute-start | bytes 786440 | tf_op jit(solution)/shard_map/ppermute | solution.py:238
  171.6 7.7 %collective-permute-start.13 = (bf16[256,512]{1,0:T(8,128)(2,1)S(1)}, bf16[256,512]{1,0:T(8,128)(2,1)S(1)}, u32[]{:S(2)}, u32[]{:S(2)}) collective-permute-start(bf16[256,512]{1,0:T(8,128)(2,1)S(1)} %get-tuple-element.54), channel_id=1, source_target_pairs={{0,3},{1,0},{2,1},{3,2},{4,7},{5,4},{6,5},{7,6},{8,11},{9,8},{10,9... | collective-permute-start | bytes 786440 | tf_op jit(solution)/shard_map/ppermute | solution.py:238

commit v5 on v4

--- a/solution.py
+++ b/solution.py
@@ -25,7 +25,7 @@
         return copy
 
 
-def expert_call(where, weights, xs=(), segs=(), carry=(), inv=None, hidden=None, jobs=(), outs=(), stash=((), ()), held=None, stored=()):
+def expert_call(where, weights, xs=(), segs=(), carry=(), inv=None, hidden=None, jobs=(), outs=(), stash=((), ()), held=(), stored=(), keep=None):
     slices = lax.axis_size("tp")
     w_gate, w_up, w_down = weights
     d_all, ff = w_gate.shape
@@ -48,15 +48,18 @@
 
     columns, later = columns_of(jobs), columns_of(stash[1])
     results = [((rows, ff), F32)] * 2 if not jobs else [((rows, ff), BF16)] * finish + [(s, BF16) for s in outs]
+    results = [(s, t) for s, t in results] + ([((rows, SIDE), BF16)] if keep else [])
+    n_out = len(results)
     results += [(s, BF16) for s in weight_shapes(stash[0], later)]
-    resident = list(xs) + list(carry) + ([] if hidden is None else [hidden]) + list(held or ())
-    streamed = ([] if held else [w_gate, w_up, w_down]) + list(stored)
-    buffers = [] if held else weight_shapes(segs, columns)
-    scratch = [pltpu.VMEM(s, BF16) for s in buffers]
+    needed = weight_shapes(segs, columns)[len(held) :]
+    streams = bool(needed) or len(results) > n_out
+    resident = list(xs) + list(carry) + ([] if hidden is None else [hidden]) + list(held)
+    streamed = ([w_gate, w_up, w_down] if streams else []) + list(stored)
+    scratch = [pltpu.VMEM(s, BF16) for s in needed]
     if finish:
         scratch += [pltpu.VMEM((rows, ff), F32)] * 2
     scratch += [pltpu.VMEM((rows, ff), F32)] * len(stored)
-    n_copies = len(stored) + len(buffers) + len(weight_shapes(stash[0], later))
+    n_copies = len(stored) + len(needed) + len(results) - n_out
     scratch += [pltpu.SemaphoreType.DMA((max(n_copies, 1),))]
 
     def body(where_ref, *refs):
@@ -64,36 +67,45 @@
         take = lambda n: [refs.pop(0) for _ in range(n)]
         x_refs, carried = take(len(xs)), take(len(carry))
         hidden_ref = take(hidden is not None)
-        held_refs = take(len(held or ()))
-        wg, wu, wd = (None,) * 3 if held else take(3)
+        held_refs = take(len(held))
+        wg, wu, wd = take(3) if streams else (None,) * 3
         stored_refs = take(len(stored))
         out_refs = take(len(results))
-        bufs = take(len(buffers)) if not held else held_refs
+        bufs = held_refs + take(len(needed))
         accs = take(2) if finish else out_refs[:2]
         stored_bufs = take(len(stored))
         copies = Copies(refs.pop(0))
         z = where_ref[0]
 
-        def bring(seg_list, column_list, into):
-            waits = []
+        def bring(seg_list, column_list, into, skip):
+            waits, n = [None] * skip, 0
             for _, step, offset, width, _ in seg_list:
                 at = pl.ds(pl.multiple_of(lax.rem(z + step, slices) * span + offset, 128), width)
-                waits += [copies.start(w.at[at, :], into[len(waits) + n]) for n, w in enumerate((wg, wu))]
+                for w in (wg, wu):
+                    if n >= skip:
+                        waits.append(copies.start(w.at[at, :], into[n]))
+                    n += 1
             for step, offset, width in column_list:
                 at = pl.ds(pl.multiple_of(lax.rem(z + step, slices) * span + offset, 128), width)
-                waits.append(copies.start(wd.at[:, at], into[len(waits)]))
+                if n >= skip:
+                    waits.append(copies.start(wd.at[:, at], into[n]))
+                n += 1
             return waits
 
-        waits = [] if held else bring(segs, columns, bufs)
+        def arrived(wait):
+            if wait is not None:
+                wait.wait()
+
+        waits = bring(segs, columns, bufs, len(held))
         stored_waits = [copies.start(r, b) for r, b in zip(stored_refs, stored_bufs)]
-        n_stash = len(weight_shapes(stash[0], later))
-        stash_waits = bring(stash[0], later, out_refs[len(out_refs) - n_stash :]) if n_stash else []
+        stash_waits = bring(stash[0], later, out_refs[n_out:], 0)
+        if keep:
+            out_refs[2][...] = x_refs[keep[0]][:, keep[1] : keep[1] + SIDE]
         for k, (index, _, _, width, col) in enumerate(segs):
             x = [x_refs[i][:, col : col + width] for i in index]
             x = x[0] if len(x) == 1 else jnp.concatenate(x, axis=0)
             for n, acc in enumerate(accs):
-                if waits:
-                    waits[2 * k + n].wait()
+                arrived(waits[2 * k + n])
                 term = jnp.dot(x, bufs[2 * k + n][...], preferred_element_type=F32)
                 if k:
                     term = acc[...] + term
@@ -104,15 +116,15 @@
                     term = stored_bufs[n][...] + term
                 acc[...] = term
         if finish:
-            scale = jnp.sum(x_refs[inv[0]][:, inv[1] : inv[1] + SIDE].astype(F32), axis=1, keepdims=True)
+            scale = jnp.sum(x_refs[inv][...].astype(F32), axis=1, keepdims=True)
             gate = accs[0][...] * scale
             hidden_ref = [out_refs.pop(0)]
             hidden_ref[0][...] = (jax.nn.silu(gate) * (accs[1][...] * scale)).astype(BF16)
         waited = set()
         for step, offset, width, row, count, targets in jobs:
             k = columns.index((step, offset, width))
-            if waits and k not in waited:
-                waits[2 * len(segs) + k].wait()
+            if k not in waited:
+                arrived(waits[2 * len(segs) + k])
                 waited.add(k)
             w = bufs[2 * len(segs) + k]
             term = jnp.dot(hidden_ref[0][row : row + count, :], w[...], preferred_element_type=F32).astype(BF16)
@@ -152,9 +164,11 @@
     tok, width = tokens.shape
     rows, bulk = window * CAP, width - EARLY
 
-    def body(tokens_hbm, gain_ref, ids_ref, pick_ref, bulk_ref, early_ref, tokens_ref, sem):
-        load = pltpu.make_async_copy(tokens_hbm, tokens_ref, sem)
-        load.start()
+    def body(ids_hbm, gain_hbm, tokens_hbm, pick_ref, bulk_ref, early_ref, ids_ref, gain_ref, tokens_ref, sems):
+        copies = Copies(sems)
+        pairs = ((ids_hbm, ids_ref), (gain_hbm, gain_ref), (tokens_hbm, tokens_ref))
+        ids_load, gain_load, load = [copies.start(*pair) for pair in pairs]
+        ids_load.wait()
         expert = lax.broadcasted_iota(jnp.int32, (window, tok), 0)
         match = jnp.zeros((window, tok), F32)
         for k in range(ids.shape[0]):
@@ -169,6 +183,7 @@
         wanted = (lax.broadcasted_iota(jnp.int32, (rows, tok), 0) % CAP).astype(F32)
         pick = jnp.where(spread == wanted, 1.0, 0.0).astype(BF16)
         pick_ref[...] = pick
+        gain_load.wait()
         gain = gain_ref[...].astype(F32).reshape(1, width)
         load.wait()
         values = tokens_ref[...].astype(F32)
@@ -179,13 +194,13 @@
 
     return pl.pallas_call(
         body,
-        in_specs=[pl.BlockSpec(memory_space=pltpu.HBM)] + [pl.BlockSpec(memory_space=pltpu.VMEM)] * 2,
-        scratch_shapes=[pltpu.VMEM((tok, width), BF16), pltpu.SemaphoreType.DMA],
+        in_specs=[pl.BlockSpec(memory_space=pltpu.HBM)] * 3,
+        scratch_shapes=[pltpu.VMEM(x.shape, x.dtype) for x in (ids, norm_gain, tokens)] + [pltpu.SemaphoreType.DMA((3,))],
         out_shape=[jax.ShapeDtypeStruct(s, BF16) for s in ((rows, tok), (rows, bulk), (tok, EARLY + SIDE))],
         cost_estimate=pl.CostEstimate(flops=2 * rows * tok * bulk, bytes_accessed=2 * tok * width, transcendentals=0),
         compiler_params=pltpu.CompilerParams(vmem_limit_bytes=24 * 2**20),
         name="head",
-    )(pltpu.with_memory_space_constraint(tokens, pltpu.HBM), norm_gain, ids)
+    )(*[pltpu.with_memory_space_constraint(x, pltpu.HBM) for x in (ids, norm_gain, tokens)])
 
 
 def join_sums(low, high):
@@ -294,17 +309,17 @@
         where, weights, [*above, *below],
         [((0, 1), 1, EARLY, bulk, 0), ((2, 3), 3, EARLY, bulk, 0)], sums,
     )
-    *sums, = expert_call(
+    early_jobs = [(k, 0, EARLY, 0, rows, ((0, 0, rows, k * EARLY),)) for k in range(n_tp)]
+    *early_sums, scale, far_gate, far_up = expert_call(
         where, weights, [early_rows],
-        [((0,), k, 0, EARLY, k * EARLY) for k in range(n_tp)], stored=sums, stash=(far_segs, far_jobs),
-    )
-    hidden, f_low, f_high, a_high, b_low = expert_call(
-        where, weights, [*far, early_rows], far_segs, sums[:2], inv=(2, n_tp * EARLY),
-        jobs=far_jobs, outs=[(half, bulk)] * 4, held=sums[2:],
+        [((0,), k, 0, EARLY, k * EARLY) for k in range(n_tp)], keep=(0, n_tp * EARLY), stash=(far_segs, ()),
+    )
+    hidden, f_low, f_high, a_high, b_low, *early_down = expert_call(
+        where, weights, [*far, scale], far_segs, early_sums, inv=2, stored=sums,
+        jobs=far_jobs, outs=[(half, bulk)] * 4, held=(far_gate, far_up), stash=((), early_jobs),
     )
     (p_early,) = expert_call(
-        where, weights, hidden=hidden,
-        jobs=[(k, 0, EARLY, 0, rows, ((0, 0, rows, k * EARLY),)) for k in range(n_tp)], outs=[(rows, n_tp * EARLY)],
+        where, weights, hidden=hidden, jobs=early_jobs, outs=[(rows, n_tp * EARLY)], held=early_down,
     )
     a_low, b_high, o_low, o_high = expert_call(
         where, weights, hidden=hidden,

time: 183 us -> 182 us (level)
  local copies, waits for them, and re-layouts: 7.62 us -> 5.35 us
    unnamed x29 -> x17, local copies, waits for them, and re-layouts: 5.32 us -> 3.04 us
  transfers between devices with their start and end apart: 24 -> 24, of which waited for: 13 -> 13; matrix products, arithmetic and copies ran while one was open for 6% -> 6% of each run, Pallas kernels for 13% -> 12%
where the time goes in v5:
time: 182 us; the launch traced here: 181 us
  waiting for transfers between devices  75.9 us (42%)
  starting transfers between devices  58.9 us (32%)
  Pallas kernels  31.6 us (17%)
  local copies, waits for them, and re-layouts  5.35 us (3%)
  matrix products  5.02 us (3%)
  other arithmetic  4.01 us (2%)
    all_to_all x4, starting transfers between devices, exchange(): lax.all_to_all(shaped, 'ep', 0, 0, tiled=True).reshape(rows, x.shape[1])  30 us
    pallas_call x6, Pallas kernels, expert_call(): pl.pallas_call(body, in_specs=[pl.BlockSpec(memory_space=pltpu.SMEM)] + [...  27.1 us
    ppermute x1, waiting for transfers between devices, spread_halves(): lax.ppermute(low, 'tp', up)  13.3 us
    all_to_all x4, waiting for transfers between devices, exchange(): lax.all_to_all(shaped, 'ep', 0, 0, tiled=True).reshape(rows, x.shape[1])  11.1 us
    ppermute x1, waiting for transfers between devices, fold_halves(): lax.ppermute(below[0], 'tp', dn)  10.1 us
    ppermute x1, waiting for transfers between devices, fold_halves(): up_high = lax.ppermute(add(below[1], got_high), 'tp', dn)  9.72 us
    ppermute x1, waiting for transfers between devices, fold_halves(): lax.ppermute(far[1], 'tp', dn)  7.37 us
    ppermute x1, waiting for transfers between devices, spread_halves(): lax.ppermute(low, 'tp', dn)  7.32 us
  transfers between devices with their start and end apart: 24, of which 13 were waited for; matrix products, arithmetic and copies ran while one was open for 6% of the time, Pallas kernels for 12%

profile of v5, /device:TPU:1, one launch (start us, length us, event | category | flops | bytes accessed | tf_op | source)
XLA Modules:
  0.0 181.0 jit_solution(5894438949743771210)
XLA Ops:
  0.0 2.9 %head.1 = (bf16[512,256]{1,0:T(8,128)(2,1)S(1)}, bf16[512,1280]{1,0:T(8,128)(2,1)}, bf16[256,640]{1,0:T(8,128)(2,1)S(1)}) custom-call(s32[8,256]{1,0:T(8,128)} %bitcast.47, bf16[1792]{0:T(1024)(128)(2,1)} %gain_hbm.1, bf16[256,1792]{1,0:T(8,128)(2,1)} %tokens_hbm.1), custom_call_target="tpu_custom_call" | custom-call | flops 335544320 | bytes 917504 | tf_op jit(solution)/shard_map/head/pallas_call | solution.py:195
  2.9 2.5 %collective-permute-start.5 = (bf16[256,640]{1,0:T(8,128)(2,1)S(1)}, bf16[256,640]{1,0:T(8,128)(2,1)S(1)}, u32[]{:S(2)}, u32[]{:S(2)}) collective-permute-start(bf16[256,640]{1,0:T(8,128)(2,1)S(1)} %get-tuple-element.32), channel_id=1, source_target_pairs={{0,1},{1,2},{2,3},{3,0},{4,5},{5,6},{6,7},{7,4},{8,9},{9,10},{10,1... | collective-permute-start | bytes 983048 | tf_op jit(solution)/shard_map/ppermute | solution.py:245
  5.4 2.2 %collective-permute-start.4 = (bf16[256,640]{1,0:T(8,128)(2,1)S(1)}, bf16[256,640]{1,0:T(8,128)(2,1)}, u32[]{:S(2)}, u32[]{:S(2)}) collective-permute-start(bf16[256,640]{1,0:T(8,128)(2,1)S(1)} %get-tuple-element.32), channel_id=1, source_target_pairs={{0,3},{1,0},{2,1},{3,2},{4,7},{5,4},{6,5},{7,6},{8,11},{9,8},{10,9... | collective-permute-start | bytes 983048 | tf_op jit(solution)/shard_map/ppermute | solution.py:245
  7.7 8.0 %all-to-all-start = ((bf16[32,16,1280]{2,1,0:T(8,128)(2,1)}), bf16[32,16,1280]{2,1,0:T(8,128)(2,1)S(1)}, u32[]{:S(2)}, u32[]{:S(2)}) async-start(bf16[32,16,1280]{2,1,0:T(8,128)(2,1)} %bitcast.4), calls=%async_computation | async-start | bytes 2621440 | tf_op jit(solution)/shard_map/all_to_all | solution.py:274
  16.0 0.9 slice.83
  16.9 2.7 %collective-permute-start.7 = (bf16[128,640]{1,0:T(8,128)(2,1)S(1)}, bf16[128,640]{1,0:T(8,128)(2,1)S(1)}, u32[]{:S(2)}, u32[]{:S(2)}) collective-permute-start(bf16[128,640]{1,0:T(8,128)(2,1)S(1)} %slice.83), channel_id=1, source_target_pairs={{0,3},{1,0},{2,1},{3,2},{4,7},{5,4},{6,5},{7,6},{8,11},{9,8},{10,9... | collective-permute-start | bytes 491528 | tf_op jit(solution)/shard_map/ppermute | solution.py:246
  19.6 1.0 slice_dynamic-update-slice_fusion.2
  20.7 1.0 convert_reduce_fusion.2
  21.7 0.9 collective-permute-done.6
  23.0 2.2 %convolution_convert_fusion = bf16[512,2176]{1,0:T(8,128)(2,1)} fusion(bf16[512,256]{1,0:T(8,128)(2,1)S(1)} %get-tuple-element.30, bf16[256,2176]{1,0:T(8,128)(2,1)S(1)} %pad_dynamic-update-slice_fusion), kind=kOutput, calls=%fused_computation | convolution fusion | flops 571539456 | bytes 3604480 | tf_op jit(solution)/shard_map/dot_general | solution.py:286
  25.2 9.8 %all-to-all-done = bf16[32,16,1280]{2,1,0:T(8,128)(2,1)S(1)} async-done(((bf16[32,16,1280]{2,1,0:T(8,128)(2,1)}), bf16[32,16,1280]{2,1,0:T(8,128)(2,1)S(1)}, u32[]{:S(2)}, u32[]{:S(2)}) %all-to-all-start) | async-done | bytes 1310752 | tf_op jit(solution)/shard_map/all_to_all | solution.py:274
  35.0 5.2 %all-to-all-start.1 = ((bf16[32,16,2176]{2,1,0:T(8,128)(2,1)}), bf16[32,16,2176]{2,1,0:T(8,128)(2,1)S(1)}, u32[]{:S(2)}, u32[]{:S(2)}) async-start(bf16[32,16,2176]{2,1,0:T(8,128)(2,1)} %bitcast.45), calls=%async_computation.1 | async-start | bytes 4456448 | tf_op jit(solution)/shard_map/all_to_all | solution.py:274
  40.2 1.1 fusion.3
  41.4 2.7 %collective-permute-start.2 = (bf16[256,1280]{1,0:T(8,128)(2,1)}, bf16[256,1280]{1,0:T(8,128)(2,1)}, u32[]{:S(2)}, u32[]{:S(2)}) collective-permute-start(bf16[256,1280]{1,0:T(8,128)(2,1)} %bitcast.6), channel_id=1, source_target_pairs={{0,3},{1,0},{2,1},{3,2},{4,7},{5,4},{6,5},{7,6},{8,11},{9,8},{10,9... | collective-permute-start | bytes 1966088 | tf_op jit(solution)/shard_map/ppermute | solution.py:257
  44.5 1.0 collective-permute-start.9
  45.5 13.3 %collective-permute-done.refs_2_ = bf16[256,1280]{1,0:T(8,128)(2,1)} collective-permute-done((bf16[256,1280]{1,0:T(8,128)(2,1)}, bf16[256,1280]{1,0:T(8,128)(2,1)}, u32[]{:S(2)}, u32[]{:S(2)}) %collective-permute-start) | collective-permute-done | bytes 655392 | tf_op jit(solution)/shard_map/ppermute | solution.py:257
  58.8 2.7 %collective-permute-start.3 = (bf16[256,1280]{1,0:T(8,128)(2,1)}, bf16[256,1280]{1,0:T(8,128)(2,1)}, u32[]{:S(2)}, u32[]{:S(2)}) collective-permute-start(bf16[256,1280]{1,0:T(8,128)(2,1)} %collective-permute-done.2.refs_1_), channel_id=1, source_target_pairs={{0,3},{1,0},{2,1},{3,2},{4,7},{5,4},{6,5},{7,6},{8,11},{9,8},{10,9... | collective-permute-start | bytes 1966088 | tf_op jit(solution)/shard_map/ppermute | solution.py:259
  61.5 3.0 %shard_map.74 = (f32[512,512]{1,0:T(8,128)S(1)}, f32[512,512]{1,0:T(8,128)S(1)}) custom-call(s32[1]{0:T(128)} %bitcast.3.where_ref, bf16[512,1280]{1,0:T(8,128)(2,1)S(1)} %bitcast.28, bf16[7168,512]{1,0:T(8,128)(2,1)} %bitcast.30, bf16[7168,512]{1,0:T(8,128)(2,1)} %bitcast.35, bf16[512,7168]{1,0:T(8,128)(2,1)} %bitcast.40), custom_call_target="tpu_custom_call" | custom-call | flops 1342177280 | bytes 5242880 | tf_op jit(solution)/shard_map/pallas_call | solution.py:138
  64.5 7.3 %collective-permute-done.8.refs_0_ = bf16[256,1280]{1,0:T(8,128)(2,1)} collective-permute-done((bf16[256,1280]{1,0:T(8,128)(2,1)}, bf16[256,1280]{1,0:T(8,128)(2,1)}, u32[]{:S(2)}, u32[]{:S(2)}) %collective-permute-start.8) | collective-permute-done | bytes 655392 | tf_op jit(solution)/shard_map/ppermute | solution.py:258
  71.8 1.0 collective-permute-done.9.refs_3_
  72.9 6.4 %shard_map.75 = (f32[512,512]{1,0:T(8,128)S(1)}, f32[512,512]{1,0:T(8,128)S(1)}) custom-call(s32[1]{0:T(128)} %bitcast.3.where_ref, bf16[256,1280]{1,0:T(8,128)(2,1)} %collective-permute-done.8.refs_0_, bf16[256,1280]{1,0:T(8,128)(2,1)} %collective-permute-done.2.refs_1_, bf16[256,1280]{1,0:T(8,128)(2,1)} %collective-permute-done.refs_2_, ...), custom_call_target="tpu_custom_call" | custom-call | flops 2684354560 | bytes 10485760 | tf_op jit(solution)/shard_map/pallas_call | solution.py:138
  79.3 1.0 copy-done
  80.3 1.0 copy-done.1
  81.2 4.1 %shard_map.73 = (f32[512,512]{1,0:T(8,128)S(1)}, f32[512,512]{1,0:T(8,128)S(1)}, bf16[512,128]{1,0:T(8,128)(2,1)S(1)}, bf16[1280,512]{1,0:T(8,128)(2,1)S(1)}, bf16[1280,512]{1,0:T(8,128)(2,1)S(1)}) custom-call(s32[1]{0:T(128)} %bitcast.3.where_ref, bf16[512,2176]{1,0:T(8,128)(2,1)S(1)} %bitcast.29, bf16[7168,512]{1,0:T(8,128)(2,1)} %bitcast.32, ...), custom_call_target="tpu_custom_call" | custom-call | flops 2147483648 | bytes 8388608 | tf_op jit(solution)/shard_map/pallas_call | solution.py:138
  85.3 1.6 collective-permute-done.1.refs_0_
  86.9 7.7 %shard_map.76 = (bf16[512,512]{1,0:T(8,128)(2,1)S(1)}, bf16[256,1280]{1,0:T(8,128)(2,1)S(1)}, bf16[256,1280]{1,0:T(8,128)(2,1)S(1)}, bf16[256,1280]{1,0:T(8,128)...) custom-call(s32[1]{0:T(128)} %bitcast.3.where_ref, ...), custom_call_target="tpu_custom_call" | custom-call | flops 2684354560 | bytes 10485760 | tf_op jit(solution)/shard_map/pallas_call | solution.py:138
  94.7 2.6 %shard_map.77 = bf16[512,2048]{1,0:T(8,128)(2,1)} custom-call(s32[1]{0:T(128)} %bitcast.3.where_ref, bf16[512,512]{1,0:T(8,128)(2,1)S(1)} %get-tuple-element.42.refs_0_, bf16[512,512]{1,0:T(8,128)(2,1)S(1)} %get-tuple-element.43.refs_1_, bf16[512,512]{1,0:T(8,128)(2,1)S(1)} %get-tuple-element.44.refs_2_, bf16[512,512]{1,0:T(8,128)(2,1)S(1)} %get-tuple-element.45.refs_3_, ...), custom_call_target="tpu_custom_call" | custom-call | flops 1073741824 | bytes 4194304 | tf_op jit(solution)/shard_map/pallas_call | solution.py:138
  97.3 8.6 %all-to-all-start.2 = ((bf16[32,16,2048]{2,1,0:T(8,128)(2,1)}), bf16[32,16,2048]{2,1,0:T(8,128)(2,1)}, u32[]{:S(2)}, u32[]{:S(2)}) async-start(bf16[32,16,2048]{2,1,0:T(8,128)(2,1)} %bitcast.14), calls=%async_computation.2 | async-start | bytes 4194304 | tf_op jit(solution)/shard_map/all_to_all | solution.py:274
  105.9 2.8 %collective-permute-start.18 = (bf16[256,1280]{1,0:T(8,128)(2,1)S(1)}, bf16[256,1280]{1,0:T(8,128)(2,1)S(1)}, u32[]{:S(2)}, u32[]{:S(2)}) collective-permute-start(bf16[256,1280]{1,0:T(8,128)(2,1)S(1)} %get-tuple-element.54), channel_id=1, source_target_pairs={{0,3},{1,0},{2,1},{3,2},{4,7},{5,4},{6,5},{7,6},{8,11},{9,8},{10,9... | collective-permute-start | bytes 1966088 | tf_op jit(solution)/shard_map/ppermute | solution.py:266
  108.7 1.5 collective-permute-start.16
  110.1 3.3 %shard_map.78 = (bf16[256,1280]{1,0:T(8,128)(2,1)S(1)}, bf16[256,1280]{1,0:T(8,128)(2,1)S(1)}, bf16[256,1280]{1,0:T(8,128)(2,1)S(1)}, bf16[256,1280]{1,0:T(8,128)(2,1)S(1)}) custom-call(s32[1]{0:T(128)} %bitcast.3.where_ref, bf16[512,512]{1,0:T(8,128)(2,1)S(1)} %get-tuple-element.42.refs_0_, bf16[7168,512]{1,0:T(8,128)(2,1)} %bitcast.34, ...), custom_call_target="tpu_custom_call" | custom-call | flops 1342177280 | bytes 5242880 | tf_op jit(solution)/shard_map/pallas_call | solution.py:138
  113.5 1.2 add_convert_fusion.1
  115.1 7.4 %collective-permute-done.18 = bf16[256,1280]{1,0:T(8,128)(2,1)S(1)} collective-permute-done((bf16[256,1280]{1,0:T(8,128)(2,1)S(1)}, bf16[256,1280]{1,0:T(8,128)(2,1)S(1)}, u32[]{:S(2)}, u32[]{:S(2)}) %collective-permute-start.18) | collective-permute-done | bytes 655392 | tf_op jit(solution)/shard_map/ppermute | solution.py:266
  122.6 3.6 %collective-permute-start.19 = (bf16[256,1280]{1,0:T(8,128)(2,1)S(1)}, bf16[256,1280]{1,0:T(8,128)(2,1)S(1)}, u32[]{:S(2)}, u32[]{:S(2)}) collective-permute-start(bf16[256,1280]{1,0:T(8,128)(2,1)S(1)} %add_convert_fusion), channel_id=1, source_target_pairs={{0,3},{1,0},{2,1},{3,2},{4,7},{5,4},{6,5},{7,6},{8,11},{9,8},{10,9... | collective-permute-start | bytes 1966088 | tf_op jit(solution)/shard_map/ppermute | solution.py:269
  126.3 10.1 %collective-permute-done.16.refs_2_ = bf16[256,1280]{1,0:T(8,128)(2,1)S(1)} collective-permute-done((bf16[256,1280]{1,0:T(8,128)(2,1)S(1)}, bf16[256,1280]{1,0:T(8,128)(2,1)S(1)}, u32[]{:S(2)}, u32[]{:S(2)}) %collective-permute-start.16) | collective-permute-done | bytes 655392 | tf_op jit(solution)/shard_map/ppermute | solution.py:267
  136.5 4.3 %collective-permute-done.15.refs_1_ = bf16[256,1280]{1,0:T(8,128)(2,1)S(1)} collective-permute-done((bf16[256,1280]{1,0:T(8,128)(2,1)S(1)}, bf16[256,1280]{1,0:T(8,128)(2,1)S(1)}, u32[]{:S(2)}, u32[]{:S(2)}) %collective-permute-start.15) | collective-permute-done | bytes 655392 | tf_op jit(solution)/shard_map/ppermute | solution.py:268
  140.8 9.7 %collective-permute-done.19.refs_5_ = bf16[256,1280]{1,0:T(8,128)(2,1)S(1)} collective-permute-done((bf16[256,1280]{1,0:T(8,128)(2,1)S(1)}, bf16[256,1280]{1,0:T(8,128)(2,1)S(1)}, u32[]{:S(2)}, u32[]{:S(2)}) %collective-permute-start.19) | collective-permute-done | bytes 655392 | tf_op jit(solution)/shard_map/ppermute | solution.py:269
  150.5 1.6 join_sums.1
  152.1 8.2 %all-to-all-start.3 = ((bf16[32,16,1280]{2,1,0:T(8,128)(2,1)}), bf16[32,16,1280]{2,1,0:T(8,128)(2,1)S(1)}, u32[]{:S(2)}, u32[]{:S(2)}) async-start(bf16[32,16,1280]{2,1,0:T(8,128)(2,1)} %bitcast.16), calls=%async_computation.3 | async-start | bytes 2621440 | tf_op jit(solution)/shard_map/all_to_all | solution.py:274
  160.3 2.3 %convolution_convert_fusion.1 = bf16[256,2048]{1,0:T(8,128)(2,1)S(1)} fusion(bf16[512,256]{1,0:T(8,128)(2,1)S(1)} %fusion, bf16[512,2048]{1,0:T(8,128)(2,1)} %bitcast.15), kind=kOutput, calls=%fused_computation.1 | convolution fusion | flops 537395200 | bytes 3407872 | tf_op jit(solution)/shard_map/dot_general | solution.py:335
  162.6 1.7 collective-permute-start.10
  164.3 1.9 %collective-permute-start.12 = (bf16[128,512]{1,0:T(8,128)(2,1)S(1)}, bf16[128,512]{1,0:T(8,128)(2,1)S(1)}, u32[]{:S(2)}, u32[]{:S(2)}) collective-permute-start(bf16[128,512]{1,0:T(8,128)(2,1)S(1)} %get-tuple-element.60), channel_id=1, source_target_pairs={{0,3},{1,0},{2,1},{3,2},{4,7},{5,4},{6,5},{7,6},{8,11},{9,8},{10,9... | collective-permute-start | bytes 393224 | tf_op jit(solution)/shard_map/ppermute | solution.py:250
  166.2 3.6 %collective-permute-done.10 = bf16[128,512]{1,0:T(8,128)(2,1)S(1)} collective-permute-done((bf16[128,512]{1,0:T(8,128)(2,1)S(1)}, bf16[128,512]{1,0:T(8,128)(2,1)S(1)}, u32[]{:S(2)}, u32[]{:S(2)}) %collective-permute-start.10) | collective-permute-done | bytes 131104 | tf_op jit(solution)/shard_map/ppermute | solution.py:250
  169.8 0.6 collective-permute-start.11
  170.5 2.1 %collective-permute-start.13 = (bf16[256,512]{1,0:T(8,128)(2,1)S(1)}, bf16[256,512]{1,0:T(8,128)(2,1)S(1)}, u32[]{:S(2)}, u32[]{:S(2)}) collective-permute-start(bf16[256,512]{1,0:T(8,128)(2,1)S(1)} %get-tuple-element.58), channel_id=1, source_target_pairs={{0,3},{1,0},{2,1},{3,2},{4,7},{5,4},{6,5},{7,6},{8,11},{9,8},{10,9... | collective-permute-start | bytes 786440 | tf_op jit(solution)/shard_map/ppermute | solution.py:253
  172.6 5.6 %collective-permute-done.11 = bf16[256,512]{1,0:T(8,128)(2,1)S(1)} collective-permute-done((bf16[256,512]{1,0:T(8,128)(2,1)S(1)}, bf16[256,512]{1,0:T(8,128)(2,1)S(1)}, u32[]{:S(2)}, u32[]{:S(2)}) %collective-permute-start.11) | collective-permute-done | bytes 262176 | tf_op jit(solution)/shard_map/ppermute | solution.py:253
  178.3 1.2 all-to-all-done.3
  180.1 1.0 pad_maximum_fusion
  (50 shorter events, 2.6 us)
Async XLA Ops:
  2.9 20.1 %copy-start.2 = (bf16[512,256]{1,0:T(8,128)(2,1)}, bf16[512,256]{1,0:T(8,128)(2,1)S(1)}, u32[]{:S(2)}) copy-start(bf16[512,256]{1,0:T(8,128)(2,1)S(1)} %get-tuple-element.30) | copy-start | bytes 786436
  2.9 12.9 %collective-permute-start.5 = (bf16[256,640]{1,0:T(8,128)(2,1)S(1)}, bf16[256,640]{1,0:T(8,128)(2,1)S(1)}, u32[]{:S(2)}, u32[]{:S(2)}) collective-permute-start(bf16[256,640]{1,0:T(8,128)(2,1)S(1)} %get-tuple-element.32), channel_id=1, source_target_pairs={{0,1},{1,2},{2,3},{3,0},{4,5},{5,6},{6,7},{7,4},{8,9},{9,10},{10,1... | collective-permute-start | bytes 983048 | tf_op jit(solution)/shard_map/ppermute | solution.py:245
  5.4 10.5 %collective-permute-start.4 = (bf16[256,640]{1,0:T(8,128)(2,1)S(1)}, bf16[256,640]{1,0:T(8,128)(2,1)}, u32[]{:S(2)}, u32[]{:S(2)}) collective-permute-start(bf16[256,640]{1,0:T(8,128)(2,1)S(1)} %get-tuple-element.32), channel_id=1, source_target_pairs={{0,3},{1,0},{2,1},{3,2},{4,7},{5,4},{6,5},{7,6},{8,11},{9,8},{10,9... | collective-permute-start | bytes 983048 | tf_op jit(solution)/shard_map/ppermute | solution.py:245
  7.7 27.3 %all-to-all-start = ((bf16[32,16,1280]{2,1,0:T(8,128)(2,1)}), bf16[32,16,1280]{2,1,0:T(8,128)(2,1)S(1)}, u32[]{:S(2)}, u32[]{:S(2)}) async-start(bf16[32,16,1280]{2,1,0:T(8,128)(2,1)} %bitcast.4), calls=%async_computation | async-start | bytes 2621440 | tf_op jit(solution)/shard_map/all_to_all | solution.py:274
  15.9 6.7 %collective-permute-start.6 = (bf16[128,640]{1,0:T(8,128)(2,1)S(1)}, bf16[128,640]{1,0:T(8,128)(2,1)S(1)}, u32[]{:S(2)}, u32[]{:S(2)}) collective-permute-start(bf16[128,640]{1,0:T(8,128)(2,1)S(1)} %slice.82), channel_id=1, source_target_pairs={{0,1},{1,2},{2,3},{3,0},{4,5},{5,6},{6,7},{7,4},{8,9},{9,10},{10,1... | collective-permute-start | bytes 491528 | tf_op jit(solution)/shard_map/ppermute | solution.py:246
  16.9 5.7 %collective-permute-start.7 = (bf16[128,640]{1,0:T(8,128)(2,1)S(1)}, bf16[128,640]{1,0:T(8,128)(2,1)S(1)}, u32[]{:S(2)}, u32[]{:S(2)}) collective-permute-start(bf16[128,640]{1,0:T(8,128)(2,1)S(1)} %slice.83), channel_id=1, source_target_pairs={{0,3},{1,0},{2,1},{3,2},{4,7},{5,4},{6,5},{7,6},{8,11},{9,8},{10,9... | collective-permute-start | bytes 491528 | tf_op jit(solution)/shard_map/ppermute | solution.py:246
  35.0 46.3 %all-to-all-start.1 = ((bf16[32,16,2176]{2,1,0:T(8,128)(2,1)}), bf16[32,16,2176]{2,1,0:T(8,128)(2,1)S(1)}, u32[]{:S(2)}, u32[]{:S(2)}) async-start(bf16[32,16,2176]{2,1,0:T(8,128)(2,1)} %bitcast.45), calls=%async_computation.1 | async-start | bytes 4456448 | tf_op jit(solution)/shard_map/all_to_all | solution.py:274
  41.3 17.5 %collective-permute-start = (bf16[256,1280]{1,0:T(8,128)(2,1)}, bf16[256,1280]{1,0:T(8,128)(2,1)}, u32[]{:S(2)}, u32[]{:S(2)}) collective-permute-start(bf16[256,1280]{1,0:T(8,128)(2,1)} %bitcast.5), channel_id=1, source_target_pairs={{0,1},{1,2},{2,3},{3,0},{4,5},{5,6},{6,7},{7,4},{8,9},{9,10},{10,1... | collective-permute-start | bytes 1966088 | tf_op jit(solution)/shard_map/ppermute | solution.py:257
  41.4 17.5 %collective-permute-start.2 = (bf16[256,1280]{1,0:T(8,128)(2,1)}, bf16[256,1280]{1,0:T(8,128)(2,1)}, u32[]{:S(2)}, u32[]{:S(2)}) collective-permute-start(bf16[256,1280]{1,0:T(8,128)(2,1)} %bitcast.6), channel_id=1, source_target_pairs={{0,3},{1,0},{2,1},{3,2},{4,7},{5,4},{6,5},{7,6},{8,11},{9,8},{10,9... | collective-permute-start | bytes 1966088 | tf_op jit(solution)/shard_map/ppermute | solution.py:257
  44.0 27.8 %collective-permute-start.8 = (bf16[256,1280]{1,0:T(8,128)(2,1)}, bf16[256,1280]{1,0:T(8,128)(2,1)}, u32[]{:S(2)}, u32[]{:S(2)}) collective-permute-start(bf16[256,1280]{1,0:T(8,128)(2,1)} %bitcast.5), channel_id=1, source_target_pairs={{0,3},{1,0},{2,1},{3,2},{4,7},{5,4},{6,5},{7,6},{8,11},{9,8},{10,9... | collective-permute-start | bytes 1966088 | tf_op jit(solution)/shard_map/ppermute | solution.py:258
  44.5 28.4 %collective-permute-start.9 = (bf16[256,1280]{1,0:T(8,128)(2,1)}, bf16[256,1280]{1,0:T(8,128)(2,1)}, u32[]{:S(2)}, u32[]{:S(2)}) collective-permute-start(bf16[256,1280]{1,0:T(8,128)(2,1)} %bitcast.6), channel_id=1, source_target_pairs={{0,1},{1,2},{2,3},{3,0},{4,5},{5,6},{6,7},{7,4},{8,9},{9,10},{10,1... | collective-permute-start | bytes 1966088 | tf_op jit(solution)/shard_map/ppermute | solution.py:258
  58.8 28.1 %collective-permute-start.1 = (bf16[256,1280]{1,0:T(8,128)(2,1)}, bf16[256,1280]{1,0:T(8,128)(2,1)}, u32[]{:S(2)}, u32[]{:S(2)}) collective-permute-start(bf16[256,1280]{1,0:T(8,128)(2,1)} %collective-permute-done.refs_2_), channel_id=1, source_target_pairs={{0,1},{1,2},{2,3},{3,0},{4,5},{5,6},{6,7},{7,4},{8,9},{9,10},{10,1... | collective-permute-start | bytes 1966088 | tf_op jit(solution)/shard_map/ppermute | solution.py:259
  58.8 28.1 %collective-permute-start.3 = (bf16[256,1280]{1,0:T(8,128)(2,1)}, bf16[256,1280]{1,0:T(8,128)(2,1)}, u32[]{:S(2)}, u32[]{:S(2)}) collective-permute-start(bf16[256,1280]{1,0:T(8,128)(2,1)} %collective-permute-done.2.refs_1_), channel_id=1, source_target_pairs={{0,3},{1,0},{2,1},{3,2},{4,7},{5,4},{6,5},{7,6},{8,11},{9,8},{10,9... | collective-permute-start | bytes 1966088 | tf_op jit(solution)/shard_map/ppermute | solution.py:259
  79.3 1.0 copy-start
  80.3 1.0 copy-start.1
  94.6 18.9 %collective-permute-start.14 = (bf16[256,1280]{1,0:T(8,128)(2,1)S(1)}, bf16[256,1280]{1,0:T(8,128)(2,1)}, u32[]{:S(2)}, u32[]{:S(2)}) collective-permute-start(bf16[256,1280]{1,0:T(8,128)(2,1)S(1)} %get-tuple-element.49), channel_id=1, source_target_pairs={{0,1},{1,2},{2,3},{3,0},{4,5},{5,6},{6,7},{7,4},{8,9},{9,10},{10,1... | collective-permute-start | bytes 1966088 | tf_op jit(solution)/shard_map/ppermute | solution.py:266
  97.3 54.8 %all-to-all-start.2 = ((bf16[32,16,2048]{2,1,0:T(8,128)(2,1)}), bf16[32,16,2048]{2,1,0:T(8,128)(2,1)}, u32[]{:S(2)}, u32[]{:S(2)}) async-start(bf16[32,16,2048]{2,1,0:T(8,128)(2,1)} %bitcast.14), calls=%async_computation.2 | async-start | bytes 4194304 | tf_op jit(solution)/shard_map/all_to_all | solution.py:274
  105.9 16.6 %collective-permute-start.18 = (bf16[256,1280]{1,0:T(8,128)(2,1)S(1)}, bf16[256,1280]{1,0:T(8,128)(2,1)S(1)}, u32[]{:S(2)}, u32[]{:S(2)}) collective-permute-start(bf16[256,1280]{1,0:T(8,128)(2,1)S(1)} %get-tuple-element.54), channel_id=1, source_target_pairs={{0,3},{1,0},{2,1},{3,2},{4,7},{5,4},{6,5},{7,6},{8,11},{9,8},{10,9... | collective-permute-start | bytes 1966088 | tf_op jit(solution)/shard_map/ppermute | solution.py:266
  108.7 27.8 %collective-permute-start.16 = (bf16[256,1280]{1,0:T(8,128)(2,1)S(1)}, bf16[256,1280]{1,0:T(8,128)(2,1)S(1)}, u32[]{:S(2)}, u32[]{:S(2)}) collective-permute-start(bf16[256,1280]{1,0:T(8,128)(2,1)S(1)} %get-tuple-element.50), channel_id=1, source_target_pairs={{0,3},{1,0},{2,1},{3,2},{4,7},{5,4},{6,5},{7,6},{8,11},{9,8},{10,9... | collective-permute-start | bytes 1966088 | tf_op jit(solution)/shard_map/ppermute | solution.py:267
  110.1 26.4 %collective-permute-start.17 = (bf16[256,1280]{1,0:T(8,128)(2,1)S(1)}, bf16[256,1280]{1,0:T(8,128)(2,1)S(1)}, u32[]{:S(2)}, u32[]{:S(2)}) collective-permute-start(bf16[256,1280]{1,0:T(8,128)(2,1)S(1)} %get-tuple-element.52), channel_id=1, source_target_pairs={{0,1},{1,2},{2,3},{3,0},{4,5},{5,6},{6,7},{7,4},{8,9},{9,10},{10,1... | collective-permute-start | bytes 1966088 | tf_op jit(solution)/shard_map/ppermute | solution.py:267
  114.7 11.5 %copy-start.5 = (bf16[256,8]{0,1:T(8,128)(2,1)S(1)}, bf16[256,8]{0,1:T(8,128)(2,1)}, u32[]{:S(2)}) copy-start(bf16[256,8]{0,1:T(8,128)(2,1)} %param.10) | copy-start | bytes 12292
  114.7 11.5 %copy-start.4 = (s32[256,8]{0,1:T(8,128)S(1)}, s32[256,8]{0,1:T(8,128)}, u32[]{:S(2)}) copy-start(s32[256,8]{0,1:T(8,128)} %param.9) | copy-start | bytes 24580
  114.7 11.5 %copy-start.3 = (bf16[512,256]{1,0:T(8,128)(2,1)S(1)}, bf16[512,256]{1,0:T(8,128)(2,1)}, u32[]{:S(2)}) copy-start(bf16[512,256]{1,0:T(8,128)(2,1)} %copy-done.2) | copy-start | bytes 786436
  114.8 26.0 %collective-permute-start.15 = (bf16[256,1280]{1,0:T(8,128)(2,1)S(1)}, bf16[256,1280]{1,0:T(8,128)(2,1)S(1)}, u32[]{:S(2)}, u32[]{:S(2)}) collective-permute-start(bf16[256,1280]{1,0:T(8,128)(2,1)S(1)} %add_convert_fusion.1), channel_id=1, source_target_pairs={{0,1},{1,2},{2,3},{3,0},{4,5},{5,6},{6,7},{7,4},{8,9},{9,10},{10,1... | collective-permute-start | bytes 1966088 | tf_op jit(solution)/shard_map/ppermute | solution.py:268
  122.6 27.9 %collective-permute-start.19 = (bf16[256,1280]{1,0:T(8,128)(2,1)S(1)}, bf16[256,1280]{1,0:T(8,128)(2,1)S(1)}, u32[]{:S(2)}, u32[]{:S(2)}) collective-permute-start(bf16[256,1280]{1,0:T(8,128)(2,1)S(1)} %add_convert_fusion), channel_id=1, source_target_pairs={{0,3},{1,0},{2,1},{3,2},{4,7},{5,4},{6,5},{7,6},{8,11},{9,8},{10,9... | collective-permute-start | bytes 1966088 | tf_op jit(solution)/shard_map/ppermute | solution.py:269
  152.1 27.4 %all-to-all-start.3 = ((bf16[32,16,1280]{2,1,0:T(8,128)(2,1)}), bf16[32,16,1280]{2,1,0:T(8,128)(2,1)S(1)}, u32[]{:S(2)}, u32[]{:S(2)}) async-start(bf16[32,16,1280]{2,1,0:T(8,128)(2,1)} %bitcast.16), calls=%async_computation.3 | async-start | bytes 2621440 | tf_op jit(solution)/shard_map/all_to_all | solution.py:274
  162.6 7.1 %collective-permute-start.10 = (bf16[128,512]{1,0:T(8,128)(2,1)S(1)}, bf16[128,512]{1,0:T(8,128)(2,1)S(1)}, u32[]{:S(2)}, u32[]{:S(2)}) collective-permute-start(bf16[128,512]{1,0:T(8,128)(2,1)S(1)} %get-tuple-element.59), channel_id=1, source_target_pairs={{0,1},{1,2},{2,3},{3,0},{4,5},{5,6},{6,7},{7,4},{8,9},{9,10},{10,1... | collective-permute-start | bytes 393224 | tf_op jit(solution)/shard_map/ppermute | solution.py:250
  164.3 5.5 %collective-permute-start.12 = (bf16[128,512]{1,0:T(8,128)(2,1)S(1)}, bf16[128,512]{1,0:T(8,128)(2,1)S(1)}, u32[]{:S(2)}, u32[]{:S(2)}) collective-permute-start(bf16[128,512]{1,0:T(8,128)(2,1)S(1)} %get-tuple-element.60), channel_id=1, source_target_pairs={{0,3},{1,0},{2,1},{3,2},{4,7},{5,4},{6,5},{7,6},{8,11},{9,8},{10,9... | collective-permute-start | bytes 393224 | tf_op jit(solution)/shard_map/ppermute | solution.py:250
  169.8 8.3 %collective-permute-start.11 = (bf16[256,512]{1,0:T(8,128)(2,1)S(1)}, bf16[256,512]{1,0:T(8,128)(2,1)S(1)}, u32[]{:S(2)}, u32[]{:S(2)}) collective-permute-start(bf16[256,512]{1,0:T(8,128)(2,1)S(1)} %get-tuple-element.57), channel_id=1, source_target_pairs={{0,1},{1,2},{2,3},{3,0},{4,5},{5,6},{6,7},{7,4},{8,9},{9,10},{10,1... | collective-permute-start | bytes 786440 | tf_op jit(solution)/shard_map/ppermute | solution.py:253
  170.5 7.7 %collective-permute-start.13 = (bf16[256,512]{1,0:T(8,128)(2,1)S(1)}, bf16[256,512]{1,0:T(8,128)(2,1)S(1)}, u32[]{:S(2)}, u32[]{:S(2)}) collective-permute-start(bf16[256,512]{1,0:T(8,128)(2,1)S(1)} %get-tuple-element.58), channel_id=1, source_target_pairs={{0,3},{1,0},{2,1},{3,2},{4,7},{5,4},{6,5},{7,6},{8,11},{9,8},{10,9... | collective-permute-start | bytes 786440 | tf_op jit(solution)/shard_map/ppermute | solution.py:253

commit v6 on v5

--- a/solution.py
+++ b/solution.py
@@ -25,7 +25,7 @@
         return copy
 
 
-def expert_call(where, weights, xs=(), segs=(), carry=(), inv=None, hidden=None, jobs=(), outs=(), stash=((), ()), held=(), stored=(), keep=None):
+def expert_call(where, weights, xs=(), segs=(), carry=(), inv=None, hidden=None, jobs=(), outs=(), stash=((), ()), held=(), stored=(), keep=None, fetch=False):
     slices = lax.axis_size("tp")
     w_gate, w_up, w_down = weights
     d_all, ff = w_gate.shape
@@ -53,27 +53,31 @@
     results += [(s, BF16) for s in weight_shapes(stash[0], later)]
     needed = weight_shapes(segs, columns)[len(held) :]
     streams = bool(needed) or len(results) > n_out
-    resident = list(xs) + list(carry) + ([] if hidden is None else [hidden]) + list(held)
-    streamed = ([w_gate, w_up, w_down] if streams else []) + list(stored)
+    resident = ([] if fetch else list(xs)) + list(carry) + ([] if hidden is None else [hidden]) + list(held)
+    streamed = ([w_gate, w_up, w_down] if streams else []) + list(stored) + (list(xs) if fetch else [])
+    fetched = [(rows, seg[3]) for seg in segs] if fetch else []
     scratch = [pltpu.VMEM(s, BF16) for s in needed]
     if finish:
         scratch += [pltpu.VMEM((rows, ff), F32)] * 2
     scratch += [pltpu.VMEM((rows, ff), F32)] * len(stored)
-    n_copies = len(stored) + len(needed) + len(results) - n_out
+    scratch += [pltpu.VMEM(shape, BF16) for shape in fetched]
+    n_copies = len(fetched) + bool(fetch and keep) + len(stored) + len(needed) + len(results) - n_out
     scratch += [pltpu.SemaphoreType.DMA((max(n_copies, 1),))]
 
     def body(where_ref, *refs):
         refs = list(refs)
         take = lambda n: [refs.pop(0) for _ in range(n)]
-        x_refs, carried = take(len(xs)), take(len(carry))
+        x_refs, carried = take(0 if fetch else len(xs)), take(len(carry))
         hidden_ref = take(hidden is not None)
         held_refs = take(len(held))
         wg, wu, wd = take(3) if streams else (None,) * 3
         stored_refs = take(len(stored))
+        x_refs = take(len(xs)) if fetch else x_refs
         out_refs = take(len(results))
         bufs = held_refs + take(len(needed))
         accs = take(2) if finish else out_refs[:2]
         stored_bufs = take(len(stored))
+        x_bufs = take(len(fetched))
         copies = Copies(refs.pop(0))
         z = where_ref[0]
 
@@ -96,13 +100,25 @@
             if wait is not None:
                 wait.wait()
 
+        x_waits = [
+            copies.start(x_refs[index[0]].at[:, pl.ds(col, width)], buf)
+            for (index, _, _, width, col), buf in zip(segs, x_bufs)
+        ]
         waits = bring(segs, columns, bufs, len(held))
         stored_waits = [copies.start(r, b) for r, b in zip(stored_refs, stored_bufs)]
         stash_waits = bring(stash[0], later, out_refs[n_out:], 0)
         if keep:
-            out_refs[2][...] = x_refs[keep[0]][:, keep[1] : keep[1] + SIDE]
+            scale_cols = x_refs[keep[0]].at[:, pl.ds(keep[1], SIDE)]
+            if fetch:
+                stash_waits.append(copies.start(scale_cols, out_refs[2]))
+            else:
+                out_refs[2][...] = scale_cols[...]
         for k, (index, _, _, width, col) in enumerate(segs):
-            x = [x_refs[i][:, col : col + width] for i in index]
+            if fetch:
+                x_waits[k].wait()
+                x = [x_bufs[k][...]]
+            else:
+                x = [x_refs[i][:, col : col + width] for i in index]
             x = x[0] if len(x) == 1 else jnp.concatenate(x, axis=0)
             for n, acc in enumerate(accs):
                 arrived(waits[2 * k + n])
@@ -310,13 +326,13 @@
         [((0, 1), 1, EARLY, bulk, 0), ((2, 3), 3, EARLY, bulk, 0)], sums,
     )
     early_jobs = [(k, 0, EARLY, 0, rows, ((0, 0, rows, k * EARLY),)) for k in range(n_tp)]
-    *early_sums, scale, far_gate, far_up = expert_call(
-        where, weights, [early_rows],
-        [((0,), k, 0, EARLY, k * EARLY) for k in range(n_tp)], keep=(0, n_tp * EARLY), stash=(far_segs, ()),
+    gate_sum, up_sum, scale, *far_held = expert_call(
+        where, weights, [early_rows], [((0,), k, 0, EARLY, k * EARLY) for k in range(n_tp)],
+        stored=sums, keep=(0, n_tp * EARLY), stash=(far_segs, far_jobs), fetch=True,
     )
     hidden, f_low, f_high, a_high, b_low, *early_down = expert_call(
-        where, weights, [*far, scale], far_segs, early_sums, inv=2, stored=sums,
-        jobs=far_jobs, outs=[(half, bulk)] * 4, held=(far_gate, far_up), stash=((), early_jobs),
+        where, weights, [*far, scale], far_segs, (gate_sum, up_sum), inv=2,
+        jobs=far_jobs, outs=[(half, bulk)] * 4, held=far_held, stash=((), early_jobs),
     )
     (p_early,) = expert_call(
         where, weights, hidden=hidden, jobs=early_jobs, outs=[(rows, n_tp * EARLY)], held=early_down,

time: 182 us -> 181 us (level)
  transfers between devices with their start and end apart: 24 -> 24, of which waited for: 13 -> 13; matrix products, arithmetic and copies ran while one was open for 6% -> 5% of each run, Pallas kernels for 12% -> 12%
where the time goes in v6:
time: 181 us
  waiting for transfers between devices  75.9 us (42%)
  starting transfers between devices  59.9 us (33%)
  Pallas kernels  31.1 us (17%)
  local copies, waits for them, and re-layouts  5.35 us (3%)
  matrix products  5.01 us (3%)
  other arithmetic  2.93 us (2%)
    all_to_all x4, starting transfers between devices, exchange(): lax.all_to_all(shaped, 'ep', 0, 0, tiled=True).reshape(rows, x.shape[1])  31.1 us
    pallas_call x6, Pallas kernels, expert_call(): pl.pallas_call(body, in_specs=[pl.BlockSpec(memory_space=pltpu.SMEM)] + [...  26.6 us
    ppermute x1, waiting for transfers between devices, spread_halves(): lax.ppermute(low, 'tp', up)  13.3 us
    all_to_all x4, waiting for transfers between devices, exchange(): lax.all_to_all(shaped, 'ep', 0, 0, tiled=True).reshape(rows, x.shape[1])  11.1 us
    ppermute x1, waiting for transfers between devices, fold_halves(): lax.ppermute(below[0], 'tp', dn)  9.94 us
    ppermute x1, waiting for transfers between devices, fold_halves(): up_high = lax.ppermute(add(below[1], got_high), 'tp', dn)  9.55 us
    ppermute x1, waiting for transfers between devices, fold_halves(): lax.ppermute(far[1], 'tp', dn)  8.5 us
    ppermute x1, waiting for transfers between devices, spread_halves(): lax.ppermute(low, 'tp', dn)  7.32 us
  transfers between devices with their start and end apart: 24, of which 13 were waited for; matrix products, arithmetic and copies ran while one was open for 5% of the time, Pallas kernels for 12%

profile of v6, /device:TPU:1, one launch (start us, length us, event | category | flops | bytes accessed | tf_op | source)
XLA Modules:
  0.0 180.6 jit_solution(5818367585683402346)
XLA Ops:
  0.0 2.9 %head.1 = (bf16[512,256]{1,0:T(8,128)(2,1)S(1)}, bf16[512,1280]{1,0:T(8,128)(2,1)}, bf16[256,640]{1,0:T(8,128)(2,1)S(1)}) custom-call(s32[8,256]{1,0:T(8,128)} %bitcast.46, bf16[1792]{0:T(1024)(128)(2,1)} %gain_hbm.1, bf16[256,1792]{1,0:T(8,128)(2,1)} %tokens_hbm.1), custom_call_target="tpu_custom_call" | custom-call | flops 335544320 | bytes 917504 | tf_op jit(solution)/shard_map/head/pallas_call | solution.py:211
  2.9 2.5 %collective-permute-start.7 = (bf16[256,640]{1,0:T(8,128)(2,1)S(1)}, bf16[256,640]{1,0:T(8,128)(2,1)S(1)}, u32[]{:S(2)}, u32[]{:S(2)}) collective-permute-start(bf16[256,640]{1,0:T(8,128)(2,1)S(1)} %get-tuple-element.39), channel_id=1, source_target_pairs={{0,1},{1,2},{2,3},{3,0},{4,5},{5,6},{6,7},{7,4},{8,9},{9,10},{10,1... | collective-permute-start | bytes 983048 | tf_op jit(solution)/shard_map/ppermute | solution.py:261
  5.5 2.2 %collective-permute-start.6 = (bf16[256,640]{1,0:T(8,128)(2,1)S(1)}, bf16[256,640]{1,0:T(8,128)(2,1)}, u32[]{:S(2)}, u32[]{:S(2)}) collective-permute-start(bf16[256,640]{1,0:T(8,128)(2,1)S(1)} %get-tuple-element.39), channel_id=1, source_target_pairs={{0,3},{1,0},{2,1},{3,2},{4,7},{5,4},{6,5},{7,6},{8,11},{9,8},{10,9... | collective-permute-start | bytes 983048 | tf_op jit(solution)/shard_map/ppermute | solution.py:261
  7.7 8.0 %all-to-all-start = ((bf16[32,16,1280]{2,1,0:T(8,128)(2,1)}), bf16[32,16,1280]{2,1,0:T(8,128)(2,1)S(1)}, u32[]{:S(2)}, u32[]{:S(2)}) async-start(bf16[32,16,1280]{2,1,0:T(8,128)(2,1)} %bitcast.4), calls=%async_computation | async-start | bytes 2621440 | tf_op jit(solution)/shard_map/all_to_all | solution.py:290
  16.0 0.9 slice.83
  16.9 2.7 %collective-permute-start.9 = (bf16[128,640]{1,0:T(8,128)(2,1)S(1)}, bf16[128,640]{1,0:T(8,128)(2,1)S(1)}, u32[]{:S(2)}, u32[]{:S(2)}) collective-permute-start(bf16[128,640]{1,0:T(8,128)(2,1)S(1)} %slice.83), channel_id=1, source_target_pairs={{0,3},{1,0},{2,1},{3,2},{4,7},{5,4},{6,5},{7,6},{8,11},{9,8},{10,9... | collective-permute-start | bytes 491528 | tf_op jit(solution)/shard_map/ppermute | solution.py:262
  19.6 1.0 slice_dynamic-update-slice_fusion.2
  20.7 1.0 convert_reduce_fusion.2
  21.7 0.9 collective-permute-done.8
  23.0 2.2 %convolution_convert_fusion = bf16[512,2176]{1,0:T(8,128)(2,1)} fusion(bf16[512,256]{1,0:T(8,128)(2,1)S(1)} %get-tuple-element.33, bf16[256,2176]{1,0:T(8,128)(2,1)S(1)} %pad_dynamic-update-slice_fusion), kind=kOutput, calls=%fused_computation | convolution fusion | flops 571539456 | bytes 3604480 | tf_op jit(solution)/shard_map/dot_general | solution.py:302
  25.1 9.8 %all-to-all-done = bf16[32,16,1280]{2,1,0:T(8,128)(2,1)S(1)} async-done(((bf16[32,16,1280]{2,1,0:T(8,128)(2,1)}), bf16[32,16,1280]{2,1,0:T(8,128)(2,1)S(1)}, u32[]{:S(2)}, u32[]{:S(2)}) %all-to-all-start) | async-done | bytes 1310752 | tf_op jit(solution)/shard_map/all_to_all | solution.py:290
  35.0 5.9 %all-to-all-start.1 = ((bf16[32,16,2176]{2,1,0:T(8,128)(2,1)}), bf16[32,16,2176]{2,1,0:T(8,128)(2,1)}, u32[]{:S(2)}, u32[]{:S(2)}) async-start(bf16[32,16,2176]{2,1,0:T(8,128)(2,1)} %bitcast.44), calls=%async_computation.1 | async-start | bytes 4456448 | tf_op jit(solution)/shard_map/all_to_all | solution.py:290
  40.9 1.1 fusion.3
  42.0 2.7 %collective-permute-start.2 = (bf16[256,1280]{1,0:T(8,128)(2,1)}, bf16[256,1280]{1,0:T(8,128)(2,1)S(1)}, u32[]{:S(2)}, u32[]{:S(2)}) collective-permute-start(bf16[256,1280]{1,0:T(8,128)(2,1)} %bitcast.6), channel_id=1, source_target_pairs={{0,3},{1,0},{2,1},{3,2},{4,7},{5,4},{6,5},{7,6},{8,11},{9,8},{10,9... | collective-permute-start | bytes 1966088 | tf_op jit(solution)/shard_map/ppermute | solution.py:273
  45.1 1.0 collective-permute-start.5
  46.2 13.3 %collective-permute-done.refs_2_ = bf16[256,1280]{1,0:T(8,128)(2,1)S(1)} collective-permute-done((bf16[256,1280]{1,0:T(8,128)(2,1)}, bf16[256,1280]{1,0:T(8,128)(2,1)S(1)}, u32[]{:S(2)}, u32[]{:S(2)}) %collective-permute-start) | collective-permute-done | bytes 655392 | tf_op jit(solution)/shard_map/ppermute | solution.py:273
  59.4 2.7 %collective-permute-start.3 = (bf16[256,1280]{1,0:T(8,128)(2,1)S(1)}, bf16[256,1280]{1,0:T(8,128)(2,1)}, u32[]{:S(2)}, u32[]{:S(2)}) collective-permute-start(bf16[256,1280]{1,0:T(8,128)(2,1)S(1)} %collective-permute-done.2.refs_1_), channel_id=1, source_target_pairs={{0,3},{1,0},{2,1},{3,2},{4,7},{5,4},{6,5},{7,6},{8,11},{9,8},{10,9... | collective-permute-start | bytes 1966088 | tf_op jit(solution)/shard_map/ppermute | solution.py:275
  62.1 3.0 %shard_map.73 = (f32[512,512]{1,0:T(8,128)S(1)}, f32[512,512]{1,0:T(8,128)S(1)}) custom-call(s32[1]{0:T(128)} %bitcast.3.where_ref, bf16[512,1280]{1,0:T(8,128)(2,1)S(1)} %bitcast.28, bf16[7168,512]{1,0:T(8,128)(2,1)} %bitcast.29, bf16[7168,512]{1,0:T(8,128)(2,1)} %bitcast.34, bf16[512,7168]{1,0:T(8,128)(2,1)} %bitcast.39), custom_call_target="tpu_custom_call" | custom-call | flops 1342177280 | bytes 5242880 | tf_op jit(solution)/shard_map/pallas_call | solution.py:154
  65.1 7.3 %collective-permute-done.4.refs_0_ = bf16[256,1280]{1,0:T(8,128)(2,1)S(1)} collective-permute-done((bf16[256,1280]{1,0:T(8,128)(2,1)}, bf16[256,1280]{1,0:T(8,128)(2,1)S(1)}, u32[]{:S(2)}, u32[]{:S(2)}) %collective-permute-start.4) | collective-permute-done | bytes 655392 | tf_op jit(solution)/shard_map/ppermute | solution.py:274
  72.4 1.0 collective-permute-done.5.refs_3_
  73.5 5.8 %shard_map.74 = (f32[512,512]{1,0:T(8,128)S(1)}, f32[512,512]{1,0:T(8,128)S(1)}) custom-call(s32[1]{0:T(128)} %bitcast.3.where_ref, bf16[256,1280]{1,0:T(8,128)(2,1)S(1)} %collective-permute-done.4.refs_0_, bf16[256,1280]{1,0:T(8,128)(2,1)S(1)} %collective-permute-done.2.refs_1_, bf16[256,1280]{1,0:T(8,128)(2,1)S(1)} %collective-permute-done.refs_2_, ...), custom_call_target="tpu_custom_call" | custom-call | flops 2684354560 | bytes 10485760 | tf_op jit(solution)/shard_map/pallas_call | solution.py:154
  79.3 1.0 copy-done
  80.3 1.0 copy-done.1
  81.3 5.5 %shard_map.75 = (f32[512,512]{1,0:T(8,128)S(1)}, f32[512,512]{1,0:T(8,128)S(1)}, bf16[512,128]{1,0:T(8,128)(2,1)S(1)}, bf16[1280,512]{1,0:T(8,128)(2,1)S(1)}, bf...) custom-call(s32[1]{0:T(128)} %bitcast.3.where_ref, ...), custom_call_target="tpu_custom_call" | custom-call | flops 2147483648 | bytes 8388608 | tf_op jit(solution)/shard_map/pallas_call | solution.py:154
  86.8 0.7 collective-permute-done.1.refs_0_
  87.5 6.4 %shard_map.76 = (bf16[512,512]{1,0:T(8,128)(2,1)S(1)}, bf16[256,1280]{1,0:T(8,128)(2,1)}, bf16[256,1280]{1,0:T(8,128)(2,1)S(1)}, bf16[256,1280]{1,0:T(8,128)(2,1...) custom-call(s32[1]{0:T(128)} %bitcast.3.where_ref, ...), custom_call_target="tpu_custom_call" | custom-call | flops 2684354560 | bytes 10485760 | tf_op jit(solution)/shard_map/pallas_call | solution.py:154
  94.0 2.6 %shard_map.77 = bf16[512,2048]{1,0:T(8,128)(2,1)} custom-call(s32[1]{0:T(128)} %bitcast.3.where_ref, bf16[512,512]{1,0:T(8,128)(2,1)S(1)} %get-tuple-element.48.refs_0_, bf16[512,512]{1,0:T(8,128)(2,1)S(1)} %get-tuple-element.49.refs_1_, bf16[512,512]{1,0:T(8,128)(2,1)S(1)} %get-tuple-element.50.refs_2_, bf16[512,512]{1,0:T(8,128)(2,1)S(1)} %get-tuple-element.51.refs_3_, ...), custom_call_target="tpu_custom_call" | custom-call | flops 1073741824 | bytes 4194304 | tf_op jit(solution)/shard_map/pallas_call | solution.py:154
  96.6 9.0 %all-to-all-start.2 = ((bf16[32,16,2048]{2,1,0:T(8,128)(2,1)}), bf16[32,16,2048]{2,1,0:T(8,128)(2,1)}, u32[]{:S(2)}, u32[]{:S(2)}) async-start(bf16[32,16,2048]{2,1,0:T(8,128)(2,1)} %bitcast.14), calls=%async_computation.2 | async-start | bytes 4194304 | tf_op jit(solution)/shard_map/all_to_all | solution.py:290
  105.6 2.6 %collective-permute-start.18 = (bf16[256,1280]{1,0:T(8,128)(2,1)S(1)}, bf16[256,1280]{1,0:T(8,128)(2,1)S(1)}, u32[]{:S(2)}, u32[]{:S(2)}) collective-permute-start(bf16[256,1280]{1,0:T(8,128)(2,1)S(1)} %get-tuple-element.60), channel_id=1, source_target_pairs={{0,3},{1,0},{2,1},{3,2},{4,7},{5,4},{6,5},{7,6},{8,11},{9,8},{10,9... | collective-permute-start | bytes 1966088 | tf_op jit(solution)/shard_map/ppermute | solution.py:282
  108.2 1.6 collective-permute-start.16
  109.8 3.3 %shard_map.78 = (bf16[256,1280]{1,0:T(8,128)(2,1)S(1)}, bf16[256,1280]{1,0:T(8,128)(2,1)S(1)}, bf16[256,1280]{1,0:T(8,128)(2,1)S(1)}, bf16[256,1280]{1,0:T(8,128)(2,1)S(1)}) custom-call(s32[1]{0:T(128)} %bitcast.3.where_ref, bf16[512,512]{1,0:T(8,128)(2,1)S(1)} %get-tuple-element.48.refs_0_, bf16[7168,512]{1,0:T(8,128)(2,1)} %bitcast.33, ...), custom_call_target="tpu_custom_call" | custom-call | flops 1342177280 | bytes 5242880 | tf_op jit(solution)/shard_map/pallas_call | solution.py:154
  113.4 8.5 %collective-permute-done.18 = bf16[256,1280]{1,0:T(8,128)(2,1)S(1)} collective-permute-done((bf16[256,1280]{1,0:T(8,128)(2,1)S(1)}, bf16[256,1280]{1,0:T(8,128)(2,1)S(1)}, u32[]{:S(2)}, u32[]{:S(2)}) %collective-permute-start.18) | collective-permute-done | bytes 655392 | tf_op jit(solution)/shard_map/ppermute | solution.py:282
  122.1 3.8 %collective-permute-start.19 = (bf16[256,1280]{1,0:T(8,128)(2,1)S(1)}, bf16[256,1280]{1,0:T(8,128)(2,1)S(1)}, u32[]{:S(2)}, u32[]{:S(2)}) collective-permute-start(bf16[256,1280]{1,0:T(8,128)(2,1)S(1)} %add_convert_fusion), channel_id=1, source_target_pairs={{0,3},{1,0},{2,1},{3,2},{4,7},{5,4},{6,5},{7,6},{8,11},{9,8},{10,9... | collective-permute-start | bytes 1966088 | tf_op jit(solution)/shard_map/ppermute | solution.py:285
  126.0 9.9 %collective-permute-done.16.refs_2_ = bf16[256,1280]{1,0:T(8,128)(2,1)S(1)} collective-permute-done((bf16[256,1280]{1,0:T(8,128)(2,1)S(1)}, bf16[256,1280]{1,0:T(8,128)(2,1)S(1)}, u32[]{:S(2)}, u32[]{:S(2)}) %collective-permute-start.16) | collective-permute-done | bytes 655392 | tf_op jit(solution)/shard_map/ppermute | solution.py:283
  136.0 4.5 %collective-permute-done.15.refs_1_ = bf16[256,1280]{1,0:T(8,128)(2,1)S(1)} collective-permute-done((bf16[256,1280]{1,0:T(8,128)(2,1)S(1)}, bf16[256,1280]{1,0:T(8,128)(2,1)S(1)}, u32[]{:S(2)}, u32[]{:S(2)}) %collective-permute-start.15) | collective-permute-done | bytes 655392 | tf_op jit(solution)/shard_map/ppermute | solution.py:284
  140.5 9.5 %collective-permute-done.19.refs_5_ = bf16[256,1280]{1,0:T(8,128)(2,1)S(1)} collective-permute-done((bf16[256,1280]{1,0:T(8,128)(2,1)S(1)}, bf16[256,1280]{1,0:T(8,128)(2,1)S(1)}, u32[]{:S(2)}, u32[]{:S(2)}) %collective-permute-start.19) | collective-permute-done | bytes 655392 | tf_op jit(solution)/shard_map/ppermute | solution.py:285
  150.0 1.6 join_sums.1
  151.6 8.2 %all-to-all-start.3 = ((bf16[32,16,1280]{2,1,0:T(8,128)(2,1)}), bf16[32,16,1280]{2,1,0:T(8,128)(2,1)S(1)}, u32[]{:S(2)}, u32[]{:S(2)}) async-start(bf16[32,16,1280]{2,1,0:T(8,128)(2,1)} %bitcast.16), calls=%async_computation.3 | async-start | bytes 2621440 | tf_op jit(solution)/shard_map/all_to_all | solution.py:290
  159.8 2.3 %convolution_convert_fusion.1 = bf16[256,2048]{1,0:T(8,128)(2,1)S(1)} fusion(bf16[512,256]{1,0:T(8,128)(2,1)S(1)} %fusion, bf16[512,2048]{1,0:T(8,128)(2,1)} %bitcast.15), kind=kOutput, calls=%fused_computation.1 | convolution fusion | flops 537395200 | bytes 3407872 | tf_op jit(solution)/shard_map/dot_general | solution.py:351
  162.1 1.8 %collective-permute-start.10 = (bf16[128,512]{1,0:T(8,128)(2,1)S(1)}, bf16[128,512]{1,0:T(8,128)(2,1)S(1)}, u32[]{:S(2)}, u32[]{:S(2)}) collective-permute-start(bf16[128,512]{1,0:T(8,128)(2,1)S(1)} %get-tuple-element.65), channel_id=1, source_target_pairs={{0,1},{1,2},{2,3},{3,0},{4,5},{5,6},{6,7},{7,4},{8,9},{9,10},{10,1... | collective-permute-start | bytes 393224 | tf_op jit(solution)/shard_map/ppermute | solution.py:266
  164.0 1.7 collective-permute-start.12
  165.7 3.6 %collective-permute-done.10 = bf16[128,512]{1,0:T(8,128)(2,1)S(1)} collective-permute-done((bf16[128,512]{1,0:T(8,128)(2,1)S(1)}, bf16[128,512]{1,0:T(8,128)(2,1)S(1)}, u32[]{:S(2)}, u32[]{:S(2)}) %collective-permute-start.10) | collective-permute-done | bytes 131104 | tf_op jit(solution)/shard_map/ppermute | solution.py:266
  169.3 0.8 collective-permute-start.11
  170.1 2.0 %collective-permute-start.13 = (bf16[256,512]{1,0:T(8,128)(2,1)S(1)}, bf16[256,512]{1,0:T(8,128)(2,1)S(1)}, u32[]{:S(2)}, u32[]{:S(2)}) collective-permute-start(bf16[256,512]{1,0:T(8,128)(2,1)S(1)} %get-tuple-element.64), channel_id=1, source_target_pairs={{0,3},{1,0},{2,1},{3,2},{4,7},{5,4},{6,5},{7,6},{8,11},{9,8},{10,9... | collective-permute-start | bytes 786440 | tf_op jit(solution)/shard_map/ppermute | solution.py:269
  172.1 5.6 %collective-permute-done.11 = bf16[256,512]{1,0:T(8,128)(2,1)S(1)} collective-permute-done((bf16[256,512]{1,0:T(8,128)(2,1)S(1)}, bf16[256,512]{1,0:T(8,128)(2,1)S(1)}, u32[]{:S(2)}, u32[]{:S(2)}) %collective-permute-start.11) | collective-permute-done | bytes 262176 | tf_op jit(solution)/shard_map/ppermute | solution.py:269
  177.8 1.2 all-to-all-done.3
  179.0 0.5 convolution_convert_fusion.2
  179.6 1.0 pad_maximum_fusion
  (46 shorter events, 2.0 us)
Async XLA Ops:
  2.9 12.9 %collective-permute-start.7 = (bf16[256,640]{1,0:T(8,128)(2,1)S(1)}, bf16[256,640]{1,0:T(8,128)(2,1)S(1)}, u32[]{:S(2)}, u32[]{:S(2)}) collective-permute-start(bf16[256,640]{1,0:T(8,128)(2,1)S(1)} %get-tuple-element.39), channel_id=1, source_target_pairs={{0,1},{1,2},{2,3},{3,0},{4,5},{5,6},{6,7},{7,4},{8,9},{9,10},{10,1... | collective-permute-start | bytes 983048 | tf_op jit(solution)/shard_map/ppermute | solution.py:261
  5.5 10.5 %collective-permute-start.6 = (bf16[256,640]{1,0:T(8,128)(2,1)S(1)}, bf16[256,640]{1,0:T(8,128)(2,1)}, u32[]{:S(2)}, u32[]{:S(2)}) collective-permute-start(bf16[256,640]{1,0:T(8,128)(2,1)S(1)} %get-tuple-element.39), channel_id=1, source_target_pairs={{0,3},{1,0},{2,1},{3,2},{4,7},{5,4},{6,5},{7,6},{8,11},{9,8},{10,9... | collective-permute-start | bytes 983048 | tf_op jit(solution)/shard_map/ppermute | solution.py:261
  7.7 27.3 %all-to-all-start = ((bf16[32,16,1280]{2,1,0:T(8,128)(2,1)}), bf16[32,16,1280]{2,1,0:T(8,128)(2,1)S(1)}, u32[]{:S(2)}, u32[]{:S(2)}) async-start(bf16[32,16,1280]{2,1,0:T(8,128)(2,1)} %bitcast.4), calls=%async_computation | async-start | bytes 2621440 | tf_op jit(solution)/shard_map/all_to_all | solution.py:290
  15.9 6.7 %collective-permute-start.8 = (bf16[128,640]{1,0:T(8,128)(2,1)S(1)}, bf16[128,640]{1,0:T(8,128)(2,1)S(1)}, u32[]{:S(2)}, u32[]{:S(2)}) collective-permute-start(bf16[128,640]{1,0:T(8,128)(2,1)S(1)} %slice.82), channel_id=1, source_target_pairs={{0,1},{1,2},{2,3},{3,0},{4,5},{5,6},{6,7},{7,4},{8,9},{9,10},{10,1... | collective-permute-start | bytes 491528 | tf_op jit(solution)/shard_map/ppermute | solution.py:262
  16.9 5.6 %collective-permute-start.9 = (bf16[128,640]{1,0:T(8,128)(2,1)S(1)}, bf16[128,640]{1,0:T(8,128)(2,1)S(1)}, u32[]{:S(2)}, u32[]{:S(2)}) collective-permute-start(bf16[128,640]{1,0:T(8,128)(2,1)S(1)} %slice.83), channel_id=1, source_target_pairs={{0,3},{1,0},{2,1},{3,2},{4,7},{5,4},{6,5},{7,6},{8,11},{9,8},{10,9... | collective-permute-start | bytes 491528 | tf_op jit(solution)/shard_map/ppermute | solution.py:262
  35.0 46.3 %all-to-all-start.1 = ((bf16[32,16,2176]{2,1,0:T(8,128)(2,1)}), bf16[32,16,2176]{2,1,0:T(8,128)(2,1)}, u32[]{:S(2)}, u32[]{:S(2)}) async-start(bf16[32,16,2176]{2,1,0:T(8,128)(2,1)} %bitcast.44), calls=%async_computation.1 | async-start | bytes 4456448 | tf_op jit(solution)/shard_map/all_to_all | solution.py:290
  42.0 17.4 %collective-permute-start = (bf16[256,1280]{1,0:T(8,128)(2,1)}, bf16[256,1280]{1,0:T(8,128)(2,1)S(1)}, u32[]{:S(2)}, u32[]{:S(2)}) collective-permute-start(bf16[256,1280]{1,0:T(8,128)(2,1)} %bitcast.5), channel_id=1, source_target_pairs={{0,1},{1,2},{2,3},{3,0},{4,5},{5,6},{6,7},{7,4},{8,9},{9,10},{10,1... | collective-permute-start | bytes 1966088 | tf_op jit(solution)/shard_map/ppermute | solution.py:273
  42.0 17.4 %collective-permute-start.2 = (bf16[256,1280]{1,0:T(8,128)(2,1)}, bf16[256,1280]{1,0:T(8,128)(2,1)S(1)}, u32[]{:S(2)}, u32[]{:S(2)}) collective-permute-start(bf16[256,1280]{1,0:T(8,128)(2,1)} %bitcast.6), channel_id=1, source_target_pairs={{0,3},{1,0},{2,1},{3,2},{4,7},{5,4},{6,5},{7,6},{8,11},{9,8},{10,9... | collective-permute-start | bytes 1966088 | tf_op jit(solution)/shard_map/ppermute | solution.py:273
  44.7 27.8 %collective-permute-start.4 = (bf16[256,1280]{1,0:T(8,128)(2,1)}, bf16[256,1280]{1,0:T(8,128)(2,1)S(1)}, u32[]{:S(2)}, u32[]{:S(2)}) collective-permute-start(bf16[256,1280]{1,0:T(8,128)(2,1)} %bitcast.5), channel_id=1, source_target_pairs={{0,3},{1,0},{2,1},{3,2},{4,7},{5,4},{6,5},{7,6},{8,11},{9,8},{10,9... | collective-permute-start | bytes 1966088 | tf_op jit(solution)/shard_map/ppermute | solution.py:274
  45.1 28.3 %collective-permute-start.5 = (bf16[256,1280]{1,0:T(8,128)(2,1)}, bf16[256,1280]{1,0:T(8,128)(2,1)}, u32[]{:S(2)}, u32[]{:S(2)}) collective-permute-start(bf16[256,1280]{1,0:T(8,128)(2,1)} %bitcast.6), channel_id=1, source_target_pairs={{0,1},{1,2},{2,3},{3,0},{4,5},{5,6},{6,7},{7,4},{8,9},{9,10},{10,1... | collective-permute-start | bytes 1966088 | tf_op jit(solution)/shard_map/ppermute | solution.py:274
  59.4 28.1 %collective-permute-start.1 = (bf16[256,1280]{1,0:T(8,128)(2,1)S(1)}, bf16[256,1280]{1,0:T(8,128)(2,1)}, u32[]{:S(2)}, u32[]{:S(2)}) collective-permute-start(bf16[256,1280]{1,0:T(8,128)(2,1)S(1)} %collective-permute-done.refs_2_), channel_id=1, source_target_pairs={{0,1},{1,2},{2,3},{3,0},{4,5},{5,6},{6,7},{7,4},{8,9},{9,10},{10,1... | collective-permute-start | bytes 1966088 | tf_op jit(solution)/shard_map/ppermute | solution.py:275
  59.4 28.1 %collective-permute-start.3 = (bf16[256,1280]{1,0:T(8,128)(2,1)S(1)}, bf16[256,1280]{1,0:T(8,128)(2,1)}, u32[]{:S(2)}, u32[]{:S(2)}) collective-permute-start(bf16[256,1280]{1,0:T(8,128)(2,1)S(1)} %collective-permute-done.2.refs_1_), channel_id=1, source_target_pairs={{0,3},{1,0},{2,1},{3,2},{4,7},{5,4},{6,5},{7,6},{8,11},{9,8},{10,9... | collective-permute-start | bytes 1966088 | tf_op jit(solution)/shard_map/ppermute | solution.py:275
  79.3 1.0 copy-start
  80.3 1.0 copy-start.1
  93.9 19.3 %collective-permute-start.14 = (bf16[256,1280]{1,0:T(8,128)(2,1)}, bf16[256,1280]{1,0:T(8,128)(2,1)S(1)}, u32[]{:S(2)}, u32[]{:S(2)}) collective-permute-start(bf16[256,1280]{1,0:T(8,128)(2,1)} %get-tuple-element.55), channel_id=1, source_target_pairs={{0,1},{1,2},{2,3},{3,0},{4,5},{5,6},{6,7},{7,4},{8,9},{9,10},{10,1... | collective-permute-start | bytes 1966088 | tf_op jit(solution)/shard_map/ppermute | solution.py:282
  96.6 55.0 %all-to-all-start.2 = ((bf16[32,16,2048]{2,1,0:T(8,128)(2,1)}), bf16[32,16,2048]{2,1,0:T(8,128)(2,1)}, u32[]{:S(2)}, u32[]{:S(2)}) async-start(bf16[32,16,2048]{2,1,0:T(8,128)(2,1)} %bitcast.14), calls=%async_computation.2 | async-start | bytes 4194304 | tf_op jit(solution)/shard_map/all_to_all | solution.py:290
  105.6 16.4 %collective-permute-start.18 = (bf16[256,1280]{1,0:T(8,128)(2,1)S(1)}, bf16[256,1280]{1,0:T(8,128)(2,1)S(1)}, u32[]{:S(2)}, u32[]{:S(2)}) collective-permute-start(bf16[256,1280]{1,0:T(8,128)(2,1)S(1)} %get-tuple-element.60), channel_id=1, source_target_pairs={{0,3},{1,0},{2,1},{3,2},{4,7},{5,4},{6,5},{7,6},{8,11},{9,8},{10,9... | collective-permute-start | bytes 1966088 | tf_op jit(solution)/shard_map/ppermute | solution.py:282
  108.2 27.8 %collective-permute-start.16 = (bf16[256,1280]{1,0:T(8,128)(2,1)S(1)}, bf16[256,1280]{1,0:T(8,128)(2,1)S(1)}, u32[]{:S(2)}, u32[]{:S(2)}) collective-permute-start(bf16[256,1280]{1,0:T(8,128)(2,1)S(1)} %get-tuple-element.56), channel_id=1, source_target_pairs={{0,3},{1,0},{2,1},{3,2},{4,7},{5,4},{6,5},{7,6},{8,11},{9,8},{10,9... | collective-permute-start | bytes 1966088 | tf_op jit(solution)/shard_map/ppermute | solution.py:283
  109.8 26.2 %collective-permute-start.17 = (bf16[256,1280]{1,0:T(8,128)(2,1)S(1)}, bf16[256,1280]{1,0:T(8,128)(2,1)S(1)}, u32[]{:S(2)}, u32[]{:S(2)}) collective-permute-start(bf16[256,1280]{1,0:T(8,128)(2,1)S(1)} %get-tuple-element.58), channel_id=1, source_target_pairs={{0,1},{1,2},{2,3},{3,0},{4,5},{5,6},{6,7},{7,4},{8,9},{9,10},{10,1... | collective-permute-start | bytes 1966088 | tf_op jit(solution)/shard_map/ppermute | solution.py:283
  113.3 12.6 %copy-start.3 = (bf16[256,8]{0,1:T(8,128)(2,1)S(1)}, bf16[256,8]{0,1:T(8,128)(2,1)}, u32[]{:S(2)}) copy-start(bf16[256,8]{0,1:T(8,128)(2,1)} %param.10) | copy-start | bytes 12292
  113.3 12.6 %copy-start.2 = (s32[256,8]{0,1:T(8,128)S(1)}, s32[256,8]{0,1:T(8,128)}, u32[]{:S(2)}) copy-start(s32[256,8]{0,1:T(8,128)} %param.9) | copy-start | bytes 24580
  113.4 27.1 %collective-permute-start.15 = (bf16[256,1280]{1,0:T(8,128)(2,1)S(1)}, bf16[256,1280]{1,0:T(8,128)(2,1)S(1)}, u32[]{:S(2)}, u32[]{:S(2)}) collective-permute-start(bf16[256,1280]{1,0:T(8,128)(2,1)S(1)} %add_convert_fusion.1), channel_id=1, source_target_pairs={{0,1},{1,2},{2,3},{3,0},{4,5},{5,6},{6,7},{7,4},{8,9},{9,10},{10,1... | collective-permute-start | bytes 1966088 | tf_op jit(solution)/shard_map/ppermute | solution.py:284
  122.1 27.9 %collective-permute-start.19 = (bf16[256,1280]{1,0:T(8,128)(2,1)S(1)}, bf16[256,1280]{1,0:T(8,128)(2,1)S(1)}, u32[]{:S(2)}, u32[]{:S(2)}) collective-permute-start(bf16[256,1280]{1,0:T(8,128)(2,1)S(1)} %add_convert_fusion), channel_id=1, source_target_pairs={{0,3},{1,0},{2,1},{3,2},{4,7},{5,4},{6,5},{7,6},{8,11},{9,8},{10,9... | collective-permute-start | bytes 1966088 | tf_op jit(solution)/shard_map/ppermute | solution.py:285
  151.6 27.4 %all-to-all-start.3 = ((bf16[32,16,1280]{2,1,0:T(8,128)(2,1)}), bf16[32,16,1280]{2,1,0:T(8,128)(2,1)S(1)}, u32[]{:S(2)}, u32[]{:S(2)}) async-start(bf16[32,16,1280]{2,1,0:T(8,128)(2,1)} %bitcast.16), calls=%async_computation.3 | async-start | bytes 2621440 | tf_op jit(solution)/shard_map/all_to_all | solution.py:290
  162.1 7.1 %collective-permute-start.10 = (bf16[128,512]{1,0:T(8,128)(2,1)S(1)}, bf16[128,512]{1,0:T(8,128)(2,1)S(1)}, u32[]{:S(2)}, u32[]{:S(2)}) collective-permute-start(bf16[128,512]{1,0:T(8,128)(2,1)S(1)} %get-tuple-element.65), channel_id=1, source_target_pairs={{0,1},{1,2},{2,3},{3,0},{4,5},{5,6},{6,7},{7,4},{8,9},{9,10},{10,1... | collective-permute-start | bytes 393224 | tf_op jit(solution)/shard_map/ppermute | solution.py:266
  164.0 5.3 %collective-permute-start.12 = (bf16[128,512]{1,0:T(8,128)(2,1)S(1)}, bf16[128,512]{1,0:T(8,128)(2,1)S(1)}, u32[]{:S(2)}, u32[]{:S(2)}) collective-permute-start(bf16[128,512]{1,0:T(8,128)(2,1)S(1)} %get-tuple-element.66), channel_id=1, source_target_pairs={{0,3},{1,0},{2,1},{3,2},{4,7},{5,4},{6,5},{7,6},{8,11},{9,8},{10,9... | collective-permute-start | bytes 393224 | tf_op jit(solution)/shard_map/ppermute | solution.py:266
  169.3 8.3 %collective-permute-start.11 = (bf16[256,512]{1,0:T(8,128)(2,1)S(1)}, bf16[256,512]{1,0:T(8,128)(2,1)S(1)}, u32[]{:S(2)}, u32[]{:S(2)}) collective-permute-start(bf16[256,512]{1,0:T(8,128)(2,1)S(1)} %get-tuple-element.63), channel_id=1, source_target_pairs={{0,1},{1,2},{2,3},{3,0},{4,5},{5,6},{6,7},{7,4},{8,9},{9,10},{10,1... | collective-permute-start | bytes 786440 | tf_op jit(solution)/shard_map/ppermute | solution.py:269
  170.1 7.5 %collective-permute-start.13 = (bf16[256,512]{1,0:T(8,128)(2,1)S(1)}, bf16[256,512]{1,0:T(8,128)(2,1)S(1)}, u32[]{:S(2)}, u32[]{:S(2)}) collective-permute-start(bf16[256,512]{1,0:T(8,128)(2,1)S(1)} %get-tuple-element.64), channel_id=1, source_target_pairs={{0,3},{1,0},{2,1},{3,2},{4,7},{5,4},{6,5},{7,6},{8,11},{9,8},{10,9... | collective-permute-start | bytes 786440 | tf_op jit(solution)/shard_map/ppermute | solution.py:269

commit v7 on v5

--- a/solution.py
+++ b/solution.py
@@ -25,7 +25,7 @@
         return copy
 
 
-def expert_call(where, weights, xs=(), segs=(), carry=(), inv=None, hidden=None, jobs=(), outs=(), stash=((), ()), held=(), stored=(), keep=None):
+def expert_call(where, weights, xs=(), segs=(), carry=(), inv=None, hidden=None, jobs=(), outs=(), stash=((), ()), held=(), stored=(), keep=None, leave=False):
     slices = lax.axis_size("tp")
     w_gate, w_up, w_down = weights
     d_all, ff = w_gate.shape
@@ -59,7 +59,8 @@
     if finish:
         scratch += [pltpu.VMEM((rows, ff), F32)] * 2
     scratch += [pltpu.VMEM((rows, ff), F32)] * len(stored)
-    n_copies = len(stored) + len(needed) + len(results) - n_out
+    scratch += [pltpu.VMEM(s, BF16) for s in outs] * leave
+    n_copies = len(jobs) * leave + len(stored) + len(needed) + len(results) - n_out
     scratch += [pltpu.SemaphoreType.DMA((max(n_copies, 1),))]
 
     def body(where_ref, *refs):
@@ -74,6 +75,7 @@
         bufs = held_refs + take(len(needed))
         accs = take(2) if finish else out_refs[:2]
         stored_bufs = take(len(stored))
+        staged = take(int(leave))
         copies = Copies(refs.pop(0))
         z = where_ref[0]
 
@@ -129,7 +131,11 @@
             w = bufs[2 * len(segs) + k]
             term = jnp.dot(hidden_ref[0][row : row + count, :], w[...], preferred_element_type=F32).astype(BF16)
             for index, top, n, col in targets:
-                out_refs[index][:, col : col + width] = term[top : top + n, :]
+                to = staged[0] if leave else out_refs[index]
+                to[:, col : col + width] = term[top : top + n, :]
+                if leave:
+                    at = pl.ds(col, width)
+                    stash_waits.append(copies.start(to.at[:, at], out_refs[index].at[:, at]))
         for w in stash_waits:
             w.wait()
 
@@ -138,8 +144,8 @@
     return pl.pallas_call(
         body,
         in_specs=[pl.BlockSpec(memory_space=pltpu.SMEM)] + [vmem] * len(resident) + [hbm] * len(streamed),
-        out_specs=[vmem] * len(results),
-        out_shape=[pltpu.VMEM(s, t) for s, t in results],
+        out_specs=[hbm if leave else vmem] * len(results),
+        out_shape=[jax.ShapeDtypeStruct(s, t) if leave else pltpu.VMEM(s, t) for s, t in results],
         scratch_shapes=scratch,
         cost_estimate=pl.CostEstimate(flops=flops, bytes_accessed=flops // 256, transcendentals=0),
         compiler_params=pltpu.CompilerParams(vmem_limit_bytes=20 * 2**20),
@@ -221,14 +227,58 @@
     )(*low, *high)
 
 
-def three_terms(value):
-    rest, terms = value, []
-    for _ in range(3):
-        term = lax.reduce_precision(rest, 8, 7)
-        terms.append(term)
-        rest = rest - term
-    stacked = jnp.stack(terms, axis=1)
-    return jnp.pad(stacked, ((0, 0), (0, SIDE - 3))).astype(BF16)
+def early_near(pick, pieces, n_slices):
+    rows = pick.shape[0]
+
+    def body(pick_ref, *refs):
+        xs, out, buf, sems = refs[: len(pieces)], refs[-3], refs[-2], refs[-1]
+        copies = Copies(sems)
+        waits = []
+        for k, (number, _) in enumerate(pieces):
+            buf[k] = jnp.dot(pick_ref[...], xs[k][:, :EARLY], preferred_element_type=F32).astype(BF16)
+            waits.append(copies.start(buf.at[k], out.at[:, pl.ds(number * EARLY, EARLY)]))
+        for w in waits:
+            w.wait()
+
+    return pl.pallas_call(
+        body,
+        out_specs=pl.BlockSpec(memory_space=pltpu.HBM),
+        out_shape=jax.ShapeDtypeStruct((rows, n_slices * EARLY + SIDE), BF16),
+        scratch_shapes=[pltpu.VMEM((len(pieces), rows, EARLY), BF16), pltpu.SemaphoreType.DMA((len(pieces),))],
+        compiler_params=pltpu.CompilerParams(vmem_limit_bytes=16 * 2**20),
+        name="early_near",
+    )(pick, *[x for _, x in pieces])
+
+
+def early_rest(pick, number, halves, others, partial, d_all):
+    rows, _ = pick.shape
+
+    def body(pick_ref, low, high, *refs):
+        xs, (_, out, buf, sems) = refs[: len(others)], refs[len(others) :]
+        copies = Copies(sems)
+        total = jnp.concatenate([r[:, EARLY:].astype(F32) for r in (low, high)], axis=0)
+        for x in xs:
+            total = total + x[:, EARLY:].astype(F32)
+        inverse = lax.rsqrt(jnp.sum(total, axis=1, keepdims=True) / d_all + epsilon)
+        x = jnp.concatenate([low[:, :EARLY], high[:, :EARLY]], axis=0)
+        buf[:, :EARLY] = jnp.dot(pick_ref[...], x, preferred_element_type=F32).astype(BF16)
+        first = copies.start(buf.at[:, pl.ds(0, EARLY)], out.at[:, pl.ds(number * EARLY, EARLY)])
+        buf[:, EARLY:] = jnp.dot(pick_ref[...], side_columns(inverse), preferred_element_type=F32).astype(BF16)
+        second = copies.start(buf.at[:, pl.ds(EARLY, SIDE)], out.at[:, pl.ds(partial.shape[1] - SIDE, SIDE)])
+        first.wait()
+        second.wait()
+
+    vmem, hbm = pl.BlockSpec(memory_space=pltpu.VMEM), pl.BlockSpec(memory_space=pltpu.HBM)
+    return pl.pallas_call(
+        body,
+        in_specs=[vmem] * (3 + len(others)) + [hbm],
+        out_specs=hbm,
+        out_shape=jax.ShapeDtypeStruct(partial.shape, BF16),
+        scratch_shapes=[pltpu.VMEM((rows, EARLY + SIDE), BF16), pltpu.SemaphoreType.DMA((2,))],
+        input_output_aliases={3 + len(others): 0},
+        compiler_params=pltpu.CompilerParams(vmem_limit_bytes=16 * 2**20),
+        name="early_rest",
+    )(pick, *halves, *others, partial)
 
 
 def local(tokens, norm_gain, expert_ids, gate_prob, w_gate, w_up, w_down):
@@ -282,17 +332,10 @@
     by_slot = jnp.broadcast_to(prob[:, None, :], (window, CAP, tok)).reshape(rows, tok)
     weight = jnp.where(pick > 0, by_slot, 0.0).astype(BF16)
 
-    def dispatch(x):
-        return jnp.dot(pick, x, preferred_element_type=F32).astype(BF16)
-
     e_below, e_above, e_far_a, e_far_b = spread(early)
     mine = exchange(picked_bulk)
-    e_far = jnp.concatenate([e_far_a, e_far_b], axis=0)
-    all_early = (early, e_above, e_far, e_below)
-    squares = sum(jnp.sum(e[:, EARLY : EARLY + 3].astype(F32), axis=1) for e in all_early)
-    inverse_rms = lax.rsqrt(squares / D + epsilon)
-    early_all = jnp.concatenate([e[:, :EARLY] for e in all_early] + [three_terms(inverse_rms)], axis=1)
-    picked = dispatch(early_all)
+    picked_near = early_near(pick, ((0, early), (1, e_above), (3, e_below)), n_tp)
+    picked = early_rest(pick, 2, (e_far_a, e_far_b), (early, e_above, e_below), picked_near, D)
     early_rows = exchange(picked)
     below, above, far = spread_halves(mine[:half], mine[half:])
 
@@ -310,17 +353,15 @@
         [((0, 1), 1, EARLY, bulk, 0), ((2, 3), 3, EARLY, bulk, 0)], sums,
     )
     early_jobs = [(k, 0, EARLY, 0, rows, ((0, 0, rows, k * EARLY),)) for k in range(n_tp)]
-    *early_sums, scale, far_gate, far_up = expert_call(
-        where, weights, [early_rows],
-        [((0,), k, 0, EARLY, k * EARLY) for k in range(n_tp)], keep=(0, n_tp * EARLY), stash=(far_segs, ()),
-    )
-    hidden, f_low, f_high, a_high, b_low, *early_down = expert_call(
-        where, weights, [*far, scale], far_segs, early_sums, inv=2, stored=sums,
-        jobs=far_jobs, outs=[(half, bulk)] * 4, held=(far_gate, far_up), stash=((), early_jobs),
-    )
-    (p_early,) = expert_call(
-        where, weights, hidden=hidden, jobs=early_jobs, outs=[(rows, n_tp * EARLY)], held=early_down,
-    )
+    gate_sum, up_sum, scale, *far_held = expert_call(
+        where, weights, [early_rows], [((0,), k, 0, EARLY, k * EARLY) for k in range(n_tp)],
+        stored=sums, keep=(0, n_tp * EARLY), stash=(far_segs, far_jobs),
+    )
+    hidden, f_low, f_high, a_high, b_low = expert_call(
+        where, weights, [*far, scale], far_segs, (gate_sum, up_sum), inv=2,
+        jobs=far_jobs, outs=[(half, bulk)] * 4, held=far_held,
+    )
+    (p_early,) = expert_call(where, weights, hidden=hidden, jobs=early_jobs, outs=[(rows, n_tp * EARLY)], leave=True)
     a_low, b_high, o_low, o_high = expert_call(
         where, weights, hidden=hidden,
         jobs=[

time: 182 us -> 182 us (level)
  starting transfers between devices: 58.9 us -> 63.4 us
  local copies, waits for them, and re-layouts: 5.35 us -> 3.15 us
  matrix products: 5.02 us -> 2.84 us
    all_to_all x4, waiting for transfers between devices: 11.1 us -> 1.26 us  [exchange(): lax.all_to_all(shaped, 'ep', 0, 0, tiled=True).reshape(rows, x.shape[1])]
    ppermute x2, waiting for transfers between devices: 0.01 us -> 6.83 us  [spread(): below, above = (lax.ppermute(x, 'tp', up), lax.ppermute(x, 'tp', dn))]
    all_to_all x4, starting transfers between devices: 30 us -> 34.2 us  [exchange(): lax.all_to_all(shaped, 'ep', 0, 0, tiled=True).reshape(rows, x.shape[1])]
    pallas_call x0 -> x2, Pallas kernels: none -> 2.87 us  [the longest x1 1.54 us: early_near(): pl.pallas_call(body, out_specs=pl.BlockSpec(memory_space=pltpu.HBM), out_...]
    ppermute x1, waiting for transfers between devices: 0.87 us -> 3.5 us  [spread(): lax.ppermute(below[:half], 'tp', up)]
    dot_general x1 -> x0, matrix products: 2.18 us -> none  [dispatch(): return jnp.dot(pick, x, preferred_element_type=F32).astype(BF16)]
  transfers between devices with their start and end apart: 24 -> 24, of which waited for: 13 -> 14; matrix products, arithmetic and copies ran while one was open for 6% -> 3% of each run, Pallas kernels for 12% -> 14%
where the time goes in v7:
time: 182 us; the launch traced here: 181 us
  waiting for transfers between devices  75.3 us (41%)
  starting transfers between devices  63.4 us (35%)
  Pallas kernels  33 us (18%)
  local copies, waits for them, and re-layouts  3.15 us (2%)
  matrix products  2.84 us (2%)
  other arithmetic  2.7 us (1%)
    all_to_all x4, starting transfers between devices, exchange(): lax.all_to_all(shaped, 'ep', 0, 0, tiled=True).reshape(rows, x.shape[1])  34.2 us
    pallas_call x6, Pallas kernels, expert_call(): pl.pallas_call(body, in_specs=[pl.BlockSpec(memory_space=pltpu.SMEM)] + [...  25.6 us
    ppermute x1, waiting for transfers between devices, spread_halves(): lax.ppermute(low, 'tp', up)  13.4 us
    ppermute x1, waiting for transfers between devices, fold_halves(): lax.ppermute(below[0], 'tp', dn)  9.95 us
    ppermute x1, waiting for transfers between devices, fold_halves(): up_high = lax.ppermute(add(below[1], got_high), 'tp', dn)  9.47 us
    ppermute x1, waiting for transfers between devices, fold_halves(): lax.ppermute(far[1], 'tp', dn)  7.33 us
    ppermute x1, waiting for transfers between devices, spread_halves(): lax.ppermute(low, 'tp', dn)  7.32 us
    ppermute x2, waiting for transfers between devices, spread(): below, above = (lax.ppermute(x, 'tp', up), lax.ppermute(x, 'tp', dn))  6.83 us
  transfers between devices with their start and end apart: 24, of which 14 were waited for; matrix products, arithmetic and copies ran while one was open for 3% of the time, Pallas kernels for 14%

profile of v7, /device:TPU:1, one launch (start us, length us, event | category | flops | bytes accessed | tf_op | source)
XLA Modules:
  0.0 180.6 jit_solution(134063790577166125)
XLA Ops:
  0.0 2.9 %head.1 = (bf16[512,256]{1,0:T(8,128)(2,1)S(1)}, bf16[512,1280]{1,0:T(8,128)(2,1)}, bf16[256,640]{1,0:T(8,128)(2,1)S(1)}) custom-call(s32[8,256]{1,0:T(8,128)} %bitcast.43, bf16[1792]{0:T(1024)(128)(2,1)} %gain_hbm.1, bf16[256,1792]{1,0:T(8,128)(2,1)} %tokens_hbm.1), custom_call_target="tpu_custom_call" | custom-call | flops 335544320 | bytes 917504 | tf_op jit(solution)/shard_map/head/pallas_call | solution.py:201
  2.9 8.6 %all-to-all-start = ((bf16[32,16,1280]{2,1,0:T(8,128)(2,1)}), bf16[32,16,1280]{2,1,0:T(8,128)(2,1)S(1)}, u32[]{:S(2)}, u32[]{:S(2)}) async-start(bf16[32,16,1280]{2,1,0:T(8,128)(2,1)} %bitcast.4), calls=%async_computation | async-start | bytes 2621440 | tf_op jit(solution)/shard_map/all_to_all | solution.py:324
  11.5 3.8 %collective-permute-start.6 = (bf16[256,640]{1,0:T(8,128)(2,1)S(1)}, bf16[256,640]{1,0:T(8,128)(2,1)S(1)}, u32[]{:S(2)}, u32[]{:S(2)}) collective-permute-start(bf16[256,640]{1,0:T(8,128)(2,1)S(1)} %get-tuple-element.31.refs_0_), channel_id=1, source_target_pairs={{0,3},{1,0},{2,1},{3,2},{4,7},{5,4},{6,5},{7,6},{8,11},{9,8},{10,9... | collective-permute-start | bytes 983048 | tf_op jit(solution)/shard_map/ppermute | solution.py:295
  15.4 6.8 %collective-permute-done.6.refs_1_ = bf16[256,640]{1,0:T(8,128)(2,1)S(1)} collective-permute-done((bf16[256,640]{1,0:T(8,128)(2,1)S(1)}, bf16[256,640]{1,0:T(8,128)(2,1)S(1)}, u32[]{:S(2)}, u32[]{:S(2)}) %collective-permute-start.6) | collective-permute-done | bytes 327712 | tf_op jit(solution)/shard_map/ppermute | solution.py:295
  22.2 3.5 %collective-permute-start.7 = (bf16[128,640]{1,0:T(8,128)(2,1)S(1)}, bf16[128,640]{1,0:T(8,128)(2,1)S(1)}, u32[]{:S(2)}, u32[]{:S(2)}) collective-permute-start(bf16[128,640]{1,0:T(8,128)(2,1)S(1)} %slice.50), channel_id=1, source_target_pairs={{0,3},{1,0},{2,1},{3,2},{4,7},{5,4},{6,5},{7,6},{8,11},{9,8},{10,9... | collective-permute-start | bytes 491528 | tf_op jit(solution)/shard_map/ppermute | solution.py:296
  25.8 1.5 early_near.1.refs_3_
  27.3 0.6 collective-permute-done.7.high
  28.0 3.5 %collective-permute-done.5.low = bf16[128,640]{1,0:T(8,128)(2,1)S(1)} collective-permute-done((bf16[128,640]{1,0:T(8,128)(2,1)S(1)}, bf16[128,640]{1,0:T(8,128)(2,1)S(1)}, u32[]{:S(2)}, u32[]{:S(2)}) %collective-permute-start.5) | collective-permute-done | bytes 163872 | tf_op jit(solution)/shard_map/ppermute | solution.py:296
  31.5 1.3 early_rest.1
  32.8 9.2 %all-to-all-start.1 = ((bf16[32,16,2176]{2,1,0:T(8,128)(2,1)}), bf16[32,16,2176]{2,1,0:T(8,128)(2,1)S(1)}, u32[]{:S(2)}, u32[]{:S(2)}) async-start(bf16[32,16,2176]{2,1,0:T(8,128)(2,1)} %bitcast.7), calls=%async_computation.1 | async-start | bytes 4456448 | tf_op jit(solution)/shard_map/all_to_all | solution.py:324
  42.0 1.1 fusion.1
  43.2 2.7 %collective-permute-start.2 = (bf16[256,1280]{1,0:T(8,128)(2,1)}, bf16[256,1280]{1,0:T(8,128)(2,1)}, u32[]{:S(2)}, u32[]{:S(2)}) collective-permute-start(bf16[256,1280]{1,0:T(8,128)(2,1)} %bitcast.6), channel_id=1, source_target_pairs={{0,3},{1,0},{2,1},{3,2},{4,7},{5,4},{6,5},{7,6},{8,11},{9,8},{10,9... | collective-permute-start | bytes 1966088 | tf_op jit(solution)/shard_map/ppermute | solution.py:307
  45.9 1.4 collective-permute-start.9
  47.3 13.4 %collective-permute-done.refs_2_ = bf16[256,1280]{1,0:T(8,128)(2,1)} collective-permute-done((bf16[256,1280]{1,0:T(8,128)(2,1)}, bf16[256,1280]{1,0:T(8,128)(2,1)}, u32[]{:S(2)}, u32[]{:S(2)}) %collective-permute-start) | collective-permute-done | bytes 655392 | tf_op jit(solution)/shard_map/ppermute | solution.py:307
  60.8 2.7 %collective-permute-start.3 = (bf16[256,1280]{1,0:T(8,128)(2,1)}, bf16[256,1280]{1,0:T(8,128)(2,1)}, u32[]{:S(2)}, u32[]{:S(2)}) collective-permute-start(bf16[256,1280]{1,0:T(8,128)(2,1)} %collective-permute-done.2.refs_1_), channel_id=1, source_target_pairs={{0,3},{1,0},{2,1},{3,2},{4,7},{5,4},{6,5},{7,6},{8,11},{9,8},{10,9... | collective-permute-start | bytes 1966088 | tf_op jit(solution)/shard_map/ppermute | solution.py:309
  63.5 3.0 %shard_map.73 = (f32[512,512]{1,0:T(8,128)S(1)}, f32[512,512]{1,0:T(8,128)S(1)}) custom-call(s32[1]{0:T(128)} %bitcast.3.where_ref, bf16[512,1280]{1,0:T(8,128)(2,1)S(1)} %bitcast.25, bf16[7168,512]{1,0:T(8,128)(2,1)} %bitcast.27, bf16[7168,512]{1,0:T(8,128)(2,1)} %bitcast.32, bf16[512,7168]{1,0:T(8,128)(2,1)} %bitcast.37), custom_call_target="tpu_custom_call" | custom-call | flops 1342177280 | bytes 5242880 | tf_op jit(solution)/shard_map/pallas_call | solution.py:144
  66.5 7.3 %collective-permute-done.8.refs_0_ = bf16[256,1280]{1,0:T(8,128)(2,1)} collective-permute-done((bf16[256,1280]{1,0:T(8,128)(2,1)}, bf16[256,1280]{1,0:T(8,128)(2,1)}, u32[]{:S(2)}, u32[]{:S(2)}) %collective-permute-start.8) | collective-permute-done | bytes 655392 | tf_op jit(solution)/shard_map/ppermute | solution.py:308
  73.8 1.0 collective-permute-done.9.refs_3_
  74.8 6.4 %shard_map.74 = (f32[512,512]{1,0:T(8,128)S(1)}, f32[512,512]{1,0:T(8,128)S(1)}) custom-call(s32[1]{0:T(128)} %bitcast.3.where_ref, bf16[256,1280]{1,0:T(8,128)(2,1)} %collective-permute-done.8.refs_0_, bf16[256,1280]{1,0:T(8,128)(2,1)} %collective-permute-done.2.refs_1_, bf16[256,1280]{1,0:T(8,128)(2,1)} %collective-permute-done.refs_2_, ...), custom_call_target="tpu_custom_call" | custom-call | flops 2684354560 | bytes 10485760 | tf_op jit(solution)/shard_map/pallas_call | solution.py:144
  81.2 1.0 copy-done.2
  82.2 1.0 copy-done.3
  83.2 4.9 %shard_map.75 = (f32[512,512]{1,0:T(8,128)S(1)}, f32[512,512]{1,0:T(8,128)S(1)}, bf16[512,128]{1,0:T(8,128)(2,1)S(1)}, bf16[1280,512]{1,0:T(8,128)(2,1)S(1)}, bf...) custom-call(s32[1]{0:T(128)} %bitcast.3.where_ref, ...), custom_call_target="tpu_custom_call" | custom-call | flops 2147483648 | bytes 8388608 | tf_op jit(solution)/shard_map/pallas_call | solution.py:144
  88.0 0.8 collective-permute-done.1.refs_0_
  88.9 4.3 %shard_map.76 = (bf16[512,512]{1,0:T(8,128)(2,1)S(1)}, bf16[256,1280]{1,0:T(8,128)(2,1)S(1)}, bf16[256,1280]{1,0:T(8,128)(2,1)S(1)}, bf16[256,1280]{1,0:T(8,128)(2,1)S(1)}, bf16[256,1280]{1,0:T(8,128)(2,1)S(1)}) custom-call(s32[1]{0:T(128)} %bitcast.3.where_ref, bf16[256,1280]{1,0:T(8,128)(2,1)} %collective-permute-done.1.refs_0_, ...), custom_call_target="tpu_custom_call" | custom-call | flops 2684354560 | bytes 10485760 | tf_op jit(solution)/shard_map/pallas_call | solution.py:144
  93.3 3.7 %shard_map.77 = bf16[512,2048]{1,0:T(8,128)(2,1)} custom-call(s32[1]{0:T(128)} %bitcast.3.where_ref, bf16[512,512]{1,0:T(8,128)(2,1)S(1)} %get-tuple-element.44.refs_0_, bf16[7168,512]{1,0:T(8,128)(2,1)} %bitcast.30, bf16[7168,512]{1,0:T(8,128)(2,1)} %bitcast.35, bf16[512,7168]{1,0:T(8,128)(2,1)} %bitcast.40), custom_call_target="tpu_custom_call" | custom-call | flops 1073741824 | bytes 4194304 | tf_op jit(solution)/shard_map/pallas_call | solution.py:144
  97.0 8.2 %all-to-all-start.2 = ((bf16[32,16,2048]{2,1,0:T(8,128)(2,1)}), bf16[32,16,2048]{2,1,0:T(8,128)(2,1)}, u32[]{:S(2)}, u32[]{:S(2)}) async-start(bf16[32,16,2048]{2,1,0:T(8,128)(2,1)} %bitcast.13), calls=%async_computation.2 | async-start | bytes 4194304 | tf_op jit(solution)/shard_map/all_to_all | solution.py:324
  105.2 3.0 %collective-permute-start.18 = (bf16[256,1280]{1,0:T(8,128)(2,1)S(1)}, bf16[256,1280]{1,0:T(8,128)(2,1)S(1)}, u32[]{:S(2)}, u32[]{:S(2)}) collective-permute-start(bf16[256,1280]{1,0:T(8,128)(2,1)S(1)} %get-tuple-element.52), channel_id=1, source_target_pairs={{0,3},{1,0},{2,1},{3,2},{4,7},{5,4},{6,5},{7,6},{8,11},{9,8},{10,9... | collective-permute-start | bytes 1966088 | tf_op jit(solution)/shard_map/ppermute | solution.py:316
  108.2 1.7 collective-permute-start.16
  109.9 3.3 %shard_map.78 = (bf16[256,1280]{1,0:T(8,128)(2,1)S(1)}, bf16[256,1280]{1,0:T(8,128)(2,1)S(1)}, bf16[256,1280]{1,0:T(8,128)(2,1)S(1)}, bf16[256,1280]{1,0:T(8,128)(2,1)S(1)}) custom-call(s32[1]{0:T(128)} %bitcast.3.where_ref, bf16[512,512]{1,0:T(8,128)(2,1)S(1)} %get-tuple-element.44.refs_0_, bf16[7168,512]{1,0:T(8,128)(2,1)} %bitcast.31, ...), custom_call_target="tpu_custom_call" | custom-call | flops 1342177280 | bytes 5242880 | tf_op jit(solution)/shard_map/pallas_call | solution.py:144
  113.3 1.2 add_convert_fusion.1
  114.7 7.3 %collective-permute-done.18 = bf16[256,1280]{1,0:T(8,128)(2,1)S(1)} collective-permute-done((bf16[256,1280]{1,0:T(8,128)(2,1)S(1)}, bf16[256,1280]{1,0:T(8,128)(2,1)S(1)}, u32[]{:S(2)}, u32[]{:S(2)}) %collective-permute-start.18) | collective-permute-done | bytes 655392 | tf_op jit(solution)/shard_map/ppermute | solution.py:316
  122.0 0.2 add_convert_fusion
  122.2 3.8 %collective-permute-start.19 = (bf16[256,1280]{1,0:T(8,128)(2,1)S(1)}, bf16[256,1280]{1,0:T(8,128)(2,1)S(1)}, u32[]{:S(2)}, u32[]{:S(2)}) collective-permute-start(bf16[256,1280]{1,0:T(8,128)(2,1)S(1)} %add_convert_fusion), channel_id=1, source_target_pairs={{0,3},{1,0},{2,1},{3,2},{4,7},{5,4},{6,5},{7,6},{8,11},{9,8},{10,9... | collective-permute-start | bytes 1966088 | tf_op jit(solution)/shard_map/ppermute | solution.py:319
  126.1 9.9 %collective-permute-done.16.refs_2_ = bf16[256,1280]{1,0:T(8,128)(2,1)S(1)} collective-permute-done((bf16[256,1280]{1,0:T(8,128)(2,1)S(1)}, bf16[256,1280]{1,0:T(8,128)(2,1)S(1)}, u32[]{:S(2)}, u32[]{:S(2)}) %collective-permute-start.16) | collective-permute-done | bytes 655392 | tf_op jit(solution)/shard_map/ppermute | solution.py:317
  136.0 4.6 %collective-permute-done.15.refs_1_ = bf16[256,1280]{1,0:T(8,128)(2,1)S(1)} collective-permute-done((bf16[256,1280]{1,0:T(8,128)(2,1)S(1)}, bf16[256,1280]{1,0:T(8,128)(2,1)S(1)}, u32[]{:S(2)}, u32[]{:S(2)}) %collective-permute-start.15) | collective-permute-done | bytes 655392 | tf_op jit(solution)/shard_map/ppermute | solution.py:318
  140.6 9.5 %collective-permute-done.19.refs_5_ = bf16[256,1280]{1,0:T(8,128)(2,1)S(1)} collective-permute-done((bf16[256,1280]{1,0:T(8,128)(2,1)S(1)}, bf16[256,1280]{1,0:T(8,128)(2,1)S(1)}, u32[]{:S(2)}, u32[]{:S(2)}) %collective-permute-start.19) | collective-permute-done | bytes 655392 | tf_op jit(solution)/shard_map/ppermute | solution.py:319
  150.1 1.6 join_sums.1
  151.7 8.2 %all-to-all-start.3 = ((bf16[32,16,1280]{2,1,0:T(8,128)(2,1)}), bf16[32,16,1280]{2,1,0:T(8,128)(2,1)S(1)}, u32[]{:S(2)}, u32[]{:S(2)}) async-start(bf16[32,16,1280]{2,1,0:T(8,128)(2,1)} %bitcast.15), calls=%async_computation.3 | async-start | bytes 2621440 | tf_op jit(solution)/shard_map/all_to_all | solution.py:324
  159.8 2.3 %convolution_convert_fusion = bf16[256,2048]{1,0:T(8,128)(2,1)S(1)} fusion(bf16[512,256]{1,0:T(8,128)(2,1)S(1)} %fusion, bf16[512,2048]{1,0:T(8,128)(2,1)} %bitcast.14), kind=kOutput, calls=%fused_computation | convolution fusion | flops 537395200 | bytes 3407872 | tf_op jit(solution)/shard_map/dot_general | solution.py:376
  162.2 1.9 %collective-permute-start.10 = (bf16[128,512]{1,0:T(8,128)(2,1)S(1)}, bf16[128,512]{1,0:T(8,128)(2,1)S(1)}, u32[]{:S(2)}, u32[]{:S(2)}) collective-permute-start(bf16[128,512]{1,0:T(8,128)(2,1)S(1)} %get-tuple-element.57), channel_id=1, source_target_pairs={{0,1},{1,2},{2,3},{3,0},{4,5},{5,6},{6,7},{7,4},{8,9},{9,10},{10,1... | collective-permute-start | bytes 393224 | tf_op jit(solution)/shard_map/ppermute | solution.py:300
  164.1 1.6 collective-permute-start.12
  165.7 3.6 %collective-permute-done.10 = bf16[128,512]{1,0:T(8,128)(2,1)S(1)} collective-permute-done((bf16[128,512]{1,0:T(8,128)(2,1)S(1)}, bf16[128,512]{1,0:T(8,128)(2,1)S(1)}, u32[]{:S(2)}, u32[]{:S(2)}) %collective-permute-start.10) | collective-permute-done | bytes 131104 | tf_op jit(solution)/shard_map/ppermute | solution.py:300
  169.4 0.9 collective-permute-start.11
  170.3 1.9 %collective-permute-start.13 = (bf16[256,512]{1,0:T(8,128)(2,1)S(1)}, bf16[256,512]{1,0:T(8,128)(2,1)S(1)}, u32[]{:S(2)}, u32[]{:S(2)}) collective-permute-start(bf16[256,512]{1,0:T(8,128)(2,1)S(1)} %get-tuple-element.56), channel_id=1, source_target_pairs={{0,3},{1,0},{2,1},{3,2},{4,7},{5,4},{6,5},{7,6},{8,11},{9,8},{10,9... | collective-permute-start | bytes 786440 | tf_op jit(solution)/shard_map/ppermute | solution.py:303
  172.2 5.6 %collective-permute-done.11 = bf16[256,512]{1,0:T(8,128)(2,1)S(1)} collective-permute-done((bf16[256,512]{1,0:T(8,128)(2,1)S(1)}, bf16[256,512]{1,0:T(8,128)(2,1)S(1)}, u32[]{:S(2)}, u32[]{:S(2)}) %collective-permute-start.11) | collective-permute-done | bytes 262176 | tf_op jit(solution)/shard_map/ppermute | solution.py:303
  177.9 1.2 all-to-all-done.3
  179.1 0.5 convolution_convert_fusion.1
  179.6 1.0 pad_maximum_fusion
  (36 shorter events, 0.7 us)
Async XLA Ops:
  2.9 28.5 %copy-start = (bf16[512,256]{1,0:T(8,128)(2,1)}, bf16[512,256]{1,0:T(8,128)(2,1)S(1)}, u32[]{:S(2)}) copy-start(bf16[512,256]{1,0:T(8,128)(2,1)S(1)} %get-tuple-element.29.pick_ref) | copy-start | bytes 786436
  2.9 29.9 %all-to-all-start = ((bf16[32,16,1280]{2,1,0:T(8,128)(2,1)}), bf16[32,16,1280]{2,1,0:T(8,128)(2,1)S(1)}, u32[]{:S(2)}, u32[]{:S(2)}) async-start(bf16[32,16,1280]{2,1,0:T(8,128)(2,1)} %bitcast.4), calls=%async_computation | async-start | bytes 2621440 | tf_op jit(solution)/shard_map/all_to_all | solution.py:324
  11.5 10.7 %collective-permute-start.6 = (bf16[256,640]{1,0:T(8,128)(2,1)S(1)}, bf16[256,640]{1,0:T(8,128)(2,1)S(1)}, u32[]{:S(2)}, u32[]{:S(2)}) collective-permute-start(bf16[256,640]{1,0:T(8,128)(2,1)S(1)} %get-tuple-element.31.refs_0_), channel_id=1, source_target_pairs={{0,3},{1,0},{2,1},{3,2},{4,7},{5,4},{6,5},{7,6},{8,11},{9,8},{10,9... | collective-permute-start | bytes 983048 | tf_op jit(solution)/shard_map/ppermute | solution.py:295
  15.4 10.3 %collective-permute-start.4 = (bf16[256,640]{1,0:T(8,128)(2,1)S(1)}, bf16[256,640]{1,0:T(8,128)(2,1)S(1)}, u32[]{:S(2)}, u32[]{:S(2)}) collective-permute-start(bf16[256,640]{1,0:T(8,128)(2,1)S(1)} %get-tuple-element.31.refs_0_), channel_id=1, source_target_pairs={{0,1},{1,2},{2,3},{3,0},{4,5},{5,6},{6,7},{7,4},{8,9},{9,10},{10,1... | collective-permute-start | bytes 983048 | tf_op jit(solution)/shard_map/ppermute | solution.py:295
  22.2 5.7 %collective-permute-start.7 = (bf16[128,640]{1,0:T(8,128)(2,1)S(1)}, bf16[128,640]{1,0:T(8,128)(2,1)S(1)}, u32[]{:S(2)}, u32[]{:S(2)}) collective-permute-start(bf16[128,640]{1,0:T(8,128)(2,1)S(1)} %slice.50), channel_id=1, source_target_pairs={{0,3},{1,0},{2,1},{3,2},{4,7},{5,4},{6,5},{7,6},{8,11},{9,8},{10,9... | collective-permute-start | bytes 491528 | tf_op jit(solution)/shard_map/ppermute | solution.py:296
  25.7 5.7 %collective-permute-start.5 = (bf16[128,640]{1,0:T(8,128)(2,1)S(1)}, bf16[128,640]{1,0:T(8,128)(2,1)S(1)}, u32[]{:S(2)}, u32[]{:S(2)}) collective-permute-start(bf16[128,640]{1,0:T(8,128)(2,1)S(1)} %slice.49), channel_id=1, source_target_pairs={{0,1},{1,2},{2,3},{3,0},{4,5},{5,6},{6,7},{7,4},{8,9},{9,10},{10,1... | collective-permute-start | bytes 491528 | tf_op jit(solution)/shard_map/ppermute | solution.py:296
  32.8 50.4 %all-to-all-start.1 = ((bf16[32,16,2176]{2,1,0:T(8,128)(2,1)}), bf16[32,16,2176]{2,1,0:T(8,128)(2,1)S(1)}, u32[]{:S(2)}, u32[]{:S(2)}) async-start(bf16[32,16,2176]{2,1,0:T(8,128)(2,1)} %bitcast.7), calls=%async_computation.1 | async-start | bytes 4456448 | tf_op jit(solution)/shard_map/all_to_all | solution.py:324
  43.2 17.6 %collective-permute-start = (bf16[256,1280]{1,0:T(8,128)(2,1)}, bf16[256,1280]{1,0:T(8,128)(2,1)}, u32[]{:S(2)}, u32[]{:S(2)}) collective-permute-start(bf16[256,1280]{1,0:T(8,128)(2,1)} %bitcast.5), channel_id=1, source_target_pairs={{0,1},{1,2},{2,3},{3,0},{4,5},{5,6},{6,7},{7,4},{8,9},{9,10},{10,1... | collective-permute-start | bytes 1966088 | tf_op jit(solution)/shard_map/ppermute | solution.py:307
  43.2 17.6 %collective-permute-start.2 = (bf16[256,1280]{1,0:T(8,128)(2,1)}, bf16[256,1280]{1,0:T(8,128)(2,1)}, u32[]{:S(2)}, u32[]{:S(2)}) collective-permute-start(bf16[256,1280]{1,0:T(8,128)(2,1)} %bitcast.6), channel_id=1, source_target_pairs={{0,3},{1,0},{2,1},{3,2},{4,7},{5,4},{6,5},{7,6},{8,11},{9,8},{10,9... | collective-permute-start | bytes 1966088 | tf_op jit(solution)/shard_map/ppermute | solution.py:307
  45.9 27.9 %collective-permute-start.8 = (bf16[256,1280]{1,0:T(8,128)(2,1)}, bf16[256,1280]{1,0:T(8,128)(2,1)}, u32[]{:S(2)}, u32[]{:S(2)}) collective-permute-start(bf16[256,1280]{1,0:T(8,128)(2,1)} %bitcast.5), channel_id=1, source_target_pairs={{0,3},{1,0},{2,1},{3,2},{4,7},{5,4},{6,5},{7,6},{8,11},{9,8},{10,9... | collective-permute-start | bytes 1966088 | tf_op jit(solution)/shard_map/ppermute | solution.py:308
  45.9 28.9 %collective-permute-start.9 = (bf16[256,1280]{1,0:T(8,128)(2,1)}, bf16[256,1280]{1,0:T(8,128)(2,1)}, u32[]{:S(2)}, u32[]{:S(2)}) collective-permute-start(bf16[256,1280]{1,0:T(8,128)(2,1)} %bitcast.6), channel_id=1, source_target_pairs={{0,1},{1,2},{2,3},{3,0},{4,5},{5,6},{6,7},{7,4},{8,9},{9,10},{10,1... | collective-permute-start | bytes 1966088 | tf_op jit(solution)/shard_map/ppermute | solution.py:308
  60.8 28.1 %collective-permute-start.1 = (bf16[256,1280]{1,0:T(8,128)(2,1)}, bf16[256,1280]{1,0:T(8,128)(2,1)}, u32[]{:S(2)}, u32[]{:S(2)}) collective-permute-start(bf16[256,1280]{1,0:T(8,128)(2,1)} %collective-permute-done.refs_2_), channel_id=1, source_target_pairs={{0,1},{1,2},{2,3},{3,0},{4,5},{5,6},{6,7},{7,4},{8,9},{9,10},{10,1... | collective-permute-start | bytes 1966088 | tf_op jit(solution)/shard_map/ppermute | solution.py:309
  60.8 28.1 %collective-permute-start.3 = (bf16[256,1280]{1,0:T(8,128)(2,1)}, bf16[256,1280]{1,0:T(8,128)(2,1)}, u32[]{:S(2)}, u32[]{:S(2)}) collective-permute-start(bf16[256,1280]{1,0:T(8,128)(2,1)} %collective-permute-done.2.refs_1_), channel_id=1, source_target_pairs={{0,3},{1,0},{2,1},{3,2},{4,7},{5,4},{6,5},{7,6},{8,11},{9,8},{10,9... | collective-permute-start | bytes 1966088 | tf_op jit(solution)/shard_map/ppermute | solution.py:309
  81.2 1.0 copy-start.2
  82.2 1.0 copy-start.3
  93.2 20.1 %collective-permute-start.14 = (bf16[256,1280]{1,0:T(8,128)(2,1)S(1)}, bf16[256,1280]{1,0:T(8,128)(2,1)}, u32[]{:S(2)}, u32[]{:S(2)}) collective-permute-start(bf16[256,1280]{1,0:T(8,128)(2,1)S(1)} %get-tuple-element.47), channel_id=1, source_target_pairs={{0,1},{1,2},{2,3},{3,0},{4,5},{5,6},{6,7},{7,4},{8,9},{9,10},{10,1... | collective-permute-start | bytes 1966088 | tf_op jit(solution)/shard_map/ppermute | solution.py:316
  97.0 54.7 %all-to-all-start.2 = ((bf16[32,16,2048]{2,1,0:T(8,128)(2,1)}), bf16[32,16,2048]{2,1,0:T(8,128)(2,1)}, u32[]{:S(2)}, u32[]{:S(2)}) async-start(bf16[32,16,2048]{2,1,0:T(8,128)(2,1)} %bitcast.13), calls=%async_computation.2 | async-start | bytes 4194304 | tf_op jit(solution)/shard_map/all_to_all | solution.py:324
  105.2 16.8 %collective-permute-start.18 = (bf16[256,1280]{1,0:T(8,128)(2,1)S(1)}, bf16[256,1280]{1,0:T(8,128)(2,1)S(1)}, u32[]{:S(2)}, u32[]{:S(2)}) collective-permute-start(bf16[256,1280]{1,0:T(8,128)(2,1)S(1)} %get-tuple-element.52), channel_id=1, source_target_pairs={{0,3},{1,0},{2,1},{3,2},{4,7},{5,4},{6,5},{7,6},{8,11},{9,8},{10,9... | collective-permute-start | bytes 1966088 | tf_op jit(solution)/shard_map/ppermute | solution.py:316
  108.2 27.8 %collective-permute-start.16 = (bf16[256,1280]{1,0:T(8,128)(2,1)S(1)}, bf16[256,1280]{1,0:T(8,128)(2,1)S(1)}, u32[]{:S(2)}, u32[]{:S(2)}) collective-permute-start(bf16[256,1280]{1,0:T(8,128)(2,1)S(1)} %get-tuple-element.48), channel_id=1, source_target_pairs={{0,3},{1,0},{2,1},{3,2},{4,7},{5,4},{6,5},{7,6},{8,11},{9,8},{10,9... | collective-permute-start | bytes 1966088 | tf_op jit(solution)/shard_map/ppermute | solution.py:317
  109.9 26.1 %collective-permute-start.17 = (bf16[256,1280]{1,0:T(8,128)(2,1)S(1)}, bf16[256,1280]{1,0:T(8,128)(2,1)S(1)}, u32[]{:S(2)}, u32[]{:S(2)}) collective-permute-start(bf16[256,1280]{1,0:T(8,128)(2,1)S(1)} %get-tuple-element.50), channel_id=1, source_target_pairs={{0,1},{1,2},{2,3},{3,0},{4,5},{5,6},{6,7},{7,4},{8,9},{9,10},{10,1... | collective-permute-start | bytes 1966088 | tf_op jit(solution)/shard_map/ppermute | solution.py:317
  114.5 11.4 %copy-start.5 = (bf16[256,8]{0,1:T(8,128)(2,1)S(1)}, bf16[256,8]{0,1:T(8,128)(2,1)}, u32[]{:S(2)}) copy-start(bf16[256,8]{0,1:T(8,128)(2,1)} %param.10) | copy-start | bytes 12292
  114.6 11.4 %copy-start.4 = (s32[256,8]{0,1:T(8,128)S(1)}, s32[256,8]{0,1:T(8,128)}, u32[]{:S(2)}) copy-start(s32[256,8]{0,1:T(8,128)} %param.9) | copy-start | bytes 24580
  114.6 11.4 %copy-start.1 = (bf16[512,256]{1,0:T(8,128)(2,1)S(1)}, bf16[512,256]{1,0:T(8,128)(2,1)}, u32[]{:S(2)}) copy-start(bf16[512,256]{1,0:T(8,128)(2,1)} %copy-done) | copy-start | bytes 786436
  114.6 26.0 %collective-permute-start.15 = (bf16[256,1280]{1,0:T(8,128)(2,1)S(1)}, bf16[256,1280]{1,0:T(8,128)(2,1)S(1)}, u32[]{:S(2)}, u32[]{:S(2)}) collective-permute-start(bf16[256,1280]{1,0:T(8,128)(2,1)S(1)} %add_convert_fusion.1), channel_id=1, source_target_pairs={{0,1},{1,2},{2,3},{3,0},{4,5},{5,6},{6,7},{7,4},{8,9},{9,10},{10,1... | collective-permute-start | bytes 1966088 | tf_op jit(solution)/shard_map/ppermute | solution.py:318
  122.2 27.9 %collective-permute-start.19 = (bf16[256,1280]{1,0:T(8,128)(2,1)S(1)}, bf16[256,1280]{1,0:T(8,128)(2,1)S(1)}, u32[]{:S(2)}, u32[]{:S(2)}) collective-permute-start(bf16[256,1280]{1,0:T(8,128)(2,1)S(1)} %add_convert_fusion), channel_id=1, source_target_pairs={{0,3},{1,0},{2,1},{3,2},{4,7},{5,4},{6,5},{7,6},{8,11},{9,8},{10,9... | collective-permute-start | bytes 1966088 | tf_op jit(solution)/shard_map/ppermute | solution.py:319
  151.7 27.4 %all-to-all-start.3 = ((bf16[32,16,1280]{2,1,0:T(8,128)(2,1)}), bf16[32,16,1280]{2,1,0:T(8,128)(2,1)S(1)}, u32[]{:S(2)}, u32[]{:S(2)}) async-start(bf16[32,16,1280]{2,1,0:T(8,128)(2,1)} %bitcast.15), calls=%async_computation.3 | async-start | bytes 2621440 | tf_op jit(solution)/shard_map/all_to_all | solution.py:324
  162.2 7.1 %collective-permute-start.10 = (bf16[128,512]{1,0:T(8,128)(2,1)S(1)}, bf16[128,512]{1,0:T(8,128)(2,1)S(1)}, u32[]{:S(2)}, u32[]{:S(2)}) collective-permute-start(bf16[128,512]{1,0:T(8,128)(2,1)S(1)} %get-tuple-element.57), channel_id=1, source_target_pairs={{0,1},{1,2},{2,3},{3,0},{4,5},{5,6},{6,7},{7,4},{8,9},{9,10},{10,1... | collective-permute-start | bytes 393224 | tf_op jit(solution)/shard_map/ppermute | solution.py:300
  164.1 5.2 %collective-permute-start.12 = (bf16[128,512]{1,0:T(8,128)(2,1)S(1)}, bf16[128,512]{1,0:T(8,128)(2,1)S(1)}, u32[]{:S(2)}, u32[]{:S(2)}) collective-permute-start(bf16[128,512]{1,0:T(8,128)(2,1)S(1)} %get-tuple-element.58), channel_id=1, source_target_pairs={{0,3},{1,0},{2,1},{3,2},{4,7},{5,4},{6,5},{7,6},{8,11},{9,8},{10,9... | collective-permute-start | bytes 393224 | tf_op jit(solution)/shard_map/ppermute | solution.py:300
  169.4 8.3 %collective-permute-start.11 = (bf16[256,512]{1,0:T(8,128)(2,1)S(1)}, bf16[256,512]{1,0:T(8,128)(2,1)S(1)}, u32[]{:S(2)}, u32[]{:S(2)}) collective-permute-start(bf16[256,512]{1,0:T(8,128)(2,1)S(1)} %get-tuple-element.55), channel_id=1, source_target_pairs={{0,1},{1,2},{2,3},{3,0},{4,5},{5,6},{6,7},{7,4},{8,9},{9,10},{10,1... | collective-permute-start | bytes 786440 | tf_op jit(solution)/shard_map/ppermute | solution.py:303
  170.3 7.5 %collective-permute-start.13 = (bf16[256,512]{1,0:T(8,128)(2,1)S(1)}, bf16[256,512]{1,0:T(8,128)(2,1)S(1)}, u32[]{:S(2)}, u32[]{:S(2)}) collective-permute-start(bf16[256,512]{1,0:T(8,128)(2,1)S(1)} %get-tuple-element.56), channel_id=1, source_target_pairs={{0,3},{1,0},{2,1},{3,2},{4,7},{5,4},{6,5},{7,6},{8,11},{9,8},{10,9... | collective-permute-start | bytes 786440 | tf_op jit(solution)/shard_map/ppermute | solution.py:303

commit v8 on v7

--- a/solution.py
+++ b/solution.py
@@ -342,11 +342,7 @@
     weights = (w_gate, w_up, w_down)
     low, high = (0, half), (half, half)
     far_segs = [((0, 1), 2, EARLY, bulk, 0)]
-    far_jobs = [
-        (2, EARLY, bulk, 0, rows, ((0, 0, half, 0), (1, half, half, 0))),
-        (1, EARLY, bulk, *high, ((2, 0, half, 0),)),
-        (3, EARLY, bulk, *low, ((3, 0, half, 0),)),
-    ]
+    far_jobs = [(2, EARLY, bulk, 0, rows, ((0, 0, half, 0), (1, half, half, 0)))]
     sums = expert_call(where, weights, [mine], [((0,), 0, EARLY, bulk, 0)])
     sums = expert_call(
         where, weights, [*above, *below],
@@ -357,11 +353,16 @@
         where, weights, [early_rows], [((0,), k, 0, EARLY, k * EARLY) for k in range(n_tp)],
         stored=sums, keep=(0, n_tp * EARLY), stash=(far_segs, far_jobs),
     )
-    hidden, f_low, f_high, a_high, b_low = expert_call(
+    hidden, f_low, f_high = expert_call(
         where, weights, [*far, scale], far_segs, (gate_sum, up_sum), inv=2,
-        jobs=far_jobs, outs=[(half, bulk)] * 4, held=far_held,
+        jobs=far_jobs, outs=[(half, bulk)] * 2, held=far_held,
     )
     (p_early,) = expert_call(where, weights, hidden=hidden, jobs=early_jobs, outs=[(rows, n_tp * EARLY)], leave=True)
+    a_high, b_low = expert_call(
+        where, weights, hidden=hidden,
+        jobs=[(1, EARLY, bulk, *high, ((0, 0, half, 0),)), (3, EARLY, bulk, *low, ((1, 0, half, 0),))],
+        outs=[(half, bulk)] * 2,
+    )
     a_low, b_high, o_low, o_high = expert_call(
         where, weights, hidden=hidden,
         jobs=[

time: 182 us -> 181 us (level)
    ppermute x1, waiting for transfers between devices: 9.47 us -> 7.17 us  [fold_halves(): up_high = lax.ppermute(add(below[1], got_high), 'tp', dn)]
    ppermute x1, waiting for transfers between devices: 4.57 us -> 6.87 us  [fold_halves(): dn_low = lax.ppermute(add(above[0], got_low), 'tp', up)]
    pallas_call x6 -> x7, Pallas kernels: 25.6 us -> 26.9 us  [expert_call(): pl.pallas_call(body, in_specs=[pl.BlockSpec(memory_space=pltpu.SMEM)] + [...]
  transfers between devices with their start and end apart: 24 -> 24, of which waited for: 14 -> 14; matrix products, arithmetic and copies ran while one was open for 3% -> 2% of each run, Pallas kernels for 14% -> 15%
where the time goes in v8:
time: 181 us; the launch traced here: 180 us
  waiting for transfers between devices  74.6 us (41%)
  starting transfers between devices  63.1 us (35%)
  Pallas kernels  34.2 us (19%)
  local copies, waits for them, and re-layouts  3.15 us (2%)
  matrix products  2.84 us (2%)
    all_to_all x4, starting transfers between devices, exchange(): lax.all_to_all(shaped, 'ep', 0, 0, tiled=True).reshape(rows, x.shape[1])  34.1 us
    pallas_call x7, Pallas kernels, expert_call(): pl.pallas_call(body, in_specs=[pl.BlockSpec(memory_space=pltpu.SMEM)] + [...  26.9 us
    ppermute x1, waiting for transfers between devices, spread_halves(): lax.ppermute(low, 'tp', up)  13.4 us
    ppermute x1, waiting for transfers between devices, fold_halves(): lax.ppermute(below[0], 'tp', dn)  10.2 us
    ppermute x1, waiting for transfers between devices, spread_halves(): lax.ppermute(low, 'tp', dn)  7.32 us
    ppermute x1, waiting for transfers between devices, fold_halves(): up_high = lax.ppermute(add(below[1], got_high), 'tp', dn)  7.17 us
    ppermute x1, waiting for transfers between devices, fold_halves(): dn_low = lax.ppermute(add(above[0], got_low), 'tp', up)  6.87 us
    ppermute x2, waiting for transfers between devices, spread(): below, above = (lax.ppermute(x, 'tp', up), lax.ppermute(x, 'tp', dn))  6.83 us
  transfers between devices with their start and end apart: 24, of which 14 were waited for; matrix products, arithmetic and copies ran while one was open for 2% of the time, Pallas kernels for 15%

profile of v8, /device:TPU:1, one launch (start us, length us, event | category | flops | bytes accessed | tf_op | source)
XLA Modules:
  0.0 179.9 jit_solution(963443045174849808)
XLA Ops:
  0.0 2.9 %head.1 = (bf16[512,256]{1,0:T(8,128)(2,1)S(1)}, bf16[512,1280]{1,0:T(8,128)(2,1)}, bf16[256,640]{1,0:T(8,128)(2,1)S(1)}) custom-call(s32[8,256]{1,0:T(8,128)} %bitcast.46, bf16[1792]{0:T(1024)(128)(2,1)} %gain_hbm.1, bf16[256,1792]{1,0:T(8,128)(2,1)} %tokens_hbm.1), custom_call_target="tpu_custom_call" | custom-call | flops 335544320 | bytes 917504 | tf_op jit(solution)/shard_map/head/pallas_call | solution.py:201
  2.9 8.6 %all-to-all-start = ((bf16[32,16,1280]{2,1,0:T(8,128)(2,1)}), bf16[32,16,1280]{2,1,0:T(8,128)(2,1)S(1)}, u32[]{:S(2)}, u32[]{:S(2)}) async-start(bf16[32,16,1280]{2,1,0:T(8,128)(2,1)} %bitcast.4), calls=%async_computation | async-start | bytes 2621440 | tf_op jit(solution)/shard_map/all_to_all | solution.py:324
  11.5 3.8 %collective-permute-start.6 = (bf16[256,640]{1,0:T(8,128)(2,1)S(1)}, bf16[256,640]{1,0:T(8,128)(2,1)S(1)}, u32[]{:S(2)}, u32[]{:S(2)}) collective-permute-start(bf16[256,640]{1,0:T(8,128)(2,1)S(1)} %get-tuple-element.29.refs_0_), channel_id=1, source_target_pairs={{0,3},{1,0},{2,1},{3,2},{4,7},{5,4},{6,5},{7,6},{8,11},{9,8},{10,9... | collective-permute-start | bytes 983048 | tf_op jit(solution)/shard_map/ppermute | solution.py:295
  15.4 6.8 %collective-permute-done.6.refs_1_ = bf16[256,640]{1,0:T(8,128)(2,1)S(1)} collective-permute-done((bf16[256,640]{1,0:T(8,128)(2,1)S(1)}, bf16[256,640]{1,0:T(8,128)(2,1)S(1)}, u32[]{:S(2)}, u32[]{:S(2)}) %collective-permute-start.6) | collective-permute-done | bytes 327712 | tf_op jit(solution)/shard_map/ppermute | solution.py:295
  22.2 3.5 %collective-permute-start.7 = (bf16[128,640]{1,0:T(8,128)(2,1)S(1)}, bf16[128,640]{1,0:T(8,128)(2,1)S(1)}, u32[]{:S(2)}, u32[]{:S(2)}) collective-permute-start(bf16[128,640]{1,0:T(8,128)(2,1)S(1)} %slice.50), channel_id=1, source_target_pairs={{0,3},{1,0},{2,1},{3,2},{4,7},{5,4},{6,5},{7,6},{8,11},{9,8},{10,9... | collective-permute-start | bytes 491528 | tf_op jit(solution)/shard_map/ppermute | solution.py:296
  25.8 1.5 early_near.1.refs_3_
  27.3 0.6 collective-permute-done.7.high
  28.0 3.5 %collective-permute-done.5.low = bf16[128,640]{1,0:T(8,128)(2,1)S(1)} collective-permute-done((bf16[128,640]{1,0:T(8,128)(2,1)S(1)}, bf16[128,640]{1,0:T(8,128)(2,1)S(1)}, u32[]{:S(2)}, u32[]{:S(2)}) %collective-permute-start.5) | collective-permute-done | bytes 163872 | tf_op jit(solution)/shard_map/ppermute | solution.py:296
  31.5 1.3 early_rest.1
  32.7 9.2 %all-to-all-start.1 = ((bf16[32,16,2176]{2,1,0:T(8,128)(2,1)}), bf16[32,16,2176]{2,1,0:T(8,128)(2,1)S(1)}, u32[]{:S(2)}, u32[]{:S(2)}) async-start(bf16[32,16,2176]{2,1,0:T(8,128)(2,1)} %bitcast.7), calls=%async_computation.1 | async-start | bytes 4456448 | tf_op jit(solution)/shard_map/all_to_all | solution.py:324
  42.0 1.2 fusion.1
  43.1 2.7 %collective-permute-start.2 = (bf16[256,1280]{1,0:T(8,128)(2,1)}, bf16[256,1280]{1,0:T(8,128)(2,1)}, u32[]{:S(2)}, u32[]{:S(2)}) collective-permute-start(bf16[256,1280]{1,0:T(8,128)(2,1)} %bitcast.6), channel_id=1, source_target_pairs={{0,3},{1,0},{2,1},{3,2},{4,7},{5,4},{6,5},{7,6},{8,11},{9,8},{10,9... | collective-permute-start | bytes 1966088 | tf_op jit(solution)/shard_map/ppermute | solution.py:307
  45.8 1.4 collective-permute-start.9
  47.3 13.4 %collective-permute-done.refs_2_ = bf16[256,1280]{1,0:T(8,128)(2,1)} collective-permute-done((bf16[256,1280]{1,0:T(8,128)(2,1)}, bf16[256,1280]{1,0:T(8,128)(2,1)}, u32[]{:S(2)}, u32[]{:S(2)}) %collective-permute-start) | collective-permute-done | bytes 655392 | tf_op jit(solution)/shard_map/ppermute | solution.py:307
  60.7 2.7 %collective-permute-start.3 = (bf16[256,1280]{1,0:T(8,128)(2,1)}, bf16[256,1280]{1,0:T(8,128)(2,1)}, u32[]{:S(2)}, u32[]{:S(2)}) collective-permute-start(bf16[256,1280]{1,0:T(8,128)(2,1)} %collective-permute-done.2.refs_1_), channel_id=1, source_target_pairs={{0,3},{1,0},{2,1},{3,2},{4,7},{5,4},{6,5},{7,6},{8,11},{9,8},{10,9... | collective-permute-start | bytes 1966088 | tf_op jit(solution)/shard_map/ppermute | solution.py:309
  63.4 3.0 %shard_map.73 = (f32[512,512]{1,0:T(8,128)S(1)}, f32[512,512]{1,0:T(8,128)S(1)}) custom-call(s32[1]{0:T(128)} %bitcast.3.where_ref, bf16[512,1280]{1,0:T(8,128)(2,1)S(1)} %bitcast.25, bf16[7168,512]{1,0:T(8,128)(2,1)} %bitcast.27, bf16[7168,512]{1,0:T(8,128)(2,1)} %bitcast.33, bf16[512,7168]{1,0:T(8,128)(2,1)} %bitcast.39), custom_call_target="tpu_custom_call" | custom-call | flops 1342177280 | bytes 5242880 | tf_op jit(solution)/shard_map/pallas_call | solution.py:144
  66.4 7.3 %collective-permute-done.8.refs_0_ = bf16[256,1280]{1,0:T(8,128)(2,1)} collective-permute-done((bf16[256,1280]{1,0:T(8,128)(2,1)}, bf16[256,1280]{1,0:T(8,128)(2,1)}, u32[]{:S(2)}, u32[]{:S(2)}) %collective-permute-start.8) | collective-permute-done | bytes 655392 | tf_op jit(solution)/shard_map/ppermute | solution.py:308
  73.7 1.0 collective-permute-done.9.refs_3_
  74.8 6.4 %shard_map.74 = (f32[512,512]{1,0:T(8,128)S(1)}, f32[512,512]{1,0:T(8,128)S(1)}) custom-call(s32[1]{0:T(128)} %bitcast.3.where_ref, bf16[256,1280]{1,0:T(8,128)(2,1)} %collective-permute-done.8.refs_0_, bf16[256,1280]{1,0:T(8,128)(2,1)} %collective-permute-done.2.refs_1_, bf16[256,1280]{1,0:T(8,128)(2,1)} %collective-permute-done.refs_2_, ...), custom_call_target="tpu_custom_call" | custom-call | flops 2684354560 | bytes 10485760 | tf_op jit(solution)/shard_map/pallas_call | solution.py:144
  81.2 1.0 copy-done.2
  82.1 1.0 copy-done.3
  83.1 4.3 %shard_map.75 = (f32[512,512]{1,0:T(8,128)S(1)}, f32[512,512]{1,0:T(8,128)S(1)}, bf16[512,128]{1,0:T(8,128)(2,1)S(1)}, bf16[1280,512]{1,0:T(8,128)(2,1)S(1)}, bf...) custom-call(s32[1]{0:T(128)} %bitcast.3.where_ref, bf16[512,2176]{1,0:T(8,128)(2,1)S(1)} %bitcast.26, ...), custom_call_target="tpu_custom_call" | custom-call | flops 2147483648 | bytes 8388608 | tf_op jit(solution)/shard_map/pallas_call | solution.py:144
  87.4 1.4 collective-permute-done.1.refs_0_
  88.8 3.7 %shard_map.76 = (bf16[512,512]{1,0:T(8,128)(2,1)S(1)}, bf16[256,1280]{1,0:T(8,128)(2,1)S(1)}, bf16[256,1280]{1,0:T(8,128)(2,1)S(1)}) custom-call(s32[1]{0:T(128)} %bitcast.3.where_ref, bf16[256,1280]{1,0:T(8,128)(2,1)} %collective-permute-done.1.refs_0_, bf16[256,1280]{1,0:T(8,128)(2,1)} %collective-permute-done.3.refs_1_, ...), custom_call_target="tpu_custom_call" | custom-call | flops 2013265920 | bytes 7864320 | tf_op jit(solution)/shard_map/pallas_call | solution.py:144
  92.6 3.7 %shard_map.77 = bf16[512,2048]{1,0:T(8,128)(2,1)} custom-call(s32[1]{0:T(128)} %bitcast.3.where_ref, bf16[512,512]{1,0:T(8,128)(2,1)S(1)} %get-tuple-element.40.refs_0_, bf16[7168,512]{1,0:T(8,128)(2,1)} %bitcast.30, bf16[7168,512]{1,0:T(8,128)(2,1)} %bitcast.36, bf16[512,7168]{1,0:T(8,128)(2,1)} %bitcast.42), custom_call_target="tpu_custom_call" | custom-call | flops 1073741824 | bytes 4194304 | tf_op jit(solution)/shard_map/pallas_call | solution.py:144
  96.3 8.2 %all-to-all-start.2 = ((bf16[32,16,2048]{2,1,0:T(8,128)(2,1)}), bf16[32,16,2048]{2,1,0:T(8,128)(2,1)}, u32[]{:S(2)}, u32[]{:S(2)}) async-start(bf16[32,16,2048]{2,1,0:T(8,128)(2,1)} %bitcast.13), calls=%async_computation.2 | async-start | bytes 4194304 | tf_op jit(solution)/shard_map/all_to_all | solution.py:324
  104.5 3.0 %collective-permute-start.18 = (bf16[256,1280]{1,0:T(8,128)(2,1)S(1)}, bf16[256,1280]{1,0:T(8,128)(2,1)S(1)}, u32[]{:S(2)}, u32[]{:S(2)}) collective-permute-start(bf16[256,1280]{1,0:T(8,128)(2,1)S(1)} %get-tuple-element.48), channel_id=1, source_target_pairs={{0,3},{1,0},{2,1},{3,2},{4,7},{5,4},{6,5},{7,6},{8,11},{9,8},{10,9... | collective-permute-start | bytes 1966088 | tf_op jit(solution)/shard_map/ppermute | solution.py:316
  107.5 2.5 %shard_map.79 = (bf16[256,1280]{1,0:T(8,128)(2,1)S(1)}, bf16[256,1280]{1,0:T(8,128)(2,1)S(1)}) custom-call(s32[1]{0:T(128)} %bitcast.3.where_ref, bf16[512,512]{1,0:T(8,128)(2,1)S(1)} %get-tuple-element.40.refs_0_, bf16[7168,512]{1,0:T(8,128)(2,1)} %bitcast.31, bf16[7168,512]{1,0:T(8,128)(2,1)} %bitcast.37, bf16[512,7168]{1,0:T(8,128)(2,1)} %bitcast.43), custom_call_target="tpu_custom_call" | custom-call | flops 671088640 | bytes 2621440 | tf_op jit(solution)/shard_map/pallas_call | solution.py:144
  110.0 1.5 collective-permute-start.16
  111.5 3.3 %shard_map.78 = (bf16[256,1280]{1,0:T(8,128)(2,1)S(1)}, bf16[256,1280]{1,0:T(8,128)(2,1)S(1)}, bf16[256,1280]{1,0:T(8,128)(2,1)S(1)}, bf16[256,1280]{1,0:T(8,128)(2,1)S(1)}) custom-call(s32[1]{0:T(128)} %bitcast.3.where_ref, bf16[512,512]{1,0:T(8,128)(2,1)S(1)} %get-tuple-element.40.refs_0_, bf16[7168,512]{1,0:T(8,128)(2,1)} %bitcast.32, ...), custom_call_target="tpu_custom_call" | custom-call | flops 1342177280 | bytes 5242880 | tf_op jit(solution)/shard_map/pallas_call | solution.py:144
  115.0 0.3 collective-permute-start.15
  115.3 5.9 %collective-permute-done.18 = bf16[256,1280]{1,0:T(8,128)(2,1)S(1)} collective-permute-done((bf16[256,1280]{1,0:T(8,128)(2,1)S(1)}, bf16[256,1280]{1,0:T(8,128)(2,1)S(1)}, u32[]{:S(2)}, u32[]{:S(2)}) %collective-permute-start.18) | collective-permute-done | bytes 655392 | tf_op jit(solution)/shard_map/ppermute | solution.py:316
  121.4 3.6 %collective-permute-start.19 = (bf16[256,1280]{1,0:T(8,128)(2,1)S(1)}, bf16[256,1280]{1,0:T(8,128)(2,1)S(1)}, u32[]{:S(2)}, u32[]{:S(2)}) collective-permute-start(bf16[256,1280]{1,0:T(8,128)(2,1)S(1)} %add_convert_fusion), channel_id=1, source_target_pairs={{0,3},{1,0},{2,1},{3,2},{4,7},{5,4},{6,5},{7,6},{8,11},{9,8},{10,9... | collective-permute-start | bytes 1966088 | tf_op jit(solution)/shard_map/ppermute | solution.py:319
  125.1 10.2 %collective-permute-done.16.refs_2_ = bf16[256,1280]{1,0:T(8,128)(2,1)S(1)} collective-permute-done((bf16[256,1280]{1,0:T(8,128)(2,1)S(1)}, bf16[256,1280]{1,0:T(8,128)(2,1)S(1)}, u32[]{:S(2)}, u32[]{:S(2)}) %collective-permute-start.16) | collective-permute-done | bytes 655392 | tf_op jit(solution)/shard_map/ppermute | solution.py:317
  135.3 6.9 %collective-permute-done.15.refs_1_ = bf16[256,1280]{1,0:T(8,128)(2,1)S(1)} collective-permute-done((bf16[256,1280]{1,0:T(8,128)(2,1)S(1)}, bf16[256,1280]{1,0:T(8,128)(2,1)S(1)}, u32[]{:S(2)}, u32[]{:S(2)}) %collective-permute-start.15) | collective-permute-done | bytes 655392 | tf_op jit(solution)/shard_map/ppermute | solution.py:318
  142.2 7.2 %collective-permute-done.19.refs_5_ = bf16[256,1280]{1,0:T(8,128)(2,1)S(1)} collective-permute-done((bf16[256,1280]{1,0:T(8,128)(2,1)S(1)}, bf16[256,1280]{1,0:T(8,128)(2,1)S(1)}, u32[]{:S(2)}, u32[]{:S(2)}) %collective-permute-start.19) | collective-permute-done | bytes 655392 | tf_op jit(solution)/shard_map/ppermute | solution.py:319
  149.3 1.6 join_sums.1
  150.9 8.2 %all-to-all-start.3 = ((bf16[32,16,1280]{2,1,0:T(8,128)(2,1)}), bf16[32,16,1280]{2,1,0:T(8,128)(2,1)S(1)}, u32[]{:S(2)}, u32[]{:S(2)}) async-start(bf16[32,16,1280]{2,1,0:T(8,128)(2,1)} %bitcast.15), calls=%async_computation.3 | async-start | bytes 2621440 | tf_op jit(solution)/shard_map/all_to_all | solution.py:324
  159.1 2.3 %convolution_convert_fusion = bf16[256,2048]{1,0:T(8,128)(2,1)S(1)} fusion(bf16[512,256]{1,0:T(8,128)(2,1)S(1)} %fusion, bf16[512,2048]{1,0:T(8,128)(2,1)} %bitcast.14), kind=kOutput, calls=%fused_computation | convolution fusion | flops 537395200 | bytes 3407872 | tf_op jit(solution)/shard_map/dot_general | solution.py:377
  161.4 1.7 collective-permute-start.10
  163.1 1.9 %collective-permute-start.12 = (bf16[128,512]{1,0:T(8,128)(2,1)S(1)}, bf16[128,512]{1,0:T(8,128)(2,1)S(1)}, u32[]{:S(2)}, u32[]{:S(2)}) collective-permute-start(bf16[128,512]{1,0:T(8,128)(2,1)S(1)} %get-tuple-element.54), channel_id=1, source_target_pairs={{0,3},{1,0},{2,1},{3,2},{4,7},{5,4},{6,5},{7,6},{8,11},{9,8},{10,9... | collective-permute-start | bytes 393224 | tf_op jit(solution)/shard_map/ppermute | solution.py:300
  165.0 3.6 %collective-permute-done.10 = bf16[128,512]{1,0:T(8,128)(2,1)S(1)} collective-permute-done((bf16[128,512]{1,0:T(8,128)(2,1)S(1)}, bf16[128,512]{1,0:T(8,128)(2,1)S(1)}, u32[]{:S(2)}, u32[]{:S(2)}) %collective-permute-start.10) | collective-permute-done | bytes 131104 | tf_op jit(solution)/shard_map/ppermute | solution.py:300
  168.6 0.6 collective-permute-start.11
  169.3 2.1 %collective-permute-start.13 = (bf16[256,512]{1,0:T(8,128)(2,1)S(1)}, bf16[256,512]{1,0:T(8,128)(2,1)S(1)}, u32[]{:S(2)}, u32[]{:S(2)}) collective-permute-start(bf16[256,512]{1,0:T(8,128)(2,1)S(1)} %get-tuple-element.52), channel_id=1, source_target_pairs={{0,3},{1,0},{2,1},{3,2},{4,7},{5,4},{6,5},{7,6},{8,11},{9,8},{10,9... | collective-permute-start | bytes 786440 | tf_op jit(solution)/shard_map/ppermute | solution.py:303
  171.4 5.6 %collective-permute-done.11 = bf16[256,512]{1,0:T(8,128)(2,1)S(1)} collective-permute-done((bf16[256,512]{1,0:T(8,128)(2,1)S(1)}, bf16[256,512]{1,0:T(8,128)(2,1)S(1)}, u32[]{:S(2)}, u32[]{:S(2)}) %collective-permute-start.11) | collective-permute-done | bytes 262176 | tf_op jit(solution)/shard_map/ppermute | solution.py:303
  177.1 1.2 all-to-all-done.3
  178.3 0.5 convolution_convert_fusion.1
  178.9 1.0 pad_maximum_fusion
  (37 shorter events, 0.9 us)
Async XLA Ops:
  2.9 28.5 %copy-start = (bf16[512,256]{1,0:T(8,128)(2,1)}, bf16[512,256]{1,0:T(8,128)(2,1)S(1)}, u32[]{:S(2)}) copy-start(bf16[512,256]{1,0:T(8,128)(2,1)S(1)} %get-tuple-element.27.pick_ref) | copy-start | bytes 786436
  2.9 29.8 %all-to-all-start = ((bf16[32,16,1280]{2,1,0:T(8,128)(2,1)}), bf16[32,16,1280]{2,1,0:T(8,128)(2,1)S(1)}, u32[]{:S(2)}, u32[]{:S(2)}) async-start(bf16[32,16,1280]{2,1,0:T(8,128)(2,1)} %bitcast.4), calls=%async_computation | async-start | bytes 2621440 | tf_op jit(solution)/shard_map/all_to_all | solution.py:324
  11.5 10.7 %collective-permute-start.6 = (bf16[256,640]{1,0:T(8,128)(2,1)S(1)}, bf16[256,640]{1,0:T(8,128)(2,1)S(1)}, u32[]{:S(2)}, u32[]{:S(2)}) collective-permute-start(bf16[256,640]{1,0:T(8,128)(2,1)S(1)} %get-tuple-element.29.refs_0_), channel_id=1, source_target_pairs={{0,3},{1,0},{2,1},{3,2},{4,7},{5,4},{6,5},{7,6},{8,11},{9,8},{10,9... | collective-permute-start | bytes 983048 | tf_op jit(solution)/shard_map/ppermute | solution.py:295
  15.4 10.3 %collective-permute-start.4 = (bf16[256,640]{1,0:T(8,128)(2,1)S(1)}, bf16[256,640]{1,0:T(8,128)(2,1)S(1)}, u32[]{:S(2)}, u32[]{:S(2)}) collective-permute-start(bf16[256,640]{1,0:T(8,128)(2,1)S(1)} %get-tuple-element.29.refs_0_), channel_id=1, source_target_pairs={{0,1},{1,2},{2,3},{3,0},{4,5},{5,6},{6,7},{7,4},{8,9},{9,10},{10,1... | collective-permute-start | bytes 983048 | tf_op jit(solution)/shard_map/ppermute | solution.py:295
  22.2 5.7 %collective-permute-start.7 = (bf16[128,640]{1,0:T(8,128)(2,1)S(1)}, bf16[128,640]{1,0:T(8,128)(2,1)S(1)}, u32[]{:S(2)}, u32[]{:S(2)}) collective-permute-start(bf16[128,640]{1,0:T(8,128)(2,1)S(1)} %slice.50), channel_id=1, source_target_pairs={{0,3},{1,0},{2,1},{3,2},{4,7},{5,4},{6,5},{7,6},{8,11},{9,8},{10,9... | collective-permute-start | bytes 491528 | tf_op jit(solution)/shard_map/ppermute | solution.py:296
  25.7 5.7 %collective-permute-start.5 = (bf16[128,640]{1,0:T(8,128)(2,1)S(1)}, bf16[128,640]{1,0:T(8,128)(2,1)S(1)}, u32[]{:S(2)}, u32[]{:S(2)}) collective-permute-start(bf16[128,640]{1,0:T(8,128)(2,1)S(1)} %slice.49), channel_id=1, source_target_pairs={{0,1},{1,2},{2,3},{3,0},{4,5},{5,6},{6,7},{7,4},{8,9},{9,10},{10,1... | collective-permute-start | bytes 491528 | tf_op jit(solution)/shard_map/ppermute | solution.py:296
  32.7 50.4 %all-to-all-start.1 = ((bf16[32,16,2176]{2,1,0:T(8,128)(2,1)}), bf16[32,16,2176]{2,1,0:T(8,128)(2,1)S(1)}, u32[]{:S(2)}, u32[]{:S(2)}) async-start(bf16[32,16,2176]{2,1,0:T(8,128)(2,1)} %bitcast.7), calls=%async_computation.1 | async-start | bytes 4456448 | tf_op jit(solution)/shard_map/all_to_all | solution.py:324
  43.1 17.6 %collective-permute-start = (bf16[256,1280]{1,0:T(8,128)(2,1)}, bf16[256,1280]{1,0:T(8,128)(2,1)}, u32[]{:S(2)}, u32[]{:S(2)}) collective-permute-start(bf16[256,1280]{1,0:T(8,128)(2,1)} %bitcast.5), channel_id=1, source_target_pairs={{0,1},{1,2},{2,3},{3,0},{4,5},{5,6},{6,7},{7,4},{8,9},{9,10},{10,1... | collective-permute-start | bytes 1966088 | tf_op jit(solution)/shard_map/ppermute | solution.py:307
  43.1 17.6 %collective-permute-start.2 = (bf16[256,1280]{1,0:T(8,128)(2,1)}, bf16[256,1280]{1,0:T(8,128)(2,1)}, u32[]{:S(2)}, u32[]{:S(2)}) collective-permute-start(bf16[256,1280]{1,0:T(8,128)(2,1)} %bitcast.6), channel_id=1, source_target_pairs={{0,3},{1,0},{2,1},{3,2},{4,7},{5,4},{6,5},{7,6},{8,11},{9,8},{10,9... | collective-permute-start | bytes 1966088 | tf_op jit(solution)/shard_map/ppermute | solution.py:307
  45.8 27.9 %collective-permute-start.8 = (bf16[256,1280]{1,0:T(8,128)(2,1)}, bf16[256,1280]{1,0:T(8,128)(2,1)}, u32[]{:S(2)}, u32[]{:S(2)}) collective-permute-start(bf16[256,1280]{1,0:T(8,128)(2,1)} %bitcast.5), channel_id=1, source_target_pairs={{0,3},{1,0},{2,1},{3,2},{4,7},{5,4},{6,5},{7,6},{8,11},{9,8},{10,9... | collective-permute-start | bytes 1966088 | tf_op jit(solution)/shard_map/ppermute | solution.py:308
  45.8 28.9 %collective-permute-start.9 = (bf16[256,1280]{1,0:T(8,128)(2,1)}, bf16[256,1280]{1,0:T(8,128)(2,1)}, u32[]{:S(2)}, u32[]{:S(2)}) collective-permute-start(bf16[256,1280]{1,0:T(8,128)(2,1)} %bitcast.6), channel_id=1, source_target_pairs={{0,1},{1,2},{2,3},{3,0},{4,5},{5,6},{6,7},{7,4},{8,9},{9,10},{10,1... | collective-permute-start | bytes 1966088 | tf_op jit(solution)/shard_map/ppermute | solution.py:308
  60.7 28.1 %collective-permute-start.1 = (bf16[256,1280]{1,0:T(8,128)(2,1)}, bf16[256,1280]{1,0:T(8,128)(2,1)}, u32[]{:S(2)}, u32[]{:S(2)}) collective-permute-start(bf16[256,1280]{1,0:T(8,128)(2,1)} %collective-permute-done.refs_2_), channel_id=1, source_target_pairs={{0,1},{1,2},{2,3},{3,0},{4,5},{5,6},{6,7},{7,4},{8,9},{9,10},{10,1... | collective-permute-start | bytes 1966088 | tf_op jit(solution)/shard_map/ppermute | solution.py:309
  60.7 28.1 %collective-permute-start.3 = (bf16[256,1280]{1,0:T(8,128)(2,1)}, bf16[256,1280]{1,0:T(8,128)(2,1)}, u32[]{:S(2)}, u32[]{:S(2)}) collective-permute-start(bf16[256,1280]{1,0:T(8,128)(2,1)} %collective-permute-done.2.refs_1_), channel_id=1, source_target_pairs={{0,3},{1,0},{2,1},{3,2},{4,7},{5,4},{6,5},{7,6},{8,11},{9,8},{10,9... | collective-permute-start | bytes 1966088 | tf_op jit(solution)/shard_map/ppermute | solution.py:309
  81.2 1.0 copy-start.2
  82.1 1.0 copy-start.3
  92.5 22.3 %collective-permute-start.14 = (bf16[256,1280]{1,0:T(8,128)(2,1)S(1)}, bf16[256,1280]{1,0:T(8,128)(2,1)S(1)}, u32[]{:S(2)}, u32[]{:S(2)}) collective-permute-start(bf16[256,1280]{1,0:T(8,128)(2,1)S(1)} %get-tuple-element.43), channel_id=1, source_target_pairs={{0,1},{1,2},{2,3},{3,0},{4,5},{5,6},{6,7},{7,4},{8,9},{9,10},{10,1... | collective-permute-start | bytes 1966088 | tf_op jit(solution)/shard_map/ppermute | solution.py:316
  96.3 54.6 %all-to-all-start.2 = ((bf16[32,16,2048]{2,1,0:T(8,128)(2,1)}), bf16[32,16,2048]{2,1,0:T(8,128)(2,1)}, u32[]{:S(2)}, u32[]{:S(2)}) async-start(bf16[32,16,2048]{2,1,0:T(8,128)(2,1)} %bitcast.13), calls=%async_computation.2 | async-start | bytes 4194304 | tf_op jit(solution)/shard_map/all_to_all | solution.py:324
  104.5 16.8 %collective-permute-start.18 = (bf16[256,1280]{1,0:T(8,128)(2,1)S(1)}, bf16[256,1280]{1,0:T(8,128)(2,1)S(1)}, u32[]{:S(2)}, u32[]{:S(2)}) collective-permute-start(bf16[256,1280]{1,0:T(8,128)(2,1)S(1)} %get-tuple-element.48), channel_id=1, source_target_pairs={{0,3},{1,0},{2,1},{3,2},{4,7},{5,4},{6,5},{7,6},{8,11},{9,8},{10,9... | collective-permute-start | bytes 1966088 | tf_op jit(solution)/shard_map/ppermute | solution.py:316
  110.0 25.3 %collective-permute-start.16 = (bf16[256,1280]{1,0:T(8,128)(2,1)S(1)}, bf16[256,1280]{1,0:T(8,128)(2,1)S(1)}, u32[]{:S(2)}, u32[]{:S(2)}) collective-permute-start(bf16[256,1280]{1,0:T(8,128)(2,1)S(1)} %get-tuple-element.44), channel_id=1, source_target_pairs={{0,3},{1,0},{2,1},{3,2},{4,7},{5,4},{6,5},{7,6},{8,11},{9,8},{10,9... | collective-permute-start | bytes 1966088 | tf_op jit(solution)/shard_map/ppermute | solution.py:317
  111.5 23.8 %collective-permute-start.17 = (bf16[256,1280]{1,0:T(8,128)(2,1)S(1)}, bf16[256,1280]{1,0:T(8,128)(2,1)S(1)}, u32[]{:S(2)}, u32[]{:S(2)}) collective-permute-start(bf16[256,1280]{1,0:T(8,128)(2,1)S(1)} %get-tuple-element.46), channel_id=1, source_target_pairs={{0,1},{1,2},{2,3},{3,0},{4,5},{5,6},{6,7},{7,4},{8,9},{9,10},{10,1... | collective-permute-start | bytes 1966088 | tf_op jit(solution)/shard_map/ppermute | solution.py:317
  115.0 10.0 %copy-start.5 = (bf16[256,8]{0,1:T(8,128)(2,1)S(1)}, bf16[256,8]{0,1:T(8,128)(2,1)}, u32[]{:S(2)}) copy-start(bf16[256,8]{0,1:T(8,128)(2,1)} %param.10) | copy-start | bytes 12292
  115.0 10.0 %copy-start.4 = (s32[256,8]{0,1:T(8,128)S(1)}, s32[256,8]{0,1:T(8,128)}, u32[]{:S(2)}) copy-start(s32[256,8]{0,1:T(8,128)} %param.9) | copy-start | bytes 24580
  115.0 10.0 %copy-start.1 = (bf16[512,256]{1,0:T(8,128)(2,1)S(1)}, bf16[512,256]{1,0:T(8,128)(2,1)}, u32[]{:S(2)}) copy-start(bf16[512,256]{1,0:T(8,128)(2,1)} %copy-done) | copy-start | bytes 786436
  115.0 27.1 %collective-permute-start.15 = (bf16[256,1280]{1,0:T(8,128)(2,1)S(1)}, bf16[256,1280]{1,0:T(8,128)(2,1)S(1)}, u32[]{:S(2)}, u32[]{:S(2)}) collective-permute-start(bf16[256,1280]{1,0:T(8,128)(2,1)S(1)} %add_convert_fusion.1), channel_id=1, source_target_pairs={{0,1},{1,2},{2,3},{3,0},{4,5},{5,6},{6,7},{7,4},{8,9},{9,10},{10,1... | collective-permute-start | bytes 1966088 | tf_op jit(solution)/shard_map/ppermute | solution.py:318
  121.4 27.9 %collective-permute-start.19 = (bf16[256,1280]{1,0:T(8,128)(2,1)S(1)}, bf16[256,1280]{1,0:T(8,128)(2,1)S(1)}, u32[]{:S(2)}, u32[]{:S(2)}) collective-permute-start(bf16[256,1280]{1,0:T(8,128)(2,1)S(1)} %add_convert_fusion), channel_id=1, source_target_pairs={{0,3},{1,0},{2,1},{3,2},{4,7},{5,4},{6,5},{7,6},{8,11},{9,8},{10,9... | collective-permute-start | bytes 1966088 | tf_op jit(solution)/shard_map/ppermute | solution.py:319
  150.9 27.4 %all-to-all-start.3 = ((bf16[32,16,1280]{2,1,0:T(8,128)(2,1)}), bf16[32,16,1280]{2,1,0:T(8,128)(2,1)S(1)}, u32[]{:S(2)}, u32[]{:S(2)}) async-start(bf16[32,16,1280]{2,1,0:T(8,128)(2,1)} %bitcast.15), calls=%async_computation.3 | async-start | bytes 2621440 | tf_op jit(solution)/shard_map/all_to_all | solution.py:324
  161.4 7.1 %collective-permute-start.10 = (bf16[128,512]{1,0:T(8,128)(2,1)S(1)}, bf16[128,512]{1,0:T(8,128)(2,1)S(1)}, u32[]{:S(2)}, u32[]{:S(2)}) collective-permute-start(bf16[128,512]{1,0:T(8,128)(2,1)S(1)} %get-tuple-element.53), channel_id=1, source_target_pairs={{0,1},{1,2},{2,3},{3,0},{4,5},{5,6},{6,7},{7,4},{8,9},{9,10},{10,1... | collective-permute-start | bytes 393224 | tf_op jit(solution)/shard_map/ppermute | solution.py:300
  163.1 5.5 %collective-permute-start.12 = (bf16[128,512]{1,0:T(8,128)(2,1)S(1)}, bf16[128,512]{1,0:T(8,128)(2,1)S(1)}, u32[]{:S(2)}, u32[]{:S(2)}) collective-permute-start(bf16[128,512]{1,0:T(8,128)(2,1)S(1)} %get-tuple-element.54), channel_id=1, source_target_pairs={{0,3},{1,0},{2,1},{3,2},{4,7},{5,4},{6,5},{7,6},{8,11},{9,8},{10,9... | collective-permute-start | bytes 393224 | tf_op jit(solution)/shard_map/ppermute | solution.py:300
  168.6 8.3 %collective-permute-start.11 = (bf16[256,512]{1,0:T(8,128)(2,1)S(1)}, bf16[256,512]{1,0:T(8,128)(2,1)S(1)}, u32[]{:S(2)}, u32[]{:S(2)}) collective-permute-start(bf16[256,512]{1,0:T(8,128)(2,1)S(1)} %get-tuple-element.51), channel_id=1, source_target_pairs={{0,1},{1,2},{2,3},{3,0},{4,5},{5,6},{6,7},{7,4},{8,9},{9,10},{10,1... | collective-permute-start | bytes 786440 | tf_op jit(solution)/shard_map/ppermute | solution.py:303
  169.3 7.7 %collective-permute-start.13 = (bf16[256,512]{1,0:T(8,128)(2,1)S(1)}, bf16[256,512]{1,0:T(8,128)(2,1)S(1)}, u32[]{:S(2)}, u32[]{:S(2)}) collective-permute-start(bf16[256,512]{1,0:T(8,128)(2,1)S(1)} %get-tuple-element.52), channel_id=1, source_target_pairs={{0,3},{1,0},{2,1},{3,2},{4,7},{5,4},{6,5},{7,6},{8,11},{9,8},{10,9... | collective-permute-start | bytes 786440 | tf_op jit(solution)/shard_map/ppermute | solution.py:303

commit v9 on v7

--- a/solution.py
+++ b/solution.py
@@ -210,18 +210,19 @@
 
 
 def join_sums(low, high):
-    half, width = low[0].shape
+    cut, width = low[0].shape
+    rows = cut + high[0].shape[0]
 
     def body(*refs):
         out = refs[-1]
-        for k in (0, 1):
+        for k, at in ((0, slice(0, cut)), (1, slice(cut, rows))):
             a, b, c = (r[...].astype(F32) for r in refs[3 * k : 3 * k + 3])
-            out[k * half : (k + 1) * half, :] = (a + b + c).astype(BF16)
+            out[at, :] = (a + b + c).astype(BF16)
 
     return pl.pallas_call(
         body,
-        out_shape=jax.ShapeDtypeStruct((2 * half, width), BF16),
-        cost_estimate=pl.CostEstimate(flops=6 * half * width, bytes_accessed=16 * half * width, transcendentals=0),
+        out_shape=jax.ShapeDtypeStruct((rows, width), BF16),
+        cost_estimate=pl.CostEstimate(flops=3 * rows * width, bytes_accessed=8 * rows * width, transcendentals=0),
         compiler_params=pltpu.CompilerParams(vmem_limit_bytes=16 * 2**20),
         name="join_sums",
     )(*low, *high)
@@ -290,33 +291,39 @@
     up = [(i, (i + 1) % n_tp) for i in range(n_tp)]
     dn = [(i, (i - 1) % n_tp) for i in range(n_tp)]
 
+    def send_up(x):
+        return lax.ppermute(x, "tp", up)
+
+    def send_dn(x):
+        return lax.ppermute(x, "tp", dn)
+
     def spread(x):
         half = x.shape[0] // 2
-        below, above = lax.ppermute(x, "tp", up), lax.ppermute(x, "tp", dn)
-        return below, above, lax.ppermute(below[:half], "tp", up), lax.ppermute(above[half:], "tp", dn)
+        below, above = send_up(x), send_dn(x)
+        return below, above, send_up(below[:half]), send_dn(above[half:])
 
     def fold(own, above, below, far_a, far_b):
         half = own.shape[0] // 2
-        got_a, got_b = lax.ppermute(far_a, "tp", up), lax.ppermute(far_b, "tp", dn)
+        got_a, got_b = send_up(far_a), send_dn(far_b)
         sum_up = (above.astype(F32) + jnp.pad(got_a.astype(F32), ((0, half), (0, 0)))).astype(BF16)
         sum_dn = (below.astype(F32) + jnp.pad(got_b.astype(F32), ((half, 0), (0, 0)))).astype(BF16)
-        from_dn, from_up = lax.ppermute(sum_up, "tp", up), lax.ppermute(sum_dn, "tp", dn)
+        from_dn, from_up = send_up(sum_up), send_dn(sum_dn)
         return (own.astype(F32) + from_dn.astype(F32) + from_up.astype(F32)).astype(BF16)
 
     def spread_halves(low, high):
-        below_low, above_high = lax.ppermute(low, "tp", up), lax.ppermute(high, "tp", dn)
-        below_high, above_low = lax.ppermute(high, "tp", up), lax.ppermute(low, "tp", dn)
-        far = lax.ppermute(below_low, "tp", up), lax.ppermute(above_high, "tp", dn)
+        below_low, above_high = send_up(low), send_dn(high)
+        below_high, above_low = send_up(high), send_dn(low)
+        far = send_up(below_low), send_dn(above_high)
         return (below_low, below_high), (above_low, above_high), far
 
     def add(*terms):
         return sum(t.astype(F32) for t in terms).astype(BF16)
 
     def fold_halves(own, above, below, far):
-        got_low, got_high = lax.ppermute(far[0], "tp", up), lax.ppermute(far[1], "tp", dn)
-        dn_high, up_low = lax.ppermute(above[1], "tp", up), lax.ppermute(below[0], "tp", dn)
-        dn_low = lax.ppermute(add(above[0], got_low), "tp", up)
-        up_high = lax.ppermute(add(below[1], got_high), "tp", dn)
+        got_low, got_high = send_up(far[0]), send_dn(far[1])
+        dn_high, up_low = send_up(above[1]), send_dn(below[0])
+        dn_low = send_up(add(above[0], got_low))
+        up_high = send_dn(add(below[1], got_high))
         return join_sums((own[0], dn_low, up_low), (own[1], dn_high, up_high))
 
     def exchange(x):
@@ -324,7 +331,7 @@
         return lax.all_to_all(shaped, "ep", 0, 0, tiled=True).reshape(rows, x.shape[1])
 
     bulk = tokens.shape[1] - EARLY
-    half = rows // 2
+    cut = rows // 2 + CAP
     ids, probs = expert_ids.T, gate_prob.T.astype(F32)
     pick, picked_bulk, early = head(tokens, norm_gain, ids, window)
     same = ids[:, None, :] == jnp.arange(window, dtype=jnp.int32)[None, :, None]
@@ -337,15 +344,15 @@
     picked_near = early_near(pick, ((0, early), (1, e_above), (3, e_below)), n_tp)
     picked = early_rest(pick, 2, (e_far_a, e_far_b), (early, e_above, e_below), picked_near, D)
     early_rows = exchange(picked)
-    below, above, far = spread_halves(mine[:half], mine[half:])
+    below, above, far = spread_halves(mine[:cut], mine[cut:])
 
     weights = (w_gate, w_up, w_down)
-    low, high = (0, half), (half, half)
+    low, high = (0, cut), (cut, rows - cut)
     far_segs = [((0, 1), 2, EARLY, bulk, 0)]
     far_jobs = [
-        (2, EARLY, bulk, 0, rows, ((0, 0, half, 0), (1, half, half, 0))),
-        (1, EARLY, bulk, *high, ((2, 0, half, 0),)),
-        (3, EARLY, bulk, *low, ((3, 0, half, 0),)),
+        (2, EARLY, bulk, 0, rows, ((0, *low, 0), (1, *high, 0))),
+        (1, EARLY, bulk, *high, ((2, 0, rows - cut, 0),)),
+        (3, EARLY, bulk, *low, ((3, 0, cut, 0),)),
     ]
     sums = expert_call(where, weights, [mine], [((0,), 0, EARLY, bulk, 0)])
     sums = expert_call(
@@ -359,17 +366,17 @@
     )
     hidden, f_low, f_high, a_high, b_low = expert_call(
         where, weights, [*far, scale], far_segs, (gate_sum, up_sum), inv=2,
-        jobs=far_jobs, outs=[(half, bulk)] * 4, held=far_held,
+        jobs=far_jobs, outs=[(cut, bulk), (rows - cut, bulk), (rows - cut, bulk), (cut, bulk)], held=far_held,
     )
     (p_early,) = expert_call(where, weights, hidden=hidden, jobs=early_jobs, outs=[(rows, n_tp * EARLY)], leave=True)
     a_low, b_high, o_low, o_high = expert_call(
         where, weights, hidden=hidden,
         jobs=[
-            (1, EARLY, bulk, *low, ((0, 0, half, 0),)),
-            (3, EARLY, bulk, *high, ((1, 0, half, 0),)),
-            (0, EARLY, bulk, 0, rows, ((2, 0, half, 0), (3, half, half, 0))),
+            (1, EARLY, bulk, *low, ((0, 0, cut, 0),)),
+            (3, EARLY, bulk, *high, ((1, 0, rows - cut, 0),)),
+            (0, EARLY, bulk, 0, rows, ((2, *low, 0), (3, *high, 0))),
         ],
-        outs=[(half, bulk)] * 4,
+        outs=[(cut, bulk), (rows - cut, bulk)] * 2,
     )
 
     def combine(back):

time: 182 us -> 183 us (level)
  waiting for transfers between devices: 75.3 us -> 78.8 us
  starting transfers between devices: 63.4 us -> 60.8 us
    ppermute x20, starting transfers between devices: 29.2 us -> 26.6 us  [the longest x10 21.9 us: send_dn(): return lax.ppermute(x, 'tp', dn)]
    ppermute x20, waiting for transfers between devices: 74 us -> 76 us  [the longest x10 41.5 us: send_dn(): return lax.ppermute(x, 'tp', dn)]
  transfers between devices with their start and end apart: 24 -> 24, of which waited for: 14 -> 12; matrix products, arithmetic and copies ran while one was open for 3% -> 3% of each run, Pallas kernels for 14% -> 14%
where the time goes in v9:
time: 183 us; the launch traced here: 182 us
  waiting for transfers between devices  78.8 us (43%)
  starting transfers between devices  60.8 us (33%)
  Pallas kernels  33 us (18%)
  local copies, waits for them, and re-layouts  3.78 us (2%)
  matrix products  2.84 us (2%)
  other arithmetic  2.73 us (1%)
    ppermute x10, waiting for transfers between devices, send_dn(): return lax.ppermute(x, 'tp', dn)  41.5 us
    ppermute x10, waiting for transfers between devices, send_up(): return lax.ppermute(x, 'tp', up)  34.5 us
    all_to_all x4, starting transfers between devices, exchange(): lax.all_to_all(shaped, 'ep', 0, 0, tiled=True).reshape(rows, x.shape[1])  34.1 us
    pallas_call x6, Pallas kernels, expert_call(): pl.pallas_call(body, in_specs=[pl.BlockSpec(memory_space=pltpu.SMEM)] + [...  25.6 us
    ppermute x10, starting transfers between devices, send_dn(): return lax.ppermute(x, 'tp', dn)  21.9 us
    ppermute x10, starting transfers between devices, send_up(): return lax.ppermute(x, 'tp', up)  4.74 us
  transfers between devices with their start and end apart: 24, of which 12 were waited for; matrix products, arithmetic and copies ran while one was open for 3% of the time, Pallas kernels for 14%

profile of v9, /device:TPU:1, one launch (start us, length us, event | category | flops | bytes accessed | tf_op | source)
XLA Modules:
  0.0 182.2 jit_solution(9115507394358093198)
XLA Ops:
  0.0 2.9 %head.1 = (bf16[512,256]{1,0:T(8,128)(2,1)S(1)}, bf16[512,1280]{1,0:T(8,128)(2,1)}, bf16[256,640]{1,0:T(8,128)(2,1)S(1)}) custom-call(s32[8,256]{1,0:T(8,128)} %bitcast.43, bf16[1792]{0:T(1024)(128)(2,1)} %gain_hbm.1, bf16[256,1792]{1,0:T(8,128)(2,1)} %tokens_hbm.1), custom_call_target="tpu_custom_call" | custom-call | flops 335544320 | bytes 917504 | tf_op jit(solution)/shard_map/head/pallas_call | solution.py:201
  2.9 8.6 %all-to-all-start = ((bf16[32,16,1280]{2,1,0:T(8,128)(2,1)}), bf16[32,16,1280]{2,1,0:T(8,128)(2,1)S(1)}, u32[]{:S(2)}, u32[]{:S(2)}) async-start(bf16[32,16,1280]{2,1,0:T(8,128)(2,1)} %bitcast.4), calls=%async_computation | async-start | bytes 2621440 | tf_op jit(solution)/shard_map/all_to_all | solution.py:331
  11.5 3.8 %collective-permute-start.6 = (bf16[256,640]{1,0:T(8,128)(2,1)S(1)}, bf16[256,640]{1,0:T(8,128)(2,1)S(1)}, u32[]{:S(2)}, u32[]{:S(2)}) collective-permute-start(bf16[256,640]{1,0:T(8,128)(2,1)S(1)} %get-tuple-element.31.refs_0_), channel_id=1, source_target_pairs={{0,3},{1,0},{2,1},{3,2},{4,7},{5,4},{6,5},{7,6},{8,11},{9,8},{10,9... | collective-permute-start | bytes 983048 | tf_op jit(solution)/shard_map/ppermute | solution.py:298
  15.4 6.8 %collective-permute-done.6.refs_1_ = bf16[256,640]{1,0:T(8,128)(2,1)S(1)} collective-permute-done((bf16[256,640]{1,0:T(8,128)(2,1)S(1)}, bf16[256,640]{1,0:T(8,128)(2,1)S(1)}, u32[]{:S(2)}, u32[]{:S(2)}) %collective-permute-start.6) | collective-permute-done | bytes 327712 | tf_op jit(solution)/shard_map/ppermute | solution.py:298
  22.2 3.5 %collective-permute-start.7 = (bf16[128,640]{1,0:T(8,128)(2,1)S(1)}, bf16[128,640]{1,0:T(8,128)(2,1)S(1)}, u32[]{:S(2)}, u32[]{:S(2)}) collective-permute-start(bf16[128,640]{1,0:T(8,128)(2,1)S(1)} %slice.50), channel_id=1, source_target_pairs={{0,3},{1,0},{2,1},{3,2},{4,7},{5,4},{6,5},{7,6},{8,11},{9,8},{10,9... | collective-permute-start | bytes 491528 | tf_op jit(solution)/shard_map/ppermute | solution.py:298
  25.8 1.6 early_near.1.refs_3_
  27.4 0.6 collective-permute-done.7.high
  28.0 3.5 %collective-permute-done.5.low = bf16[128,640]{1,0:T(8,128)(2,1)S(1)} collective-permute-done((bf16[128,640]{1,0:T(8,128)(2,1)S(1)}, bf16[128,640]{1,0:T(8,128)(2,1)S(1)}, u32[]{:S(2)}, u32[]{:S(2)}) %collective-permute-start.5) | collective-permute-done | bytes 163872 | tf_op jit(solution)/shard_map/ppermute | solution.py:295
  31.5 1.3 early_rest.1
  32.8 9.2 %all-to-all-start.1 = ((bf16[32,16,2176]{2,1,0:T(8,128)(2,1)}), bf16[32,16,2176]{2,1,0:T(8,128)(2,1)S(1)}, u32[]{:S(2)}, u32[]{:S(2)}) async-start(bf16[32,16,2176]{2,1,0:T(8,128)(2,1)} %bitcast.7), calls=%async_computation.1 | async-start | bytes 4456448 | tf_op jit(solution)/shard_map/all_to_all | solution.py:331
  42.0 0.9 slice.47
  42.9 0.9 slice.48
  43.8 2.7 %collective-permute-start.2 = (bf16[240,1280]{1,0:T(8,128)(2,1)}, bf16[240,1280]{1,0:T(8,128)(2,1)}, u32[]{:S(2)}, u32[]{:S(2)}) collective-permute-start(bf16[240,1280]{1,0:T(8,128)(2,1)} %bitcast.6), channel_id=1, source_target_pairs={{0,3},{1,0},{2,1},{3,2},{4,7},{5,4},{6,5},{7,6},{8,11},{9,8},{10,9... | collective-permute-start | bytes 1843208 | tf_op jit(solution)/shard_map/ppermute | solution.py:298
  46.5 1.4 collective-permute-start.9
  47.9 13.4 %collective-permute-done.refs_2_ = bf16[272,1280]{1,0:T(8,128)(2,1)} collective-permute-done((bf16[272,1280]{1,0:T(8,128)(2,1)}, bf16[272,1280]{1,0:T(8,128)(2,1)}, u32[]{:S(2)}, u32[]{:S(2)}) %collective-permute-start) | collective-permute-done | bytes 696352 | tf_op jit(solution)/shard_map/ppermute | solution.py:295
  61.4 2.7 %collective-permute-start.3 = (bf16[240,1280]{1,0:T(8,128)(2,1)}, bf16[240,1280]{1,0:T(8,128)(2,1)}, u32[]{:S(2)}, u32[]{:S(2)}) collective-permute-start(bf16[240,1280]{1,0:T(8,128)(2,1)} %collective-permute-done.2.refs_1_), channel_id=1, source_target_pairs={{0,3},{1,0},{2,1},{3,2},{4,7},{5,4},{6,5},{7,6},{8,11},{9,8},{10,9... | collective-permute-start | bytes 1843208 | tf_op jit(solution)/shard_map/ppermute | solution.py:298
  64.1 3.0 %shard_map.73 = (f32[512,512]{1,0:T(8,128)S(1)}, f32[512,512]{1,0:T(8,128)S(1)}) custom-call(s32[1]{0:T(128)} %bitcast.3.where_ref, bf16[512,1280]{1,0:T(8,128)(2,1)S(1)} %bitcast.25, bf16[7168,512]{1,0:T(8,128)(2,1)} %bitcast.27, bf16[7168,512]{1,0:T(8,128)(2,1)} %bitcast.32, bf16[512,7168]{1,0:T(8,128)(2,1)} %bitcast.37), custom_call_target="tpu_custom_call" | custom-call | flops 1342177280 | bytes 5242880 | tf_op jit(solution)/shard_map/pallas_call | solution.py:144
  67.1 7.5 %collective-permute-done.9.refs_3_ = bf16[240,1280]{1,0:T(8,128)(2,1)} collective-permute-done((bf16[240,1280]{1,0:T(8,128)(2,1)}, bf16[240,1280]{1,0:T(8,128)(2,1)}, u32[]{:S(2)}, u32[]{:S(2)}) %collective-permute-start.9) | collective-permute-done | bytes 614432 | tf_op jit(solution)/shard_map/ppermute | solution.py:295
  74.5 6.4 %shard_map.74 = (f32[512,512]{1,0:T(8,128)S(1)}, f32[512,512]{1,0:T(8,128)S(1)}) custom-call(s32[1]{0:T(128)} %bitcast.3.where_ref, bf16[272,1280]{1,0:T(8,128)(2,1)} %collective-permute-done.8.refs_0_, bf16[240,1280]{1,0:T(8,128)(2,1)} %collective-permute-done.2.refs_1_, bf16[272,1280]{1,0:T(8,128)(2,1)} %collective-permute-done.refs_2_, ...), custom_call_target="tpu_custom_call" | custom-call | flops 2684354560 | bytes 10485760 | tf_op jit(solution)/shard_map/pallas_call | solution.py:144
  80.9 1.0 copy-done.2
  81.9 1.0 copy-done.3
  82.9 4.9 %shard_map.75 = (f32[512,512]{1,0:T(8,128)S(1)}, f32[512,512]{1,0:T(8,128)S(1)}, bf16[512,128]{1,0:T(8,128)(2,1)S(1)}, bf16[1280,512]{1,0:T(8,128)(2,1)S(1)}, bf...) custom-call(s32[1]{0:T(128)} %bitcast.3.where_ref, ...), custom_call_target="tpu_custom_call" | custom-call | flops 2147483648 | bytes 8388608 | tf_op jit(solution)/shard_map/pallas_call | solution.py:144
  87.8 1.7 collective-permute-done.1.refs_0_
  89.5 4.3 %shard_map.76 = (bf16[512,512]{1,0:T(8,128)(2,1)S(1)}, bf16[272,1280]{1,0:T(8,128)(2,1)S(1)}, bf16[240,1280]{1,0:T(8,128)(2,1)S(1)}, bf16[240,1280]{1,0:T(8,128)(2,1)S(1)}, bf16[272,1280]{1,0:T(8,128)(2,1)S(1)}) custom-call(s32[1]{0:T(128)} %bitcast.3.where_ref, bf16[272,1280]{1,0:T(8,128)(2,1)} %collective-permute-done.1.refs_0_, ...), custom_call_target="tpu_custom_call" | custom-call | flops 2684354560 | bytes 10485760 | tf_op jit(solution)/shard_map/pallas_call | solution.py:144
  93.9 3.7 %shard_map.77 = bf16[512,2048]{1,0:T(8,128)(2,1)} custom-call(s32[1]{0:T(128)} %bitcast.3.where_ref, bf16[512,512]{1,0:T(8,128)(2,1)S(1)} %get-tuple-element.44.refs_0_, bf16[7168,512]{1,0:T(8,128)(2,1)} %bitcast.30, bf16[7168,512]{1,0:T(8,128)(2,1)} %bitcast.35, bf16[512,7168]{1,0:T(8,128)(2,1)} %bitcast.40), custom_call_target="tpu_custom_call" | custom-call | flops 1073741824 | bytes 4194304 | tf_op jit(solution)/shard_map/pallas_call | solution.py:144
  97.6 8.2 %all-to-all-start.2 = ((bf16[32,16,2048]{2,1,0:T(8,128)(2,1)}), bf16[32,16,2048]{2,1,0:T(8,128)(2,1)}, u32[]{:S(2)}, u32[]{:S(2)}) async-start(bf16[32,16,2048]{2,1,0:T(8,128)(2,1)} %bitcast.13), calls=%async_computation.2 | async-start | bytes 4194304 | tf_op jit(solution)/shard_map/all_to_all | solution.py:331
  105.7 1.2 collective-permute-start.17
  106.9 1.9 %collective-permute-start.18 = (bf16[240,1280]{1,0:T(8,128)(2,1)S(1)}, bf16[240,1280]{1,0:T(8,128)(2,1)S(1)}, u32[]{:S(2)}, u32[]{:S(2)}) collective-permute-start(bf16[240,1280]{1,0:T(8,128)(2,1)S(1)} %get-tuple-element.52), channel_id=1, source_target_pairs={{0,3},{1,0},{2,1},{3,2},{4,7},{5,4},{6,5},{7,6},{8,11},{9,8},{10,9... | collective-permute-start | bytes 1843208 | tf_op jit(solution)/shard_map/ppermute | solution.py:298
  108.9 1.7 collective-permute-start.16
  110.6 3.4 %shard_map.78 = (bf16[272,1280]{1,0:T(8,128)(2,1)S(1)}, bf16[240,1280]{1,0:T(8,128)(2,1)S(1)}, bf16[272,1280]{1,0:T(8,128)(2,1)S(1)}, bf16[240,1280]{1,0:T(8,128)(2,1)S(1)}) custom-call(s32[1]{0:T(128)} %bitcast.3.where_ref, bf16[512,512]{1,0:T(8,128)(2,1)S(1)} %get-tuple-element.44.refs_0_, bf16[7168,512]{1,0:T(8,128)(2,1)} %bitcast.31, ...), custom_call_target="tpu_custom_call" | custom-call | flops 1342177280 | bytes 5242880 | tf_op jit(solution)/shard_map/pallas_call | solution.py:144
  114.0 1.3 add_convert_fusion
  115.4 8.3 %collective-permute-done.18 = bf16[240,1280]{1,0:T(8,128)(2,1)S(1)} collective-permute-done((bf16[240,1280]{1,0:T(8,128)(2,1)S(1)}, bf16[240,1280]{1,0:T(8,128)(2,1)S(1)}, u32[]{:S(2)}, u32[]{:S(2)}) %collective-permute-start.18) | collective-permute-done | bytes 614432 | tf_op jit(solution)/shard_map/ppermute | solution.py:298
  123.6 0.2 add_convert_fusion.1
  123.8 1.9 %collective-permute-start.19 = (bf16[240,1280]{1,0:T(8,128)(2,1)S(1)}, bf16[240,1280]{1,0:T(8,128)(2,1)S(1)}, u32[]{:S(2)}, u32[]{:S(2)}) collective-permute-start(bf16[240,1280]{1,0:T(8,128)(2,1)S(1)} %add_convert_fusion.1), channel_id=1, source_target_pairs={{0,3},{1,0},{2,1},{3,2},{4,7},{5,4},{6,5},{7,6},{8,11},{9,8},{10,9... | collective-permute-start | bytes 1843208 | tf_op jit(solution)/shard_map/ppermute | solution.py:298
  125.9 12.6 %collective-permute-done.16.refs_2_ = bf16[272,1280]{1,0:T(8,128)(2,1)S(1)} collective-permute-done((bf16[272,1280]{1,0:T(8,128)(2,1)S(1)}, bf16[272,1280]{1,0:T(8,128)(2,1)S(1)}, u32[]{:S(2)}, u32[]{:S(2)}) %collective-permute-start.16) | collective-permute-done | bytes 696352 | tf_op jit(solution)/shard_map/ppermute | solution.py:298
  138.5 13.2 %collective-permute-done.19.refs_5_ = bf16[240,1280]{1,0:T(8,128)(2,1)S(1)} collective-permute-done((bf16[240,1280]{1,0:T(8,128)(2,1)S(1)}, bf16[240,1280]{1,0:T(8,128)(2,1)S(1)}, u32[]{:S(2)}, u32[]{:S(2)}) %collective-permute-start.19) | collective-permute-done | bytes 614432 | tf_op jit(solution)/shard_map/ppermute | solution.py:298
  151.6 1.6 join_sums.1
  153.2 8.2 %all-to-all-start.3 = ((bf16[32,16,1280]{2,1,0:T(8,128)(2,1)}), bf16[32,16,1280]{2,1,0:T(8,128)(2,1)S(1)}, u32[]{:S(2)}, u32[]{:S(2)}) async-start(bf16[32,16,1280]{2,1,0:T(8,128)(2,1)} %bitcast.15), calls=%async_computation.3 | async-start | bytes 2621440 | tf_op jit(solution)/shard_map/all_to_all | solution.py:331
  161.4 2.3 %convolution_convert_fusion = bf16[256,2048]{1,0:T(8,128)(2,1)S(1)} fusion(bf16[512,256]{1,0:T(8,128)(2,1)S(1)} %fusion, bf16[512,2048]{1,0:T(8,128)(2,1)} %bitcast.14), kind=kOutput, calls=%fused_computation | convolution fusion | flops 537395200 | bytes 3407872 | tf_op jit(solution)/shard_map/dot_general | solution.py:383
  163.8 1.5 collective-permute-start.10
  165.3 1.2 collective-permute-start.12
  166.5 3.4 %collective-permute-done.10 = bf16[128,512]{1,0:T(8,128)(2,1)S(1)} collective-permute-done((bf16[128,512]{1,0:T(8,128)(2,1)S(1)}, bf16[128,512]{1,0:T(8,128)(2,1)S(1)}, u32[]{:S(2)}, u32[]{:S(2)}) %collective-permute-start.10) | collective-permute-done | bytes 131104 | tf_op jit(solution)/shard_map/ppermute | solution.py:295
  170.0 0.3 collective-permute-start.11
  170.3 2.4 %collective-permute-start.13 = (bf16[256,512]{1,0:T(8,128)(2,1)S(1)}, bf16[256,512]{1,0:T(8,128)(2,1)S(1)}, u32[]{:S(2)}, u32[]{:S(2)}) collective-permute-start(bf16[256,512]{1,0:T(8,128)(2,1)S(1)} %get-tuple-element.54), channel_id=1, source_target_pairs={{0,3},{1,0},{2,1},{3,2},{4,7},{5,4},{6,5},{7,6},{8,11},{9,8},{10,9... | collective-permute-start | bytes 786440 | tf_op jit(solution)/shard_map/ppermute | solution.py:298
  172.7 5.1 %collective-permute-done.11 = bf16[256,512]{1,0:T(8,128)(2,1)S(1)} collective-permute-done((bf16[256,512]{1,0:T(8,128)(2,1)S(1)}, bf16[256,512]{1,0:T(8,128)(2,1)S(1)}, u32[]{:S(2)}, u32[]{:S(2)}) %collective-permute-start.11) | collective-permute-done | bytes 262176 | tf_op jit(solution)/shard_map/ppermute | solution.py:295
  177.9 2.8 %all-to-all-done.3 = bf16[32,16,1280]{2,1,0:T(8,128)(2,1)S(1)} async-done(((bf16[32,16,1280]{2,1,0:T(8,128)(2,1)}), bf16[32,16,1280]{2,1,0:T(8,128)(2,1)S(1)}, u32[]{:S(2)}, u32[]{:S(2)}) %all-to-all-start.3) | async-done | bytes 1310752 | tf_op jit(solution)/shard_map/all_to_all | solution.py:331
  180.7 0.5 convolution_convert_fusion.1
  181.2 1.0 pad_maximum_fusion
  (37 shorter events, 0.7 us)
Async XLA Ops:
  2.9 28.5 %copy-start = (bf16[512,256]{1,0:T(8,128)(2,1)}, bf16[512,256]{1,0:T(8,128)(2,1)S(1)}, u32[]{:S(2)}) copy-start(bf16[512,256]{1,0:T(8,128)(2,1)S(1)} %get-tuple-element.29.pick_ref) | copy-start | bytes 786436
  2.9 29.8 %all-to-all-start = ((bf16[32,16,1280]{2,1,0:T(8,128)(2,1)}), bf16[32,16,1280]{2,1,0:T(8,128)(2,1)S(1)}, u32[]{:S(2)}, u32[]{:S(2)}) async-start(bf16[32,16,1280]{2,1,0:T(8,128)(2,1)} %bitcast.4), calls=%async_computation | async-start | bytes 2621440 | tf_op jit(solution)/shard_map/all_to_all | solution.py:331
  11.5 10.7 %collective-permute-start.6 = (bf16[256,640]{1,0:T(8,128)(2,1)S(1)}, bf16[256,640]{1,0:T(8,128)(2,1)S(1)}, u32[]{:S(2)}, u32[]{:S(2)}) collective-permute-start(bf16[256,640]{1,0:T(8,128)(2,1)S(1)} %get-tuple-element.31.refs_0_), channel_id=1, source_target_pairs={{0,3},{1,0},{2,1},{3,2},{4,7},{5,4},{6,5},{7,6},{8,11},{9,8},{10,9... | collective-permute-start | bytes 983048 | tf_op jit(solution)/shard_map/ppermute | solution.py:298
  15.4 10.3 %collective-permute-start.4 = (bf16[256,640]{1,0:T(8,128)(2,1)S(1)}, bf16[256,640]{1,0:T(8,128)(2,1)S(1)}, u32[]{:S(2)}, u32[]{:S(2)}) collective-permute-start(bf16[256,640]{1,0:T(8,128)(2,1)S(1)} %get-tuple-element.31.refs_0_), channel_id=1, source_target_pairs={{0,1},{1,2},{2,3},{3,0},{4,5},{5,6},{6,7},{7,4},{8,9},{9,10},{10,1... | collective-permute-start | bytes 983048 | tf_op jit(solution)/shard_map/ppermute | solution.py:295
  22.2 5.7 %collective-permute-start.7 = (bf16[128,640]{1,0:T(8,128)(2,1)S(1)}, bf16[128,640]{1,0:T(8,128)(2,1)S(1)}, u32[]{:S(2)}, u32[]{:S(2)}) collective-permute-start(bf16[128,640]{1,0:T(8,128)(2,1)S(1)} %slice.50), channel_id=1, source_target_pairs={{0,3},{1,0},{2,1},{3,2},{4,7},{5,4},{6,5},{7,6},{8,11},{9,8},{10,9... | collective-permute-start | bytes 491528 | tf_op jit(solution)/shard_map/ppermute | solution.py:298
  25.7 5.7 %collective-permute-start.5 = (bf16[128,640]{1,0:T(8,128)(2,1)S(1)}, bf16[128,640]{1,0:T(8,128)(2,1)S(1)}, u32[]{:S(2)}, u32[]{:S(2)}) collective-permute-start(bf16[128,640]{1,0:T(8,128)(2,1)S(1)} %slice.49), channel_id=1, source_target_pairs={{0,1},{1,2},{2,3},{3,0},{4,5},{5,6},{6,7},{7,4},{8,9},{9,10},{10,1... | collective-permute-start | bytes 491528 | tf_op jit(solution)/shard_map/ppermute | solution.py:295
  32.8 50.1 %all-to-all-start.1 = ((bf16[32,16,2176]{2,1,0:T(8,128)(2,1)}), bf16[32,16,2176]{2,1,0:T(8,128)(2,1)S(1)}, u32[]{:S(2)}, u32[]{:S(2)}) async-start(bf16[32,16,2176]{2,1,0:T(8,128)(2,1)} %bitcast.7), calls=%async_computation.1 | async-start | bytes 4456448 | tf_op jit(solution)/shard_map/all_to_all | solution.py:331
  42.9 18.5 %collective-permute-start = (bf16[272,1280]{1,0:T(8,128)(2,1)}, bf16[272,1280]{1,0:T(8,128)(2,1)}, u32[]{:S(2)}, u32[]{:S(2)}) collective-permute-start(bf16[272,1280]{1,0:T(8,128)(2,1)} %bitcast.5), channel_id=1, source_target_pairs={{0,1},{1,2},{2,3},{3,0},{4,5},{5,6},{6,7},{7,4},{8,9},{9,10},{10,1... | collective-permute-start | bytes 2088968 | tf_op jit(solution)/shard_map/ppermute | solution.py:295
  43.8 17.6 %collective-permute-start.2 = (bf16[240,1280]{1,0:T(8,128)(2,1)}, bf16[240,1280]{1,0:T(8,128)(2,1)}, u32[]{:S(2)}, u32[]{:S(2)}) collective-permute-start(bf16[240,1280]{1,0:T(8,128)(2,1)} %bitcast.6), channel_id=1, source_target_pairs={{0,3},{1,0},{2,1},{3,2},{4,7},{5,4},{6,5},{7,6},{8,11},{9,8},{10,9... | collective-permute-start | bytes 1843208 | tf_op jit(solution)/shard_map/ppermute | solution.py:298
  46.5 28.1 %collective-permute-start.8 = (bf16[272,1280]{1,0:T(8,128)(2,1)}, bf16[272,1280]{1,0:T(8,128)(2,1)}, u32[]{:S(2)}, u32[]{:S(2)}) collective-permute-start(bf16[272,1280]{1,0:T(8,128)(2,1)} %bitcast.5), channel_id=1, source_target_pairs={{0,3},{1,0},{2,1},{3,2},{4,7},{5,4},{6,5},{7,6},{8,11},{9,8},{10,9... | collective-permute-start | bytes 2088968 | tf_op jit(solution)/shard_map/ppermute | solution.py:298
  46.5 28.1 %collective-permute-start.9 = (bf16[240,1280]{1,0:T(8,128)(2,1)}, bf16[240,1280]{1,0:T(8,128)(2,1)}, u32[]{:S(2)}, u32[]{:S(2)}) collective-permute-start(bf16[240,1280]{1,0:T(8,128)(2,1)} %bitcast.6), channel_id=1, source_target_pairs={{0,1},{1,2},{2,3},{3,0},{4,5},{5,6},{6,7},{7,4},{8,9},{9,10},{10,1... | collective-permute-start | bytes 1843208 | tf_op jit(solution)/shard_map/ppermute | solution.py:295
  61.4 28.1 %collective-permute-start.1 = (bf16[272,1280]{1,0:T(8,128)(2,1)}, bf16[272,1280]{1,0:T(8,128)(2,1)}, u32[]{:S(2)}, u32[]{:S(2)}) collective-permute-start(bf16[272,1280]{1,0:T(8,128)(2,1)} %collective-permute-done.refs_2_), channel_id=1, source_target_pairs={{0,1},{1,2},{2,3},{3,0},{4,5},{5,6},{6,7},{7,4},{8,9},{9,10},{10,1... | collective-permute-start | bytes 2088968 | tf_op jit(solution)/shard_map/ppermute | solution.py:295
  61.4 26.4 %collective-permute-start.3 = (bf16[240,1280]{1,0:T(8,128)(2,1)}, bf16[240,1280]{1,0:T(8,128)(2,1)}, u32[]{:S(2)}, u32[]{:S(2)}) collective-permute-start(bf16[240,1280]{1,0:T(8,128)(2,1)} %collective-permute-done.2.refs_1_), channel_id=1, source_target_pairs={{0,3},{1,0},{2,1},{3,2},{4,7},{5,4},{6,5},{7,6},{8,11},{9,8},{10,9... | collective-permute-start | bytes 1843208 | tf_op jit(solution)/shard_map/ppermute | solution.py:298
  80.9 1.0 copy-start.2
  81.9 1.0 copy-start.3
  93.8 20.2 %collective-permute-start.14 = (bf16[272,1280]{1,0:T(8,128)(2,1)S(1)}, bf16[272,1280]{1,0:T(8,128)(2,1)}, u32[]{:S(2)}, u32[]{:S(2)}) collective-permute-start(bf16[272,1280]{1,0:T(8,128)(2,1)S(1)} %get-tuple-element.47), channel_id=1, source_target_pairs={{0,1},{1,2},{2,3},{3,0},{4,5},{5,6},{6,7},{7,4},{8,9},{9,10},{10,1... | collective-permute-start | bytes 2088968 | tf_op jit(solution)/shard_map/ppermute | solution.py:295
  97.6 55.7 %all-to-all-start.2 = ((bf16[32,16,2048]{2,1,0:T(8,128)(2,1)}), bf16[32,16,2048]{2,1,0:T(8,128)(2,1)}, u32[]{:S(2)}, u32[]{:S(2)}) async-start(bf16[32,16,2048]{2,1,0:T(8,128)(2,1)} %bitcast.13), calls=%async_computation.2 | async-start | bytes 4194304 | tf_op jit(solution)/shard_map/all_to_all | solution.py:331
  105.7 20.1 %collective-permute-start.17 = (bf16[240,1280]{1,0:T(8,128)(2,1)S(1)}, bf16[240,1280]{1,0:T(8,128)(2,1)S(1)}, u32[]{:S(2)}, u32[]{:S(2)}) collective-permute-start(bf16[240,1280]{1,0:T(8,128)(2,1)S(1)} %get-tuple-element.50), channel_id=1, source_target_pairs={{0,1},{1,2},{2,3},{3,0},{4,5},{5,6},{6,7},{7,4},{8,9},{9,10},{10,1... | collective-permute-start | bytes 1843208 | tf_op jit(solution)/shard_map/ppermute | solution.py:295
  106.9 16.7 %collective-permute-start.18 = (bf16[240,1280]{1,0:T(8,128)(2,1)S(1)}, bf16[240,1280]{1,0:T(8,128)(2,1)S(1)}, u32[]{:S(2)}, u32[]{:S(2)}) collective-permute-start(bf16[240,1280]{1,0:T(8,128)(2,1)S(1)} %get-tuple-element.52), channel_id=1, source_target_pairs={{0,3},{1,0},{2,1},{3,2},{4,7},{5,4},{6,5},{7,6},{8,11},{9,8},{10,9... | collective-permute-start | bytes 1843208 | tf_op jit(solution)/shard_map/ppermute | solution.py:298
  108.9 29.6 %collective-permute-start.16 = (bf16[272,1280]{1,0:T(8,128)(2,1)S(1)}, bf16[272,1280]{1,0:T(8,128)(2,1)S(1)}, u32[]{:S(2)}, u32[]{:S(2)}) collective-permute-start(bf16[272,1280]{1,0:T(8,128)(2,1)S(1)} %get-tuple-element.48), channel_id=1, source_target_pairs={{0,3},{1,0},{2,1},{3,2},{4,7},{5,4},{6,5},{7,6},{8,11},{9,8},{10,9... | collective-permute-start | bytes 2088968 | tf_op jit(solution)/shard_map/ppermute | solution.py:298
  115.2 10.5 %copy-start.5 = (bf16[256,8]{0,1:T(8,128)(2,1)S(1)}, bf16[256,8]{0,1:T(8,128)(2,1)}, u32[]{:S(2)}) copy-start(bf16[256,8]{0,1:T(8,128)(2,1)} %param.10) | copy-start | bytes 12292
  115.3 10.5 %copy-start.4 = (s32[256,8]{0,1:T(8,128)S(1)}, s32[256,8]{0,1:T(8,128)}, u32[]{:S(2)}) copy-start(s32[256,8]{0,1:T(8,128)} %param.9) | copy-start | bytes 24580
  115.3 10.5 %copy-start.1 = (bf16[512,256]{1,0:T(8,128)(2,1)S(1)}, bf16[512,256]{1,0:T(8,128)(2,1)}, u32[]{:S(2)}) copy-start(bf16[512,256]{1,0:T(8,128)(2,1)} %copy-done) | copy-start | bytes 786436
  115.3 36.4 %collective-permute-start.15 = (bf16[272,1280]{1,0:T(8,128)(2,1)S(1)}, bf16[272,1280]{1,0:T(8,128)(2,1)S(1)}, u32[]{:S(2)}, u32[]{:S(2)}) collective-permute-start(bf16[272,1280]{1,0:T(8,128)(2,1)S(1)} %add_convert_fusion), channel_id=1, source_target_pairs={{0,1},{1,2},{2,3},{3,0},{4,5},{5,6},{6,7},{7,4},{8,9},{9,10},{10,1... | collective-permute-start | bytes 2088968 | tf_op jit(solution)/shard_map/ppermute | solution.py:295
  123.8 27.8 %collective-permute-start.19 = (bf16[240,1280]{1,0:T(8,128)(2,1)S(1)}, bf16[240,1280]{1,0:T(8,128)(2,1)S(1)}, u32[]{:S(2)}, u32[]{:S(2)}) collective-permute-start(bf16[240,1280]{1,0:T(8,128)(2,1)S(1)} %add_convert_fusion.1), channel_id=1, source_target_pairs={{0,3},{1,0},{2,1},{3,2},{4,7},{5,4},{6,5},{7,6},{8,11},{9,8},{10,9... | collective-permute-start | bytes 1843208 | tf_op jit(solution)/shard_map/ppermute | solution.py:298
  153.2 27.4 %all-to-all-start.3 = ((bf16[32,16,1280]{2,1,0:T(8,128)(2,1)}), bf16[32,16,1280]{2,1,0:T(8,128)(2,1)S(1)}, u32[]{:S(2)}, u32[]{:S(2)}) async-start(bf16[32,16,1280]{2,1,0:T(8,128)(2,1)} %bitcast.15), calls=%async_computation.3 | async-start | bytes 2621440 | tf_op jit(solution)/shard_map/all_to_all | solution.py:331
  163.8 6.1 %collective-permute-start.10 = (bf16[128,512]{1,0:T(8,128)(2,1)S(1)}, bf16[128,512]{1,0:T(8,128)(2,1)S(1)}, u32[]{:S(2)}, u32[]{:S(2)}) collective-permute-start(bf16[128,512]{1,0:T(8,128)(2,1)S(1)} %get-tuple-element.55), channel_id=1, source_target_pairs={{0,1},{1,2},{2,3},{3,0},{4,5},{5,6},{6,7},{7,4},{8,9},{9,10},{10,1... | collective-permute-start | bytes 393224 | tf_op jit(solution)/shard_map/ppermute | solution.py:295
  165.3 4.6 %collective-permute-start.12 = (bf16[128,512]{1,0:T(8,128)(2,1)S(1)}, bf16[128,512]{1,0:T(8,128)(2,1)S(1)}, u32[]{:S(2)}, u32[]{:S(2)}) collective-permute-start(bf16[128,512]{1,0:T(8,128)(2,1)S(1)} %get-tuple-element.56), channel_id=1, source_target_pairs={{0,3},{1,0},{2,1},{3,2},{4,7},{5,4},{6,5},{7,6},{8,11},{9,8},{10,9... | collective-permute-start | bytes 393224 | tf_op jit(solution)/shard_map/ppermute | solution.py:298
  170.0 7.8 %collective-permute-start.11 = (bf16[256,512]{1,0:T(8,128)(2,1)S(1)}, bf16[256,512]{1,0:T(8,128)(2,1)S(1)}, u32[]{:S(2)}, u32[]{:S(2)}) collective-permute-start(bf16[256,512]{1,0:T(8,128)(2,1)S(1)} %get-tuple-element.53), channel_id=1, source_target_pairs={{0,1},{1,2},{2,3},{3,0},{4,5},{5,6},{6,7},{7,4},{8,9},{9,10},{10,1... | collective-permute-start | bytes 786440 | tf_op jit(solution)/shard_map/ppermute | solution.py:295
  170.3 7.5 %collective-permute-start.13 = (bf16[256,512]{1,0:T(8,128)(2,1)S(1)}, bf16[256,512]{1,0:T(8,128)(2,1)S(1)}, u32[]{:S(2)}, u32[]{:S(2)}) collective-permute-start(bf16[256,512]{1,0:T(8,128)(2,1)S(1)} %get-tuple-element.54), channel_id=1, source_target_pairs={{0,3},{1,0},{2,1},{3,2},{4,7},{5,4},{6,5},{7,6},{8,11},{9,8},{10,9... | collective-permute-start | bytes 786440 | tf_op jit(solution)/shard_map/ppermute | solution.py:298

commit v10 on v9

--- a/solution.py
+++ b/solution.py
@@ -59,8 +59,8 @@
     if finish:
         scratch += [pltpu.VMEM((rows, ff), F32)] * 2
     scratch += [pltpu.VMEM((rows, ff), F32)] * len(stored)
-    scratch += [pltpu.VMEM(s, BF16) for s in outs] * leave
-    n_copies = len(jobs) * leave + len(stored) + len(needed) + len(results) - n_out
+    scratch += ([pltpu.VMEM(s, BF16) for s in outs] or [pltpu.VMEM((rows, ff), F32)] * 2) * leave
+    n_copies = (len(jobs) or 2) * leave + len(stored) + len(needed) + len(results) - n_out
     scratch += [pltpu.SemaphoreType.DMA((max(n_copies, 1),))]
 
     def body(where_ref, *refs):
@@ -75,7 +75,8 @@
         bufs = held_refs + take(len(needed))
         accs = take(2) if finish else out_refs[:2]
         stored_bufs = take(len(stored))
-        staged = take(int(leave))
+        staged = take(leave * (len(outs) or 2))
+        accs = staged if leave and not jobs else accs
         copies = Copies(refs.pop(0))
         z = where_ref[0]
 
@@ -117,6 +118,8 @@
                     stored_waits[n].wait()
                     term = stored_bufs[n][...] + term
                 acc[...] = term
+                if leave and not jobs and k == len(segs) - 1:
+                    stash_waits.append(copies.start(acc, out_refs[n]))
         if finish:
             scale = jnp.sum(x_refs[inv][...].astype(F32), axis=1, keepdims=True)
             gate = accs[0][...] * scale
@@ -357,12 +360,12 @@
     sums = expert_call(where, weights, [mine], [((0,), 0, EARLY, bulk, 0)])
     sums = expert_call(
         where, weights, [*above, *below],
-        [((0, 1), 1, EARLY, bulk, 0), ((2, 3), 3, EARLY, bulk, 0)], sums,
+        [((0, 1), 1, EARLY, bulk, 0), ((2, 3), 3, EARLY, bulk, 0)], sums, leave=True,
     )
     early_jobs = [(k, 0, EARLY, 0, rows, ((0, 0, rows, k * EARLY),)) for k in range(n_tp)]
     gate_sum, up_sum, scale, *far_held = expert_call(
         where, weights, [early_rows], [((0,), k, 0, EARLY, k * EARLY) for k in range(n_tp)],
-        stored=sums, keep=(0, n_tp * EARLY), stash=(far_segs, far_jobs),
+        stored=sums, keep=(0, n_tp * EARLY), stash=(far_segs, far_jobs[:1]),
     )
     hidden, f_low, f_high, a_high, b_low = expert_call(
         where, weights, [*far, scale], far_segs, (gate_sum, up_sum), inv=2,

time: 183 us -> 184 us (level)
  transfers between devices with their start and end apart: 24 -> 24, of which waited for: 12 -> 13; matrix products, arithmetic and copies ran while one was open for 3% -> 3% of each run, Pallas kernels for 14% -> 14%
where the time goes in v10:
time: 184 us; the launch traced here: 183 us
  waiting for transfers between devices  78.8 us (43%)
  starting transfers between devices  60.8 us (33%)
  Pallas kernels  33.8 us (18%)
  local copies, waits for them, and re-layouts  3.78 us (2%)
  matrix products  2.84 us (2%)
  other arithmetic  2.73 us (1%)
    ppermute x10, waiting for transfers between devices, send_dn(): return lax.ppermute(x, 'tp', dn)  41.3 us
    ppermute x10, waiting for transfers between devices, send_up(): return lax.ppermute(x, 'tp', up)  34.7 us
    all_to_all x4, starting transfers between devices, exchange(): lax.all_to_all(shaped, 'ep', 0, 0, tiled=True).reshape(rows, x.shape[1])  34.1 us
    pallas_call x6, Pallas kernels, expert_call(): pl.pallas_call(body, in_specs=[pl.BlockSpec(memory_space=pltpu.SMEM)] + [...  26.5 us
    ppermute x10, starting transfers between devices, send_dn(): return lax.ppermute(x, 'tp', dn)  22 us
    ppermute x10, starting transfers between devices, send_up(): return lax.ppermute(x, 'tp', up)  4.65 us
  transfers between devices with their start and end apart: 24, of which 13 were waited for; matrix products, arithmetic and copies ran while one was open for 3% of the time, Pallas kernels for 14%

profile of v10, /device:TPU:1, one launch (start us, length us, event | category | flops | bytes accessed | tf_op | source)
XLA Modules:
  0.0 183.0 jit_solution(4382918478199013921)
XLA Ops:
  0.0 2.9 %head.1 = (bf16[512,256]{1,0:T(8,128)(2,1)S(1)}, bf16[512,1280]{1,0:T(8,128)(2,1)}, bf16[256,640]{1,0:T(8,128)(2,1)S(1)}) custom-call(s32[8,256]{1,0:T(8,128)} %bitcast.46, bf16[1792]{0:T(1024)(128)(2,1)} %gain_hbm.1, bf16[256,1792]{1,0:T(8,128)(2,1)} %tokens_hbm.1), custom_call_target="tpu_custom_call" | custom-call | flops 335544320 | bytes 917504 | tf_op jit(solution)/shard_map/head/pallas_call | solution.py:204
  2.9 8.6 %all-to-all-start = ((bf16[32,16,1280]{2,1,0:T(8,128)(2,1)}), bf16[32,16,1280]{2,1,0:T(8,128)(2,1)S(1)}, u32[]{:S(2)}, u32[]{:S(2)}) async-start(bf16[32,16,1280]{2,1,0:T(8,128)(2,1)} %bitcast.4), calls=%async_computation | async-start | bytes 2621440 | tf_op jit(solution)/shard_map/all_to_all | solution.py:334
  11.5 3.8 %collective-permute-start.6 = (bf16[256,640]{1,0:T(8,128)(2,1)S(1)}, bf16[256,640]{1,0:T(8,128)(2,1)S(1)}, u32[]{:S(2)}, u32[]{:S(2)}) collective-permute-start(bf16[256,640]{1,0:T(8,128)(2,1)S(1)} %get-tuple-element.29.refs_0_), channel_id=1, source_target_pairs={{0,3},{1,0},{2,1},{3,2},{4,7},{5,4},{6,5},{7,6},{8,11},{9,8},{10,9... | collective-permute-start | bytes 983048 | tf_op jit(solution)/shard_map/ppermute | solution.py:301
  15.4 6.8 %collective-permute-done.6.refs_1_ = bf16[256,640]{1,0:T(8,128)(2,1)S(1)} collective-permute-done((bf16[256,640]{1,0:T(8,128)(2,1)S(1)}, bf16[256,640]{1,0:T(8,128)(2,1)S(1)}, u32[]{:S(2)}, u32[]{:S(2)}) %collective-permute-start.6) | collective-permute-done | bytes 327712 | tf_op jit(solution)/shard_map/ppermute | solution.py:301
  22.2 3.5 %collective-permute-start.7 = (bf16[128,640]{1,0:T(8,128)(2,1)S(1)}, bf16[128,640]{1,0:T(8,128)(2,1)S(1)}, u32[]{:S(2)}, u32[]{:S(2)}) collective-permute-start(bf16[128,640]{1,0:T(8,128)(2,1)S(1)} %slice.50), channel_id=1, source_target_pairs={{0,3},{1,0},{2,1},{3,2},{4,7},{5,4},{6,5},{7,6},{8,11},{9,8},{10,9... | collective-permute-start | bytes 491528 | tf_op jit(solution)/shard_map/ppermute | solution.py:301
  25.8 1.6 early_near.1.refs_3_
  27.4 0.6 collective-permute-done.7.high
  28.0 3.5 %collective-permute-done.5.low = bf16[128,640]{1,0:T(8,128)(2,1)S(1)} collective-permute-done((bf16[128,640]{1,0:T(8,128)(2,1)S(1)}, bf16[128,640]{1,0:T(8,128)(2,1)S(1)}, u32[]{:S(2)}, u32[]{:S(2)}) %collective-permute-start.5) | collective-permute-done | bytes 163872 | tf_op jit(solution)/shard_map/ppermute | solution.py:298
  31.5 1.3 early_rest.1
  32.8 9.2 %all-to-all-start.1 = ((bf16[32,16,2176]{2,1,0:T(8,128)(2,1)}), bf16[32,16,2176]{2,1,0:T(8,128)(2,1)S(1)}, u32[]{:S(2)}, u32[]{:S(2)}) async-start(bf16[32,16,2176]{2,1,0:T(8,128)(2,1)} %bitcast.7), calls=%async_computation.1 | async-start | bytes 4456448 | tf_op jit(solution)/shard_map/all_to_all | solution.py:334
  42.0 0.9 slice.47
  42.9 0.9 slice.48
  43.8 2.7 %collective-permute-start.2 = (bf16[240,1280]{1,0:T(8,128)(2,1)}, bf16[240,1280]{1,0:T(8,128)(2,1)}, u32[]{:S(2)}, u32[]{:S(2)}) collective-permute-start(bf16[240,1280]{1,0:T(8,128)(2,1)} %bitcast.6), channel_id=1, source_target_pairs={{0,3},{1,0},{2,1},{3,2},{4,7},{5,4},{6,5},{7,6},{8,11},{9,8},{10,9... | collective-permute-start | bytes 1843208 | tf_op jit(solution)/shard_map/ppermute | solution.py:301
  46.5 1.4 collective-permute-start.9
  47.9 13.4 %collective-permute-done.refs_2_ = bf16[272,1280]{1,0:T(8,128)(2,1)} collective-permute-done((bf16[272,1280]{1,0:T(8,128)(2,1)}, bf16[272,1280]{1,0:T(8,128)(2,1)}, u32[]{:S(2)}, u32[]{:S(2)}) %collective-permute-start) | collective-permute-done | bytes 696352 | tf_op jit(solution)/shard_map/ppermute | solution.py:298
  61.4 2.7 %collective-permute-start.3 = (bf16[240,1280]{1,0:T(8,128)(2,1)}, bf16[240,1280]{1,0:T(8,128)(2,1)}, u32[]{:S(2)}, u32[]{:S(2)}) collective-permute-start(bf16[240,1280]{1,0:T(8,128)(2,1)} %collective-permute-done.2.refs_1_), channel_id=1, source_target_pairs={{0,3},{1,0},{2,1},{3,2},{4,7},{5,4},{6,5},{7,6},{8,11},{9,8},{10,9... | collective-permute-start | bytes 1843208 | tf_op jit(solution)/shard_map/ppermute | solution.py:301
  64.1 3.0 %shard_map.73 = (f32[512,512]{1,0:T(8,128)S(1)}, f32[512,512]{1,0:T(8,128)S(1)}) custom-call(s32[1]{0:T(128)} %bitcast.3.where_ref, bf16[512,1280]{1,0:T(8,128)(2,1)S(1)} %bitcast.25, bf16[7168,512]{1,0:T(8,128)(2,1)} %bitcast.27, bf16[7168,512]{1,0:T(8,128)(2,1)} %bitcast.33, bf16[512,7168]{1,0:T(8,128)(2,1)} %bitcast.39), custom_call_target="tpu_custom_call" | custom-call | flops 1342177280 | bytes 5242880 | tf_op jit(solution)/shard_map/pallas_call | solution.py:147
  67.1 7.5 %collective-permute-done.9.refs_3_ = bf16[240,1280]{1,0:T(8,128)(2,1)} collective-permute-done((bf16[240,1280]{1,0:T(8,128)(2,1)}, bf16[240,1280]{1,0:T(8,128)(2,1)}, u32[]{:S(2)}, u32[]{:S(2)}) %collective-permute-start.9) | collective-permute-done | bytes 614432 | tf_op jit(solution)/shard_map/ppermute | solution.py:298
  74.5 6.6 %shard_map.74 = (f32[512,512]{1,0:T(8,128)S(1)}, f32[512,512]{1,0:T(8,128)S(1)}) custom-call(s32[1]{0:T(128)} %bitcast.3.where_ref, bf16[272,1280]{1,0:T(8,128)(2,1)} %collective-permute-done.8.refs_0_, bf16[240,1280]{1,0:T(8,128)(2,1)} %collective-permute-done.2.refs_1_, bf16[272,1280]{1,0:T(8,128)(2,1)} %collective-permute-done.refs_2_, ...), custom_call_target="tpu_custom_call" | custom-call | flops 2684354560 | bytes 10485760 | tf_op jit(solution)/shard_map/pallas_call | solution.py:147
  81.1 1.0 copy-done.2
  82.1 1.0 copy-done.3
  83.1 4.3 %shard_map.75 = (f32[512,512]{1,0:T(8,128)S(1)}, f32[512,512]{1,0:T(8,128)S(1)}, bf16[512,128]{1,0:T(8,128)(2,1)S(1)}, bf16[1280,512]{1,0:T(8,128)(2,1)S(1)}, bf...) custom-call(s32[1]{0:T(128)} %bitcast.3.where_ref, bf16[512,2176]{1,0:T(8,128)(2,1)S(1)} %bitcast.26, ...), custom_call_target="tpu_custom_call" | custom-call | flops 2147483648 | bytes 8388608 | tf_op jit(solution)/shard_map/pallas_call | solution.py:147
  87.6 1.9 %collective-permute-done.1.refs_0_ = bf16[272,1280]{1,0:T(8,128)(2,1)} collective-permute-done((bf16[272,1280]{1,0:T(8,128)(2,1)}, bf16[272,1280]{1,0:T(8,128)(2,1)}, u32[]{:S(2)}, u32[]{:S(2)}) %collective-permute-start.1) | collective-permute-done | bytes 696352 | tf_op jit(solution)/shard_map/ppermute | solution.py:298
  89.5 5.5 %shard_map.76 = (bf16[512,512]{1,0:T(8,128)(2,1)S(1)}, bf16[272,1280]{1,0:T(8,128)(2,1)S(1)}, bf16[240,1280]{1,0:T(8,128)(2,1)S(1)}, bf16[240,1280]{1,0:T(8,128)(2,1)S(1)}, bf16[272,1280]{1,0:T(8,128)(2,1)S(1)}) custom-call(s32[1]{0:T(128)} %bitcast.3.where_ref, bf16[272,1280]{1,0:T(8,128)(2,1)} %collective-permute-done.1.refs_0_, ...), custom_call_target="tpu_custom_call" | custom-call | flops 2684354560 | bytes 10485760 | tf_op jit(solution)/shard_map/pallas_call | solution.py:147
  95.1 3.7 %shard_map.77 = bf16[512,2048]{1,0:T(8,128)(2,1)} custom-call(s32[1]{0:T(128)} %bitcast.3.where_ref, bf16[512,512]{1,0:T(8,128)(2,1)S(1)} %get-tuple-element.40.refs_0_, bf16[7168,512]{1,0:T(8,128)(2,1)} %bitcast.31, bf16[7168,512]{1,0:T(8,128)(2,1)} %bitcast.37, bf16[512,7168]{1,0:T(8,128)(2,1)} %bitcast.43), custom_call_target="tpu_custom_call" | custom-call | flops 1073741824 | bytes 4194304 | tf_op jit(solution)/shard_map/pallas_call | solution.py:147
  98.8 8.2 %all-to-all-start.2 = ((bf16[32,16,2048]{2,1,0:T(8,128)(2,1)}), bf16[32,16,2048]{2,1,0:T(8,128)(2,1)}, u32[]{:S(2)}, u32[]{:S(2)}) async-start(bf16[32,16,2048]{2,1,0:T(8,128)(2,1)} %bitcast.13), calls=%async_computation.2 | async-start | bytes 4194304 | tf_op jit(solution)/shard_map/all_to_all | solution.py:334
  106.9 0.9 collective-permute-start.17
  107.8 2.2 %collective-permute-start.18 = (bf16[240,1280]{1,0:T(8,128)(2,1)S(1)}, bf16[240,1280]{1,0:T(8,128)(2,1)S(1)}, u32[]{:S(2)}, u32[]{:S(2)}) collective-permute-start(bf16[240,1280]{1,0:T(8,128)(2,1)S(1)} %get-tuple-element.48), channel_id=1, source_target_pairs={{0,3},{1,0},{2,1},{3,2},{4,7},{5,4},{6,5},{7,6},{8,11},{9,8},{10,9... | collective-permute-start | bytes 1843208 | tf_op jit(solution)/shard_map/ppermute | solution.py:301
  110.0 1.4 collective-permute-start.16
  111.4 3.4 %shard_map.78 = (bf16[272,1280]{1,0:T(8,128)(2,1)S(1)}, bf16[240,1280]{1,0:T(8,128)(2,1)S(1)}, bf16[272,1280]{1,0:T(8,128)(2,1)S(1)}, bf16[240,1280]{1,0:T(8,128)(2,1)S(1)}) custom-call(s32[1]{0:T(128)} %bitcast.3.where_ref, bf16[512,512]{1,0:T(8,128)(2,1)S(1)} %get-tuple-element.40.refs_0_, bf16[7168,512]{1,0:T(8,128)(2,1)} %bitcast.32, ...), custom_call_target="tpu_custom_call" | custom-call | flops 1342177280 | bytes 5242880 | tf_op jit(solution)/shard_map/pallas_call | solution.py:147
  114.8 1.3 add_convert_fusion
  116.1 0.3 collective-permute-start.15
  116.5 8.0 %collective-permute-done.18 = bf16[240,1280]{1,0:T(8,128)(2,1)S(1)} collective-permute-done((bf16[240,1280]{1,0:T(8,128)(2,1)S(1)}, bf16[240,1280]{1,0:T(8,128)(2,1)S(1)}, u32[]{:S(2)}, u32[]{:S(2)}) %collective-permute-start.18) | collective-permute-done | bytes 614432 | tf_op jit(solution)/shard_map/ppermute | solution.py:301
  124.6 2.0 %collective-permute-start.19 = (bf16[240,1280]{1,0:T(8,128)(2,1)S(1)}, bf16[240,1280]{1,0:T(8,128)(2,1)S(1)}, u32[]{:S(2)}, u32[]{:S(2)}) collective-permute-start(bf16[240,1280]{1,0:T(8,128)(2,1)S(1)} %add_convert_fusion.1), channel_id=1, source_target_pairs={{0,3},{1,0},{2,1},{3,2},{4,7},{5,4},{6,5},{7,6},{8,11},{9,8},{10,9... | collective-permute-start | bytes 1843208 | tf_op jit(solution)/shard_map/ppermute | solution.py:301
  126.8 12.5 %collective-permute-done.16.refs_2_ = bf16[272,1280]{1,0:T(8,128)(2,1)S(1)} collective-permute-done((bf16[272,1280]{1,0:T(8,128)(2,1)S(1)}, bf16[272,1280]{1,0:T(8,128)(2,1)S(1)}, u32[]{:S(2)}, u32[]{:S(2)}) %collective-permute-start.16) | collective-permute-done | bytes 696352 | tf_op jit(solution)/shard_map/ppermute | solution.py:301
  139.3 13.2 %collective-permute-done.19.refs_5_ = bf16[240,1280]{1,0:T(8,128)(2,1)S(1)} collective-permute-done((bf16[240,1280]{1,0:T(8,128)(2,1)S(1)}, bf16[240,1280]{1,0:T(8,128)(2,1)S(1)}, u32[]{:S(2)}, u32[]{:S(2)}) %collective-permute-start.19) | collective-permute-done | bytes 614432 | tf_op jit(solution)/shard_map/ppermute | solution.py:301
  152.5 1.6 join_sums.1
  154.1 8.2 %all-to-all-start.3 = ((bf16[32,16,1280]{2,1,0:T(8,128)(2,1)}), bf16[32,16,1280]{2,1,0:T(8,128)(2,1)S(1)}, u32[]{:S(2)}, u32[]{:S(2)}) async-start(bf16[32,16,1280]{2,1,0:T(8,128)(2,1)} %bitcast.15), calls=%async_computation.3 | async-start | bytes 2621440 | tf_op jit(solution)/shard_map/all_to_all | solution.py:334
  162.2 2.3 %convolution_convert_fusion = bf16[256,2048]{1,0:T(8,128)(2,1)S(1)} fusion(bf16[512,256]{1,0:T(8,128)(2,1)S(1)} %fusion, bf16[512,2048]{1,0:T(8,128)(2,1)} %bitcast.14), kind=kOutput, calls=%fused_computation | convolution fusion | flops 537395200 | bytes 3407872 | tf_op jit(solution)/shard_map/dot_general | solution.py:386
  164.6 1.5 collective-permute-start.10
  166.1 1.2 collective-permute-start.12
  167.3 3.4 %collective-permute-done.10 = bf16[128,512]{1,0:T(8,128)(2,1)S(1)} collective-permute-done((bf16[128,512]{1,0:T(8,128)(2,1)S(1)}, bf16[128,512]{1,0:T(8,128)(2,1)S(1)}, u32[]{:S(2)}, u32[]{:S(2)}) %collective-permute-start.10) | collective-permute-done | bytes 131104 | tf_op jit(solution)/shard_map/ppermute | solution.py:298
  170.8 0.3 collective-permute-start.11
  171.1 2.4 %collective-permute-start.13 = (bf16[256,512]{1,0:T(8,128)(2,1)S(1)}, bf16[256,512]{1,0:T(8,128)(2,1)S(1)}, u32[]{:S(2)}, u32[]{:S(2)}) collective-permute-start(bf16[256,512]{1,0:T(8,128)(2,1)S(1)} %get-tuple-element.50), channel_id=1, source_target_pairs={{0,3},{1,0},{2,1},{3,2},{4,7},{5,4},{6,5},{7,6},{8,11},{9,8},{10,9... | collective-permute-start | bytes 786440 | tf_op jit(solution)/shard_map/ppermute | solution.py:301
  173.5 5.1 %collective-permute-done.11 = bf16[256,512]{1,0:T(8,128)(2,1)S(1)} collective-permute-done((bf16[256,512]{1,0:T(8,128)(2,1)S(1)}, bf16[256,512]{1,0:T(8,128)(2,1)S(1)}, u32[]{:S(2)}, u32[]{:S(2)}) %collective-permute-start.11) | collective-permute-done | bytes 262176 | tf_op jit(solution)/shard_map/ppermute | solution.py:298
  178.7 2.8 %all-to-all-done.3 = bf16[32,16,1280]{2,1,0:T(8,128)(2,1)S(1)} async-done(((bf16[32,16,1280]{2,1,0:T(8,128)(2,1)}), bf16[32,16,1280]{2,1,0:T(8,128)(2,1)S(1)}, u32[]{:S(2)}, u32[]{:S(2)}) %all-to-all-start.3) | async-done | bytes 1310752 | tf_op jit(solution)/shard_map/all_to_all | solution.py:334
  181.5 0.5 convolution_convert_fusion.1
  182.0 1.0 pad_maximum_fusion
  (37 shorter events, 0.9 us)
Async XLA Ops:
  2.9 28.5 %copy-start = (bf16[512,256]{1,0:T(8,128)(2,1)}, bf16[512,256]{1,0:T(8,128)(2,1)S(1)}, u32[]{:S(2)}) copy-start(bf16[512,256]{1,0:T(8,128)(2,1)S(1)} %get-tuple-element.27.pick_ref) | copy-start | bytes 786436
  2.9 29.8 %all-to-all-start = ((bf16[32,16,1280]{2,1,0:T(8,128)(2,1)}), bf16[32,16,1280]{2,1,0:T(8,128)(2,1)S(1)}, u32[]{:S(2)}, u32[]{:S(2)}) async-start(bf16[32,16,1280]{2,1,0:T(8,128)(2,1)} %bitcast.4), calls=%async_computation | async-start | bytes 2621440 | tf_op jit(solution)/shard_map/all_to_all | solution.py:334
  11.5 10.7 %collective-permute-start.6 = (bf16[256,640]{1,0:T(8,128)(2,1)S(1)}, bf16[256,640]{1,0:T(8,128)(2,1)S(1)}, u32[]{:S(2)}, u32[]{:S(2)}) collective-permute-start(bf16[256,640]{1,0:T(8,128)(2,1)S(1)} %get-tuple-element.29.refs_0_), channel_id=1, source_target_pairs={{0,3},{1,0},{2,1},{3,2},{4,7},{5,4},{6,5},{7,6},{8,11},{9,8},{10,9... | collective-permute-start | bytes 983048 | tf_op jit(solution)/shard_map/ppermute | solution.py:301
  15.4 10.3 %collective-permute-start.4 = (bf16[256,640]{1,0:T(8,128)(2,1)S(1)}, bf16[256,640]{1,0:T(8,128)(2,1)S(1)}, u32[]{:S(2)}, u32[]{:S(2)}) collective-permute-start(bf16[256,640]{1,0:T(8,128)(2,1)S(1)} %get-tuple-element.29.refs_0_), channel_id=1, source_target_pairs={{0,1},{1,2},{2,3},{3,0},{4,5},{5,6},{6,7},{7,4},{8,9},{9,10},{10,1... | collective-permute-start | bytes 983048 | tf_op jit(solution)/shard_map/ppermute | solution.py:298
  22.2 5.7 %collective-permute-start.7 = (bf16[128,640]{1,0:T(8,128)(2,1)S(1)}, bf16[128,640]{1,0:T(8,128)(2,1)S(1)}, u32[]{:S(2)}, u32[]{:S(2)}) collective-permute-start(bf16[128,640]{1,0:T(8,128)(2,1)S(1)} %slice.50), channel_id=1, source_target_pairs={{0,3},{1,0},{2,1},{3,2},{4,7},{5,4},{6,5},{7,6},{8,11},{9,8},{10,9... | collective-permute-start | bytes 491528 | tf_op jit(solution)/shard_map/ppermute | solution.py:301
  25.7 5.7 %collective-permute-start.5 = (bf16[128,640]{1,0:T(8,128)(2,1)S(1)}, bf16[128,640]{1,0:T(8,128)(2,1)S(1)}, u32[]{:S(2)}, u32[]{:S(2)}) collective-permute-start(bf16[128,640]{1,0:T(8,128)(2,1)S(1)} %slice.49), channel_id=1, source_target_pairs={{0,1},{1,2},{2,3},{3,0},{4,5},{5,6},{6,7},{7,4},{8,9},{9,10},{10,1... | collective-permute-start | bytes 491528 | tf_op jit(solution)/shard_map/ppermute | solution.py:298
  32.8 50.3 %all-to-all-start.1 = ((bf16[32,16,2176]{2,1,0:T(8,128)(2,1)}), bf16[32,16,2176]{2,1,0:T(8,128)(2,1)S(1)}, u32[]{:S(2)}, u32[]{:S(2)}) async-start(bf16[32,16,2176]{2,1,0:T(8,128)(2,1)} %bitcast.7), calls=%async_computation.1 | async-start | bytes 4456448 | tf_op jit(solution)/shard_map/all_to_all | solution.py:334
  42.9 18.5 %collective-permute-start = (bf16[272,1280]{1,0:T(8,128)(2,1)}, bf16[272,1280]{1,0:T(8,128)(2,1)}, u32[]{:S(2)}, u32[]{:S(2)}) collective-permute-start(bf16[272,1280]{1,0:T(8,128)(2,1)} %bitcast.5), channel_id=1, source_target_pairs={{0,1},{1,2},{2,3},{3,0},{4,5},{5,6},{6,7},{7,4},{8,9},{9,10},{10,1... | collective-permute-start | bytes 2088968 | tf_op jit(solution)/shard_map/ppermute | solution.py:298
  43.8 17.6 %collective-permute-start.2 = (bf16[240,1280]{1,0:T(8,128)(2,1)}, bf16[240,1280]{1,0:T(8,128)(2,1)}, u32[]{:S(2)}, u32[]{:S(2)}) collective-permute-start(bf16[240,1280]{1,0:T(8,128)(2,1)} %bitcast.6), channel_id=1, source_target_pairs={{0,3},{1,0},{2,1},{3,2},{4,7},{5,4},{6,5},{7,6},{8,11},{9,8},{10,9... | collective-permute-start | bytes 1843208 | tf_op jit(solution)/shard_map/ppermute | solution.py:301
  46.5 28.1 %collective-permute-start.8 = (bf16[272,1280]{1,0:T(8,128)(2,1)}, bf16[272,1280]{1,0:T(8,128)(2,1)}, u32[]{:S(2)}, u32[]{:S(2)}) collective-permute-start(bf16[272,1280]{1,0:T(8,128)(2,1)} %bitcast.5), channel_id=1, source_target_pairs={{0,3},{1,0},{2,1},{3,2},{4,7},{5,4},{6,5},{7,6},{8,11},{9,8},{10,9... | collective-permute-start | bytes 2088968 | tf_op jit(solution)/shard_map/ppermute | solution.py:301
  46.5 28.1 %collective-permute-start.9 = (bf16[240,1280]{1,0:T(8,128)(2,1)}, bf16[240,1280]{1,0:T(8,128)(2,1)}, u32[]{:S(2)}, u32[]{:S(2)}) collective-permute-start(bf16[240,1280]{1,0:T(8,128)(2,1)} %bitcast.6), channel_id=1, source_target_pairs={{0,1},{1,2},{2,3},{3,0},{4,5},{5,6},{6,7},{7,4},{8,9},{9,10},{10,1... | collective-permute-start | bytes 1843208 | tf_op jit(solution)/shard_map/ppermute | solution.py:298
  61.4 28.1 %collective-permute-start.1 = (bf16[272,1280]{1,0:T(8,128)(2,1)}, bf16[272,1280]{1,0:T(8,128)(2,1)}, u32[]{:S(2)}, u32[]{:S(2)}) collective-permute-start(bf16[272,1280]{1,0:T(8,128)(2,1)} %collective-permute-done.refs_2_), channel_id=1, source_target_pairs={{0,1},{1,2},{2,3},{3,0},{4,5},{5,6},{6,7},{7,4},{8,9},{9,10},{10,1... | collective-permute-start | bytes 2088968 | tf_op jit(solution)/shard_map/ppermute | solution.py:298
  61.4 26.2 %collective-permute-start.3 = (bf16[240,1280]{1,0:T(8,128)(2,1)}, bf16[240,1280]{1,0:T(8,128)(2,1)}, u32[]{:S(2)}, u32[]{:S(2)}) collective-permute-start(bf16[240,1280]{1,0:T(8,128)(2,1)} %collective-permute-done.2.refs_1_), channel_id=1, source_target_pairs={{0,3},{1,0},{2,1},{3,2},{4,7},{5,4},{6,5},{7,6},{8,11},{9,8},{10,9... | collective-permute-start | bytes 1843208 | tf_op jit(solution)/shard_map/ppermute | solution.py:301
  81.1 1.0 copy-start.2
  82.1 1.0 copy-start.3
  95.0 19.8 %collective-permute-start.14 = (bf16[272,1280]{1,0:T(8,128)(2,1)S(1)}, bf16[272,1280]{1,0:T(8,128)(2,1)}, u32[]{:S(2)}, u32[]{:S(2)}) collective-permute-start(bf16[272,1280]{1,0:T(8,128)(2,1)S(1)} %get-tuple-element.43), channel_id=1, source_target_pairs={{0,1},{1,2},{2,3},{3,0},{4,5},{5,6},{6,7},{7,4},{8,9},{9,10},{10,1... | collective-permute-start | bytes 2088968 | tf_op jit(solution)/shard_map/ppermute | solution.py:298
  98.8 55.3 %all-to-all-start.2 = ((bf16[32,16,2048]{2,1,0:T(8,128)(2,1)}), bf16[32,16,2048]{2,1,0:T(8,128)(2,1)}, u32[]{:S(2)}, u32[]{:S(2)}) async-start(bf16[32,16,2048]{2,1,0:T(8,128)(2,1)} %bitcast.13), calls=%async_computation.2 | async-start | bytes 4194304 | tf_op jit(solution)/shard_map/all_to_all | solution.py:334
  106.9 19.9 %collective-permute-start.17 = (bf16[240,1280]{1,0:T(8,128)(2,1)S(1)}, bf16[240,1280]{1,0:T(8,128)(2,1)S(1)}, u32[]{:S(2)}, u32[]{:S(2)}) collective-permute-start(bf16[240,1280]{1,0:T(8,128)(2,1)S(1)} %get-tuple-element.46), channel_id=1, source_target_pairs={{0,1},{1,2},{2,3},{3,0},{4,5},{5,6},{6,7},{7,4},{8,9},{9,10},{10,1... | collective-permute-start | bytes 1843208 | tf_op jit(solution)/shard_map/ppermute | solution.py:298
  107.8 16.7 %collective-permute-start.18 = (bf16[240,1280]{1,0:T(8,128)(2,1)S(1)}, bf16[240,1280]{1,0:T(8,128)(2,1)S(1)}, u32[]{:S(2)}, u32[]{:S(2)}) collective-permute-start(bf16[240,1280]{1,0:T(8,128)(2,1)S(1)} %get-tuple-element.48), channel_id=1, source_target_pairs={{0,3},{1,0},{2,1},{3,2},{4,7},{5,4},{6,5},{7,6},{8,11},{9,8},{10,9... | collective-permute-start | bytes 1843208 | tf_op jit(solution)/shard_map/ppermute | solution.py:301
  110.0 29.3 %collective-permute-start.16 = (bf16[272,1280]{1,0:T(8,128)(2,1)S(1)}, bf16[272,1280]{1,0:T(8,128)(2,1)S(1)}, u32[]{:S(2)}, u32[]{:S(2)}) collective-permute-start(bf16[272,1280]{1,0:T(8,128)(2,1)S(1)} %get-tuple-element.44), channel_id=1, source_target_pairs={{0,3},{1,0},{2,1},{3,2},{4,7},{5,4},{6,5},{7,6},{8,11},{9,8},{10,9... | collective-permute-start | bytes 2088968 | tf_op jit(solution)/shard_map/ppermute | solution.py:301
  116.1 10.6 %copy-start.5 = (bf16[256,8]{0,1:T(8,128)(2,1)S(1)}, bf16[256,8]{0,1:T(8,128)(2,1)}, u32[]{:S(2)}) copy-start(bf16[256,8]{0,1:T(8,128)(2,1)} %param.10) | copy-start | bytes 12292
  116.1 10.6 %copy-start.4 = (s32[256,8]{0,1:T(8,128)S(1)}, s32[256,8]{0,1:T(8,128)}, u32[]{:S(2)}) copy-start(s32[256,8]{0,1:T(8,128)} %param.9) | copy-start | bytes 24580
  116.1 10.6 %copy-start.1 = (bf16[512,256]{1,0:T(8,128)(2,1)S(1)}, bf16[512,256]{1,0:T(8,128)(2,1)}, u32[]{:S(2)}) copy-start(bf16[512,256]{1,0:T(8,128)(2,1)} %copy-done) | copy-start | bytes 786436
  116.1 36.4 %collective-permute-start.15 = (bf16[272,1280]{1,0:T(8,128)(2,1)S(1)}, bf16[272,1280]{1,0:T(8,128)(2,1)S(1)}, u32[]{:S(2)}, u32[]{:S(2)}) collective-permute-start(bf16[272,1280]{1,0:T(8,128)(2,1)S(1)} %add_convert_fusion), channel_id=1, source_target_pairs={{0,1},{1,2},{2,3},{3,0},{4,5},{5,6},{6,7},{7,4},{8,9},{9,10},{10,1... | collective-permute-start | bytes 2088968 | tf_op jit(solution)/shard_map/ppermute | solution.py:298
  124.6 27.8 %collective-permute-start.19 = (bf16[240,1280]{1,0:T(8,128)(2,1)S(1)}, bf16[240,1280]{1,0:T(8,128)(2,1)S(1)}, u32[]{:S(2)}, u32[]{:S(2)}) collective-permute-start(bf16[240,1280]{1,0:T(8,128)(2,1)S(1)} %add_convert_fusion.1), channel_id=1, source_target_pairs={{0,3},{1,0},{2,1},{3,2},{4,7},{5,4},{6,5},{7,6},{8,11},{9,8},{10,9... | collective-permute-start | bytes 1843208 | tf_op jit(solution)/shard_map/ppermute | solution.py:301
  154.1 27.4 %all-to-all-start.3 = ((bf16[32,16,1280]{2,1,0:T(8,128)(2,1)}), bf16[32,16,1280]{2,1,0:T(8,128)(2,1)S(1)}, u32[]{:S(2)}, u32[]{:S(2)}) async-start(bf16[32,16,1280]{2,1,0:T(8,128)(2,1)} %bitcast.15), calls=%async_computation.3 | async-start | bytes 2621440 | tf_op jit(solution)/shard_map/all_to_all | solution.py:334
  164.6 6.1 %collective-permute-start.10 = (bf16[128,512]{1,0:T(8,128)(2,1)S(1)}, bf16[128,512]{1,0:T(8,128)(2,1)S(1)}, u32[]{:S(2)}, u32[]{:S(2)}) collective-permute-start(bf16[128,512]{1,0:T(8,128)(2,1)S(1)} %get-tuple-element.51), channel_id=1, source_target_pairs={{0,1},{1,2},{2,3},{3,0},{4,5},{5,6},{6,7},{7,4},{8,9},{9,10},{10,1... | collective-permute-start | bytes 393224 | tf_op jit(solution)/shard_map/ppermute | solution.py:298
  166.1 4.6 %collective-permute-start.12 = (bf16[128,512]{1,0:T(8,128)(2,1)S(1)}, bf16[128,512]{1,0:T(8,128)(2,1)S(1)}, u32[]{:S(2)}, u32[]{:S(2)}) collective-permute-start(bf16[128,512]{1,0:T(8,128)(2,1)S(1)} %get-tuple-element.52), channel_id=1, source_target_pairs={{0,3},{1,0},{2,1},{3,2},{4,7},{5,4},{6,5},{7,6},{8,11},{9,8},{10,9... | collective-permute-start | bytes 393224 | tf_op jit(solution)/shard_map/ppermute | solution.py:301
  170.8 7.8 %collective-permute-start.11 = (bf16[256,512]{1,0:T(8,128)(2,1)S(1)}, bf16[256,512]{1,0:T(8,128)(2,1)S(1)}, u32[]{:S(2)}, u32[]{:S(2)}) collective-permute-start(bf16[256,512]{1,0:T(8,128)(2,1)S(1)} %get-tuple-element.49), channel_id=1, source_target_pairs={{0,1},{1,2},{2,3},{3,0},{4,5},{5,6},{6,7},{7,4},{8,9},{9,10},{10,1... | collective-permute-start | bytes 786440 | tf_op jit(solution)/shard_map/ppermute | solution.py:298
  171.1 7.5 %collective-permute-start.13 = (bf16[256,512]{1,0:T(8,128)(2,1)S(1)}, bf16[256,512]{1,0:T(8,128)(2,1)S(1)}, u32[]{:S(2)}, u32[]{:S(2)}) collective-permute-start(bf16[256,512]{1,0:T(8,128)(2,1)S(1)} %get-tuple-element.50), channel_id=1, source_target_pairs={{0,3},{1,0},{2,1},{3,2},{4,7},{5,4},{6,5},{7,6},{8,11},{9,8},{10,9... | collective-permute-start | bytes 786440 | tf_op jit(solution)/shard_map/ppermute | solution.py:301

commit v11 on v10

--- a/solution.py
+++ b/solution.py
@@ -148,7 +148,7 @@
         body,
         in_specs=[pl.BlockSpec(memory_space=pltpu.SMEM)] + [vmem] * len(resident) + [hbm] * len(streamed),
         out_specs=[hbm if leave else vmem] * len(results),
-        out_shape=[jax.ShapeDtypeStruct(s, t) if leave else pltpu.VMEM(s, t) for s, t in results],
+        out_shape=[(pltpu.HBM if leave else pltpu.VMEM)(s, t) for s, t in results],
         scratch_shapes=scratch,
         cost_estimate=pl.CostEstimate(flops=flops, bytes_accessed=flops // 256, transcendentals=0),
         compiler_params=pltpu.CompilerParams(vmem_limit_bytes=20 * 2**20),
@@ -334,7 +334,7 @@
         return lax.all_to_all(shaped, "ep", 0, 0, tiled=True).reshape(rows, x.shape[1])
 
     bulk = tokens.shape[1] - EARLY
-    cut = rows // 2 + CAP
+    cut = rows // 2
     ids, probs = expert_ids.T, gate_prob.T.astype(F32)
     pick, picked_bulk, early = head(tokens, norm_gain, ids, window)
     same = ids[:, None, :] == jnp.arange(window, dtype=jnp.int32)[None, :, None]
@@ -365,10 +365,10 @@
     early_jobs = [(k, 0, EARLY, 0, rows, ((0, 0, rows, k * EARLY),)) for k in range(n_tp)]
     gate_sum, up_sum, scale, *far_held = expert_call(
         where, weights, [early_rows], [((0,), k, 0, EARLY, k * EARLY) for k in range(n_tp)],
-        stored=sums, keep=(0, n_tp * EARLY), stash=(far_segs, far_jobs[:1]),
+        keep=(0, n_tp * EARLY), stash=(far_segs, far_jobs),
     )
     hidden, f_low, f_high, a_high, b_low = expert_call(
-        where, weights, [*far, scale], far_segs, (gate_sum, up_sum), inv=2,
+        where, weights, [*far, scale], far_segs, (gate_sum, up_sum), inv=2, stored=sums,
         jobs=far_jobs, outs=[(cut, bulk), (rows - cut, bulk), (rows - cut, bulk), (cut, bulk)], held=far_held,
     )
     (p_early,) = expert_call(where, weights, hidden=hidden, jobs=early_jobs, outs=[(rows, n_tp * EARLY)], leave=True)

time: 184 us -> 182 us (0.989)
  local copies, waits for them, and re-layouts: 3.78 us -> 1.22 us
  starting transfers between devices: 60.8 us -> 63.1 us
    ppermute x10, starting transfers between devices: 22 us -> 25 us  [send_dn(): return lax.ppermute(x, 'tp', dn)]
    unnamed x12 -> x8, local copies, waits for them, and re-layouts: 1.96 us -> 0.02 us
  transfers between devices with their start and end apart: 24 -> 24, of which waited for: 13 -> 14; matrix products, arithmetic and copies ran while one was open for 3% -> 3% of each run, Pallas kernels for 14% -> 14%
where the time goes in v11:
time: 182 us; the launch traced here: 181 us
  waiting for transfers between devices  77 us (42%)
  starting transfers between devices  63.1 us (35%)
  Pallas kernels  34.3 us (19%)
  matrix products  2.84 us (2%)
  other arithmetic  2.71 us (1%)
    ppermute x10, waiting for transfers between devices, send_dn(): return lax.ppermute(x, 'tp', dn)  42 us
    all_to_all x4, starting transfers between devices, exchange(): lax.all_to_all(shaped, 'ep', 0, 0, tiled=True).reshape(rows, x.shape[1])  34.1 us
    ppermute x10, waiting for transfers between devices, send_up(): return lax.ppermute(x, 'tp', up)  33.8 us
    pallas_call x6, Pallas kernels, expert_call(): pl.pallas_call(body, in_specs=[pl.BlockSpec(memory_space=pltpu.SMEM)] + [...  26.9 us
    ppermute x10, starting transfers between devices, send_dn(): return lax.ppermute(x, 'tp', dn)  25 us
    ppermute x10, starting transfers between devices, send_up(): return lax.ppermute(x, 'tp', up)  3.98 us
  transfers between devices with their start and end apart: 24, of which 14 were waited for; matrix products, arithmetic and copies ran while one was open for 3% of the time, Pallas kernels for 14%

profile of v11, /device:TPU:1, one launch (start us, length us, event | category | flops | bytes accessed | tf_op | source)
XLA Modules:
  0.0 181.4 jit_solution(10976397095790105721)
XLA Ops:
  0.0 2.9 %head.1 = (bf16[512,256]{1,0:T(8,128)(2,1)S(1)}, bf16[512,1280]{1,0:T(8,128)(2,1)}, bf16[256,640]{1,0:T(8,128)(2,1)S(1)}) custom-call(s32[8,256]{1,0:T(8,128)} %bitcast.44, bf16[1792]{0:T(1024)(128)(2,1)} %gain_hbm.1, bf16[256,1792]{1,0:T(8,128)(2,1)} %tokens_hbm.1), custom_call_target="tpu_custom_call" | custom-call | flops 335544320 | bytes 917504 | tf_op jit(solution)/shard_map/head/pallas_call | solution.py:204
  2.9 8.6 %all-to-all-start = ((bf16[32,16,1280]{2,1,0:T(8,128)(2,1)}), bf16[32,16,1280]{2,1,0:T(8,128)(2,1)S(1)}, u32[]{:S(2)}, u32[]{:S(2)}) async-start(bf16[32,16,1280]{2,1,0:T(8,128)(2,1)} %bitcast.4), calls=%async_computation | async-start | bytes 2621440 | tf_op jit(solution)/shard_map/all_to_all | solution.py:334
  11.5 3.8 %collective-permute-start.6 = (bf16[256,640]{1,0:T(8,128)(2,1)S(1)}, bf16[256,640]{1,0:T(8,128)(2,1)S(1)}, u32[]{:S(2)}, u32[]{:S(2)}) collective-permute-start(bf16[256,640]{1,0:T(8,128)(2,1)S(1)} %get-tuple-element.31.refs_0_), channel_id=1, source_target_pairs={{0,3},{1,0},{2,1},{3,2},{4,7},{5,4},{6,5},{7,6},{8,11},{9,8},{10,9... | collective-permute-start | bytes 983048 | tf_op jit(solution)/shard_map/ppermute | solution.py:301
  15.4 6.8 %collective-permute-done.6.refs_1_ = bf16[256,640]{1,0:T(8,128)(2,1)S(1)} collective-permute-done((bf16[256,640]{1,0:T(8,128)(2,1)S(1)}, bf16[256,640]{1,0:T(8,128)(2,1)S(1)}, u32[]{:S(2)}, u32[]{:S(2)}) %collective-permute-start.6) | collective-permute-done | bytes 327712 | tf_op jit(solution)/shard_map/ppermute | solution.py:301
  22.2 3.5 %collective-permute-start.7 = (bf16[128,640]{1,0:T(8,128)(2,1)S(1)}, bf16[128,640]{1,0:T(8,128)(2,1)S(1)}, u32[]{:S(2)}, u32[]{:S(2)}) collective-permute-start(bf16[128,640]{1,0:T(8,128)(2,1)S(1)} %slice.50), channel_id=1, source_target_pairs={{0,3},{1,0},{2,1},{3,2},{4,7},{5,4},{6,5},{7,6},{8,11},{9,8},{10,9... | collective-permute-start | bytes 491528 | tf_op jit(solution)/shard_map/ppermute | solution.py:301
  25.8 1.6 early_near.1.refs_3_
  27.4 0.6 collective-permute-done.7.high
  27.9 3.5 %collective-permute-done.5.low = bf16[128,640]{1,0:T(8,128)(2,1)S(1)} collective-permute-done((bf16[128,640]{1,0:T(8,128)(2,1)S(1)}, bf16[128,640]{1,0:T(8,128)(2,1)S(1)}, u32[]{:S(2)}, u32[]{:S(2)}) %collective-permute-start.5) | collective-permute-done | bytes 163872 | tf_op jit(solution)/shard_map/ppermute | solution.py:298
  31.5 1.3 early_rest.1
  32.8 9.2 %all-to-all-start.1 = ((bf16[32,16,2176]{2,1,0:T(8,128)(2,1)}), bf16[32,16,2176]{2,1,0:T(8,128)(2,1)S(1)}, u32[]{:S(2)}, u32[]{:S(2)}) async-start(bf16[32,16,2176]{2,1,0:T(8,128)(2,1)} %bitcast.7), calls=%async_computation.1 | async-start | bytes 4456448 | tf_op jit(solution)/shard_map/all_to_all | solution.py:334
  42.0 1.1 fusion.1
  43.2 2.7 %collective-permute-start.2 = (bf16[256,1280]{1,0:T(8,128)(2,1)}, bf16[256,1280]{1,0:T(8,128)(2,1)}, u32[]{:S(2)}, u32[]{:S(2)}) collective-permute-start(bf16[256,1280]{1,0:T(8,128)(2,1)} %bitcast.6), channel_id=1, source_target_pairs={{0,3},{1,0},{2,1},{3,2},{4,7},{5,4},{6,5},{7,6},{8,11},{9,8},{10,9... | collective-permute-start | bytes 1966088 | tf_op jit(solution)/shard_map/ppermute | solution.py:301
  45.9 1.4 collective-permute-start.9
  47.3 13.4 %collective-permute-done.refs_2_ = bf16[256,1280]{1,0:T(8,128)(2,1)} collective-permute-done((bf16[256,1280]{1,0:T(8,128)(2,1)}, bf16[256,1280]{1,0:T(8,128)(2,1)}, u32[]{:S(2)}, u32[]{:S(2)}) %collective-permute-start) | collective-permute-done | bytes 655392 | tf_op jit(solution)/shard_map/ppermute | solution.py:298
  60.8 2.7 %collective-permute-start.3 = (bf16[256,1280]{1,0:T(8,128)(2,1)}, bf16[256,1280]{1,0:T(8,128)(2,1)}, u32[]{:S(2)}, u32[]{:S(2)}) collective-permute-start(bf16[256,1280]{1,0:T(8,128)(2,1)} %collective-permute-done.2.refs_1_), channel_id=1, source_target_pairs={{0,3},{1,0},{2,1},{3,2},{4,7},{5,4},{6,5},{7,6},{8,11},{9,8},{10,9... | collective-permute-start | bytes 1966088 | tf_op jit(solution)/shard_map/ppermute | solution.py:301
  63.4 3.0 %shard_map.74 = (f32[512,512]{1,0:T(8,128)S(1)}, f32[512,512]{1,0:T(8,128)S(1)}) custom-call(s32[1]{0:T(128)} %bitcast.3.where_ref, bf16[512,1280]{1,0:T(8,128)(2,1)S(1)} %bitcast.25, bf16[7168,512]{1,0:T(8,128)(2,1)} %bitcast.27, bf16[7168,512]{1,0:T(8,128)(2,1)} %bitcast.32, bf16[512,7168]{1,0:T(8,128)(2,1)} %bitcast.37), custom_call_target="tpu_custom_call" | custom-call | flops 1342177280 | bytes 5242880 | tf_op jit(solution)/shard_map/pallas_call | solution.py:147
  66.5 7.3 %collective-permute-done.8.refs_0_ = bf16[256,1280]{1,0:T(8,128)(2,1)} collective-permute-done((bf16[256,1280]{1,0:T(8,128)(2,1)}, bf16[256,1280]{1,0:T(8,128)(2,1)}, u32[]{:S(2)}, u32[]{:S(2)}) %collective-permute-start.8) | collective-permute-done | bytes 655392 | tf_op jit(solution)/shard_map/ppermute | solution.py:301
  73.8 1.0 collective-permute-done.9.refs_3_
  74.8 7.4 %shard_map.75 = (f32[512,512]{1,0:T(8,128)}, f32[512,512]{1,0:T(8,128)}) custom-call(s32[1]{0:T(128)} %bitcast.3.where_ref, bf16[256,1280]{1,0:T(8,128)(2,1)} %collective-permute-done.8.refs_0_, bf16[256,1280]{1,0:T(8,128)(2,1)} %collective-permute-done.2.refs_1_, bf16[256,1280]{1,0:T(8,128)(2,1)} %collective-permute-done.refs_2_, ...), custom_call_target="tpu_custom_call" | custom-call | flops 2684354560 | bytes 10485760 | tf_op jit(solution)/shard_map/pallas_call | solution.py:147
  82.2 4.2 %shard_map.73 = (f32[512,512]{1,0:T(8,128)S(1)}, f32[512,512]{1,0:T(8,128)S(1)}, bf16[512,128]{1,0:T(8,128)(2,1)S(1)}, bf16[1280,512]{1,0:T(8,128)(2,1)S(1)}, bf...) custom-call(s32[1]{0:T(128)} %bitcast.3.where_ref, ...), custom_call_target="tpu_custom_call" | custom-call | flops 2147483648 | bytes 8388608 | tf_op jit(solution)/shard_map/pallas_call | solution.py:147
  86.4 2.4 %collective-permute-done.1.refs_0_ = bf16[256,1280]{1,0:T(8,128)(2,1)} collective-permute-done((bf16[256,1280]{1,0:T(8,128)(2,1)}, bf16[256,1280]{1,0:T(8,128)(2,1)}, u32[]{:S(2)}, u32[]{:S(2)}) %collective-permute-start.1) | collective-permute-done | bytes 655392 | tf_op jit(solution)/shard_map/ppermute | solution.py:298
  88.8 5.2 %shard_map.76 = (bf16[512,512]{1,0:T(8,128)(2,1)S(1)}, bf16[256,1280]{1,0:T(8,128)(2,1)S(1)}, bf16[256,1280]{1,0:T(8,128)(2,1)S(1)}, bf16[256,1280]{1,0:T(8,128)(2,1)S(1)}, bf16[256,1280]{1,0:T(8,128)(2,1)S(1)}) custom-call(s32[1]{0:T(128)} %bitcast.3.where_ref, bf16[256,1280]{1,0:T(8,128)(2,1)} %collective-permute-done.1.refs_0_, ...), custom_call_target="tpu_custom_call" | custom-call | flops 2684354560 | bytes 10485760 | tf_op jit(solution)/shard_map/pallas_call | solution.py:147
  94.1 3.7 %shard_map.77 = bf16[512,2048]{1,0:T(8,128)(2,1)} custom-call(s32[1]{0:T(128)} %bitcast.3.where_ref, bf16[512,512]{1,0:T(8,128)(2,1)S(1)} %get-tuple-element.44.refs_0_, bf16[7168,512]{1,0:T(8,128)(2,1)} %bitcast.30, bf16[7168,512]{1,0:T(8,128)(2,1)} %bitcast.35, bf16[512,7168]{1,0:T(8,128)(2,1)} %bitcast.40), custom_call_target="tpu_custom_call" | custom-call | flops 1073741824 | bytes 4194304 | tf_op jit(solution)/shard_map/pallas_call | solution.py:147
  97.9 8.2 %all-to-all-start.2 = ((bf16[32,16,2048]{2,1,0:T(8,128)(2,1)}), bf16[32,16,2048]{2,1,0:T(8,128)(2,1)}, u32[]{:S(2)}, u32[]{:S(2)}) async-start(bf16[32,16,2048]{2,1,0:T(8,128)(2,1)} %bitcast.42), calls=%async_computation.2 | async-start | bytes 4194304 | tf_op jit(solution)/shard_map/all_to_all | solution.py:334
  106.0 3.0 %collective-permute-start.18 = (bf16[256,1280]{1,0:T(8,128)(2,1)S(1)}, bf16[256,1280]{1,0:T(8,128)(2,1)S(1)}, u32[]{:S(2)}, u32[]{:S(2)}) collective-permute-start(bf16[256,1280]{1,0:T(8,128)(2,1)S(1)} %get-tuple-element.52), channel_id=1, source_target_pairs={{0,3},{1,0},{2,1},{3,2},{4,7},{5,4},{6,5},{7,6},{8,11},{9,8},{10,9... | collective-permute-start | bytes 1966088 | tf_op jit(solution)/shard_map/ppermute | solution.py:301
  109.0 1.5 collective-permute-start.16
  110.5 3.3 %shard_map.78 = (bf16[256,1280]{1,0:T(8,128)(2,1)S(1)}, bf16[256,1280]{1,0:T(8,128)(2,1)S(1)}, bf16[256,1280]{1,0:T(8,128)(2,1)S(1)}, bf16[256,1280]{1,0:T(8,128)(2,1)S(1)}) custom-call(s32[1]{0:T(128)} %bitcast.3.where_ref, bf16[512,512]{1,0:T(8,128)(2,1)S(1)} %get-tuple-element.44.refs_0_, bf16[7168,512]{1,0:T(8,128)(2,1)} %bitcast.31, ...), custom_call_target="tpu_custom_call" | custom-call | flops 1342177280 | bytes 5242880 | tf_op jit(solution)/shard_map/pallas_call | solution.py:147
  113.9 1.2 add_convert_fusion.1
  115.2 7.6 %collective-permute-done.18 = bf16[256,1280]{1,0:T(8,128)(2,1)S(1)} collective-permute-done((bf16[256,1280]{1,0:T(8,128)(2,1)S(1)}, bf16[256,1280]{1,0:T(8,128)(2,1)S(1)}, u32[]{:S(2)}, u32[]{:S(2)}) %collective-permute-start.18) | collective-permute-done | bytes 655392 | tf_op jit(solution)/shard_map/ppermute | solution.py:301
  122.8 0.2 add_convert_fusion
  123.0 3.8 %collective-permute-start.19 = (bf16[256,1280]{1,0:T(8,128)(2,1)S(1)}, bf16[256,1280]{1,0:T(8,128)(2,1)S(1)}, u32[]{:S(2)}, u32[]{:S(2)}) collective-permute-start(bf16[256,1280]{1,0:T(8,128)(2,1)S(1)} %add_convert_fusion), channel_id=1, source_target_pairs={{0,3},{1,0},{2,1},{3,2},{4,7},{5,4},{6,5},{7,6},{8,11},{9,8},{10,9... | collective-permute-start | bytes 1966088 | tf_op jit(solution)/shard_map/ppermute | solution.py:301
  126.9 9.9 %collective-permute-done.16.refs_2_ = bf16[256,1280]{1,0:T(8,128)(2,1)S(1)} collective-permute-done((bf16[256,1280]{1,0:T(8,128)(2,1)S(1)}, bf16[256,1280]{1,0:T(8,128)(2,1)S(1)}, u32[]{:S(2)}, u32[]{:S(2)}) %collective-permute-start.16) | collective-permute-done | bytes 655392 | tf_op jit(solution)/shard_map/ppermute | solution.py:301
  136.8 4.3 %collective-permute-done.15.refs_1_ = bf16[256,1280]{1,0:T(8,128)(2,1)S(1)} collective-permute-done((bf16[256,1280]{1,0:T(8,128)(2,1)S(1)}, bf16[256,1280]{1,0:T(8,128)(2,1)S(1)}, u32[]{:S(2)}, u32[]{:S(2)}) %collective-permute-start.15) | collective-permute-done | bytes 655392 | tf_op jit(solution)/shard_map/ppermute | solution.py:298
  141.2 9.7 %collective-permute-done.19.refs_5_ = bf16[256,1280]{1,0:T(8,128)(2,1)S(1)} collective-permute-done((bf16[256,1280]{1,0:T(8,128)(2,1)S(1)}, bf16[256,1280]{1,0:T(8,128)(2,1)S(1)}, u32[]{:S(2)}, u32[]{:S(2)}) %collective-permute-start.19) | collective-permute-done | bytes 655392 | tf_op jit(solution)/shard_map/ppermute | solution.py:301
  150.9 1.6 join_sums.1
  152.5 8.2 %all-to-all-start.3 = ((bf16[32,16,1280]{2,1,0:T(8,128)(2,1)}), bf16[32,16,1280]{2,1,0:T(8,128)(2,1)S(1)}, u32[]{:S(2)}, u32[]{:S(2)}) async-start(bf16[32,16,1280]{2,1,0:T(8,128)(2,1)} %bitcast.15), calls=%async_computation.3 | async-start | bytes 2621440 | tf_op jit(solution)/shard_map/all_to_all | solution.py:334
  160.6 2.3 %convolution_convert_fusion = bf16[256,2048]{1,0:T(8,128)(2,1)S(1)} fusion(bf16[512,256]{1,0:T(8,128)(2,1)S(1)} %fusion, bf16[512,2048]{1,0:T(8,128)(2,1)} %bitcast.14), kind=kOutput, calls=%fused_computation | convolution fusion | flops 537395200 | bytes 3407872 | tf_op jit(solution)/shard_map/dot_general | solution.py:386
  163.0 1.7 collective-permute-start.10
  164.7 1.9 %collective-permute-start.12 = (bf16[128,512]{1,0:T(8,128)(2,1)S(1)}, bf16[128,512]{1,0:T(8,128)(2,1)S(1)}, u32[]{:S(2)}, u32[]{:S(2)}) collective-permute-start(bf16[128,512]{1,0:T(8,128)(2,1)S(1)} %get-tuple-element.58), channel_id=1, source_target_pairs={{0,3},{1,0},{2,1},{3,2},{4,7},{5,4},{6,5},{7,6},{8,11},{9,8},{10,9... | collective-permute-start | bytes 393224 | tf_op jit(solution)/shard_map/ppermute | solution.py:301
  166.6 3.6 %collective-permute-done.10 = bf16[128,512]{1,0:T(8,128)(2,1)S(1)} collective-permute-done((bf16[128,512]{1,0:T(8,128)(2,1)S(1)}, bf16[128,512]{1,0:T(8,128)(2,1)S(1)}, u32[]{:S(2)}, u32[]{:S(2)}) %collective-permute-start.10) | collective-permute-done | bytes 131104 | tf_op jit(solution)/shard_map/ppermute | solution.py:298
  170.1 0.1 add_convert_fusion.4
  170.2 0.6 collective-permute-start.11
  170.8 2.1 %collective-permute-start.13 = (bf16[256,512]{1,0:T(8,128)(2,1)S(1)}, bf16[256,512]{1,0:T(8,128)(2,1)S(1)}, u32[]{:S(2)}, u32[]{:S(2)}) collective-permute-start(bf16[256,512]{1,0:T(8,128)(2,1)S(1)} %get-tuple-element.56), channel_id=1, source_target_pairs={{0,3},{1,0},{2,1},{3,2},{4,7},{5,4},{6,5},{7,6},{8,11},{9,8},{10,9... | collective-permute-start | bytes 786440 | tf_op jit(solution)/shard_map/ppermute | solution.py:301
  173.0 5.6 %collective-permute-done.11 = bf16[256,512]{1,0:T(8,128)(2,1)S(1)} collective-permute-done((bf16[256,512]{1,0:T(8,128)(2,1)S(1)}, bf16[256,512]{1,0:T(8,128)(2,1)S(1)}, u32[]{:S(2)}, u32[]{:S(2)}) %collective-permute-start.11) | collective-permute-done | bytes 262176 | tf_op jit(solution)/shard_map/ppermute | solution.py:298
  178.6 0.1 add_convert_fusion.2
  178.7 1.2 all-to-all-done.3
  179.9 0.5 convolution_convert_fusion.1
  180.4 1.0 pad_maximum_fusion
  (32 shorter events, 0.5 us)
Async XLA Ops:
  2.9 28.5 %copy-start = (bf16[512,256]{1,0:T(8,128)(2,1)}, bf16[512,256]{1,0:T(8,128)(2,1)S(1)}, u32[]{:S(2)}) copy-start(bf16[512,256]{1,0:T(8,128)(2,1)S(1)} %get-tuple-element.29.pick_ref) | copy-start | bytes 786436
  2.9 29.8 %all-to-all-start = ((bf16[32,16,1280]{2,1,0:T(8,128)(2,1)}), bf16[32,16,1280]{2,1,0:T(8,128)(2,1)S(1)}, u32[]{:S(2)}, u32[]{:S(2)}) async-start(bf16[32,16,1280]{2,1,0:T(8,128)(2,1)} %bitcast.4), calls=%async_computation | async-start | bytes 2621440 | tf_op jit(solution)/shard_map/all_to_all | solution.py:334
  11.5 10.7 %collective-permute-start.6 = (bf16[256,640]{1,0:T(8,128)(2,1)S(1)}, bf16[256,640]{1,0:T(8,128)(2,1)S(1)}, u32[]{:S(2)}, u32[]{:S(2)}) collective-permute-start(bf16[256,640]{1,0:T(8,128)(2,1)S(1)} %get-tuple-element.31.refs_0_), channel_id=1, source_target_pairs={{0,3},{1,0},{2,1},{3,2},{4,7},{5,4},{6,5},{7,6},{8,11},{9,8},{10,9... | collective-permute-start | bytes 983048 | tf_op jit(solution)/shard_map/ppermute | solution.py:301
  15.4 10.3 %collective-permute-start.4 = (bf16[256,640]{1,0:T(8,128)(2,1)S(1)}, bf16[256,640]{1,0:T(8,128)(2,1)S(1)}, u32[]{:S(2)}, u32[]{:S(2)}) collective-permute-start(bf16[256,640]{1,0:T(8,128)(2,1)S(1)} %get-tuple-element.31.refs_0_), channel_id=1, source_target_pairs={{0,1},{1,2},{2,3},{3,0},{4,5},{5,6},{6,7},{7,4},{8,9},{9,10},{10,1... | collective-permute-start | bytes 983048 | tf_op jit(solution)/shard_map/ppermute | solution.py:298
  22.2 5.7 %collective-permute-start.7 = (bf16[128,640]{1,0:T(8,128)(2,1)S(1)}, bf16[128,640]{1,0:T(8,128)(2,1)S(1)}, u32[]{:S(2)}, u32[]{:S(2)}) collective-permute-start(bf16[128,640]{1,0:T(8,128)(2,1)S(1)} %slice.50), channel_id=1, source_target_pairs={{0,3},{1,0},{2,1},{3,2},{4,7},{5,4},{6,5},{7,6},{8,11},{9,8},{10,9... | collective-permute-start | bytes 491528 | tf_op jit(solution)/shard_map/ppermute | solution.py:301
  25.7 5.7 %collective-permute-start.5 = (bf16[128,640]{1,0:T(8,128)(2,1)S(1)}, bf16[128,640]{1,0:T(8,128)(2,1)S(1)}, u32[]{:S(2)}, u32[]{:S(2)}) collective-permute-start(bf16[128,640]{1,0:T(8,128)(2,1)S(1)} %slice.49), channel_id=1, source_target_pairs={{0,1},{1,2},{2,3},{3,0},{4,5},{5,6},{6,7},{7,4},{8,9},{9,10},{10,1... | collective-permute-start | bytes 491528 | tf_op jit(solution)/shard_map/ppermute | solution.py:298
  32.8 49.4 %all-to-all-start.1 = ((bf16[32,16,2176]{2,1,0:T(8,128)(2,1)}), bf16[32,16,2176]{2,1,0:T(8,128)(2,1)S(1)}, u32[]{:S(2)}, u32[]{:S(2)}) async-start(bf16[32,16,2176]{2,1,0:T(8,128)(2,1)} %bitcast.7), calls=%async_computation.1 | async-start | bytes 4456448 | tf_op jit(solution)/shard_map/all_to_all | solution.py:334
  43.2 17.6 %collective-permute-start = (bf16[256,1280]{1,0:T(8,128)(2,1)}, bf16[256,1280]{1,0:T(8,128)(2,1)}, u32[]{:S(2)}, u32[]{:S(2)}) collective-permute-start(bf16[256,1280]{1,0:T(8,128)(2,1)} %bitcast.5), channel_id=1, source_target_pairs={{0,1},{1,2},{2,3},{3,0},{4,5},{5,6},{6,7},{7,4},{8,9},{9,10},{10,1... | collective-permute-start | bytes 1966088 | tf_op jit(solution)/shard_map/ppermute | solution.py:298
  43.2 17.6 %collective-permute-start.2 = (bf16[256,1280]{1,0:T(8,128)(2,1)}, bf16[256,1280]{1,0:T(8,128)(2,1)}, u32[]{:S(2)}, u32[]{:S(2)}) collective-permute-start(bf16[256,1280]{1,0:T(8,128)(2,1)} %bitcast.6), channel_id=1, source_target_pairs={{0,3},{1,0},{2,1},{3,2},{4,7},{5,4},{6,5},{7,6},{8,11},{9,8},{10,9... | collective-permute-start | bytes 1966088 | tf_op jit(solution)/shard_map/ppermute | solution.py:301
  45.8 27.9 %collective-permute-start.8 = (bf16[256,1280]{1,0:T(8,128)(2,1)}, bf16[256,1280]{1,0:T(8,128)(2,1)}, u32[]{:S(2)}, u32[]{:S(2)}) collective-permute-start(bf16[256,1280]{1,0:T(8,128)(2,1)} %bitcast.5), channel_id=1, source_target_pairs={{0,3},{1,0},{2,1},{3,2},{4,7},{5,4},{6,5},{7,6},{8,11},{9,8},{10,9... | collective-permute-start | bytes 1966088 | tf_op jit(solution)/shard_map/ppermute | solution.py:301
  45.9 28.9 %collective-permute-start.9 = (bf16[256,1280]{1,0:T(8,128)(2,1)}, bf16[256,1280]{1,0:T(8,128)(2,1)}, u32[]{:S(2)}, u32[]{:S(2)}) collective-permute-start(bf16[256,1280]{1,0:T(8,128)(2,1)} %bitcast.6), channel_id=1, source_target_pairs={{0,1},{1,2},{2,3},{3,0},{4,5},{5,6},{6,7},{7,4},{8,9},{9,10},{10,1... | collective-permute-start | bytes 1966088 | tf_op jit(solution)/shard_map/ppermute | solution.py:298
  60.8 28.1 %collective-permute-start.1 = (bf16[256,1280]{1,0:T(8,128)(2,1)}, bf16[256,1280]{1,0:T(8,128)(2,1)}, u32[]{:S(2)}, u32[]{:S(2)}) collective-permute-start(bf16[256,1280]{1,0:T(8,128)(2,1)} %collective-permute-done.refs_2_), channel_id=1, source_target_pairs={{0,1},{1,2},{2,3},{3,0},{4,5},{5,6},{6,7},{7,4},{8,9},{9,10},{10,1... | collective-permute-start | bytes 1966088 | tf_op jit(solution)/shard_map/ppermute | solution.py:298
  60.8 28.1 %collective-permute-start.3 = (bf16[256,1280]{1,0:T(8,128)(2,1)}, bf16[256,1280]{1,0:T(8,128)(2,1)}, u32[]{:S(2)}, u32[]{:S(2)}) collective-permute-start(bf16[256,1280]{1,0:T(8,128)(2,1)} %collective-permute-done.2.refs_1_), channel_id=1, source_target_pairs={{0,3},{1,0},{2,1},{3,2},{4,7},{5,4},{6,5},{7,6},{8,11},{9,8},{10,9... | collective-permute-start | bytes 1966088 | tf_op jit(solution)/shard_map/ppermute | solution.py:301
  94.1 19.8 %collective-permute-start.14 = (bf16[256,1280]{1,0:T(8,128)(2,1)S(1)}, bf16[256,1280]{1,0:T(8,128)(2,1)}, u32[]{:S(2)}, u32[]{:S(2)}) collective-permute-start(bf16[256,1280]{1,0:T(8,128)(2,1)S(1)} %get-tuple-element.47), channel_id=1, source_target_pairs={{0,1},{1,2},{2,3},{3,0},{4,5},{5,6},{6,7},{7,4},{8,9},{9,10},{10,1... | collective-permute-start | bytes 1966088 | tf_op jit(solution)/shard_map/ppermute | solution.py:298
  97.9 54.6 %all-to-all-start.2 = ((bf16[32,16,2048]{2,1,0:T(8,128)(2,1)}), bf16[32,16,2048]{2,1,0:T(8,128)(2,1)}, u32[]{:S(2)}, u32[]{:S(2)}) async-start(bf16[32,16,2048]{2,1,0:T(8,128)(2,1)} %bitcast.42), calls=%async_computation.2 | async-start | bytes 4194304 | tf_op jit(solution)/shard_map/all_to_all | solution.py:334
  106.0 16.8 %collective-permute-start.18 = (bf16[256,1280]{1,0:T(8,128)(2,1)S(1)}, bf16[256,1280]{1,0:T(8,128)(2,1)S(1)}, u32[]{:S(2)}, u32[]{:S(2)}) collective-permute-start(bf16[256,1280]{1,0:T(8,128)(2,1)S(1)} %get-tuple-element.52), channel_id=1, source_target_pairs={{0,3},{1,0},{2,1},{3,2},{4,7},{5,4},{6,5},{7,6},{8,11},{9,8},{10,9... | collective-permute-start | bytes 1966088 | tf_op jit(solution)/shard_map/ppermute | solution.py:301
  109.0 27.8 %collective-permute-start.16 = (bf16[256,1280]{1,0:T(8,128)(2,1)S(1)}, bf16[256,1280]{1,0:T(8,128)(2,1)S(1)}, u32[]{:S(2)}, u32[]{:S(2)}) collective-permute-start(bf16[256,1280]{1,0:T(8,128)(2,1)S(1)} %get-tuple-element.48), channel_id=1, source_target_pairs={{0,3},{1,0},{2,1},{3,2},{4,7},{5,4},{6,5},{7,6},{8,11},{9,8},{10,9... | collective-permute-start | bytes 1966088 | tf_op jit(solution)/shard_map/ppermute | solution.py:301
  110.5 26.4 %collective-permute-start.17 = (bf16[256,1280]{1,0:T(8,128)(2,1)S(1)}, bf16[256,1280]{1,0:T(8,128)(2,1)S(1)}, u32[]{:S(2)}, u32[]{:S(2)}) collective-permute-start(bf16[256,1280]{1,0:T(8,128)(2,1)S(1)} %get-tuple-element.50), channel_id=1, source_target_pairs={{0,1},{1,2},{2,3},{3,0},{4,5},{5,6},{6,7},{7,4},{8,9},{9,10},{10,1... | collective-permute-start | bytes 1966088 | tf_op jit(solution)/shard_map/ppermute | solution.py:298
  115.1 11.7 %copy-start.3 = (bf16[256,8]{0,1:T(8,128)(2,1)S(1)}, bf16[256,8]{0,1:T(8,128)(2,1)}, u32[]{:S(2)}) copy-start(bf16[256,8]{0,1:T(8,128)(2,1)} %param.10) | copy-start | bytes 12292
  115.1 11.7 %copy-start.2 = (s32[256,8]{0,1:T(8,128)S(1)}, s32[256,8]{0,1:T(8,128)}, u32[]{:S(2)}) copy-start(s32[256,8]{0,1:T(8,128)} %param.9) | copy-start | bytes 24580
  115.1 11.7 %copy-start.1 = (bf16[512,256]{1,0:T(8,128)(2,1)S(1)}, bf16[512,256]{1,0:T(8,128)(2,1)}, u32[]{:S(2)}) copy-start(bf16[512,256]{1,0:T(8,128)(2,1)} %copy-done) | copy-start | bytes 786436
  115.1 26.0 %collective-permute-start.15 = (bf16[256,1280]{1,0:T(8,128)(2,1)S(1)}, bf16[256,1280]{1,0:T(8,128)(2,1)S(1)}, u32[]{:S(2)}, u32[]{:S(2)}) collective-permute-start(bf16[256,1280]{1,0:T(8,128)(2,1)S(1)} %add_convert_fusion.1), channel_id=1, source_target_pairs={{0,1},{1,2},{2,3},{3,0},{4,5},{5,6},{6,7},{7,4},{8,9},{9,10},{10,1... | collective-permute-start | bytes 1966088 | tf_op jit(solution)/shard_map/ppermute | solution.py:298
  123.0 27.9 %collective-permute-start.19 = (bf16[256,1280]{1,0:T(8,128)(2,1)S(1)}, bf16[256,1280]{1,0:T(8,128)(2,1)S(1)}, u32[]{:S(2)}, u32[]{:S(2)}) collective-permute-start(bf16[256,1280]{1,0:T(8,128)(2,1)S(1)} %add_convert_fusion), channel_id=1, source_target_pairs={{0,3},{1,0},{2,1},{3,2},{4,7},{5,4},{6,5},{7,6},{8,11},{9,8},{10,9... | collective-permute-start | bytes 1966088 | tf_op jit(solution)/shard_map/ppermute | solution.py:301
  152.5 27.4 %all-to-all-start.3 = ((bf16[32,16,1280]{2,1,0:T(8,128)(2,1)}), bf16[32,16,1280]{2,1,0:T(8,128)(2,1)S(1)}, u32[]{:S(2)}, u32[]{:S(2)}) async-start(bf16[32,16,1280]{2,1,0:T(8,128)(2,1)} %bitcast.15), calls=%async_computation.3 | async-start | bytes 2621440 | tf_op jit(solution)/shard_map/all_to_all | solution.py:334
  163.0 7.1 %collective-permute-start.10 = (bf16[128,512]{1,0:T(8,128)(2,1)S(1)}, bf16[128,512]{1,0:T(8,128)(2,1)S(1)}, u32[]{:S(2)}, u32[]{:S(2)}) collective-permute-start(bf16[128,512]{1,0:T(8,128)(2,1)S(1)} %get-tuple-element.57), channel_id=1, source_target_pairs={{0,1},{1,2},{2,3},{3,0},{4,5},{5,6},{6,7},{7,4},{8,9},{9,10},{10,1... | collective-permute-start | bytes 393224 | tf_op jit(solution)/shard_map/ppermute | solution.py:298
  164.7 5.4 %collective-permute-start.12 = (bf16[128,512]{1,0:T(8,128)(2,1)S(1)}, bf16[128,512]{1,0:T(8,128)(2,1)S(1)}, u32[]{:S(2)}, u32[]{:S(2)}) collective-permute-start(bf16[128,512]{1,0:T(8,128)(2,1)S(1)} %get-tuple-element.58), channel_id=1, source_target_pairs={{0,3},{1,0},{2,1},{3,2},{4,7},{5,4},{6,5},{7,6},{8,11},{9,8},{10,9... | collective-permute-start | bytes 393224 | tf_op jit(solution)/shard_map/ppermute | solution.py:301
  170.2 8.3 %collective-permute-start.11 = (bf16[256,512]{1,0:T(8,128)(2,1)S(1)}, bf16[256,512]{1,0:T(8,128)(2,1)S(1)}, u32[]{:S(2)}, u32[]{:S(2)}) collective-permute-start(bf16[256,512]{1,0:T(8,128)(2,1)S(1)} %get-tuple-element.55), channel_id=1, source_target_pairs={{0,1},{1,2},{2,3},{3,0},{4,5},{5,6},{6,7},{7,4},{8,9},{9,10},{10,1... | collective-permute-start | bytes 786440 | tf_op jit(solution)/shard_map/ppermute | solution.py:298
  170.8 7.7 %collective-permute-start.13 = (bf16[256,512]{1,0:T(8,128)(2,1)S(1)}, bf16[256,512]{1,0:T(8,128)(2,1)S(1)}, u32[]{:S(2)}, u32[]{:S(2)}) collective-permute-start(bf16[256,512]{1,0:T(8,128)(2,1)S(1)} %get-tuple-element.56), channel_id=1, source_target_pairs={{0,3},{1,0},{2,1},{3,2},{4,7},{5,4},{6,5},{7,6},{8,11},{9,8},{10,9... | collective-permute-start | bytes 786440 | tf_op jit(solution)/shard_map/ppermute | solution.py:301
